TPU v7x, 256 devices: a whole 4x4x8 slice. The times are simulated.
256 devices in a mesh: tok: 64 (over x, z, core), head: 4 (over y).
Axes of the slice: x: 4, y: 4, z: 8, core: 2. Of those that a mesh axis runs over, the one named last changes fastest.
Arguments:
- head_inputs: bfloat16 [32768, 2048], P('tok', 'head'), may hold values from -6 to 6
- state_keys: bfloat16 [32768, 128], P('tok'), may hold values from -2 to 2
- state_queries: bfloat16 [32768, 128], P('tok'), may hold values from -2 to 2
- log_decay: float32 [32768, 32], P('tok', 'head'), may hold values from -1.6 to 0, as said below
- level_weight: float32 [32768, 32, 18], P('tok', 'head'), may hold values from 0.2 to 2
- skip_scale: float32 [32], P('head'), may hold values from 0.5 to 2
- gate_input: bfloat16 [32768, 2048], P('tok', 'head'), may hold values from -500 to 500
- norm_gain: float32 [2048], P('head'), may hold values from 0.5 to 1.5
Outputs:
- mixer_out: bfloat16 [32768, 2048], P('tok', 'head')
Inputs may be any that keep to these rules, and one draw needn't show every extreme that they name: `log_decay`: every entry is negative.
All inputs are finite; a program needn't handle non-finite values.
Results may differ from a plain program's by a relative error of at most 0.0038.
Values sent between devices are 32-bit elements; how exact they have to be, the bound alone decides.
No kernel may reach another device: no remote copies, remote signals or barrier semaphores. Data moves between devices by JAX's collectives and lax.ppermute only.
A program may use at most 64 MiB of HBM per device.

v0:
```python
import jax
import jax.numpy as jnp
from jax import lax
from jax.sharding import PartitionSpec as P

epsilon = 1e-05


def partner_2(block, axis, distance):
    count = lax.axis_size(axis)
    route = []
    for low in range(count):
        high = low | 1 << distance
        if high != low and high < count:
            route += [(low, high), (high, low)]
    return lax.ppermute(block, axis, route)


def from_everyone(array, axis):
    copies = jnp.broadcast_to(array, (lax.axis_size(axis), *array.shape))
    return lax.all_to_all(copies, axis, split_axis=0, concat_axis=0, tiled=True)


def of_everyone(array, axis):
    everything = from_everyone(array, axis)
    return jnp.sum(everything, axis=0)


def block_levels(row_count, col_count, local_bits):
    query_pos = jnp.arange(row_count, dtype=jnp.int32)
    key_pos = jnp.arange(col_count, dtype=jnp.int32)
    crossing = jnp.bitwise_xor(query_pos[:, None], key_pos[None, :])
    level_map = jnp.zeros((row_count, col_count), jnp.int32)
    for shift_bit in range(local_bits):
        level_map = level_map + (crossing >= 1 << shift_bit).astype(jnp.int32)
    return (level_map, key_pos[None, :] <= query_pos[:, None])


def local_mix(queries, key_rows, values, decays, scales, local_bits):
    block_len = queries.shape[0]
    row_block = min(512, block_len)
    scores = jnp.dot(queries, key_rows.T, preferred_element_type=jnp.float32)
    level_map, causal = block_levels(row_block, row_block, local_bits)

    def local_one_head(inputs):
        decay_row, scale_row, value_row = inputs
        spread = jnp.where(
            causal, decay_row[0:row_block, None] - decay_row[None, :row_block], -jnp.inf
        )
        chosen = jnp.zeros((row_block, row_block), jnp.float32)
        for level_index in range(local_bits + 1):
            chosen = chosen + jnp.where(
                level_map == level_index, scale_row[0:row_block, level_index : level_index + 1], 0.0
            )
        weighted = (scores * jnp.exp(spread) * chosen).astype(jnp.bfloat16)
        return jnp.dot(weighted, value_row, preferred_element_type=jnp.float32)

    pieces_out = lax.map(local_one_head, (decays, scales, values))
    return pieces_out


def make_state(key_rows, values, decays):
    scaled = (
        key_rows.astype(jnp.float32)[None] * jnp.exp(decays[:, -1:] - decays)[:, :, None]
    ).astype(jnp.bfloat16)
    return jnp.einsum("htn,htp->hnp", scaled, values, preferred_element_type=jnp.float32)


def far_mix(queries, decays, scales, crossed, first_level):
    query_wide = queries.astype(jnp.float32)
    tree_bits = crossed.shape[1]

    def far_one_head(inputs):
        decay_row, scale_row, state_row = inputs
        stacked = state_row.transpose(1, 0, 2).reshape(state_row.shape[1], -1)
        readout = jnp.dot(query_wide, stacked, precision=lax.Precision.HIGHEST).reshape(
            query_wide.shape[0], tree_bits, -1
        )
        level_scale = scale_row[:, first_level : first_level + tree_bits]
        return jnp.exp(decay_row)[:, None] * jnp.sum(level_scale[:, :, None] * readout, axis=1)

    return lax.map(far_one_head, (decays, scales, crossed))


def head_mix(queries, key_rows, values, decays, scales, crossed, gates, skip_scale, local_bits):
    nearby = local_mix(queries, key_rows, values, decays, scales, local_bits)
    distant = far_mix(queries, decays, scales, crossed, local_bits + 1)
    mixed_out = nearby + distant + skip_scale[:, None, None] * values.astype(jnp.float32)
    head_count, block_len, head_size = mixed_out.shape
    mixed_out = mixed_out.transpose(1, 0, 2).reshape(block_len, head_count * head_size)
    return mixed_out * jax.nn.silu(gates.astype(jnp.float32))


def shards(
    head_inputs,
    state_keys,
    state_queries,
    log_decay,
    level_weight,
    skip_scale,
    gate_input,
    norm_gain,
):
    block_len = head_inputs.shape[0]
    head_count = log_decay.shape[1]
    head_size = head_inputs.shape[1] // head_count
    local_bits = block_len.bit_length() - 1
    tree_bits = lax.axis_size("tok").bit_length() - 1
    head_values = head_inputs.reshape(block_len, head_count, head_size).transpose(1, 0, 2)
    decay_sum = jnp.cumsum(log_decay, axis=0).T
    weights = level_weight.transpose(1, 0, 2)
    block_state = make_state(state_keys, head_values, decay_sum)
    block_total = decay_sum[:, -1]
    position = lax.axis_index("tok")
    aggregate = block_state
    extent = block_total
    leading = jnp.zeros_like(block_total)
    collected = []
    for level_bit in range(tree_bits):
        partner, partner_extent = partner_2((aggregate, extent), "tok", level_bit)
        upper_half = jnp.bitwise_and(jnp.right_shift(position, level_bit), 1) == 1
        collected.append(jnp.where(upper_half, partner * jnp.exp(leading)[:, None, None], 0.0))
        merged_upper = partner * jnp.exp(extent)[:, None, None] + aggregate
        merged_lower = aggregate * jnp.exp(partner_extent)[:, None, None] + partner
        aggregate = jnp.where(upper_half, merged_upper, merged_lower)
        leading = jnp.where(upper_half, leading + partner_extent, leading)
        extent = extent + partner_extent
    crossed = jnp.stack(collected, axis=0)
    crossed = crossed.transpose(1, 0, 2, 3)
    gated_out = head_mix(
        state_queries,
        state_keys,
        head_values,
        decay_sum,
        weights,
        crossed,
        gate_input,
        skip_scale,
        local_bits,
    )
    squares = of_everyone(jnp.sum(gated_out * gated_out, axis=1), "head")
    norm_width = head_count * head_size * lax.axis_size("head")
    scaling = lax.rsqrt(squares / norm_width + epsilon)
    return (gated_out * scaling[:, None] * norm_gain[None, :]).astype(jnp.bfloat16)


def solution(mesh):
    return jax.shard_map(
        shards,
        mesh=mesh,
        in_specs=(
            P("tok", "head"),
            P("tok", None),
            P("tok", None),
            P("tok", "head"),
            P("tok", "head", None),
            P("head"),
            P("tok", "head"),
            P("head"),
        ),
        out_specs=P("tok", "head"),
        check_vma=False,
    )
```

profile of v0, /device:TPU:32, one launch (start us, length us, event | category | flops | bytes accessed | tf_op | source)
XLA Modules:
  0.0 117.9 jit_solution(9075145442034801537)
XLA Ops:
  0.0 2.2 %reduce-window.6 = f32[8,4,128]{2,0,1:T(8,128)S(1)} reduce-window(f32[8,4,128]{2,0,1:T(8,128)} %bitcast.134, f32[]{:T(128)} %constant.20.clone.1), window={size=1x1x128 pad=0_0x0_0x127_0}, to_apply=%region_0.0 | reduce-window | flops 520192 | bytes 32772 | tf_op jit(solution)/shard_map/reduce-window
  2.8 1.3 %copy.37 = bf16[512,512]{0,1:T(8,128)(2,1)S(1)} copy(bf16[512,512]{1,0:T(8,128)(2,1)} %param.12) | data formatting | bytes 1048576 | tf_op args[0]
  4.2 1.0 convert_element_type.219
  5.2 0.8 fusion.67
  6.5 1.9 %collective-permute-start.3 = (f32[8]{0:T(128)S(1)}, f32[8]{0:T(128)S(1)}, u32[]{:S(2)}, u32[]{:S(2)}) collective-permute-start(f32[8]{0:T(128)S(1)} %get-tuple-element.245), channel_id=1, source_target_pairs={{0,8},{8,0},{4,12},{12,4},{16,24},{24,16},{20,28},{28,20},{32,40},... | collective-permute-start | bytes 104 | tf_op jit(solution)/shard_map/ppermute | solution.py:16
  8.4 1.8 %collective-permute-done.3 = f32[8]{0:T(128)S(1)} collective-permute-done((f32[8]{0:T(128)S(1)}, f32[8]{0:T(128)S(1)}, u32[]{:S(2)}, u32[]{:S(2)}) %collective-permute-start.3) | collective-permute-done | bytes 64 | tf_op jit(solution)/shard_map/ppermute | solution.py:16
  10.8 3.3 %collective-permute-start.5 = (f32[8]{0:T(128)S(1)}, f32[8]{0:T(128)S(1)}, u32[]{:S(2)}, u32[]{:S(2)}) collective-permute-start(f32[8]{0:T(128)S(1)} %get-tuple-element.243), channel_id=1, source_target_pairs={{0,16},{16,0},{4,20},{20,4},{8,24},{24,8},{12,28},{28,12},{32,48},... | collective-permute-start | bytes 104 | tf_op jit(solution)/shard_map/ppermute | solution.py:16
  14.1 1.5 %collective-permute-done.5 = f32[8]{0:T(128)S(1)} collective-permute-done((f32[8]{0:T(128)S(1)}, f32[8]{0:T(128)S(1)}, u32[]{:S(2)}, u32[]{:S(2)}) %collective-permute-start.5) | collective-permute-done | bytes 64 | tf_op jit(solution)/shard_map/ppermute | solution.py:16
  16.2 5.9 %collective-permute-start.7 = (f32[8]{0:T(128)S(1)}, f32[8]{0:T(128)S(1)}, u32[]{:S(2)}, u32[]{:S(2)}) collective-permute-start(f32[8]{0:T(128)S(1)} %get-tuple-element.241), channel_id=1, source_target_pairs={{0,32},{32,0},{4,36},{36,4},{8,40},{40,8},{12,44},{44,12},{16,48},... | collective-permute-start | bytes 104 | tf_op jit(solution)/shard_map/ppermute | solution.py:16
  22.1 1.5 %collective-permute-done.7 = f32[8]{0:T(128)S(1)} collective-permute-done((f32[8]{0:T(128)S(1)}, f32[8]{0:T(128)S(1)}, u32[]{:S(2)}, u32[]{:S(2)}) %collective-permute-start.7) | collective-permute-done | bytes 64 | tf_op jit(solution)/shard_map/ppermute | solution.py:16
  24.3 1.5 %collective-permute-start.9 = (f32[8]{0:T(128)S(1)}, f32[8]{0:T(128)S(1)}, u32[]{:S(2)}, u32[]{:S(2)}) collective-permute-start(f32[8]{0:T(128)S(1)} %get-tuple-element.239), channel_id=1, source_target_pairs={{0,64},{64,0},{4,68},{68,4},{8,72},{72,8},{12,76},{76,12},{16,80},... | collective-permute-start | bytes 104 | tf_op jit(solution)/shard_map/ppermute | solution.py:16
  25.8 2.1 %collective-permute-done.9 = f32[8]{0:T(128)S(1)} collective-permute-done((f32[8]{0:T(128)S(1)}, f32[8]{0:T(128)S(1)}, u32[]{:S(2)}, u32[]{:S(2)}) %collective-permute-start.9) | collective-permute-done | bytes 64 | tf_op jit(solution)/shard_map/ppermute | solution.py:16
  28.6 1.5 %collective-permute-start.2 = (f32[8,128,64]{1,2,0:T(8,128)S(1)}, f32[8,128,64]{1,2,0:T(8,128)S(1)}, u32[]{:S(2)}, u32[]{:S(2)}) collective-permute-start(f32[8,128,64]{1,2,0:T(8,128)S(1)} %add_select_fusion.4), channel_id=1, source_target_pairs={{0,8},{8,0},{4,12},{12,4},{16,24},{24,16},{20,28},{28,20},{32,40},... | collective-permute-start | bytes 786440 | tf_op jit(solution)/shard_map/ppermute | solution.py:16
  30.6 5.3 %collective-permute-done.2 = f32[8,128,64]{1,2,0:T(8,128)S(1)} collective-permute-done((f32[8,128,64]{1,2,0:T(8,128)S(1)}, f32[8,128,64]{1,2,0:T(8,128)S(1)}, u32[]{:S(2)}, u32[]{:S(2)}) %collective-permute-start.2) | collective-permute-done | bytes 262176 | tf_op jit(solution)/shard_map/ppermute | solution.py:16
  35.9 0.8 add_select_fusion.3
  36.7 2.9 %collective-permute-start.4 = (f32[8,128,64]{1,2,0:T(8,128)}, f32[8,128,64]{1,2,0:T(8,128)}, u32[]{:S(2)}, u32[]{:S(2)}) collective-permute-start(f32[8,128,64]{1,2,0:T(8,128)} %add_select_fusion.3), channel_id=1, source_target_pairs={{0,16},{16,0},{4,20},{20,4},{8,24},{24,8},{12,28},{28,12},{32,48},... | collective-permute-start | bytes 786440 | tf_op jit(solution)/shard_map/ppermute | solution.py:16
  39.7 8.4 %while.23 = (s32[]{:T(128)}, f32[8,512,64]{1,2,0:T(8,128)S(1)}, f32[8,512]{1,0:T(8,128)S(1)}, f32[512,512]{1,0:T(8,128)S(1)}, f32[8,512,18]{1,2,0:T(8,128)S(1)}, /*index=5*/bf16[8,512,64]{1,2,0:T(8,128)(2,1)S(1)}, s32[]{:T(128)}) while((s32[]{:T(128)}, f32[8,512,64]{1,2,0:T(8,128)S(1)}, f32[8,512]{1,0:T(8,128)S(1)}, ...), condition=%wide.region_3.4_spmd.clone.clone, body=%wide.region_2.3_spmd.clone.clone.sunk | while | flops 49807360 | bytes 1389653 | solution.py:58
  39.8 1.0 fusion.98
  40.9 1.0 fusion.98
  41.9 1.0 fusion.98
  43.0 1.0 fusion.98
  44.0 1.0 fusion.98
  45.1 1.0 fusion.98
  46.1 1.0 fusion.98
  47.2 1.0 fusion.98
  48.2 0.9 convert_element_type.221
  49.1 1.3 %copy.40 = bf16[512,512]{0,1:T(8,128)(2,1)S(1)} copy(bf16[512,512]{1,0:T(8,128)(2,1)} %param.18) | data formatting | bytes 1048576 | tf_op args[6]
  50.4 1.1 add_select_fusion.2
  51.6 5.5 %collective-permute-start.6 = (f32[8,128,64]{1,2,0:T(8,128)S(1)}, f32[8,128,64]{1,2,0:T(8,128)S(1)}, u32[]{:S(2)}, u32[]{:S(2)}) collective-permute-start(f32[8,128,64]{1,2,0:T(8,128)S(1)} %add_select_fusion.2), channel_id=1, source_target_pairs={{0,32},{32,0},{4,36},{36,4},{8,40},{40,8},{12,44},{44,12},{16,48},... | collective-permute-start | bytes 786440 | tf_op jit(solution)/shard_map/ppermute | solution.py:16
  58.3 0.7 bitcast_dynamic-update-slice_fusion.5
  59.0 5.6 %collective-permute-done.6 = f32[8,128,64]{1,2,0:T(8,128)S(1)} collective-permute-done((f32[8,128,64]{1,2,0:T(8,128)S(1)}, f32[8,128,64]{1,2,0:T(8,128)S(1)}, u32[]{:S(2)}, u32[]{:S(2)}) %collective-permute-start.6) | collective-permute-done | bytes 262176 | tf_op jit(solution)/shard_map/ppermute | solution.py:16
  64.6 0.8 add_select_fusion.1
  65.4 1.6 %collective-permute-start.8 = (f32[8,128,64]{1,2,0:T(8,128)S(1)}, f32[8,128,64]{1,2,0:T(8,128)S(1)}, u32[]{:S(2)}, u32[]{:S(2)}) collective-permute-start(f32[8,128,64]{1,2,0:T(8,128)S(1)} %add_select_fusion.1), channel_id=1, source_target_pairs={{0,64},{64,0},{4,68},{68,4},{8,72},{72,8},{12,76},{76,12},{16,80},... | collective-permute-start | bytes 786440 | tf_op jit(solution)/shard_map/ppermute | solution.py:16
  67.0 0.8 bitcast_dynamic-update-slice_fusion.4
  67.8 1.7 %bitcast_dynamic-update-slice_fusion.3 = f32[6,8,128,64]{2,3,1,0:T(8,128)} fusion(f32[6,8,128,64]{2,3,1,0:T(8,128)} %bitcast_dynamic-update-slice_fusion.4, f32[8,128,64]{1,2,0:T(8,128)} %collective-permute-done.4, f32[8]{0:T(128)S(1)} %get-tuple-element.263, pred[]{:T(512)S(6)} %eq.50), kind=kLoop, calls=%fused_computation.90 | loop fusion | flops 131072 | bytes 524321
  69.6 5.0 %collective-permute-done.8 = f32[8,128,64]{1,2,0:T(8,128)S(1)} collective-permute-done((f32[8,128,64]{1,2,0:T(8,128)S(1)}, f32[8,128,64]{1,2,0:T(8,128)S(1)}, u32[]{:S(2)}, u32[]{:S(2)}) %collective-permute-start.8) | collective-permute-done | bytes 262176 | tf_op jit(solution)/shard_map/ppermute | solution.py:16
  74.7 2.1 %collective-permute-start.10 = (f32[8,128,64]{1,2,0:T(8,128)S(1)}, f32[8,128,64]{1,2,0:T(8,128)S(1)}, u32[]{:S(2)}, u32[]{:S(2)}) collective-permute-start(f32[8,128,64]{1,2,0:T(8,128)S(1)} %add_select_fusion), channel_id=1, source_target_pairs={{0,128},{128,0},{4,132},{132,4},{8,136},{136,8},{12,140},{140,12},... | collective-permute-start | bytes 786440 | tf_op jit(solution)/shard_map/ppermute | solution.py:16
  76.8 0.8 bitcast_dynamic-update-slice_fusion.2
  77.6 0.8 bitcast_dynamic-update-slice_fusion.1
  78.4 4.3 %collective-permute-done.10 = f32[8,128,64]{1,2,0:T(8,128)S(1)} collective-permute-done((f32[8,128,64]{1,2,0:T(8,128)S(1)}, f32[8,128,64]{1,2,0:T(8,128)S(1)}, u32[]{:S(2)}, u32[]{:S(2)}) %collective-permute-start.10) | collective-permute-done | bytes 262176 | tf_op jit(solution)/shard_map/ppermute | solution.py:16
  82.6 0.8 bitcast_dynamic-update-slice_fusion
  83.4 1.1 broadcast.111.clone.1
  84.5 20.4 %while.22 = (s32[]{:T(128)}, f32[8,512,64]{1,2,0:T(8,128)}, f32[8,512]{1,0:T(8,128)S(1)}, f32[8,512,18]{1,2,0:T(8,128)S(1)}, f32[8,6,128,64]{2,3,0,1:T(8,128)}, /*index=5*/f32[512,128]{1,0:T(8,128)S(1)}, s32[]{:T(128)}) while((s32[]{:T(128)}, f32[8,512,64]{1,2,0:T(8,128)}, f32[8,512]{1,0:T(8,128)S(1)}, f32[8,512,18]{1,2,0:T(8,128)S(1)}, ...), condition=%wide.region_6.7_spmd, body=%wide.region_4.6_spmd.sunk | while | flops 302383104 | bytes 2935385 | solution.py:82
  84.5 0.9 constant_dynamic-slice_fusion.4
  85.5 0.8 fusion.94
  87.1 0.9 constant_dynamic-slice_fusion.4
  88.0 0.8 fusion.94
  89.6 0.9 constant_dynamic-slice_fusion.4
  90.6 0.8 fusion.94
  92.2 0.9 constant_dynamic-slice_fusion.4
  93.1 0.8 fusion.94
  94.1 0.7 fusion.95
  94.7 0.9 constant_dynamic-slice_fusion.4
  95.7 0.8 fusion.94
  97.3 0.9 constant_dynamic-slice_fusion.4
  98.2 0.8 fusion.94
  99.8 0.9 constant_dynamic-slice_fusion.4
  100.8 0.8 fusion.94
  101.7 0.7 fusion.95
  102.4 0.9 constant_dynamic-slice_fusion.4
  103.4 0.8 fusion.94
  105.0 1.6 %multiply_add_fusion = f32[8,512,64]{1,2,0:T(8,128)S(1)} fusion(bf16[8,512,64]{1,2,0:T(8,128)(2,1)S(1)} %get-tuple-element.401, f32[8,512,64]{1,2,0:T(8,128)S(1)} %get-tuple-element.106, f32[8,512,64]{1,2,0:T(8,128)} %get-tuple-element.107, f32[8]{0:T(128)} %param.17), kind=kLoop, calls=%fused_computation.83 | loop fusion | flops 1048576 | bytes 3670048 | tf_op jit(solution)/shard_map/add | solution.py:88
  106.9 9.6 %all_to_all.6 = f32[4,1,512]{2,1,0:T(1,128)S(1)} all-to-all(f32[4,1,512]{2,1,0:T(1,128)S(1)} %broadcast_in_dim.136), channel_id=1, replica_groups=mesh['tok'=64,'head'=4] {'head'}, dimensions={0} | all-to-all | bytes 16384 | tf_op jit(solution)/shard_map/all_to_all | solution.py:21
  116.9 1.0 copy.42
  (108 shorter events, 11.7 us)
Async XLA Ops:
  2.7 3.9 %collective-permute-start.1 = (f32[8]{0:T(128)S(1)}, f32[8]{0:T(128)S(1)}, u32[]{:S(2)}, u32[]{:S(2)}) collective-permute-start(f32[8]{0:T(128)S(1)} %slice_reduce_fusion.1), channel_id=1, source_target_pairs={{0,4},{4,0},{8,12},{12,8},{16,20},{20,16},{24,28},{28,24},{32,36},... | collective-permute-start | bytes 104 | tf_op jit(solution)/shard_map/ppermute | solution.py:16
  2.8 27.3 %copy-start.2 = (f32[512,8,18]{0,1,2:T(8,128)S(1)}, f32[512,8,18]{0,1,2:T(8,128)}, u32[]{:S(2)}) copy-start(f32[512,8,18]{0,1,2:T(8,128)} %param.16) | copy-start | bytes 884740
  4.2 26.1 %copy-start = (bf16[512,128]{1,0:T(8,128)(2,1)S(1)}, bf16[512,128]{1,0:T(8,128)(2,1)}, u32[]{:S(2)}) copy-start(bf16[512,128]{1,0:T(8,128)(2,1)} %param.13) | copy-start | bytes 393220
  4.2 26.1 %copy-start.1 = (bf16[512,128]{1,0:T(8,128)(2,1)S(1)}, bf16[512,128]{1,0:T(8,128)(2,1)}, u32[]{:S(2)}) copy-start(bf16[512,128]{1,0:T(8,128)(2,1)} %param.14) | copy-start | bytes 393220
  5.9 22.5 %collective-permute-start = (f32[8,128,64]{1,2,0:T(8,128)S(1)}, f32[8,128,64]{1,2,0:T(8,128)S(1)}, u32[]{:S(2)}, u32[]{:S(2)}) collective-permute-start(f32[8,128,64]{1,2,0:T(8,128)S(1)} %fusion.67), channel_id=1, source_target_pairs={{0,4},{4,0},{8,12},{12,8},{16,20},{20,16},{24,28},{28,24},{32,36},... | collective-permute-start | bytes 786440 | tf_op jit(solution)/shard_map/ppermute | solution.py:16
  6.5 3.7 %collective-permute-start.3 = (f32[8]{0:T(128)S(1)}, f32[8]{0:T(128)S(1)}, u32[]{:S(2)}, u32[]{:S(2)}) collective-permute-start(f32[8]{0:T(128)S(1)} %get-tuple-element.245), channel_id=1, source_target_pairs={{0,8},{8,0},{4,12},{12,4},{16,24},{24,16},{20,28},{28,20},{32,40},... | collective-permute-start | bytes 104 | tf_op jit(solution)/shard_map/ppermute | solution.py:16
  10.8 4.8 %collective-permute-start.5 = (f32[8]{0:T(128)S(1)}, f32[8]{0:T(128)S(1)}, u32[]{:S(2)}, u32[]{:S(2)}) collective-permute-start(f32[8]{0:T(128)S(1)} %get-tuple-element.243), channel_id=1, source_target_pairs={{0,16},{16,0},{4,20},{20,4},{8,24},{24,8},{12,28},{28,12},{32,48},... | collective-permute-start | bytes 104 | tf_op jit(solution)/shard_map/ppermute | solution.py:16
  15.6 12.8 %copy-start.3 = (f32[8]{0:T(128)}, f32[8]{0:T(128)S(1)}, u32[]{:S(2)}) copy-start(f32[8]{0:T(128)S(1)} %collective-permute-done.5) | copy-start | bytes 100
  16.2 7.5 %collective-permute-start.7 = (f32[8]{0:T(128)S(1)}, f32[8]{0:T(128)S(1)}, u32[]{:S(2)}, u32[]{:S(2)}) collective-permute-start(f32[8]{0:T(128)S(1)} %get-tuple-element.241), channel_id=1, source_target_pairs={{0,32},{32,0},{4,36},{36,4},{8,40},{40,8},{12,44},{44,12},{16,48},... | collective-permute-start | bytes 104 | tf_op jit(solution)/shard_map/ppermute | solution.py:16
  24.3 3.6 %collective-permute-start.9 = (f32[8]{0:T(128)S(1)}, f32[8]{0:T(128)S(1)}, u32[]{:S(2)}, u32[]{:S(2)}) collective-permute-start(f32[8]{0:T(128)S(1)} %get-tuple-element.239), channel_id=1, source_target_pairs={{0,64},{64,0},{4,68},{68,4},{8,72},{72,8},{12,76},{76,12},{16,80},... | collective-permute-start | bytes 104 | tf_op jit(solution)/shard_map/ppermute | solution.py:16
  28.6 7.4 %collective-permute-start.2 = (f32[8,128,64]{1,2,0:T(8,128)S(1)}, f32[8,128,64]{1,2,0:T(8,128)S(1)}, u32[]{:S(2)}, u32[]{:S(2)}) collective-permute-start(f32[8,128,64]{1,2,0:T(8,128)S(1)} %add_select_fusion.4), channel_id=1, source_target_pairs={{0,8},{8,0},{4,12},{12,4},{16,24},{24,16},{20,28},{28,20},{32,40},... | collective-permute-start | bytes 786440 | tf_op jit(solution)/shard_map/ppermute | solution.py:16
  36.7 13.6 %collective-permute-start.4 = (f32[8,128,64]{1,2,0:T(8,128)}, f32[8,128,64]{1,2,0:T(8,128)}, u32[]{:S(2)}, u32[]{:S(2)}) collective-permute-start(f32[8,128,64]{1,2,0:T(8,128)} %add_select_fusion.3), channel_id=1, source_target_pairs={{0,16},{16,0},{4,20},{20,4},{8,24},{24,8},{12,28},{28,12},{32,48},... | collective-permute-start | bytes 786440 | tf_op jit(solution)/shard_map/ppermute | solution.py:16
  50.4 16.6 %copy-start.6 = (f32[8]{0:T(128)S(1)}, f32[8]{0:T(128)}, u32[]{:S(2)}) copy-start(f32[8]{0:T(128)} %get-tuple-element.259) | copy-start | bytes 100
  50.4 24.1 %copy-start.5 = (f32[8]{0:T(128)S(1)}, f32[8]{0:T(128)}, u32[]{:S(2)}) copy-start(f32[8]{0:T(128)} %get-tuple-element.256) | copy-start | bytes 100
  50.4 24.1 %copy-start.7 = (f32[8]{0:T(128)S(1)}, f32[8]{0:T(128)}, u32[]{:S(2)}) copy-start(f32[8]{0:T(128)} %get-tuple-element.238) | copy-start | bytes 100
  51.6 13.1 %collective-permute-start.6 = (f32[8,128,64]{1,2,0:T(8,128)S(1)}, f32[8,128,64]{1,2,0:T(8,128)S(1)}, u32[]{:S(2)}, u32[]{:S(2)}) collective-permute-start(f32[8,128,64]{1,2,0:T(8,128)S(1)} %add_select_fusion.2), channel_id=1, source_target_pairs={{0,32},{32,0},{4,36},{36,4},{8,40},{40,8},{12,44},{44,12},{16,48},... | collective-permute-start | bytes 786440 | tf_op jit(solution)/shard_map/ppermute | solution.py:16
  65.4 17.2 %copy-start.4 = (f32[8]{0:T(128)S(1)}, f32[8]{0:T(128)}, u32[]{:S(2)}) copy-start(f32[8]{0:T(128)} %get-tuple-element.235) | copy-start | bytes 100
  65.4 9.1 %collective-permute-start.8 = (f32[8,128,64]{1,2,0:T(8,128)S(1)}, f32[8,128,64]{1,2,0:T(8,128)S(1)}, u32[]{:S(2)}, u32[]{:S(2)}) collective-permute-start(f32[8,128,64]{1,2,0:T(8,128)S(1)} %add_select_fusion.1), channel_id=1, source_target_pairs={{0,64},{64,0},{4,68},{68,4},{8,72},{72,8},{12,76},{76,12},{16,80},... | collective-permute-start | bytes 786440 | tf_op jit(solution)/shard_map/ppermute | solution.py:16
  74.7 8.0 %collective-permute-start.10 = (f32[8,128,64]{1,2,0:T(8,128)S(1)}, f32[8,128,64]{1,2,0:T(8,128)S(1)}, u32[]{:S(2)}, u32[]{:S(2)}) collective-permute-start(f32[8,128,64]{1,2,0:T(8,128)S(1)} %add_select_fusion), channel_id=1, source_target_pairs={{0,128},{128,0},{4,132},{132,4},{8,136},{136,8},{12,140},{140,12},... | collective-permute-start | bytes 786440 | tf_op jit(solution)/shard_map/ppermute | solution.py:16
  106.5 10.0 %copy-start.8 = (f32[512]{0:T(512)S(1)}, f32[512]{0:T(512)}, u32[]{:S(2)}) copy-start(f32[512]{0:T(512)} %param.19) | copy-start | bytes 6148
where the time goes:
time: 119 us; the launch traced here: 118 us
  waiting for transfers between devices  27.1 us (23%)
  starting transfers between devices  26.8 us (23%)
  other arithmetic  24.3 us (20%)
  matrix products  15.1 us (13%)
  local copies, waits for them, and re-layouts  14.1 us (12%)
  blocking collectives  9.58 us (8%)
    ppermute x11, waiting for transfers between devices, partner_2(): return lax.ppermute(block, axis, route)  27.1 us
    ppermute x11, starting transfers between devices, partner_2(): return lax.ppermute(block, axis, route)  26.8 us
    all_to_all x1, blocking collectives, from_everyone(): return lax.all_to_all(copies, axis, split_axis=0, concat_axis=0, tiled=True)  9.58 us
    dot_general x8, matrix products, local_one_head(): return jnp.dot(weighted, value_row, preferred_element_type=jnp.float32)  7.76 us
    dynamic_slice x8, local copies, waits for them, and re-layouts, far_mix(): return lax.map(far_one_head, (decays, scales, crossed))  7.52 us
    dot_general x8, matrix products, far_one_head(): jnp.dot(query_wide, stacked, precision=lax.Precision.HIGHEST)  6.28 us
    dynamic_update_slice x8, other arithmetic, local_mix(): pieces_out = lax.map(local_one_head, (decays, scales, values))  5.38 us
    unnamed x5, other arithmetic  4.85 us
  transfers between devices with their start and end apart: 11, of which 8 were waited for; matrix products, arithmetic and copies ran while one was open for 19% of the time, Pallas kernels for 0%

commit v1 on v0

v1 whole, which is shorter than its diff:
```python
import functools

import jax
import jax.numpy as jnp
from jax import lax
from jax.experimental import pallas as pl
from jax.experimental.pallas import tpu as pltpu
from jax.sharding import PartitionSpec as P

epsilon = 1e-05
BLOCK = 512
HEADS = 8
WIDTH = 64
STATE = 128
CHUNKS = 2
CHUNK_HEADS = HEADS // 2 // CHUNKS
CHUNK_ROWS = CHUNK_HEADS * WIDTH
BUF_ROWS = CHUNK_ROWS + HEADS
LOCAL_BITS = 9
TREE_BITS = 6
F32 = jnp.float32
BF16 = jnp.bfloat16
VM = pl.BlockSpec(memory_space=pltpu.VMEM)
SM = pl.BlockSpec(memory_space=pltpu.SMEM)
MIB = 1024 * 1024


def call(body, outs, ins, name, flops, aliases=None, scratch=(), vmem=12):
    return pl.pallas_call(
        body,
        out_shape=outs,
        in_specs=ins,
        out_specs=jax.tree.map(lambda _: VM, outs),
        scratch_shapes=list(scratch),
        input_output_aliases=aliases or {},
        name=name,
        cost_estimate=pl.CostEstimate(flops=flops, bytes_accessed=MIB, transcendentals=0),
        compiler_params=pltpu.CompilerParams(vmem_limit_bytes=vmem * MIB),
    )


def sds(shape, dtype=F32):
    return jax.ShapeDtypeStruct(shape, dtype)


def core_index():
    return lax.axis_index("tok") & 1


def split3(x):
    hi = x.astype(BF16).astype(F32)
    rest = x - hi
    mid = rest.astype(BF16).astype(F32)
    return hi, mid, rest - mid


def prep_body(ld_ref, v_ref, k_ref, d_ref, dcol_ref, vt_ref, *rest):
    own_refs, send_refs, state_ref = rest[:CHUNKS], rest[CHUNKS : 2 * CHUNKS], rest[-1]
    core = core_index()
    ld = ld_ref[...]
    parts = jnp.concatenate([*split3(ld), jnp.zeros_like(ld)], axis=0).astype(BF16)
    row = lax.broadcasted_iota(jnp.int32, (BLOCK, BLOCK), 0)
    col = lax.broadcasted_iota(jnp.int32, (BLOCK, BLOCK), 1)
    upto = (row <= col).astype(F32).astype(BF16)
    sums = jnp.dot(parts, upto, preferred_element_type=F32)
    d = sums[0:8] + sums[8:16] + sums[16:24]
    d_ref[...] = d
    total = jnp.broadcast_to(d[:, BLOCK - 1 : BLOCK], (HEADS, BLOCK))
    toend = jnp.exp(total - d)
    vt = v_ref[...].T
    vt_ref[...] = vt
    scaled = [
        (vt[h * WIDTH : (h + 1) * WIDTH].astype(F32) * toend[h : h + 1]).astype(BF16)
        for h in range(HEADS)
    ]
    state_ref[...] = jnp.dot(
        jnp.concatenate(scaled, axis=0), k_ref[...], preferred_element_type=F32
    )
    for k in range(CHUNKS):
        mine = pl.multiple_of(core * (HEADS // 2 * WIDTH) + k * CHUNK_ROWS, CHUNK_ROWS)
        other = pl.multiple_of((1 - core) * (HEADS // 2 * WIDTH) + k * CHUNK_ROWS, CHUNK_ROWS)
        own_refs[k][0:CHUNK_ROWS] = state_ref[pl.ds(mine, CHUNK_ROWS), :]
        own_refs[k][CHUNK_ROWS:BUF_ROWS] = total[:, 0:STATE]
        send_refs[k][0:CHUNK_ROWS] = state_ref[pl.ds(other, CHUNK_ROWS), :]
        send_refs[k][CHUNK_ROWS:BUF_ROWS] = total[:, 0:STATE]
    dcol_ref[...] = d.T


def prep(ld, v, k):
    buf = sds((BUF_ROWS, STATE))
    outs = [sds((HEADS, BLOCK)), sds((BLOCK, HEADS)), sds((BLOCK, BLOCK), BF16)]
    outs += [buf] * (2 * CHUNKS)
    got = call(
        prep_body, outs, [VM] * 3, "prep", 10**9,
        scratch=[pltpu.VMEM((HEADS * WIDTH, STATE), F32)],
    )(ld, v, k)
    return got[0], got[1], got[2], got[3 : 3 + CHUNKS], got[3 + CHUNKS :]


def merge_body(level, chunk, own_ref, got_ref, out_ref, fac_ref):
    upper = ((lax.axis_index("tok") >> level) & 1) == 1
    own_ext = own_ref[CHUNK_ROWS:BUF_ROWS]
    got_ext = got_ref[CHUNK_ROWS:BUF_ROWS]
    one = jnp.ones_like(own_ext)
    fac_ref[0:HEADS] = jnp.where(upper, one, jnp.exp(got_ext))
    fac_ref[HEADS : 2 * HEADS] = jnp.where(upper, jnp.exp(own_ext), one)
    first = core_index() * (HEADS // 2) + chunk * CHUNK_HEADS
    for j in range(CHUNK_HEADS):
        rows = slice(j * WIDTH, (j + 1) * WIDTH)
        fa = fac_ref[pl.ds(first + j, 1), :]
        fb = fac_ref[pl.ds(first + (HEADS + j), 1), :]
        out_ref[rows] = own_ref[rows] * fa + got_ref[rows] * fb
    out_ref[CHUNK_ROWS:BUF_ROWS] = own_ext + got_ext


def merge(level, chunk, own, got):
    return call(
        functools.partial(merge_body, level, chunk), sds((BUF_ROWS, STATE)), [VM] * 2,
        "merge", 10**7, scratch=[pltpu.VMEM((2 * HEADS, STATE), F32)], vmem=4,
    )(own, got)


def aux_body(q_ref, gate_ref, qt_ref, gt_ref):
    qt = q_ref[...].T
    qt_ref[0:STATE] = qt
    qt_ref[STATE : 2 * STATE] = qt
    for j in range(4):
        cols = slice(j * 128, (j + 1) * 128)
        v = gate_ref[:, cols].T.astype(F32)
        gt_ref[cols] = v / (1.0 + jnp.exp(-v))


def aux(q, gate):
    return call(
        aux_body, [sds((2 * STATE, BLOCK), BF16), sds((BLOCK, BLOCK))], [VM] * 2, "aux", 10**9
    )(q, gate)


def near_body(first, k_ref, qt_ref, vt_ref, d_ref, dcol_ref, w_ref, skip_ref, out_ref, sc_ref, mix_ref):
    sc_ref[...] = jnp.dot(k_ref[...], qt_ref[0:STATE], preferred_element_type=F32)
    half = BLOCK // 2
    mix_ref[half:BLOCK, 0:half] = jnp.zeros((half, half), BF16)
    mix_ref[128:256, 0:128] = jnp.zeros((128, 128), BF16)
    mix_ref[384:512, 256:384] = jnp.zeros((128, 128), BF16)
    srow = lax.broadcasted_iota(jnp.int32, (128, 128), 0)
    tcol = lax.broadcasted_iota(jnp.int32, (128, 128), 1)
    cross = srow ^ tcol
    causal = srow <= tcol
    for n in range(2):
        h = first + n
        for i in range(4):
            rows = slice(i * 128, (i + 1) * 128)
            dcol = jnp.broadcast_to(dcol_ref[rows, h : h + 1], (128, 128))
            for j in range(i, 4):
                cols = slice(j * 128, (j + 1) * 128)
                spread = d_ref[h : h + 1, cols] - dcol
                if i == j:
                    spread = jnp.where(causal, spread, -jnp.inf)
                    chosen = jnp.broadcast_to(w_ref[0, h : h + 1, cols], (128, 128))
                    for level in range(1, 8):
                        chosen = jnp.where(
                            cross >= 1 << (level - 1), w_ref[level, h : h + 1, cols], chosen
                        )
                else:
                    chosen = w_ref[7 + (i ^ j).bit_length(), h : h + 1, cols]
                mix_ref[rows, cols] = (sc_ref[rows, cols] * jnp.exp(spread) * chosen).astype(BF16)
        mine = slice(h * WIDTH, (h + 1) * WIDTH)
        here = slice(n * WIDTH, (n + 1) * WIDTH)
        vt = vt_ref[mine]
        skip = vt.astype(F32) * skip_ref[h]
        out_ref[here, 0:half] = skip[:, 0:half] + jnp.dot(
            vt[:, 0:half], mix_ref[0:half, 0:half], preferred_element_type=F32
        )
        out_ref[here, half:BLOCK] = skip[:, half:BLOCK] + jnp.dot(
            vt, mix_ref[:, half:BLOCK], preferred_element_type=F32
        )


def near(first, k, qt, vt, d, dcol, w, skip):
    return call(
        functools.partial(near_body, first), sds((2 * WIDTH, BLOCK)), [VM] * 6 + [SM],
        f"near{first}", 10**9,
        scratch=[pltpu.VMEM((BLOCK, BLOCK), F32), pltpu.VMEM((BLOCK, BLOCK), BF16)],
    )(k, qt, vt, d, dcol, w, skip)


def readout(level, acc_rows, emit, qt_ref, d_ref, w_ref, lead_ref, buf_refs, coef_ref):
    upper = ((lax.axis_index("tok") >> level) & 1) == 1
    lead = lead_ref[...]
    gain = jnp.where(upper, jnp.exp(lead), 0.0)[:, 0:1]
    coef_ref[...] = w_ref[LOCAL_BITS + 1 + level] * jnp.exp(d_ref[...]) * gain
    core = core_index()
    for side in range(2):
        base = (core if side == 0 else 1 - core) * (HEADS // 2)
        for k in range(CHUNKS):
            states = buf_refs[side * CHUNKS + k][0:CHUNK_ROWS]
            hi = states.astype(BF16)
            lo = (states - hi.astype(F32)).astype(BF16)
            read = jnp.dot(
                jnp.concatenate([hi, lo], axis=1), qt_ref[...], preferred_element_type=F32
            )
            for j in range(CHUNK_HEADS):
                head = base + (k * CHUNK_HEADS + j)
                row = pl.multiple_of(head * WIDTH, WIDTH)
                term = read[j * WIDTH : (j + 1) * WIDTH] * coef_ref[pl.ds(head, 1), :]
                emit(row, acc_rows(row) + term)
    got = buf_refs[0][CHUNK_ROWS:BUF_ROWS]
    return lead + jnp.where(upper, got, 0.0)


def far_body(level, qt_ref, d_ref, w_ref, lead_ref, acc_ref, *rest):
    bufs, out_ref, next_ref, coef_ref = rest[: 2 * CHUNKS], rest[-3], rest[-2], rest[-1]

    def emit(row, value):
        out_ref[pl.ds(row, WIDTH), :] = value

    next_ref[...] = readout(
        level, lambda row: acc_ref[pl.ds(row, WIDTH), :], emit,
        qt_ref, d_ref, w_ref, lead_ref, bufs, coef_ref,
    )


def far(level, qt, d, w, lead, acc, bufs):
    return call(
        functools.partial(far_body, level), [sds((BLOCK, BLOCK)), sds((HEADS, STATE))],
        [VM] * (5 + 2 * CHUNKS), f"far{level}", 10**9, aliases={4: 0},
        scratch=[pltpu.VMEM((HEADS, BLOCK), F32)],
    )(qt, d, w, lead, acc, *bufs)


def close_body(level, qt_ref, d_ref, w_ref, lead_ref, acc_ref, gt_ref, *rest):
    bufs, out_ref, sq_ref, coef_ref = rest[: 2 * CHUNKS], rest[-3], rest[-2], rest[-1]
    sums = []

    def emit(row, value):
        gated = value * gt_ref[pl.ds(row, WIDTH), :]
        out_ref[pl.ds(row, WIDTH), :] = gated
        sums.append(jnp.sum(gated * gated, axis=0, keepdims=True))

    readout(
        level, lambda row: acc_ref[pl.ds(row, WIDTH), :], emit,
        qt_ref, d_ref, w_ref, lead_ref, bufs, coef_ref,
    )
    sq_ref[...] = sum(sums[1:], sums[0])


def close(level, qt, d, w, lead, acc, gt, bufs):
    return call(
        functools.partial(close_body, level), [sds((BLOCK, BLOCK)), sds((1, BLOCK))],
        [VM] * (6 + 2 * CHUNKS), "close", 10**9,
        scratch=[pltpu.VMEM((HEADS, BLOCK), F32)],
    )(qt, d, w, lead, acc, gt, *bufs)


def turn_body(g_ref, gain_ref, out_ref):
    for j in range(4):
        rows = slice(j * 128, (j + 1) * 128)
        out_ref[rows] = g_ref[:, rows].T * gain_ref[...]


def turn(g, gain):
    return call(turn_body, sds((BLOCK, BLOCK)), [VM] * 2, "turn", 10**8)(g, gain)


def finish_body(width, g_ref, a_ref, b_ref, c_ref, e_ref, out_ref):
    total = a_ref[...] + b_ref[...] + c_ref[...] + e_ref[...]
    scale = lax.rsqrt(total / width + epsilon)
    column = jnp.broadcast_to(scale, (8, BLOCK)).T[:, 0:1]
    out_ref[...] = (g_ref[...] * column).astype(BF16)


def finish(width, g, sums):
    return call(
        functools.partial(finish_body, width), sds((BLOCK, BLOCK), BF16), [VM] * 5, "finish", 10**8
    )(g, *sums)


def route_of(partner):
    return [(i, partner(i)) for i in range(1 << TREE_BITS)]


def partner_of(level):
    flip = (1, 2, 6, 14, 16, 48)[level]
    return route_of(lambda i: i ^ flip)


def shards(head_inputs, state_keys, state_queries, log_decay, level_weight, skip_scale, gate_input, norm_gain):
    w = level_weight.transpose(2, 1, 0)
    d, dcol, vt, own, send = prep(log_decay.T, head_inputs, state_keys)
    swap = lambda x: lax.ppermute(x, "tok", partner_of(0))
    got = [swap(x) for x in send]
    other = [swap(x) for x in own]
    qt, gt = aux(state_queries, gate_input)
    levels = [(got, other)]
    sums = [merge(0, k, own[k], got[k]) for k in range(CHUNKS)]
    for level in range(1, TREE_BITS):
        got = [lax.ppermute(x, "tok", partner_of(level)) for x in sums]
        if level + 1 < TREE_BITS:
            sums = [merge(level, k, sums[k], got[k]) for k in range(CHUNKS)]
        levels.append((got, [swap(x) for x in got]))
    acc = jnp.concatenate(
        [near(h, state_keys, qt, vt, d, dcol, w, skip_scale) for h in range(0, HEADS, 2)], axis=0
    )
    lead = jnp.zeros((HEADS, STATE), F32)
    for level in range(TREE_BITS - 1):
        acc, lead = far(level, qt, d, w, lead, acc, (*levels[level][0], *levels[level][1]))
    last = TREE_BITS - 1
    gated, squares = close(last, qt, d, w, lead, acc, gt, (*levels[last][0], *levels[last][1]))
    count = lax.axis_size("head")
    shares = [
        lax.ppermute(squares, "head", [(i, (i + s) % count) for i in range(count)])
        for s in range(1, count)
    ]
    turned = turn(gated, norm_gain[None])
    return finish(HEADS * WIDTH * count, turned, [squares, *shares])


def solution(mesh):
    return jax.shard_map(
        shards,
        mesh=mesh,
        in_specs=(
            P("tok", "head"),
            P("tok", None),
            P("tok", None),
            P("tok", "head"),
            P("tok", "head", None),
            P("head"),
            P("tok", "head"),
            P("head"),
        ),
        out_specs=P("tok", "head"),
        check_vma=False,
    )
```

time: 119 us -> 57 us (0.48)
  other arithmetic: 24.3 us -> 0.07 us
  waiting for transfers between devices: 27.1 us -> 12 us
  matrix products: 15.1 us -> 0 us
  local copies, waits for them, and re-layouts: 14.1 us -> 3.37 us
  Pallas kernels: 0 us -> 10.3 us
  blocking collectives: 9.58 us -> 0 us
  starting transfers between devices: 26.8 us -> 31 us
    ppermute x11 -> x27, waiting for transfers between devices: 27.1 us -> 12 us  [the longest x10 9.14 us: shards(): got = [lax.ppermute(x, 'tok', partner_of(level)) for x in sums]]
    dot_general x18 -> x0, matrix products: 15.1 us -> none  [the longest x8 7.76 us: local_one_head(): return jnp.dot(weighted, value_row, preferred_element_type=jnp.float32)]
    pallas_call x0 -> x24, Pallas kernels: none -> 10.3 us  [the longest x4 5.56 us: near(): call(functools.partial(near_body, first), sds((2 * WIDTH, BLOCK)), [VM] *...]
    all_to_all x1 -> x0, blocking collectives: 9.58 us -> none  [from_everyone(): return lax.all_to_all(copies, axis, split_axis=0, concat_axis=0, tiled=True)]
    dynamic_slice x16 -> x0, local copies, waits for them, and re-layouts: 7.61 us -> none  [the longest x8 7.52 us: far_mix(): return lax.map(far_one_head, (decays, scales, crossed))]
    dynamic_update_slice x8 -> x0, other arithmetic: 5.38 us -> none  [local_mix(): pieces_out = lax.map(local_one_head, (decays, scales, values))]
    unnamed x5 -> x0, other arithmetic: 4.85 us -> none
    ppermute x11 -> x27, starting transfers between devices: 26.8 us -> 31 us  [the longest x10 21.8 us: shards(): got = [lax.ppermute(x, 'tok', partner_of(level)) for x in sums]]
  transfers between devices with their start and end apart: 11 -> 27, of which waited for: 8 -> 8; matrix products, arithmetic and copies ran while one was open for 19% -> 0% of each run, Pallas kernels for 0% -> 14%
where the time goes in v1:
time: 57 us; the launch traced here: 56.8 us
  starting transfers between devices  31 us (54%)
  waiting for transfers between devices  12 us (21%)
  Pallas kernels  10.3 us (18%)
  local copies, waits for them, and re-layouts  3.37 us (6%)
    ppermute x10, starting transfers between devices, shards(): got = [lax.ppermute(x, 'tok', partner_of(level)) for x in sums]  21.8 us
    ppermute x10, waiting for transfers between devices, shards(): got = [lax.ppermute(x, 'tok', partner_of(level)) for x in sums]  9.14 us
    ppermute x3, starting transfers between devices, shards(): lax.ppermute(squares, 'head', [(i, (i + s) % count) for i in range(count)])  5.9 us
    pallas_call x4, Pallas kernels, near(): call(functools.partial(near_body, first), sds((2 * WIDTH, BLOCK)), [VM] *...  5.56 us
    unnamed x18, local copies, waits for them, and re-layouts  3.37 us
    ppermute x14, starting transfers between devices, shards(): swap = lambda x: lax.ppermute(x, 'tok', partner_of(0))  3.24 us
    ppermute x3, waiting for transfers between devices, shards(): lax.ppermute(squares, 'head', [(i, (i + s) % count) for i in range(count)])  1.88 us
    pallas_call x5, Pallas kernels, far(): call(functools.partial(far_body, level), [sds((BLOCK, BLOCK)), sds((HEADS...  1.67 us
  transfers between devices with their start and end apart: 27, of which 8 were waited for; matrix products, arithmetic and copies ran while one was open for 0% of the time, Pallas kernels for 14%

profile of v1, /device:TPU:32, one launch (start us, length us, event | category | flops | bytes accessed | tf_op | source)
XLA Modules:
  0.0 56.8 jit_solution(10260292663630986844)
XLA Ops:
  0.0 1.0 %copy-done.1 = bf16[512,512]{1,0:T(8,128)(2,1)S(1)} copy-done((bf16[512,512]{1,0:T(8,128)(2,1)S(1)}, bf16[512,512]{1,0:T(8,128)(2,1)}, u32[]{:S(2)}) %copy-start.1) | copy-done | bytes 524312
  1.0 0.9 %copy-done.5 = bf16[512,128]{1,0:T(8,128)(2,1)S(1)} copy-done((bf16[512,128]{1,0:T(8,128)(2,1)S(1)}, bf16[512,128]{1,0:T(8,128)(2,1)}, u32[]{:S(2)}) %copy-start.5) | copy-done | bytes 131096
  1.9 0.7 %copy-done.7 = f32[512,8]{0,1:T(8,128)S(1)} copy-done((f32[512,8]{0,1:T(8,128)S(1)}, f32[512,8]{0,1:T(8,128)}, u32[]{:S(2)}) %copy-start.7) | copy-done | bytes 16408
  2.7 0.6 %prep.1 = (f32[8,512]{1,0:T(8,128)S(1)}, f32[512,8]{1,0:T(8,128)S(1)}, bf16[512,512]{1,0:T(8,128)(2,1)S(1)}, f32[136,128]{1,0:T(8,128)S(1)}, f32[136,128]{1,0:T(...) custom-call(f32[8,512]{1,0:T(8,128)S(1)} %bitcast.14, bf16[512,512]{1,0:T(8,128)(2,1)S(1)} %copy-done.1, ...), custom_call_target="tpu_custom_call" | custom-call | flops 1000000000 | bytes 1048576 | tf_op jit(solution)/shard_map/prep/pallas_call | solution.py:93
  3.3 0.1 collective-permute-start
  3.4 0.5 collective-permute-start.1
  3.9 0.1 collective-permute-start.2
  4.0 0.4 collective-permute-start.3
  4.4 0.4 aux.1
  4.8 0.0 copy-start.8
  4.8 0.2 copy-done.3
  4.9 0.0 copy-done.6
  5.0 0.5 copy-done.8
  5.5 1.4 %near6.1 = f32[128,512]{1,0:T(8,128)S(1)} custom-call(bf16[512,128]{1,0:T(8,128)(2,1)S(1)} %copy-done.6, bf16[256,512]{1,0:T(8,128)(2,1)S(1)} %get-tuple-element.26.qt_ref, bf16[512,512]{1,0:T(8,128)(2,1)S(1)} %get-tuple-element.28.vt_ref, f32[8,512]{1,0:T(8,128)S(1)} %get-tuple-element.27.d_ref, f32[512,8]{1,0:T(8,128)S(1)} %get-tuple-element.29.dcol_ref, ...), custom_call_target="tpu_custom_call" | custom-call | flops 1000000000 | bytes 1048576 | tf_op jit(solution)/shard_map/near6/pallas_call | solution.py:180
  6.8 1.4 %near4.1 = f32[128,512]{1,0:T(8,128)S(1)} custom-call(bf16[512,128]{1,0:T(8,128)(2,1)S(1)} %copy-done.6, bf16[256,512]{1,0:T(8,128)(2,1)S(1)} %get-tuple-element.26.qt_ref, bf16[512,512]{1,0:T(8,128)(2,1)S(1)} %get-tuple-element.28.vt_ref, f32[8,512]{1,0:T(8,128)S(1)} %get-tuple-element.27.d_ref, f32[512,8]{1,0:T(8,128)S(1)} %get-tuple-element.29.dcol_ref, ...), custom_call_target="tpu_custom_call" | custom-call | flops 1000000000 | bytes 1048576 | tf_op jit(solution)/shard_map/near4/pallas_call | solution.py:180
  8.2 1.4 %near2.1 = f32[128,512]{1,0:T(8,128)S(1)} custom-call(bf16[512,128]{1,0:T(8,128)(2,1)S(1)} %copy-done.6, bf16[256,512]{1,0:T(8,128)(2,1)S(1)} %get-tuple-element.26.qt_ref, bf16[512,512]{1,0:T(8,128)(2,1)S(1)} %get-tuple-element.28.vt_ref, f32[8,512]{1,0:T(8,128)S(1)} %get-tuple-element.27.d_ref, f32[512,8]{1,0:T(8,128)S(1)} %get-tuple-element.29.dcol_ref, ...), custom_call_target="tpu_custom_call" | custom-call | flops 1000000000 | bytes 1048576 | tf_op jit(solution)/shard_map/near2/pallas_call | solution.py:180
  9.6 1.4 %near0.1 = f32[128,512]{1,0:T(8,128)S(1)} custom-call(bf16[512,128]{1,0:T(8,128)(2,1)S(1)} %copy-done.6, bf16[256,512]{1,0:T(8,128)(2,1)S(1)} %get-tuple-element.26.qt_ref, bf16[512,512]{1,0:T(8,128)(2,1)S(1)} %get-tuple-element.28.vt_ref, f32[8,512]{1,0:T(8,128)S(1)} %get-tuple-element.27.d_ref, f32[512,8]{1,0:T(8,128)S(1)} %get-tuple-element.29.dcol_ref, ...), custom_call_target="tpu_custom_call" | custom-call | flops 1000000000 | bytes 1048576 | tf_op jit(solution)/shard_map/near0/pallas_call | solution.py:180
  11.1 1.9 %collective-permute-start.4 = (f32[136,128]{1,0:T(8,128)S(1)}, f32[136,128]{1,0:T(8,128)S(1)}, u32[]{:S(2)}, u32[]{:S(2)}) collective-permute-start(f32[136,128]{1,0:T(8,128)S(1)} %merge.10.own_ref), channel_id=1, source_target_pairs={{0,8},{4,12},{8,0},{12,4},{16,24},{20,28},{24,16},{28,20},{32,40},... | collective-permute-start | bytes 208904 | tf_op jit(solution)/shard_map/ppermute | solution.py:297
  13.0 0.0 collective-permute-done.1.rest_1_.got_ref
  13.0 0.3 collective-permute-start.5
  13.3 0.1 pad_maximum_fusion.acc_ref
  13.4 2.1 %collective-permute-done.4.rest_0_.got_ref = f32[136,128]{1,0:T(8,128)S(1)} collective-permute-done((f32[136,128]{1,0:T(8,128)S(1)}, f32[136,128]{1,0:T(8,128)S(1)}, u32[]{:S(2)}, u32[]{:S(2)}) %collective-permute-start.4) | collective-permute-done | bytes 69664 | tf_op jit(solution)/shard_map/ppermute | solution.py:297
  15.5 2.1 %collective-permute-start.8 = (f32[136,128]{1,0:T(8,128)S(1)}, f32[136,128]{1,0:T(8,128)S(1)}, u32[]{:S(2)}, u32[]{:S(2)}) collective-permute-start(f32[136,128]{1,0:T(8,128)S(1)} %merge.12.own_ref), channel_id=1, source_target_pairs={{0,24},{4,28},{8,16},{12,20},{16,8},{20,12},{24,0},{28,4},{32,56},... | collective-permute-start | bytes 208904 | tf_op jit(solution)/shard_map/ppermute | solution.py:297
  17.6 1.9 %collective-permute-start.9 = (f32[136,128]{1,0:T(8,128)S(1)}, f32[136,128]{1,0:T(8,128)S(1)}, u32[]{:S(2)}, u32[]{:S(2)}) collective-permute-start(f32[136,128]{1,0:T(8,128)S(1)} %merge.13.own_ref), channel_id=1, source_target_pairs={{0,24},{4,28},{8,16},{12,20},{16,8},{20,12},{24,0},{28,4},{32,56},... | collective-permute-start | bytes 208904 | tf_op jit(solution)/shard_map/ppermute | solution.py:297
  19.5 0.5 collective-permute-start.7
  20.0 0.3 far0.1
  20.4 0.8 %collective-permute-done.8.rest_0_.got_ref = f32[136,128]{1,0:T(8,128)S(1)} collective-permute-done((f32[136,128]{1,0:T(8,128)S(1)}, f32[136,128]{1,0:T(8,128)S(1)}, u32[]{:S(2)}, u32[]{:S(2)}) %collective-permute-start.8) | collective-permute-done | bytes 69664 | tf_op jit(solution)/shard_map/ppermute | solution.py:297
  21.2 7.0 %collective-permute-start.12 = (f32[136,128]{1,0:T(8,128)S(1)}, f32[136,128]{1,0:T(8,128)S(1)}, u32[]{:S(2)}, u32[]{:S(2)}) collective-permute-start(f32[136,128]{1,0:T(8,128)S(1)} %merge.14.own_ref), channel_id=1, source_target_pairs={{0,56},{4,60},{8,48},{12,52},{16,40},{20,44},{24,32},{28,36},{32,2... | collective-permute-start | bytes 208904 | tf_op jit(solution)/shard_map/ppermute | solution.py:297
  28.2 0.0 collective-permute-done.9.rest_1_.got_ref
  28.2 0.7 %collective-permute-start.13 = (f32[136,128]{1,0:T(8,128)S(1)}, f32[136,128]{1,0:T(8,128)S(1)}, u32[]{:S(2)}, u32[]{:S(2)}) collective-permute-start(f32[136,128]{1,0:T(8,128)S(1)} %merge.15.own_ref), channel_id=1, source_target_pairs={{0,56},{4,60},{8,48},{12,52},{16,40},{20,44},{24,32},{28,36},{32,2... | collective-permute-start | bytes 208904 | tf_op jit(solution)/shard_map/ppermute | solution.py:297
  28.9 0.0 collective-permute-start.10
  28.9 0.0 collective-permute-done.6.rest_2_
  28.9 0.5 collective-permute-start.11
  29.4 0.0 collective-permute-done.7.rest_3_
  29.4 0.3 far1.1
  29.8 0.8 %collective-permute-done.12.rest_0_.got_ref = f32[136,128]{1,0:T(8,128)S(1)} collective-permute-done((f32[136,128]{1,0:T(8,128)S(1)}, f32[136,128]{1,0:T(8,128)S(1)}, u32[]{:S(2)}, u32[]{:S(2)}) %collective-permute-start.12) | collective-permute-done | bytes 69664 | tf_op jit(solution)/shard_map/ppermute | solution.py:297
  30.6 1.6 %collective-permute-start.16 = (f32[136,128]{1,0:T(8,128)S(1)}, f32[136,128]{1,0:T(8,128)S(1)}, u32[]{:S(2)}, u32[]{:S(2)}) collective-permute-start(f32[136,128]{1,0:T(8,128)S(1)} %merge.16.own_ref), channel_id=1, source_target_pairs={{0,64},{4,68},{8,72},{12,76},{16,80},{20,84},{24,88},{28,92},{32,9... | collective-permute-start | bytes 208904 | tf_op jit(solution)/shard_map/ppermute | solution.py:297
  32.1 3.4 %collective-permute-done.13.rest_1_.got_ref = f32[136,128]{1,0:T(8,128)S(1)} collective-permute-done((f32[136,128]{1,0:T(8,128)S(1)}, f32[136,128]{1,0:T(8,128)S(1)}, u32[]{:S(2)}, u32[]{:S(2)}) %collective-permute-start.13) | collective-permute-done | bytes 69664 | tf_op jit(solution)/shard_map/ppermute | solution.py:297
  35.6 1.6 %collective-permute-start.17 = (f32[136,128]{1,0:T(8,128)S(1)}, f32[136,128]{1,0:T(8,128)S(1)}, u32[]{:S(2)}, u32[]{:S(2)}) collective-permute-start(f32[136,128]{1,0:T(8,128)S(1)} %merge.17.own_ref), channel_id=1, source_target_pairs={{0,64},{4,68},{8,72},{12,76},{16,80},{20,84},{24,88},{28,92},{32,9... | collective-permute-start | bytes 208904 | tf_op jit(solution)/shard_map/ppermute | solution.py:297
  37.2 0.0 collective-permute-start.14
  37.2 0.0 collective-permute-done.10.rest_2_
  37.2 0.5 collective-permute-start.15
  37.7 0.0 collective-permute-done.11.rest_3_
  37.7 0.3 far2.1
  38.1 2.2 %collective-permute-start.20 = (f32[136,128]{1,0:T(8,128)S(1)}, f32[136,128]{1,0:T(8,128)S(1)}, u32[]{:S(2)}, u32[]{:S(2)}) collective-permute-start(f32[136,128]{1,0:T(8,128)S(1)} %merge.18), channel_id=1, source_target_pairs={{0,192},{4,196},{8,200},{12,204},{16,208},{20,212},{24,216},{28,22... | collective-permute-start | bytes 208904 | tf_op jit(solution)/shard_map/ppermute | solution.py:297
  40.3 2.6 %collective-permute-start.21 = (f32[136,128]{1,0:T(8,128)S(1)}, f32[136,128]{1,0:T(8,128)S(1)}, u32[]{:S(2)}, u32[]{:S(2)}) collective-permute-start(f32[136,128]{1,0:T(8,128)S(1)} %merge.19), channel_id=1, source_target_pairs={{0,192},{4,196},{8,200},{12,204},{16,208},{20,212},{24,216},{28,22... | collective-permute-start | bytes 208904 | tf_op jit(solution)/shard_map/ppermute | solution.py:297
  42.9 0.0 collective-permute-start.18
  42.9 0.0 collective-permute-done.14.rest_2_
  42.9 0.5 collective-permute-start.19
  43.4 0.0 collective-permute-done.15.rest_3_
  43.4 0.3 far3.1
  43.8 0.1 collective-permute-start.22
  43.9 2.1 %collective-permute-done.21.rest_1_ = f32[136,128]{1,0:T(8,128)S(1)} collective-permute-done((f32[136,128]{1,0:T(8,128)S(1)}, f32[136,128]{1,0:T(8,128)S(1)}, u32[]{:S(2)}, u32[]{:S(2)}) %collective-permute-start.21) | collective-permute-done | bytes 69664 | tf_op jit(solution)/shard_map/ppermute | solution.py:297
  45.9 0.3 far4.1
  46.3 0.9 %collective-permute-done.23.rest_3_ = f32[136,128]{1,0:T(8,128)S(1)} collective-permute-done((f32[136,128]{1,0:T(8,128)S(1)}, f32[136,128]{1,0:T(8,128)S(1)}, u32[]{:S(2)}, u32[]{:S(2)}) %collective-permute-start.23) | collective-permute-done | bytes 69664 | tf_op jit(solution)/shard_map/ppermute | solution.py:290
  47.2 0.4 close.1
  47.6 0.0 copy-start
  47.6 1.7 %collective-permute-start.24 = (f32[1,512]{1,0:T(1,128)S(1)}, f32[1,512]{1,0:T(1,128)S(1)}, u32[]{:S(2)}, u32[]{:S(2)}) collective-permute-start(f32[1,512]{1,0:T(1,128)S(1)} %get-tuple-element.46.a_ref), channel_id=1, source_target_pairs={{0,1},{1,2},{2,3},{3,0},{4,5},{5,6},{6,7},{7,4},{8,9},{9,10},{10,1... | collective-permute-start | bytes 6152 | tf_op jit(solution)/shard_map/ppermute | solution.py:311
  49.3 2.9 %collective-permute-start.25 = (f32[1,512]{1,0:T(1,128)S(1)}, f32[1,512]{1,0:T(1,128)S(1)}, u32[]{:S(2)}, u32[]{:S(2)}) collective-permute-start(f32[1,512]{1,0:T(1,128)S(1)} %get-tuple-element.46.a_ref), channel_id=1, source_target_pairs={{0,2},{1,3},{2,0},{3,1},{4,6},{5,7},{6,4},{7,5},{8,10},{9,11},{10,... | collective-permute-start | bytes 6152 | tf_op jit(solution)/shard_map/ppermute | solution.py:311
  52.2 1.3 %collective-permute-start.26 = (f32[1,512]{1,0:T(1,128)S(1)}, f32[1,512]{1,0:T(1,128)S(1)}, u32[]{:S(2)}, u32[]{:S(2)}) collective-permute-start(f32[1,512]{1,0:T(1,128)S(1)} %get-tuple-element.46.a_ref), channel_id=1, source_target_pairs={{0,3},{1,0},{2,1},{3,2},{4,7},{5,4},{6,5},{7,6},{8,11},{9,8},{10,9... | collective-permute-start | bytes 6152 | tf_op jit(solution)/shard_map/ppermute | solution.py:311
  53.5 0.3 turn.1.g_ref
  53.9 0.5 collective-permute-done.25.c_ref
  54.4 1.4 %collective-permute-done.26.e_ref = f32[1,512]{1,0:T(1,128)S(1)} collective-permute-done((f32[1,512]{1,0:T(1,128)S(1)}, f32[1,512]{1,0:T(1,128)S(1)}, u32[]{:S(2)}, u32[]{:S(2)}) %collective-permute-start.26) | collective-permute-done | bytes 2080 | tf_op jit(solution)/shard_map/ppermute | solution.py:311
  55.7 1.1 %finish.1 = bf16[512,512]{1,0:T(8,128)(2,1)} custom-call(f32[512,512]{1,0:T(8,128)S(1)} %turn.1.g_ref, f32[1,512]{1,0:T(1,128)S(1)} %get-tuple-element.46.a_ref, f32[1,512]{1,0:T(1,128)S(1)} %collective-permute-done.24.b_ref, f32[1,512]{1,0:T(1,128)S(1)} %collective-permute-done.25.c_ref, f32[1,512]{1,0:T(1,128)S(1)} %collective-permute-done.26.e_ref), custom_call_target="tpu_custom_call" | custom-call | flops 100000000 | bytes 1048576 | tf_op jit(solution)/shard_map/finish/pallas_call | solution.py:273
  (34 shorter events, 0.3 us)
Async XLA Ops:
  0.0 1.0 %copy-start.1 = (bf16[512,512]{1,0:T(8,128)(2,1)S(1)}, bf16[512,512]{1,0:T(8,128)(2,1)}, u32[]{:S(2)}) copy-start(bf16[512,512]{1,0:T(8,128)(2,1)} %v_ref.1) | copy-start | bytes 1572868
  1.0 0.9 %copy-start.5 = (bf16[512,128]{1,0:T(8,128)(2,1)S(1)}, bf16[512,128]{1,0:T(8,128)(2,1)}, u32[]{:S(2)}) copy-start(bf16[512,128]{1,0:T(8,128)(2,1)} %k_ref.9) | copy-start | bytes 393220
  1.9 0.7 %copy-start.7 = (f32[512,8]{0,1:T(8,128)S(1)}, f32[512,8]{0,1:T(8,128)}, u32[]{:S(2)}) copy-start(f32[512,8]{0,1:T(8,128)} %param.11) | copy-start | bytes 49156
  2.7 1.7 %copy-start.2 = (bf16[512,512]{1,0:T(8,128)(2,1)S(1)}, bf16[512,512]{1,0:T(8,128)(2,1)}, u32[]{:S(2)}) copy-start(bf16[512,512]{1,0:T(8,128)(2,1)} %gate_ref.1) | copy-start | bytes 1572868
  2.7 1.7 %copy-start.4 = (bf16[512,128]{1,0:T(8,128)(2,1)S(1)}, bf16[512,128]{1,0:T(8,128)(2,1)}, u32[]{:S(2)}) copy-start(bf16[512,128]{1,0:T(8,128)(2,1)} %q_ref.1) | copy-start | bytes 393220
  3.3 7.8 %collective-permute-start = (f32[136,128]{1,0:T(8,128)S(1)}, f32[136,128]{1,0:T(8,128)S(1)}, u32[]{:S(2)}, u32[]{:S(2)}) collective-permute-start(f32[136,128]{1,0:T(8,128)S(1)} %get-tuple-element.30), channel_id=1, source_target_pairs={{0,4},{4,0},{8,12},{12,8},{16,20},{20,16},{24,28},{28,24},{32,36},... | collective-permute-start | bytes 208904 | tf_op jit(solution)/shard_map/ppermute | solution.py:290
  3.4 9.6 %collective-permute-start.1 = (f32[136,128]{1,0:T(8,128)S(1)}, f32[136,128]{1,0:T(8,128)S(1)}, u32[]{:S(2)}, u32[]{:S(2)}) collective-permute-start(f32[136,128]{1,0:T(8,128)S(1)} %get-tuple-element.31), channel_id=1, source_target_pairs={{0,4},{4,0},{8,12},{12,8},{16,20},{20,16},{24,28},{28,24},{32,36},... | collective-permute-start | bytes 208904 | tf_op jit(solution)/shard_map/ppermute | solution.py:290
  3.9 15.7 %collective-permute-start.2 = (f32[136,128]{1,0:T(8,128)S(1)}, f32[136,128]{1,0:T(8,128)S(1)}, u32[]{:S(2)}, u32[]{:S(2)}) collective-permute-start(f32[136,128]{1,0:T(8,128)S(1)} %get-tuple-element.32.own_ref), channel_id=1, source_target_pairs={{0,4},{4,0},{8,12},{12,8},{16,20},{20,16},{24,28},{28,24},{32,36},... | collective-permute-start | bytes 208904 | tf_op jit(solution)/shard_map/ppermute | solution.py:290
  4.0 1.0 %copy-start.3 = (f32[512,8,18]{0,1,2:T(8,128)S(1)}, f32[512,8,18]{0,1,2:T(8,128)}, u32[]{:S(2)}) copy-start(f32[512,8,18]{0,1,2:T(8,128)} %param.12) | copy-start | bytes 884740
  4.0 1.0 %copy-start.6 = (bf16[512,128]{1,0:T(8,128)(2,1)S(1)}, bf16[512,128]{1,0:T(8,128)(2,1)}, u32[]{:S(2)}) copy-start(bf16[512,128]{1,0:T(8,128)(2,1)} %k_ref.9) | copy-start | bytes 393220
  4.0 16.1 %collective-permute-start.3 = (f32[136,128]{1,0:T(8,128)S(1)}, f32[136,128]{1,0:T(8,128)S(1)}, u32[]{:S(2)}, u32[]{:S(2)}) collective-permute-start(f32[136,128]{1,0:T(8,128)S(1)} %get-tuple-element.33.own_ref), channel_id=1, source_target_pairs={{0,4},{4,0},{8,12},{12,8},{16,20},{20,16},{24,28},{28,24},{32,36},... | collective-permute-start | bytes 208904 | tf_op jit(solution)/shard_map/ppermute | solution.py:290
  4.8 0.7 %copy-start.8 = (f32[8]{0:T(128)S(1)}, f32[8]{0:T(128)}, u32[]{:S(2)}) copy-start(f32[8]{0:T(128)} %skip_ref.7) | copy-start | bytes 100
  11.1 4.4 %collective-permute-start.4 = (f32[136,128]{1,0:T(8,128)S(1)}, f32[136,128]{1,0:T(8,128)S(1)}, u32[]{:S(2)}, u32[]{:S(2)}) collective-permute-start(f32[136,128]{1,0:T(8,128)S(1)} %merge.10.own_ref), channel_id=1, source_target_pairs={{0,8},{4,12},{8,0},{12,4},{16,24},{20,28},{24,16},{28,20},{32,40},... | collective-permute-start | bytes 208904 | tf_op jit(solution)/shard_map/ppermute | solution.py:297
  13.0 4.5 %collective-permute-start.5 = (f32[136,128]{1,0:T(8,128)S(1)}, f32[136,128]{1,0:T(8,128)S(1)}, u32[]{:S(2)}, u32[]{:S(2)}) collective-permute-start(f32[136,128]{1,0:T(8,128)S(1)} %merge.11.own_ref), channel_id=1, source_target_pairs={{0,8},{4,12},{8,0},{12,4},{16,24},{20,28},{24,16},{28,20},{32,40},... | collective-permute-start | bytes 208904 | tf_op jit(solution)/shard_map/ppermute | solution.py:297
  15.5 5.7 %collective-permute-start.8 = (f32[136,128]{1,0:T(8,128)S(1)}, f32[136,128]{1,0:T(8,128)S(1)}, u32[]{:S(2)}, u32[]{:S(2)}) collective-permute-start(f32[136,128]{1,0:T(8,128)S(1)} %merge.12.own_ref), channel_id=1, source_target_pairs={{0,24},{4,28},{8,16},{12,20},{16,8},{20,12},{24,0},{28,4},{32,56},... | collective-permute-start | bytes 208904 | tf_op jit(solution)/shard_map/ppermute | solution.py:297
  17.6 10.6 %collective-permute-start.9 = (f32[136,128]{1,0:T(8,128)S(1)}, f32[136,128]{1,0:T(8,128)S(1)}, u32[]{:S(2)}, u32[]{:S(2)}) collective-permute-start(f32[136,128]{1,0:T(8,128)S(1)} %merge.13.own_ref), channel_id=1, source_target_pairs={{0,24},{4,28},{8,16},{12,20},{16,8},{20,12},{24,0},{28,4},{32,56},... | collective-permute-start | bytes 208904 | tf_op jit(solution)/shard_map/ppermute | solution.py:297
  19.5 9.4 %collective-permute-start.6 = (f32[136,128]{1,0:T(8,128)S(1)}, f32[136,128]{1,0:T(8,128)S(1)}, u32[]{:S(2)}, u32[]{:S(2)}) collective-permute-start(f32[136,128]{1,0:T(8,128)S(1)} %collective-permute-done.4.rest_0_.got_ref), channel_id=1, source_target_pairs={{0,4},{4,0},{8,12},{12,8},{16,20},{20,16},{24,28},{28,24},{32,36},... | collective-permute-start | bytes 208904 | tf_op jit(solution)/shard_map/ppermute | solution.py:290
  19.5 9.9 %collective-permute-start.7 = (f32[136,128]{1,0:T(8,128)S(1)}, f32[136,128]{1,0:T(8,128)S(1)}, u32[]{:S(2)}, u32[]{:S(2)}) collective-permute-start(f32[136,128]{1,0:T(8,128)S(1)} %collective-permute-done.5.rest_1_.got_ref), channel_id=1, source_target_pairs={{0,4},{4,0},{8,12},{12,8},{16,20},{20,16},{24,28},{28,24},{32,36},... | collective-permute-start | bytes 208904 | tf_op jit(solution)/shard_map/ppermute | solution.py:290
  21.2 9.4 %collective-permute-start.12 = (f32[136,128]{1,0:T(8,128)S(1)}, f32[136,128]{1,0:T(8,128)S(1)}, u32[]{:S(2)}, u32[]{:S(2)}) collective-permute-start(f32[136,128]{1,0:T(8,128)S(1)} %merge.14.own_ref), channel_id=1, source_target_pairs={{0,56},{4,60},{8,48},{12,52},{16,40},{20,44},{24,32},{28,36},{32,2... | collective-permute-start | bytes 208904 | tf_op jit(solution)/shard_map/ppermute | solution.py:297
  28.2 7.4 %collective-permute-start.13 = (f32[136,128]{1,0:T(8,128)S(1)}, f32[136,128]{1,0:T(8,128)S(1)}, u32[]{:S(2)}, u32[]{:S(2)}) collective-permute-start(f32[136,128]{1,0:T(8,128)S(1)} %merge.15.own_ref), channel_id=1, source_target_pairs={{0,56},{4,60},{8,48},{12,52},{16,40},{20,44},{24,32},{28,36},{32,2... | collective-permute-start | bytes 208904 | tf_op jit(solution)/shard_map/ppermute | solution.py:297
  28.9 8.3 %collective-permute-start.10 = (f32[136,128]{1,0:T(8,128)S(1)}, f32[136,128]{1,0:T(8,128)S(1)}, u32[]{:S(2)}, u32[]{:S(2)}) collective-permute-start(f32[136,128]{1,0:T(8,128)S(1)} %collective-permute-done.8.rest_0_.got_ref), channel_id=1, source_target_pairs={{0,4},{4,0},{8,12},{12,8},{16,20},{20,16},{24,28},{28,24},{32,36},... | collective-permute-start | bytes 208904 | tf_op jit(solution)/shard_map/ppermute | solution.py:290
  28.9 8.8 %collective-permute-start.11 = (f32[136,128]{1,0:T(8,128)S(1)}, f32[136,128]{1,0:T(8,128)S(1)}, u32[]{:S(2)}, u32[]{:S(2)}) collective-permute-start(f32[136,128]{1,0:T(8,128)S(1)} %collective-permute-done.9.rest_1_.got_ref), channel_id=1, source_target_pairs={{0,4},{4,0},{8,12},{12,8},{16,20},{20,16},{24,28},{28,24},{32,36},... | collective-permute-start | bytes 208904 | tf_op jit(solution)/shard_map/ppermute | solution.py:290
  30.6 7.5 %collective-permute-start.16 = (f32[136,128]{1,0:T(8,128)S(1)}, f32[136,128]{1,0:T(8,128)S(1)}, u32[]{:S(2)}, u32[]{:S(2)}) collective-permute-start(f32[136,128]{1,0:T(8,128)S(1)} %merge.16.own_ref), channel_id=1, source_target_pairs={{0,64},{4,68},{8,72},{12,76},{16,80},{20,84},{24,88},{28,92},{32,9... | collective-permute-start | bytes 208904 | tf_op jit(solution)/shard_map/ppermute | solution.py:297
  35.6 4.7 %collective-permute-start.17 = (f32[136,128]{1,0:T(8,128)S(1)}, f32[136,128]{1,0:T(8,128)S(1)}, u32[]{:S(2)}, u32[]{:S(2)}) collective-permute-start(f32[136,128]{1,0:T(8,128)S(1)} %merge.17.own_ref), channel_id=1, source_target_pairs={{0,64},{4,68},{8,72},{12,76},{16,80},{20,84},{24,88},{28,92},{32,9... | collective-permute-start | bytes 208904 | tf_op jit(solution)/shard_map/ppermute | solution.py:297
  37.2 5.7 %collective-permute-start.14 = (f32[136,128]{1,0:T(8,128)S(1)}, f32[136,128]{1,0:T(8,128)S(1)}, u32[]{:S(2)}, u32[]{:S(2)}) collective-permute-start(f32[136,128]{1,0:T(8,128)S(1)} %collective-permute-done.12.rest_0_.got_ref), channel_id=1, source_target_pairs={{0,4},{4,0},{8,12},{12,8},{16,20},{20,16},{24,28},{28,24},{32,36},... | collective-permute-start | bytes 208904 | tf_op jit(solution)/shard_map/ppermute | solution.py:290
  37.2 6.2 %collective-permute-start.15 = (f32[136,128]{1,0:T(8,128)S(1)}, f32[136,128]{1,0:T(8,128)S(1)}, u32[]{:S(2)}, u32[]{:S(2)}) collective-permute-start(f32[136,128]{1,0:T(8,128)S(1)} %collective-permute-done.13.rest_1_.got_ref), channel_id=1, source_target_pairs={{0,4},{4,0},{8,12},{12,8},{16,20},{20,16},{24,28},{28,24},{32,36},... | collective-permute-start | bytes 208904 | tf_op jit(solution)/shard_map/ppermute | solution.py:290
  38.1 5.7 %collective-permute-start.20 = (f32[136,128]{1,0:T(8,128)S(1)}, f32[136,128]{1,0:T(8,128)S(1)}, u32[]{:S(2)}, u32[]{:S(2)}) collective-permute-start(f32[136,128]{1,0:T(8,128)S(1)} %merge.18), channel_id=1, source_target_pairs={{0,192},{4,196},{8,200},{12,204},{16,208},{20,212},{24,216},{28,22... | collective-permute-start | bytes 208904 | tf_op jit(solution)/shard_map/ppermute | solution.py:297
  40.3 5.6 %collective-permute-start.21 = (f32[136,128]{1,0:T(8,128)S(1)}, f32[136,128]{1,0:T(8,128)S(1)}, u32[]{:S(2)}, u32[]{:S(2)}) collective-permute-start(f32[136,128]{1,0:T(8,128)S(1)} %merge.19), channel_id=1, source_target_pairs={{0,192},{4,196},{8,200},{12,204},{16,208},{20,212},{24,216},{28,22... | collective-permute-start | bytes 208904 | tf_op jit(solution)/shard_map/ppermute | solution.py:297
  42.9 3.0 %collective-permute-start.18 = (f32[136,128]{1,0:T(8,128)S(1)}, f32[136,128]{1,0:T(8,128)S(1)}, u32[]{:S(2)}, u32[]{:S(2)}) collective-permute-start(f32[136,128]{1,0:T(8,128)S(1)} %collective-permute-done.16.rest_0_.got_ref), channel_id=1, source_target_pairs={{0,4},{4,0},{8,12},{12,8},{16,20},{20,16},{24,28},{28,24},{32,36},... | collective-permute-start | bytes 208904 | tf_op jit(solution)/shard_map/ppermute | solution.py:290
  42.9 3.0 %collective-permute-start.19 = (f32[136,128]{1,0:T(8,128)S(1)}, f32[136,128]{1,0:T(8,128)S(1)}, u32[]{:S(2)}, u32[]{:S(2)}) collective-permute-start(f32[136,128]{1,0:T(8,128)S(1)} %collective-permute-done.17.rest_1_.got_ref), channel_id=1, source_target_pairs={{0,4},{4,0},{8,12},{12,8},{16,20},{20,16},{24,28},{28,24},{32,36},... | collective-permute-start | bytes 208904 | tf_op jit(solution)/shard_map/ppermute | solution.py:290
  43.8 2.5 %collective-permute-start.22 = (f32[136,128]{1,0:T(8,128)S(1)}, f32[136,128]{1,0:T(8,128)S(1)}, u32[]{:S(2)}, u32[]{:S(2)}) collective-permute-start(f32[136,128]{1,0:T(8,128)S(1)} %collective-permute-done.20.rest_0_), channel_id=1, source_target_pairs={{0,4},{4,0},{8,12},{12,8},{16,20},{20,16},{24,28},{28,24},{32,36},... | collective-permute-start | bytes 208904 | tf_op jit(solution)/shard_map/ppermute | solution.py:290
  45.9 1.3 %collective-permute-start.23 = (f32[136,128]{1,0:T(8,128)S(1)}, f32[136,128]{1,0:T(8,128)S(1)}, u32[]{:S(2)}, u32[]{:S(2)}) collective-permute-start(f32[136,128]{1,0:T(8,128)S(1)} %collective-permute-done.21.rest_1_), channel_id=1, source_target_pairs={{0,4},{4,0},{8,12},{12,8},{16,20},{20,16},{24,28},{28,24},{32,36},... | collective-permute-start | bytes 208904 | tf_op jit(solution)/shard_map/ppermute | solution.py:290
  47.6 5.9 %copy-start = (f32[512]{0:T(512)S(1)}, f32[512]{0:T(512)}, u32[]{:S(2)}) copy-start(f32[512]{0:T(512)} %param.15) | copy-start | bytes 6148
  47.6 6.2 %collective-permute-start.24 = (f32[1,512]{1,0:T(1,128)S(1)}, f32[1,512]{1,0:T(1,128)S(1)}, u32[]{:S(2)}, u32[]{:S(2)}) collective-permute-start(f32[1,512]{1,0:T(1,128)S(1)} %get-tuple-element.46.a_ref), channel_id=1, source_target_pairs={{0,1},{1,2},{2,3},{3,0},{4,5},{5,6},{6,7},{7,4},{8,9},{9,10},{10,1... | collective-permute-start | bytes 6152 | tf_op jit(solution)/shard_map/ppermute | solution.py:311
  49.3 5.1 %collective-permute-start.25 = (f32[1,512]{1,0:T(1,128)S(1)}, f32[1,512]{1,0:T(1,128)S(1)}, u32[]{:S(2)}, u32[]{:S(2)}) collective-permute-start(f32[1,512]{1,0:T(1,128)S(1)} %get-tuple-element.46.a_ref), channel_id=1, source_target_pairs={{0,2},{1,3},{2,0},{3,1},{4,6},{5,7},{6,4},{7,5},{8,10},{9,11},{10,... | collective-permute-start | bytes 6152 | tf_op jit(solution)/shard_map/ppermute | solution.py:311
  52.2 3.6 %collective-permute-start.26 = (f32[1,512]{1,0:T(1,128)S(1)}, f32[1,512]{1,0:T(1,128)S(1)}, u32[]{:S(2)}, u32[]{:S(2)}) collective-permute-start(f32[1,512]{1,0:T(1,128)S(1)} %get-tuple-element.46.a_ref), channel_id=1, source_target_pairs={{0,3},{1,0},{2,1},{3,2},{4,7},{5,4},{6,5},{7,6},{8,11},{9,8},{10,9... | collective-permute-start | bytes 6152 | tf_op jit(solution)/shard_map/ppermute | solution.py:311

commit v2 on v1

--- a/solution.py
+++ b/solution.py
@@ -12,7 +12,7 @@
 HEADS = 8
 WIDTH = 64
 STATE = 128
-CHUNKS = 2
+CHUNKS = 1
 CHUNK_HEADS = HEADS // 2 // CHUNKS
 CHUNK_ROWS = CHUNK_HEADS * WIDTH
 BUF_ROWS = CHUNK_ROWS + HEADS
@@ -22,15 +22,16 @@
 BF16 = jnp.bfloat16
 VM = pl.BlockSpec(memory_space=pltpu.VMEM)
 SM = pl.BlockSpec(memory_space=pltpu.SMEM)
+HB = pl.BlockSpec(memory_space=pltpu.HBM)
 MIB = 1024 * 1024
 
 
-def call(body, outs, ins, name, flops, aliases=None, scratch=(), vmem=12):
+def call(body, outs, ins, name, flops, aliases=None, scratch=(), vmem=12, out_space=VM):
     return pl.pallas_call(
         body,
         out_shape=outs,
         in_specs=ins,
-        out_specs=jax.tree.map(lambda _: VM, outs),
+        out_specs=jax.tree.map(lambda _: out_space, outs),
         scratch_shapes=list(scratch),
         input_output_aliases=aliases or {},
         name=name,
@@ -54,9 +55,15 @@
     return hi, mid, rest - mid
 
 
-def prep_body(ld_ref, v_ref, k_ref, d_ref, dcol_ref, vt_ref, *rest):
-    own_refs, send_refs, state_ref = rest[:CHUNKS], rest[CHUNKS : 2 * CHUNKS], rest[-1]
+def prep_body(ld_hbm, v_hbm, k_hbm, d_ref, dcol_ref, vt_ref, *rest):
+    own_refs, send_refs = rest[:CHUNKS], rest[CHUNKS : 2 * CHUNKS]
+    state_ref, ld_ref, v_ref, k_ref, sems = rest[2 * CHUNKS :]
+    pairs = ((ld_hbm, ld_ref), (v_hbm, v_ref), (k_hbm, k_ref))
+    copies = [pltpu.make_async_copy(a, b, sems.at[i]) for i, (a, b) in enumerate(pairs)]
+    for copy in copies:
+        copy.start()
     core = core_index()
+    copies[0].wait()
     ld = ld_ref[...]
     parts = jnp.concatenate([*split3(ld), jnp.zeros_like(ld)], axis=0).astype(BF16)
     row = lax.broadcasted_iota(jnp.int32, (BLOCK, BLOCK), 0)
@@ -67,12 +74,14 @@
     d_ref[...] = d
     total = jnp.broadcast_to(d[:, BLOCK - 1 : BLOCK], (HEADS, BLOCK))
     toend = jnp.exp(total - d)
+    copies[1].wait()
     vt = v_ref[...].T
     vt_ref[...] = vt
     scaled = [
         (vt[h * WIDTH : (h + 1) * WIDTH].astype(F32) * toend[h : h + 1]).astype(BF16)
         for h in range(HEADS)
     ]
+    copies[2].wait()
     state_ref[...] = jnp.dot(
         jnp.concatenate(scaled, axis=0), k_ref[...], preferred_element_type=F32
     )
@@ -91,9 +100,15 @@
     outs = [sds((HEADS, BLOCK)), sds((BLOCK, HEADS)), sds((BLOCK, BLOCK), BF16)]
     outs += [buf] * (2 * CHUNKS)
     got = call(
-        prep_body, outs, [VM] * 3, "prep", 10**9,
-        scratch=[pltpu.VMEM((HEADS * WIDTH, STATE), F32)],
-    )(ld, v, k)
+        prep_body, outs, [HB] * 3, "prep", 10**9,
+        scratch=[
+            pltpu.VMEM((HEADS * WIDTH, STATE), F32),
+            pltpu.VMEM((HEADS, BLOCK), F32),
+            pltpu.VMEM((BLOCK, HEADS * WIDTH), BF16),
+            pltpu.VMEM((BLOCK, STATE), BF16),
+            pltpu.SemaphoreType.DMA((3,)),
+        ],
+    )(*(pltpu.with_memory_space_constraint(x, pltpu.HBM) for x in (ld, v, k)))
     return got[0], got[1], got[2], got[3 : 3 + CHUNKS], got[3 + CHUNKS :]
 
 
@@ -136,7 +151,7 @@
     )(q, gate)
 
 
-def near_body(first, k_ref, qt_ref, vt_ref, d_ref, dcol_ref, w_ref, skip_ref, out_ref, sc_ref, mix_ref):
+def near_body(first, k_ref, qt_ref, vt_ref, d_ref, dcol_ref, w_ref, skip_ref, token_ref, out_ref, sc_ref, mix_ref):
     sc_ref[...] = jnp.dot(k_ref[...], qt_ref[0:STATE], preferred_element_type=F32)
     half = BLOCK // 2
     mix_ref[half:BLOCK, 0:half] = jnp.zeros((half, half), BF16)
@@ -176,12 +191,12 @@
         )
 
 
-def near(first, k, qt, vt, d, dcol, w, skip):
-    return call(
-        functools.partial(near_body, first), sds((2 * WIDTH, BLOCK)), [VM] * 6 + [SM],
+def near(first, k, qt, vt, d, dcol, w, skip, token):
+    return call(
+        functools.partial(near_body, first), sds((2 * WIDTH, BLOCK)), [VM] * 6 + [SM, VM],
         f"near{first}", 10**9,
         scratch=[pltpu.VMEM((BLOCK, BLOCK), F32), pltpu.VMEM((BLOCK, BLOCK), BF16)],
-    )(k, qt, vt, d, dcol, w, skip)
+    )(k, qt, vt, d, dcol, w, skip, token)
 
 
 def readout(level, acc_rows, emit, qt_ref, d_ref, w_ref, lead_ref, buf_refs, coef_ref):
@@ -208,24 +223,29 @@
     return lead + jnp.where(upper, got, 0.0)
 
 
-def far_body(level, qt_ref, d_ref, w_ref, lead_ref, acc_ref, *rest):
-    bufs, out_ref, next_ref, coef_ref = rest[: 2 * CHUNKS], rest[-3], rest[-2], rest[-1]
+def far_body(level, qt_ref, d_ref, w_ref, lead_ref, *rest):
+    coef_ref, next_ref, out_ref = rest[-1], rest[-2], rest[-3]
+    bufs = rest[: 2 * CHUNKS]
 
     def emit(row, value):
         out_ref[pl.ds(row, WIDTH), :] = value
 
-    next_ref[...] = readout(
-        level, lambda row: acc_ref[pl.ds(row, WIDTH), :], emit,
-        qt_ref, d_ref, w_ref, lead_ref, bufs, coef_ref,
-    )
-
-
-def far(level, qt, d, w, lead, acc, bufs):
+    def start(row):
+        return rest[2 * CHUNKS][pl.ds(row, WIDTH), :] if level > 0 else 0.0
+
+    next_ref[...] = readout(level, start, emit, qt_ref, d_ref, w_ref, lead_ref, bufs, coef_ref)
+    if level > 0:
+        rows = slice((level - 1) * 2 * WIDTH, level * 2 * WIDTH)
+        out_ref[rows] = out_ref[rows] + rest[2 * CHUNKS + 1][...]
+
+
+def far(level, qt, d, w, lead, bufs, *more):
     return call(
         functools.partial(far_body, level), [sds((BLOCK, BLOCK)), sds((HEADS, STATE))],
-        [VM] * (5 + 2 * CHUNKS), f"far{level}", 10**9, aliases={4: 0},
+        [VM] * (4 + 2 * CHUNKS + len(more)), f"far{level}", 10**9,
+        aliases={4 + 2 * CHUNKS: 0} if more else None,
         scratch=[pltpu.VMEM((HEADS, BLOCK), F32)],
-    )(qt, d, w, lead, acc, *bufs)
+    )(qt, d, w, lead, *bufs, *more)
 
 
 def close_body(level, qt_ref, d_ref, w_ref, lead_ref, acc_ref, gt_ref, *rest):
@@ -262,16 +282,27 @@
     return call(turn_body, sds((BLOCK, BLOCK)), [VM] * 2, "turn", 10**8)(g, gain)
 
 
-def finish_body(width, g_ref, a_ref, b_ref, c_ref, e_ref, out_ref):
+def finish_body(width, g_ref, a_ref, b_ref, c_ref, e_ref, out_hbm, out_ref, sems):
     total = a_ref[...] + b_ref[...] + c_ref[...] + e_ref[...]
     scale = lax.rsqrt(total / width + epsilon)
-    column = jnp.broadcast_to(scale, (8, BLOCK)).T[:, 0:1]
-    out_ref[...] = (g_ref[...] * column).astype(BF16)
+    copies = []
+    for j in range(4):
+        rows = slice(j * 128, (j + 1) * 128)
+        column = jnp.broadcast_to(scale[:, rows], (128, 128)).T
+        for i in range(4):
+            cols = slice(i * 128, (i + 1) * 128)
+            out_ref[rows, cols] = (g_ref[rows, cols] * column).astype(BF16)
+        copies.append(pltpu.make_async_copy(out_ref.at[rows], out_hbm.at[rows], sems.at[j]))
+        copies[-1].start()
+    for copy in copies:
+        copy.wait()
 
 
 def finish(width, g, sums):
     return call(
-        functools.partial(finish_body, width), sds((BLOCK, BLOCK), BF16), [VM] * 5, "finish", 10**8
+        functools.partial(finish_body, width), sds((BLOCK, BLOCK), BF16), [VM] * 5, "finish",
+        10**8, out_space=HB,
+        scratch=[pltpu.VMEM((BLOCK, BLOCK), BF16), pltpu.SemaphoreType.DMA((4,))],
     )(g, *sums)
 
 
@@ -293,17 +324,21 @@
     qt, gt = aux(state_queries, gate_input)
     levels = [(got, other)]
     sums = [merge(0, k, own[k], got[k]) for k in range(CHUNKS)]
+    parts = []
     for level in range(1, TREE_BITS):
+        if level < 5:
+            parts.append(
+                near(2 * (level - 1), state_keys, qt, vt, d, dcol, w, skip_scale, sums[-1])
+            )
         got = [lax.ppermute(x, "tok", partner_of(level)) for x in sums]
         if level + 1 < TREE_BITS:
             sums = [merge(level, k, sums[k], got[k]) for k in range(CHUNKS)]
         levels.append((got, [swap(x) for x in got]))
-    acc = jnp.concatenate(
-        [near(h, state_keys, qt, vt, d, dcol, w, skip_scale) for h in range(0, HEADS, 2)], axis=0
-    )
     lead = jnp.zeros((HEADS, STATE), F32)
-    for level in range(TREE_BITS - 1):
-        acc, lead = far(level, qt, d, w, lead, acc, (*levels[level][0], *levels[level][1]))
+    acc, lead = far(0, qt, d, w, lead, (*levels[0][0], *levels[0][1]))
+    for level in range(1, TREE_BITS - 1):
+        bufs = (*levels[level][0], *levels[level][1])
+        acc, lead = far(level, qt, d, w, lead, bufs, acc, parts[level - 1])
     last = TREE_BITS - 1
     gated, squares = close(last, qt, d, w, lead, acc, gt, (*levels[last][0], *levels[last][1]))
     count = lax.axis_size("head")

time: 57 us -> 49.4 us (0.87)
  the two profiles are of different devices: /device:TPU:32 before, /device:TPU:6 now
where the time goes in v2:
time: 49.4 us; the launch traced here: 49.3 us
  starting transfers between devices  19.7 us (40%)
  waiting for transfers between devices  17.4 us (35%)
  Pallas kernels  11.1 us (22%)
  local copies, waits for them, and re-layouts  0.66 us (1%)
    ppermute x5, waiting for transfers between devices, shards(): got = [lax.ppermute(x, 'tok', partner_of(level)) for x in sums]  13.6 us
    ppermute x5, starting transfers between devices, shards(): got = [lax.ppermute(x, 'tok', partner_of(level)) for x in sums]  12.8 us
    ppermute x3, starting transfers between devices, shards(): lax.ppermute(squares, 'head', [(i, (i + s) % count) for i in range(count)])  5.9 us
    pallas_call x4, Pallas kernels, near(): call(functools.partial(near_body, first), sds((2 * WIDTH, BLOCK)), [VM] *...  5.49 us
    ppermute x7, waiting for transfers between devices, shards(): swap = lambda x: lax.ppermute(x, 'tok', partner_of(0))  1.95 us
    ppermute x3, waiting for transfers between devices, shards(): lax.ppermute(squares, 'head', [(i, (i + s) % count) for i in range(count)])  1.88 us
    pallas_call x5, Pallas kernels, far(): call(functools.partial(far_body, level), [sds((BLOCK, BLOCK)), sds((HEADS...  1.75 us
    pallas_call x1, Pallas kernels, prep(): call(prep_body, outs, [HB] * 3, 'prep', 10 ** 9, scratch=[pltpu.VMEM((HEA...  1.64 us
  transfers between devices with their start and end apart: 15, of which 9 were waited for; matrix products, arithmetic and copies ran while one was open for 0% of the time, Pallas kernels for 16%

profile of v2, /device:TPU:6, one launch (start us, length us, event | category | flops | bytes accessed | tf_op | source)
XLA Modules:
  0.0 49.3 jit_solution(11871996192052928376)
XLA Ops:
  0.0 1.6 %prep.1 = (f32[8,512]{1,0:T(8,128)S(1)}, f32[512,8]{1,0:T(8,128)S(1)}, bf16[512,512]{1,0:T(8,128)(2,1)S(1)}, f32[264,128]{1,0:T(8,128)S(1)}, f32[264,128]{1,0:T(8,128)S(1)}) custom-call(f32[8,512]{1,0:T(8,128)} %bitcast.14, bf16[512,512]{1,0:T(8,128)(2,1)} %v_hbm.1, bf16[512,128]{1,0:T(8,128)(2,1)} %k_ref.7), custom_call_target="tpu_custom_call" | custom-call | flops 1000000000 | bytes 1048576 | tf_op jit(solution)/shard_map/prep/pallas_call | solution.py:102
  1.6 0.0 copy-start.1
  1.7 0.1 collective-permute-start
  1.8 1.3 %collective-permute-done.rest_0_.got_ref = f32[264,128]{1,0:T(8,128)S(1)} collective-permute-done((f32[264,128]{1,0:T(8,128)S(1)}, f32[264,128]{1,0:T(8,128)S(1)}, u32[]{:S(2)}, u32[]{:S(2)}) %collective-permute-start) | collective-permute-done | bytes 135200 | tf_op jit(solution)/shard_map/ppermute | solution.py:321
  3.1 0.0 copy-start.3
  3.1 2.0 %collective-permute-start.2 = (f32[264,128]{1,0:T(8,128)S(1)}, f32[264,128]{1,0:T(8,128)S(1)}, u32[]{:S(2)}, u32[]{:S(2)}) collective-permute-start(f32[264,128]{1,0:T(8,128)S(1)} %merge.5.token_ref.own_ref), channel_id=1, source_target_pairs={{0,8},{4,12},{8,0},{12,4},{16,24},{20,28},{24,16},{28,20},{32,40},... | collective-permute-start | bytes 405512 | tf_op jit(solution)/shard_map/ppermute | solution.py:333
  5.2 0.0 collective-permute-start.1
  5.2 3.9 %collective-permute-done.2.rest_0_.got_ref = f32[264,128]{1,0:T(8,128)S(1)} collective-permute-done((f32[264,128]{1,0:T(8,128)S(1)}, f32[264,128]{1,0:T(8,128)S(1)}, u32[]{:S(2)}, u32[]{:S(2)}) %collective-permute-start.2) | collective-permute-done | bytes 135200 | tf_op jit(solution)/shard_map/ppermute | solution.py:333
  9.1 0.0 copy-start.2
  9.1 0.0 copy-start.4
  9.1 4.5 %collective-permute-start.4 = (f32[264,128]{1,0:T(8,128)S(1)}, f32[264,128]{1,0:T(8,128)S(1)}, u32[]{:S(2)}, u32[]{:S(2)}) collective-permute-start(f32[264,128]{1,0:T(8,128)S(1)} %merge.6.token_ref.own_ref), channel_id=1, source_target_pairs={{0,24},{4,28},{8,16},{12,20},{16,8},{20,12},{24,0},{28,4},{32,56},... | collective-permute-start | bytes 405512 | tf_op jit(solution)/shard_map/ppermute | solution.py:333
  13.6 0.0 copy-done.1
  13.6 0.0 copy-done.3
  13.7 0.4 aux.1
  14.0 0.0 copy-start.5
  14.0 0.0 copy-done.2
  14.0 0.0 copy-done.4
  14.1 0.6 %copy-done.5 = f32[8]{0:T(128)S(1)} copy-done((f32[8]{0:T(128)S(1)}, f32[8]{0:T(128)}, u32[]{:S(2)}) %copy-start.5) | copy-done | bytes 56
  14.7 1.4 %near0.1.rest_3_ = f32[128,512]{1,0:T(8,128)S(1)} custom-call(bf16[512,128]{1,0:T(8,128)(2,1)S(1)} %copy-done.4, bf16[256,512]{1,0:T(8,128)(2,1)S(1)} %get-tuple-element.24.qt_ref, bf16[512,512]{1,0:T(8,128)(2,1)S(1)} %get-tuple-element.30.vt_ref, f32[8,512]{1,0:T(8,128)S(1)} %get-tuple-element.25.d_ref, f32[512,8]{1,0:T(8,128)S(1)} %get-tuple-element.31.dcol_ref, ...), custom_call_target="tpu_custom_call" | custom-call | flops 1000000000 | bytes 1048576 | tf_op jit(solution)/shard_map/near0/pallas_call | solution.py:195
  16.1 0.7 %collective-permute-done.4.rest_0_.got_ref = f32[264,128]{1,0:T(8,128)S(1)} collective-permute-done((f32[264,128]{1,0:T(8,128)S(1)}, f32[264,128]{1,0:T(8,128)S(1)}, u32[]{:S(2)}, u32[]{:S(2)}) %collective-permute-start.4) | collective-permute-done | bytes 135200 | tf_op jit(solution)/shard_map/ppermute | solution.py:333
  16.8 5.0 %collective-permute-start.6 = (f32[264,128]{1,0:T(8,128)S(1)}, f32[264,128]{1,0:T(8,128)S(1)}, u32[]{:S(2)}, u32[]{:S(2)}) collective-permute-start(f32[264,128]{1,0:T(8,128)S(1)} %merge.7.token_ref.own_ref), channel_id=1, source_target_pairs={{0,56},{4,60},{8,48},{12,52},{16,40},{20,44},{24,32},{28,36},{32,2... | collective-permute-start | bytes 405512 | tf_op jit(solution)/shard_map/ppermute | solution.py:333
  21.8 0.0 collective-permute-done.1.rest_1_
  21.8 0.3 far0.1
  22.1 0.1 collective-permute-start.3
  22.2 1.4 %near2.1.rest_3_ = f32[128,512]{1,0:T(8,128)S(1)} custom-call(bf16[512,128]{1,0:T(8,128)(2,1)S(1)} %copy-done.4, bf16[256,512]{1,0:T(8,128)(2,1)S(1)} %get-tuple-element.24.qt_ref, bf16[512,512]{1,0:T(8,128)(2,1)S(1)} %get-tuple-element.30.vt_ref, f32[8,512]{1,0:T(8,128)S(1)} %get-tuple-element.25.d_ref, f32[512,8]{1,0:T(8,128)S(1)} %get-tuple-element.31.dcol_ref, ...), custom_call_target="tpu_custom_call" | custom-call | flops 1000000000 | bytes 1048576 | tf_op jit(solution)/shard_map/near2/pallas_call | solution.py:195
  23.6 3.2 %collective-permute-done.6.rest_0_.got_ref = f32[264,128]{1,0:T(8,128)S(1)} collective-permute-done((f32[264,128]{1,0:T(8,128)S(1)}, f32[264,128]{1,0:T(8,128)S(1)}, u32[]{:S(2)}, u32[]{:S(2)}) %collective-permute-start.6) | collective-permute-done | bytes 135200 | tf_op jit(solution)/shard_map/ppermute | solution.py:333
  26.8 0.9 %collective-permute-start.8 = (f32[264,128]{1,0:T(8,128)S(1)}, f32[264,128]{1,0:T(8,128)S(1)}, u32[]{:S(2)}, u32[]{:S(2)}) collective-permute-start(f32[264,128]{1,0:T(8,128)S(1)} %merge.8.token_ref.own_ref), channel_id=1, source_target_pairs={{0,64},{4,68},{8,72},{12,76},{16,80},{20,84},{24,88},{28,92},{32,9... | collective-permute-start | bytes 405512 | tf_op jit(solution)/shard_map/ppermute | solution.py:333
  27.7 1.4 %near4.1.rest_3_ = f32[128,512]{1,0:T(8,128)S(1)} custom-call(bf16[512,128]{1,0:T(8,128)(2,1)S(1)} %copy-done.4, bf16[256,512]{1,0:T(8,128)(2,1)S(1)} %get-tuple-element.24.qt_ref, bf16[512,512]{1,0:T(8,128)(2,1)S(1)} %get-tuple-element.30.vt_ref, f32[8,512]{1,0:T(8,128)S(1)} %get-tuple-element.25.d_ref, f32[512,8]{1,0:T(8,128)S(1)} %get-tuple-element.31.dcol_ref, ...), custom_call_target="tpu_custom_call" | custom-call | flops 1000000000 | bytes 1048576 | tf_op jit(solution)/shard_map/near4/pallas_call | solution.py:195
  29.1 0.1 collective-permute-start.5
  29.2 0.0 collective-permute-done.3.rest_1_
  29.2 0.4 far1.1
  29.6 0.6 %collective-permute-start.7 = (f32[264,128]{1,0:T(8,128)S(1)}, f32[264,128]{1,0:T(8,128)S(1)}, u32[]{:S(2)}, u32[]{:S(2)}) collective-permute-start(f32[264,128]{1,0:T(8,128)S(1)} %collective-permute-done.6.rest_0_.got_ref), channel_id=1, source_target_pairs={{0,4},{4,0},{8,12},{12,8},{16,20},{20,16},{24,28},{28,24},{32,36},... | collective-permute-start | bytes 405512 | tf_op jit(solution)/shard_map/ppermute | solution.py:321
  30.2 1.8 %collective-permute-done.8.rest_0_.got_ref = f32[264,128]{1,0:T(8,128)S(1)} collective-permute-done((f32[264,128]{1,0:T(8,128)S(1)}, f32[264,128]{1,0:T(8,128)S(1)}, u32[]{:S(2)}, u32[]{:S(2)}) %collective-permute-start.8) | collective-permute-done | bytes 135200 | tf_op jit(solution)/shard_map/ppermute | solution.py:333
  31.9 0.4 collective-permute-start.10
  32.3 1.4 %near6.1.rest_3_ = f32[128,512]{1,0:T(8,128)S(1)} custom-call(bf16[512,128]{1,0:T(8,128)(2,1)S(1)} %copy-done.4, bf16[256,512]{1,0:T(8,128)(2,1)S(1)} %get-tuple-element.24.qt_ref, bf16[512,512]{1,0:T(8,128)(2,1)S(1)} %get-tuple-element.30.vt_ref, f32[8,512]{1,0:T(8,128)S(1)} %get-tuple-element.25.d_ref, f32[512,8]{1,0:T(8,128)S(1)} %get-tuple-element.31.dcol_ref, ...), custom_call_target="tpu_custom_call" | custom-call | flops 1000000000 | bytes 1048576 | tf_op jit(solution)/shard_map/near6/pallas_call | solution.py:195
  33.7 0.1 collective-permute-start.9
  33.8 0.0 collective-permute-done.5.rest_1_
  33.8 0.4 far2.1
  34.2 4.1 %collective-permute-done.10.rest_0_ = f32[264,128]{1,0:T(8,128)S(1)} collective-permute-done((f32[264,128]{1,0:T(8,128)S(1)}, f32[264,128]{1,0:T(8,128)S(1)}, u32[]{:S(2)}, u32[]{:S(2)}) %collective-permute-start.10) | collective-permute-done | bytes 135200 | tf_op jit(solution)/shard_map/ppermute | solution.py:333
  38.3 0.0 collective-permute-start.11
  38.3 0.0 collective-permute-done.7.rest_1_
  38.3 0.4 far3.1
  38.6 0.0 collective-permute-done.9.rest_1_
  38.6 0.4 far4.1
  39.0 0.6 %collective-permute-done.11.rest_1_ = f32[264,128]{1,0:T(8,128)S(1)} collective-permute-done((f32[264,128]{1,0:T(8,128)S(1)}, f32[264,128]{1,0:T(8,128)S(1)}, u32[]{:S(2)}, u32[]{:S(2)}) %collective-permute-start.11) | collective-permute-done | bytes 135200 | tf_op jit(solution)/shard_map/ppermute | solution.py:321
  39.6 0.4 close.1
  40.0 0.0 copy-start
  40.0 1.7 %collective-permute-start.12 = (f32[1,512]{1,0:T(1,128)S(1)}, f32[1,512]{1,0:T(1,128)S(1)}, u32[]{:S(2)}, u32[]{:S(2)}) collective-permute-start(f32[1,512]{1,0:T(1,128)S(1)} %get-tuple-element.42.a_ref), channel_id=1, source_target_pairs={{0,1},{1,2},{2,3},{3,0},{4,5},{5,6},{6,7},{7,4},{8,9},{9,10},{10,1... | collective-permute-start | bytes 6152 | tf_op jit(solution)/shard_map/ppermute | solution.py:346
  41.7 2.9 %collective-permute-start.13 = (f32[1,512]{1,0:T(1,128)S(1)}, f32[1,512]{1,0:T(1,128)S(1)}, u32[]{:S(2)}, u32[]{:S(2)}) collective-permute-start(f32[1,512]{1,0:T(1,128)S(1)} %get-tuple-element.42.a_ref), channel_id=1, source_target_pairs={{0,2},{1,3},{2,0},{3,1},{4,6},{5,7},{6,4},{7,5},{8,10},{9,11},{10,... | collective-permute-start | bytes 6152 | tf_op jit(solution)/shard_map/ppermute | solution.py:346
  44.6 1.3 %collective-permute-start.14 = (f32[1,512]{1,0:T(1,128)S(1)}, f32[1,512]{1,0:T(1,128)S(1)}, u32[]{:S(2)}, u32[]{:S(2)}) collective-permute-start(f32[1,512]{1,0:T(1,128)S(1)} %get-tuple-element.42.a_ref), channel_id=1, source_target_pairs={{0,3},{1,0},{2,1},{3,2},{4,7},{5,4},{6,5},{7,6},{8,11},{9,8},{10,9... | collective-permute-start | bytes 6152 | tf_op jit(solution)/shard_map/ppermute | solution.py:346
  45.9 0.0 copy-done
  45.9 0.3 turn.1.g_ref
  46.3 0.0 collective-permute-done.12.b_ref
  46.3 0.5 collective-permute-done.13.c_ref
  46.8 1.4 %collective-permute-done.14.e_ref = f32[1,512]{1,0:T(1,128)S(1)} collective-permute-done((f32[1,512]{1,0:T(1,128)S(1)}, f32[1,512]{1,0:T(1,128)S(1)}, u32[]{:S(2)}, u32[]{:S(2)}) %collective-permute-start.14) | collective-permute-done | bytes 2080 | tf_op jit(solution)/shard_map/ppermute | solution.py:346
  48.2 0.9 %finish.1 = bf16[512,512]{1,0:T(8,128)(2,1)} custom-call(f32[512,512]{1,0:T(8,128)S(1)} %turn.1.g_ref, f32[1,512]{1,0:T(1,128)S(1)} %get-tuple-element.42.a_ref, f32[1,512]{1,0:T(1,128)S(1)} %collective-permute-done.12.b_ref, f32[1,512]{1,0:T(1,128)S(1)} %collective-permute-done.13.c_ref, f32[1,512]{1,0:T(1,128)S(1)} %collective-permute-done.14.e_ref), custom_call_target="tpu_custom_call" | custom-call | flops 100000000 | bytes 1048576 | tf_op jit(solution)/shard_map/finish/pallas_call | solution.py:302
  (6 shorter events, 0.2 us)
Async XLA Ops:
  1.6 12.0 %copy-start.1 = (bf16[512,512]{1,0:T(8,128)(2,1)S(1)}, bf16[512,512]{1,0:T(8,128)(2,1)}, u32[]{:S(2)}) copy-start(bf16[512,512]{1,0:T(8,128)(2,1)} %gate_ref.1) | copy-start | bytes 1572868
  1.7 1.4 %collective-permute-start = (f32[264,128]{1,0:T(8,128)S(1)}, f32[264,128]{1,0:T(8,128)S(1)}, u32[]{:S(2)}, u32[]{:S(2)}) collective-permute-start(f32[264,128]{1,0:T(8,128)S(1)} %get-tuple-element.26), channel_id=1, source_target_pairs={{0,4},{4,0},{8,12},{12,8},{16,20},{20,16},{24,28},{28,24},{32,36},... | collective-permute-start | bytes 405512 | tf_op jit(solution)/shard_map/ppermute | solution.py:321
  3.1 10.5 %copy-start.3 = (bf16[512,128]{1,0:T(8,128)(2,1)S(1)}, bf16[512,128]{1,0:T(8,128)(2,1)}, u32[]{:S(2)}) copy-start(bf16[512,128]{1,0:T(8,128)(2,1)} %q_ref.1) | copy-start | bytes 393220
  3.1 5.9 %collective-permute-start.2 = (f32[264,128]{1,0:T(8,128)S(1)}, f32[264,128]{1,0:T(8,128)S(1)}, u32[]{:S(2)}, u32[]{:S(2)}) collective-permute-start(f32[264,128]{1,0:T(8,128)S(1)} %merge.5.token_ref.own_ref), channel_id=1, source_target_pairs={{0,8},{4,12},{8,0},{12,4},{16,24},{20,28},{24,16},{28,20},{32,40},... | collective-permute-start | bytes 405512 | tf_op jit(solution)/shard_map/ppermute | solution.py:333
  5.2 16.7 %collective-permute-start.1 = (f32[264,128]{1,0:T(8,128)S(1)}, f32[264,128]{1,0:T(8,128)S(1)}, u32[]{:S(2)}, u32[]{:S(2)}) collective-permute-start(f32[264,128]{1,0:T(8,128)S(1)} %get-tuple-element.27.own_ref), channel_id=1, source_target_pairs={{0,4},{4,0},{8,12},{12,8},{16,20},{20,16},{24,28},{28,24},{32,36},... | collective-permute-start | bytes 405512 | tf_op jit(solution)/shard_map/ppermute | solution.py:321
  9.1 5.0 %copy-start.2 = (f32[512,8,18]{0,1,2:T(8,128)S(1)}, f32[512,8,18]{0,1,2:T(8,128)}, u32[]{:S(2)}) copy-start(f32[512,8,18]{0,1,2:T(8,128)} %param.12) | copy-start | bytes 884740
  9.1 5.0 %copy-start.4 = (bf16[512,128]{1,0:T(8,128)(2,1)S(1)}, bf16[512,128]{1,0:T(8,128)(2,1)}, u32[]{:S(2)}) copy-start(bf16[512,128]{1,0:T(8,128)(2,1)} %k_ref.7) | copy-start | bytes 393220
  9.1 7.7 %collective-permute-start.4 = (f32[264,128]{1,0:T(8,128)S(1)}, f32[264,128]{1,0:T(8,128)S(1)}, u32[]{:S(2)}, u32[]{:S(2)}) collective-permute-start(f32[264,128]{1,0:T(8,128)S(1)} %merge.6.token_ref.own_ref), channel_id=1, source_target_pairs={{0,24},{4,28},{8,16},{12,20},{16,8},{20,12},{24,0},{28,4},{32,56},... | collective-permute-start | bytes 405512 | tf_op jit(solution)/shard_map/ppermute | solution.py:333
  14.0 0.7 %copy-start.5 = (f32[8]{0:T(128)S(1)}, f32[8]{0:T(128)}, u32[]{:S(2)}) copy-start(f32[8]{0:T(128)} %skip_ref.7) | copy-start | bytes 100
  16.8 9.9 %collective-permute-start.6 = (f32[264,128]{1,0:T(8,128)S(1)}, f32[264,128]{1,0:T(8,128)S(1)}, u32[]{:S(2)}, u32[]{:S(2)}) collective-permute-start(f32[264,128]{1,0:T(8,128)S(1)} %merge.7.token_ref.own_ref), channel_id=1, source_target_pairs={{0,56},{4,60},{8,48},{12,52},{16,40},{20,44},{24,32},{28,36},{32,2... | collective-permute-start | bytes 405512 | tf_op jit(solution)/shard_map/ppermute | solution.py:333
  22.1 7.1 %collective-permute-start.3 = (f32[264,128]{1,0:T(8,128)S(1)}, f32[264,128]{1,0:T(8,128)S(1)}, u32[]{:S(2)}, u32[]{:S(2)}) collective-permute-start(f32[264,128]{1,0:T(8,128)S(1)} %collective-permute-done.2.rest_0_.got_ref), channel_id=1, source_target_pairs={{0,4},{4,0},{8,12},{12,8},{16,20},{20,16},{24,28},{28,24},{32,36},... | collective-permute-start | bytes 405512 | tf_op jit(solution)/shard_map/ppermute | solution.py:321
  26.8 5.1 %collective-permute-start.8 = (f32[264,128]{1,0:T(8,128)S(1)}, f32[264,128]{1,0:T(8,128)S(1)}, u32[]{:S(2)}, u32[]{:S(2)}) collective-permute-start(f32[264,128]{1,0:T(8,128)S(1)} %merge.8.token_ref.own_ref), channel_id=1, source_target_pairs={{0,64},{4,68},{8,72},{12,76},{16,80},{20,84},{24,88},{28,92},{32,9... | collective-permute-start | bytes 405512 | tf_op jit(solution)/shard_map/ppermute | solution.py:333
  29.1 4.7 %collective-permute-start.5 = (f32[264,128]{1,0:T(8,128)S(1)}, f32[264,128]{1,0:T(8,128)S(1)}, u32[]{:S(2)}, u32[]{:S(2)}) collective-permute-start(f32[264,128]{1,0:T(8,128)S(1)} %collective-permute-done.4.rest_0_.got_ref), channel_id=1, source_target_pairs={{0,4},{4,0},{8,12},{12,8},{16,20},{20,16},{24,28},{28,24},{32,36},... | collective-permute-start | bytes 405512 | tf_op jit(solution)/shard_map/ppermute | solution.py:321
  29.6 8.7 %collective-permute-start.7 = (f32[264,128]{1,0:T(8,128)S(1)}, f32[264,128]{1,0:T(8,128)S(1)}, u32[]{:S(2)}, u32[]{:S(2)}) collective-permute-start(f32[264,128]{1,0:T(8,128)S(1)} %collective-permute-done.6.rest_0_.got_ref), channel_id=1, source_target_pairs={{0,4},{4,0},{8,12},{12,8},{16,20},{20,16},{24,28},{28,24},{32,36},... | collective-permute-start | bytes 405512 | tf_op jit(solution)/shard_map/ppermute | solution.py:321
  31.9 6.3 %collective-permute-start.10 = (f32[264,128]{1,0:T(8,128)S(1)}, f32[264,128]{1,0:T(8,128)S(1)}, u32[]{:S(2)}, u32[]{:S(2)}) collective-permute-start(f32[264,128]{1,0:T(8,128)S(1)} %merge.9), channel_id=1, source_target_pairs={{0,192},{4,196},{8,200},{12,204},{16,208},{20,212},{24,216},{28,22... | collective-permute-start | bytes 405512 | tf_op jit(solution)/shard_map/ppermute | solution.py:333
  33.7 4.9 %collective-permute-start.9 = (f32[264,128]{1,0:T(8,128)S(1)}, f32[264,128]{1,0:T(8,128)S(1)}, u32[]{:S(2)}, u32[]{:S(2)}) collective-permute-start(f32[264,128]{1,0:T(8,128)S(1)} %collective-permute-done.8.rest_0_.got_ref), channel_id=1, source_target_pairs={{0,4},{4,0},{8,12},{12,8},{16,20},{20,16},{24,28},{28,24},{32,36},... | collective-permute-start | bytes 405512 | tf_op jit(solution)/shard_map/ppermute | solution.py:321
  38.3 1.4 %collective-permute-start.11 = (f32[264,128]{1,0:T(8,128)S(1)}, f32[264,128]{1,0:T(8,128)S(1)}, u32[]{:S(2)}, u32[]{:S(2)}) collective-permute-start(f32[264,128]{1,0:T(8,128)S(1)} %collective-permute-done.10.rest_0_), channel_id=1, source_target_pairs={{0,4},{4,0},{8,12},{12,8},{16,20},{20,16},{24,28},{28,24},{32,36},... | collective-permute-start | bytes 405512 | tf_op jit(solution)/shard_map/ppermute | solution.py:321
  40.0 5.9 %copy-start = (f32[512]{0:T(512)S(1)}, f32[512]{0:T(512)}, u32[]{:S(2)}) copy-start(f32[512]{0:T(512)} %param.15) | copy-start | bytes 6148
  40.0 6.3 %collective-permute-start.12 = (f32[1,512]{1,0:T(1,128)S(1)}, f32[1,512]{1,0:T(1,128)S(1)}, u32[]{:S(2)}, u32[]{:S(2)}) collective-permute-start(f32[1,512]{1,0:T(1,128)S(1)} %get-tuple-element.42.a_ref), channel_id=1, source_target_pairs={{0,1},{1,2},{2,3},{3,0},{4,5},{5,6},{6,7},{7,4},{8,9},{9,10},{10,1... | collective-permute-start | bytes 6152 | tf_op jit(solution)/shard_map/ppermute | solution.py:346
  41.7 5.1 %collective-permute-start.13 = (f32[1,512]{1,0:T(1,128)S(1)}, f32[1,512]{1,0:T(1,128)S(1)}, u32[]{:S(2)}, u32[]{:S(2)}) collective-permute-start(f32[1,512]{1,0:T(1,128)S(1)} %get-tuple-element.42.a_ref), channel_id=1, source_target_pairs={{0,2},{1,3},{2,0},{3,1},{4,6},{5,7},{6,4},{7,5},{8,10},{9,11},{10,... | collective-permute-start | bytes 6152 | tf_op jit(solution)/shard_map/ppermute | solution.py:346
  44.6 3.6 %collective-permute-start.14 = (f32[1,512]{1,0:T(1,128)S(1)}, f32[1,512]{1,0:T(1,128)S(1)}, u32[]{:S(2)}, u32[]{:S(2)}) collective-permute-start(f32[1,512]{1,0:T(1,128)S(1)} %get-tuple-element.42.a_ref), channel_id=1, source_target_pairs={{0,3},{1,0},{2,1},{3,2},{4,7},{5,4},{6,5},{7,6},{8,11},{9,8},{10,9... | collective-permute-start | bytes 6152 | tf_op jit(solution)/shard_map/ppermute | solution.py:346

commit v3 on v2

--- a/solution.py
+++ b/solution.py
@@ -7,15 +7,17 @@
 from jax.experimental.pallas import tpu as pltpu
 from jax.sharding import PartitionSpec as P
 
+
 epsilon = 1e-05
 BLOCK = 512
 HEADS = 8
 WIDTH = 64
 STATE = 128
-CHUNKS = 1
+CHUNKS = 2
 CHUNK_HEADS = HEADS // 2 // CHUNKS
 CHUNK_ROWS = CHUNK_HEADS * WIDTH
 BUF_ROWS = CHUNK_ROWS + HEADS
+HALF_ROWS = CHUNKS * CHUNK_ROWS
 LOCAL_BITS = 9
 TREE_BITS = 6
 F32 = jnp.float32
@@ -26,7 +28,7 @@
 MIB = 1024 * 1024
 
 
-def call(body, outs, ins, name, flops, aliases=None, scratch=(), vmem=12, out_space=VM):
+def call(body, outs, ins, flops, aliases=None, scratch=(), vmem=12, out_space=VM):
     return pl.pallas_call(
         body,
         out_shape=outs,
@@ -34,7 +36,6 @@
         out_specs=jax.tree.map(lambda _: out_space, outs),
         scratch_shapes=list(scratch),
         input_output_aliases=aliases or {},
-        name=name,
         cost_estimate=pl.CostEstimate(flops=flops, bytes_accessed=MIB, transcendentals=0),
         compiler_params=pltpu.CompilerParams(vmem_limit_bytes=vmem * MIB),
     )
@@ -57,7 +58,7 @@
 
 def prep_body(ld_hbm, v_hbm, k_hbm, d_ref, dcol_ref, vt_ref, *rest):
     own_refs, send_refs = rest[:CHUNKS], rest[CHUNKS : 2 * CHUNKS]
-    state_ref, ld_ref, v_ref, k_ref, sems = rest[2 * CHUNKS :]
+    pack_ref, state_ref, ld_ref, v_ref, k_ref, sems = rest[2 * CHUNKS :]
     pairs = ((ld_hbm, ld_ref), (v_hbm, v_ref), (k_hbm, k_ref))
     copies = [pltpu.make_async_copy(a, b, sems.at[i]) for i, (a, b) in enumerate(pairs)]
     for copy in copies:
@@ -92,15 +93,16 @@
         own_refs[k][CHUNK_ROWS:BUF_ROWS] = total[:, 0:STATE]
         send_refs[k][0:CHUNK_ROWS] = state_ref[pl.ds(other, CHUNK_ROWS), :]
         send_refs[k][CHUNK_ROWS:BUF_ROWS] = total[:, 0:STATE]
+    pack_ref[...] = state_ref[pl.ds(pl.multiple_of(core * HALF_ROWS, HALF_ROWS), HALF_ROWS), :]
     dcol_ref[...] = d.T
 
 
 def prep(ld, v, k):
     buf = sds((BUF_ROWS, STATE))
     outs = [sds((HEADS, BLOCK)), sds((BLOCK, HEADS)), sds((BLOCK, BLOCK), BF16)]
-    outs += [buf] * (2 * CHUNKS)
+    outs += [buf] * (2 * CHUNKS) + [sds((HALF_ROWS, STATE))]
     got = call(
-        prep_body, outs, [HB] * 3, "prep", 10**9,
+        prep_body, outs, [HB] * 3, 10**7,
         scratch=[
             pltpu.VMEM((HEADS * WIDTH, STATE), F32),
             pltpu.VMEM((HEADS, BLOCK), F32),
@@ -109,10 +111,11 @@
             pltpu.SemaphoreType.DMA((3,)),
         ],
     )(*(pltpu.with_memory_space_constraint(x, pltpu.HBM) for x in (ld, v, k)))
-    return got[0], got[1], got[2], got[3 : 3 + CHUNKS], got[3 + CHUNKS :]
-
-
-def merge_body(level, chunk, own_ref, got_ref, out_ref, fac_ref):
+    return got[0], got[1], got[2], got[3 : 3 + CHUNKS], got[3 + CHUNKS : -1], got[-1]
+
+
+def merge_body(level, chunk, own_ref, got_ref, *refs):
+    out_ref, fac_ref = refs[-2:]
     upper = ((lax.axis_index("tok") >> level) & 1) == 1
     own_ext = own_ref[CHUNK_ROWS:BUF_ROWS]
     got_ext = got_ref[CHUNK_ROWS:BUF_ROWS]
@@ -128,11 +131,29 @@
     out_ref[CHUNK_ROWS:BUF_ROWS] = own_ext + got_ext
 
 
-def merge(level, chunk, own, got):
-    return call(
-        functools.partial(merge_body, level, chunk), sds((BUF_ROWS, STATE)), [VM] * 2,
-        "merge", 10**7, scratch=[pltpu.VMEM((2 * HEADS, STATE), F32)], vmem=4,
-    )(own, got)
+def merge(level, chunk, own, got, tokens):
+    return call(
+        functools.partial(merge_body, level, chunk), sds((BUF_ROWS, STATE)),
+        [VM] * (2 + len(tokens)), 10**5,
+        scratch=[pltpu.VMEM((2 * HEADS, STATE), F32)], vmem=4,
+    )(own, got, *tokens)
+
+
+def merge_all(level, own, got, tokens):
+    out = []
+    for k in range(CHUNKS):
+        out.append(merge(level, k, own[k], got[k], tokens))
+        tokens = out[-1:]
+    return out
+
+
+def pack_body(*refs):
+    for k, ref in enumerate(refs[:CHUNKS]):
+        refs[-1][k * CHUNK_ROWS : (k + 1) * CHUNK_ROWS] = ref[0:CHUNK_ROWS]
+
+
+def pack(got, token):
+    return call(pack_body, sds((HALF_ROWS, STATE)), [VM] * (CHUNKS + 1), 10**5, vmem=4)(*got, token)
 
 
 def aux_body(q_ref, gate_ref, qt_ref, gt_ref):
@@ -147,7 +168,7 @@
 
 def aux(q, gate):
     return call(
-        aux_body, [sds((2 * STATE, BLOCK), BF16), sds((BLOCK, BLOCK))], [VM] * 2, "aux", 10**9
+        aux_body, [sds((2 * STATE, BLOCK), BF16), sds((BLOCK, BLOCK))], [VM] * 2, 10**7
     )(q, gate)
 
 
@@ -194,7 +215,7 @@
 def near(first, k, qt, vt, d, dcol, w, skip, token):
     return call(
         functools.partial(near_body, first), sds((2 * WIDTH, BLOCK)), [VM] * 6 + [SM, VM],
-        f"near{first}", 10**9,
+        10**7,
         scratch=[pltpu.VMEM((BLOCK, BLOCK), F32), pltpu.VMEM((BLOCK, BLOCK), BF16)],
     )(k, qt, vt, d, dcol, w, skip, token)
 
@@ -205,45 +226,46 @@
     gain = jnp.where(upper, jnp.exp(lead), 0.0)[:, 0:1]
     coef_ref[...] = w_ref[LOCAL_BITS + 1 + level] * jnp.exp(d_ref[...]) * gain
     core = core_index()
-    for side in range(2):
-        base = (core if side == 0 else 1 - core) * (HEADS // 2)
-        for k in range(CHUNKS):
-            states = buf_refs[side * CHUNKS + k][0:CHUNK_ROWS]
-            hi = states.astype(BF16)
-            lo = (states - hi.astype(F32)).astype(BF16)
-            read = jnp.dot(
-                jnp.concatenate([hi, lo], axis=1), qt_ref[...], preferred_element_type=F32
-            )
-            for j in range(CHUNK_HEADS):
-                head = base + (k * CHUNK_HEADS + j)
-                row = pl.multiple_of(head * WIDTH, WIDTH)
-                term = read[j * WIDTH : (j + 1) * WIDTH] * coef_ref[pl.ds(head, 1), :]
-                emit(row, acc_rows(row) + term)
+    places = [(core, k * CHUNK_HEADS, CHUNK_HEADS) for k in range(CHUNKS)]
+    if len(buf_refs) == 2 * CHUNKS:
+        places += [(1 - core, k * CHUNK_HEADS, CHUNK_HEADS) for k in range(CHUNKS)]
+    else:
+        places += [(1 - core, 0, HEADS // 2)]
+    for ref, (side, first, heads) in zip(buf_refs, places):
+        states = ref[0 : heads * WIDTH]
+        hi = states.astype(BF16)
+        lo = (states - hi.astype(F32)).astype(BF16)
+        read = jnp.dot(jnp.concatenate([hi, lo], axis=1), qt_ref[...], preferred_element_type=F32)
+        for j in range(heads):
+            head = side * (HEADS // 2) + (first + j)
+            row = pl.multiple_of(head * WIDTH, WIDTH)
+            term = read[j * WIDTH : (j + 1) * WIDTH] * coef_ref[pl.ds(head, 1), :]
+            emit(row, acc_rows(row) + term)
     got = buf_refs[0][CHUNK_ROWS:BUF_ROWS]
     return lead + jnp.where(upper, got, 0.0)
 
 
 def far_body(level, qt_ref, d_ref, w_ref, lead_ref, *rest):
     coef_ref, next_ref, out_ref = rest[-1], rest[-2], rest[-3]
-    bufs = rest[: 2 * CHUNKS]
+    bufs = rest[: CHUNKS + 1]
 
     def emit(row, value):
         out_ref[pl.ds(row, WIDTH), :] = value
 
     def start(row):
-        return rest[2 * CHUNKS][pl.ds(row, WIDTH), :] if level > 0 else 0.0
+        return rest[CHUNKS + 1][pl.ds(row, WIDTH), :] if level > 0 else 0.0
 
     next_ref[...] = readout(level, start, emit, qt_ref, d_ref, w_ref, lead_ref, bufs, coef_ref)
     if level > 0:
         rows = slice((level - 1) * 2 * WIDTH, level * 2 * WIDTH)
-        out_ref[rows] = out_ref[rows] + rest[2 * CHUNKS + 1][...]
+        out_ref[rows] = out_ref[rows] + rest[CHUNKS + 2][...]
 
 
 def far(level, qt, d, w, lead, bufs, *more):
     return call(
         functools.partial(far_body, level), [sds((BLOCK, BLOCK)), sds((HEADS, STATE))],
-        [VM] * (4 + 2 * CHUNKS + len(more)), f"far{level}", 10**9,
-        aliases={4 + 2 * CHUNKS: 0} if more else None,
+        [VM] * (5 + CHUNKS + len(more)), 10**7,
+        aliases={5 + CHUNKS: 0} if more else None,
         scratch=[pltpu.VMEM((HEADS, BLOCK), F32)],
     )(qt, d, w, lead, *bufs, *more)
 
@@ -267,7 +289,7 @@
 def close(level, qt, d, w, lead, acc, gt, bufs):
     return call(
         functools.partial(close_body, level), [sds((BLOCK, BLOCK)), sds((1, BLOCK))],
-        [VM] * (6 + 2 * CHUNKS), "close", 10**9,
+        [VM] * (6 + 2 * CHUNKS), 10**7,
         scratch=[pltpu.VMEM((HEADS, BLOCK), F32)],
     )(qt, d, w, lead, acc, gt, *bufs)
 
@@ -279,7 +301,7 @@
 
 
 def turn(g, gain):
-    return call(turn_body, sds((BLOCK, BLOCK)), [VM] * 2, "turn", 10**8)(g, gain)
+    return call(turn_body, sds((BLOCK, BLOCK)), [VM] * 2, 10**7)(g, gain)
 
 
 def finish_body(width, g_ref, a_ref, b_ref, c_ref, e_ref, out_hbm, out_ref, sems):
@@ -300,7 +322,7 @@
 
 def finish(width, g, sums):
     return call(
-        functools.partial(finish_body, width), sds((BLOCK, BLOCK), BF16), [VM] * 5, "finish",
+        functools.partial(finish_body, width), sds((BLOCK, BLOCK), BF16), [VM] * 5,
         10**8, out_space=HB,
         scratch=[pltpu.VMEM((BLOCK, BLOCK), BF16), pltpu.SemaphoreType.DMA((4,))],
     )(g, *sums)
@@ -315,32 +337,37 @@
     return route_of(lambda i: i ^ flip)
 
 
-def shards(head_inputs, state_keys, state_queries, log_decay, level_weight, skip_scale, gate_input, norm_gain):
+def work(head_inputs, state_keys, state_queries, log_decay, level_weight, skip_scale, gate_input, norm_gain):
     w = level_weight.transpose(2, 1, 0)
-    d, dcol, vt, own, send = prep(log_decay.T, head_inputs, state_keys)
+    d, dcol, vt, own, send, packed = prep(log_decay.T, head_inputs, state_keys)
     swap = lambda x: lax.ppermute(x, "tok", partner_of(0))
     got = [swap(x) for x in send]
-    other = [swap(x) for x in own]
     qt, gt = aux(state_queries, gate_input)
-    levels = [(got, other)]
-    sums = [merge(0, k, own[k], got[k]) for k in range(CHUNKS)]
+    sums = merge_all(0, own, got, [gt])
+    levels = [(*got, swap(packed))]
+    acc, lead = None, jnp.zeros((HEADS, STATE), F32)
     parts = []
     for level in range(1, TREE_BITS):
+        before = []
         if level < 5:
-            parts.append(
-                near(2 * (level - 1), state_keys, qt, vt, d, dcol, w, skip_scale, sums[-1])
-            )
-        got = [lax.ppermute(x, "tok", partner_of(level)) for x in sums]
+            first = 2 * (level - 1)
+            parts.append(near(first, state_keys, qt, vt, d, dcol, w, skip_scale, sums[-1]))
+            before.append(parts[-1])
+        if level > 1:
+            more = () if acc is None else (acc, parts[level - 3])
+            acc, lead = far(level - 2, qt, d, w, lead, levels[level - 2], *more)
+            before.append(acc)
+        got = []
+        for x in sums:
+            got.append(lax.ppermute(x, "tok", partner_of(level)))
         if level + 1 < TREE_BITS:
-            sums = [merge(level, k, sums[k], got[k]) for k in range(CHUNKS)]
-        levels.append((got, [swap(x) for x in got]))
-    lead = jnp.zeros((HEADS, STATE), F32)
-    acc, lead = far(0, qt, d, w, lead, (*levels[0][0], *levels[0][1]))
-    for level in range(1, TREE_BITS - 1):
-        bufs = (*levels[level][0], *levels[level][1])
-        acc, lead = far(level, qt, d, w, lead, bufs, acc, parts[level - 1])
+            sums = merge_all(level, sums, got, before)
+            levels.append((*got, swap(pack(got, sums[-1]))))
+        else:
+            levels.append((*got, *[swap(x) for x in got]))
+    acc, lead = far(TREE_BITS - 2, qt, d, w, lead, levels[TREE_BITS - 2], acc, parts[-1])
     last = TREE_BITS - 1
-    gated, squares = close(last, qt, d, w, lead, acc, gt, (*levels[last][0], *levels[last][1]))
+    gated, squares = close(last, qt, d, w, lead, acc, gt, levels[last])
     count = lax.axis_size("head")
     shares = [
         lax.ppermute(squares, "head", [(i, (i + s) % count) for i in range(count)])
@@ -352,7 +379,7 @@
 
 def solution(mesh):
     return jax.shard_map(
-        shards,
+        work,
         mesh=mesh,
         in_specs=(
             P("tok", "head"),

time: 49.4 us -> 53 us (1.073)
  the two profiles are of different devices: /device:TPU:6 before, /device:TPU:32 now
where the time goes in v3:
time: 53 us; the launch traced here: 52.9 us
  starting transfers between devices  28.2 us (53%)
  waiting for transfers between devices  12.3 us (23%)
  Pallas kernels  11.4 us (22%)
  local copies, waits for them, and re-layouts  0.69 us (1%)
    ppermute x10, starting transfers between devices, work(): got.append(lax.ppermute(x, 'tok', partner_of(level)))  22 us
    ppermute x10, waiting for transfers between devices, work(): got.append(lax.ppermute(x, 'tok', partner_of(level)))  7.92 us
    pallas_call x4, Pallas kernels, near(): call(functools.partial(near_body, first), sds((2 * WIDTH, BLOCK)), [VM] *...  5.52 us
    ppermute x3, starting transfers between devices, work(): lax.ppermute(squares, 'head', [(i, (i + s) % count) for i in range(count)])  4.69 us
    ppermute x3, waiting for transfers between devices, work(): lax.ppermute(squares, 'head', [(i, (i + s) % count) for i in range(count)])  3.47 us
    pallas_call x5, Pallas kernels, far(): call(functools.partial(far_body, level), [sds((BLOCK, BLOCK)), sds((HEADS...  1.77 us
    pallas_call x1, Pallas kernels, prep(): call(prep_body, outs, [HB] * 3, 10 ** 7, scratch=[pltpu.VMEM((HEADS * WID...  1.71 us
    ppermute x9, starting transfers between devices, work(): swap = lambda x: lax.ppermute(x, 'tok', partner_of(0))  1.45 us
  transfers between devices with their start and end apart: 22, of which 9 were waited for; matrix products, arithmetic and copies ran while one was open for 0% of the time, Pallas kernels for 16%

profile of v3, /device:TPU:32, one launch (start us, length us, event | category | flops | bytes accessed | tf_op | source)
XLA Modules:
  0.0 52.9 jit_solution(15819262621454927021)
XLA Ops:
  0.0 1.7 %shard_map.83 = (f32[8,512]{1,0:T(8,128)S(1)}, f32[512,8]{1,0:T(8,128)S(1)}, bf16[512,512]{1,0:T(8,128)(2,1)S(1)}, f32[136,128]{1,0:T(8,128)S(1)}, f32[136,128]{...) custom-call(f32[8,512]{1,0:T(8,128)} %bitcast.14, ...), custom_call_target="tpu_custom_call" | custom-call | flops 10000000 | bytes 1048576 | tf_op jit(solution)/shard_map/pallas_call | solution.py:104
  1.7 0.1 collective-permute-start
  1.8 0.5 collective-permute-start.1
  2.3 0.0 copy-done.2
  2.3 0.0 copy-done.3
  2.3 0.4 shard_map.82
  2.7 0.4 collective-permute-done.rest_0_.got_ref
  3.1 1.9 %collective-permute-start.3 = (f32[136,128]{1,0:T(8,128)S(1)}, f32[136,128]{1,0:T(8,128)S(1)}, u32[]{:S(2)}, u32[]{:S(2)}) collective-permute-start(f32[136,128]{1,0:T(8,128)S(1)} %shard_map.85.refs_0_.own_ref), channel_id=1, source_target_pairs={{0,8},{4,12},{8,0},{12,4},{16,24},{20,28},{24,16},{28,20},{32,40},... | collective-permute-start | bytes 208904 | tf_op jit(solution)/shard_map/ppermute | solution.py:362
  5.0 0.0 collective-permute-done.1.rest_1_.got_ref
  5.0 0.3 collective-permute-start.4
  5.3 0.0 collective-permute-start.2
  5.3 0.0 copy-done
  5.3 0.6 %copy-done.1 = bf16[512,128]{1,0:T(8,128)(2,1)S(1)} copy-done((bf16[512,128]{1,0:T(8,128)(2,1)S(1)}, bf16[512,128]{1,0:T(8,128)(2,1)}, u32[]{:S(2)}) %copy-start.1) | copy-done | bytes 131096
  5.9 0.1 copy-done.4
  6.0 1.4 %shard_map.87.refs_0_.rest_4_ = f32[128,512]{1,0:T(8,128)S(1)} custom-call(bf16[512,128]{1,0:T(8,128)(2,1)S(1)} %copy-done.1, bf16[256,512]{1,0:T(8,128)(2,1)S(1)} %get-tuple-element.27.qt_ref, bf16[512,512]{1,0:T(8,128)(2,1)S(1)} %get-tuple-element.36.vt_ref, f32[8,512]{1,0:T(8,128)S(1)} %get-tuple-element.28.d_ref, ...), custom_call_target="tpu_custom_call" | custom-call | flops 10000000 | bytes 1048576 | tf_op jit(solution)/shard_map/pallas_call | solution.py:216
  7.4 0.1 collective-permute-done.3.got_ref.refs_0_.rest_0_
  7.5 2.1 %collective-permute-start.6 = (f32[136,128]{1,0:T(8,128)S(1)}, f32[136,128]{1,0:T(8,128)S(1)}, u32[]{:S(2)}, u32[]{:S(2)}) collective-permute-start(f32[136,128]{1,0:T(8,128)S(1)} %shard_map.88.refs_0_.own_ref), channel_id=1, source_target_pairs={{0,24},{4,28},{8,16},{12,20},{16,8},{20,12},{24,0},{28,4},{32,56},... | collective-permute-start | bytes 208904 | tf_op jit(solution)/shard_map/ppermute | solution.py:362
  9.6 0.0 collective-permute-done.4.got_ref.refs_1_.rest_1_
  9.7 1.9 %collective-permute-start.7 = (f32[136,128]{1,0:T(8,128)S(1)}, f32[136,128]{1,0:T(8,128)S(1)}, u32[]{:S(2)}, u32[]{:S(2)}) collective-permute-start(f32[136,128]{1,0:T(8,128)S(1)} %shard_map.89.refs_2_.token_ref.own_ref), channel_id=1, source_target_pairs={{0,24},{4,28},{8,16},{12,20},{16,8},{20,12},{24,0},{28,4},{32,56},... | collective-permute-start | bytes 208904 | tf_op jit(solution)/shard_map/ppermute | solution.py:362
  11.6 0.1 collective-permute-start.5
  11.7 0.0 collective-permute-done.2.rest_2_
  11.7 0.3 shard_map.84
  12.0 1.4 %shard_map.92.refs_0_.rest_4_ = f32[128,512]{1,0:T(8,128)S(1)} custom-call(bf16[512,128]{1,0:T(8,128)(2,1)S(1)} %copy-done.1, bf16[256,512]{1,0:T(8,128)(2,1)S(1)} %get-tuple-element.27.qt_ref, bf16[512,512]{1,0:T(8,128)(2,1)S(1)} %get-tuple-element.36.vt_ref, f32[8,512]{1,0:T(8,128)S(1)} %get-tuple-element.28.d_ref, ...), custom_call_target="tpu_custom_call" | custom-call | flops 10000000 | bytes 1048576 | tf_op jit(solution)/shard_map/pallas_call | solution.py:216
  13.4 0.0 collective-permute-done.6.got_ref.refs_0_.rest_0_
  13.4 7.7 %collective-permute-start.9 = (f32[136,128]{1,0:T(8,128)S(1)}, f32[136,128]{1,0:T(8,128)S(1)}, u32[]{:S(2)}, u32[]{:S(2)}) collective-permute-start(f32[136,128]{1,0:T(8,128)S(1)} %shard_map.93.refs_0_.own_ref), channel_id=1, source_target_pairs={{0,56},{4,60},{8,48},{12,52},{16,40},{20,44},{24,32},{28,36},{32,2... | collective-permute-start | bytes 208904 | tf_op jit(solution)/shard_map/ppermute | solution.py:362
  21.1 0.0 collective-permute-done.7.got_ref.refs_1_.rest_1_
  21.2 1.5 %collective-permute-start.10 = (f32[136,128]{1,0:T(8,128)S(1)}, f32[136,128]{1,0:T(8,128)S(1)}, u32[]{:S(2)}, u32[]{:S(2)}) collective-permute-start(f32[136,128]{1,0:T(8,128)S(1)} %shard_map.94.refs_2_.token_ref.own_ref), channel_id=1, source_target_pairs={{0,56},{4,60},{8,48},{12,52},{16,40},{20,44},{24,32},{28,36},{32,2... | collective-permute-start | bytes 208904 | tf_op jit(solution)/shard_map/ppermute | solution.py:362
  22.6 0.1 collective-permute-start.8
  22.7 1.4 %shard_map.97.refs_0_.rest_4_ = f32[128,512]{1,0:T(8,128)S(1)} custom-call(bf16[512,128]{1,0:T(8,128)(2,1)S(1)} %copy-done.1, bf16[256,512]{1,0:T(8,128)(2,1)S(1)} %get-tuple-element.27.qt_ref, bf16[512,512]{1,0:T(8,128)(2,1)S(1)} %get-tuple-element.36.vt_ref, f32[8,512]{1,0:T(8,128)S(1)} %get-tuple-element.28.d_ref, ...), custom_call_target="tpu_custom_call" | custom-call | flops 10000000 | bytes 1048576 | tf_op jit(solution)/shard_map/pallas_call | solution.py:216
  24.1 0.0 collective-permute-done.5.rest_2_
  24.1 0.4 shard_map.91
  24.5 0.0 collective-permute-done.9.got_ref.refs_0_.rest_0_
  24.5 1.6 %collective-permute-start.12 = (f32[136,128]{1,0:T(8,128)S(1)}, f32[136,128]{1,0:T(8,128)S(1)}, u32[]{:S(2)}, u32[]{:S(2)}) collective-permute-start(f32[136,128]{1,0:T(8,128)S(1)} %shard_map.98.refs_0_.own_ref), channel_id=1, source_target_pairs={{0,64},{4,68},{8,72},{12,76},{16,80},{20,84},{24,88},{28,92},{32,9... | collective-permute-start | bytes 208904 | tf_op jit(solution)/shard_map/ppermute | solution.py:362
  26.1 2.4 %collective-permute-done.10.got_ref.refs_1_.rest_1_ = f32[136,128]{1,0:T(8,128)S(1)} collective-permute-done((f32[136,128]{1,0:T(8,128)S(1)}, f32[136,128]{1,0:T(8,128)S(1)}, u32[]{:S(2)}, u32[]{:S(2)}) %collective-permute-start.10) | collective-permute-done | bytes 69664 | tf_op jit(solution)/shard_map/ppermute | solution.py:362
  28.6 1.6 %collective-permute-start.13 = (f32[136,128]{1,0:T(8,128)S(1)}, f32[136,128]{1,0:T(8,128)S(1)}, u32[]{:S(2)}, u32[]{:S(2)}) collective-permute-start(f32[136,128]{1,0:T(8,128)S(1)} %shard_map.99.refs_2_.token_ref.own_ref), channel_id=1, source_target_pairs={{0,64},{4,68},{8,72},{12,76},{16,80},{20,84},{24,88},{28,92},{32,9... | collective-permute-start | bytes 208904 | tf_op jit(solution)/shard_map/ppermute | solution.py:362
  30.2 1.4 %shard_map.102.refs_0_.rest_4_ = f32[128,512]{1,0:T(8,128)S(1)} custom-call(bf16[512,128]{1,0:T(8,128)(2,1)S(1)} %copy-done.1, bf16[256,512]{1,0:T(8,128)(2,1)S(1)} %get-tuple-element.27.qt_ref, bf16[512,512]{1,0:T(8,128)(2,1)S(1)} %get-tuple-element.36.vt_ref, f32[8,512]{1,0:T(8,128)S(1)} %get-tuple-element.28.d_ref, ...), custom_call_target="tpu_custom_call" | custom-call | flops 10000000 | bytes 1048576 | tf_op jit(solution)/shard_map/pallas_call | solution.py:216
  31.5 0.0 collective-permute-done.8.rest_2_
  31.6 0.4 shard_map.96
  31.9 0.0 collective-permute-done.12.got_ref.refs_0_.rest_0_
  32.0 1.0 %collective-permute-done.13.got_ref.refs_1_.rest_1_ = f32[136,128]{1,0:T(8,128)S(1)} collective-permute-done((f32[136,128]{1,0:T(8,128)S(1)}, f32[136,128]{1,0:T(8,128)S(1)}, u32[]{:S(2)}, u32[]{:S(2)}) %collective-permute-start.13) | collective-permute-done | bytes 69664 | tf_op jit(solution)/shard_map/ppermute | solution.py:362
  33.0 3.0 %collective-permute-start.16 = (f32[136,128]{1,0:T(8,128)S(1)}, f32[136,128]{1,0:T(8,128)S(1)}, u32[]{:S(2)}, u32[]{:S(2)}) collective-permute-start(f32[136,128]{1,0:T(8,128)S(1)} %shard_map.104.refs_2_), channel_id=1, source_target_pairs={{0,192},{4,196},{8,200},{12,204},{16,208},{20,212},{24,216},{28,22... | collective-permute-start | bytes 208904 | tf_op jit(solution)/shard_map/ppermute | solution.py:362
  36.0 0.5 collective-permute-start.15
  36.5 0.1 collective-permute-start.11
  36.6 0.6 %collective-permute-start.14 = (f32[256,128]{1,0:T(8,128)S(1)}, f32[256,128]{1,0:T(8,128)S(1)}, u32[]{:S(2)}, u32[]{:S(2)}) collective-permute-start(f32[256,128]{1,0:T(8,128)S(1)} %shard_map.105), channel_id=1, source_target_pairs={{0,4},{4,0},{8,12},{12,8},{16,20},{20,16},{24,28},{28,24},{32,36},... | collective-permute-start | bytes 393224 | tf_op jit(solution)/shard_map/ppermute | solution.py:343
  37.2 1.6 %collective-permute-done.16.rest_1_ = f32[136,128]{1,0:T(8,128)S(1)} collective-permute-done((f32[136,128]{1,0:T(8,128)S(1)}, f32[136,128]{1,0:T(8,128)S(1)}, u32[]{:S(2)}, u32[]{:S(2)}) %collective-permute-start.16) | collective-permute-done | bytes 69664 | tf_op jit(solution)/shard_map/ppermute | solution.py:362
  38.8 0.0 collective-permute-start.18
  38.8 2.8 %collective-permute-done.15.rest_0_ = f32[136,128]{1,0:T(8,128)S(1)} collective-permute-done((f32[136,128]{1,0:T(8,128)S(1)}, f32[136,128]{1,0:T(8,128)S(1)}, u32[]{:S(2)}, u32[]{:S(2)}) %collective-permute-start.15) | collective-permute-done | bytes 69664 | tf_op jit(solution)/shard_map/ppermute | solution.py:362
  41.6 0.0 collective-permute-start.17
  41.6 0.0 collective-permute-done.11.rest_2_
  41.6 0.4 shard_map.101
  41.9 0.0 collective-permute-done.14.rest_2_
  41.9 0.4 shard_map.106
  42.3 0.0 collective-permute-done.18.rest_3_
  42.3 0.5 collective-permute-done.17.rest_2_
  42.8 0.4 shard_map.107
  43.2 0.0 copy-start.5
  43.3 3.1 %collective-permute-start.21 = (f32[1,512]{1,0:T(1,128)S(1)}, f32[1,512]{1,0:T(1,128)S(1)}, u32[]{:S(2)}, u32[]{:S(2)}) collective-permute-start(f32[1,512]{1,0:T(1,128)S(1)} %get-tuple-element.48.a_ref), channel_id=1, source_target_pairs={{0,3},{1,0},{2,1},{3,2},{4,7},{5,4},{6,5},{7,6},{8,11},{9,8},{10,9... | collective-permute-start | bytes 6152 | tf_op jit(solution)/shard_map/ppermute | solution.py:373
  46.3 0.6 %collective-permute-start.20 = (f32[1,512]{1,0:T(1,128)S(1)}, f32[1,512]{1,0:T(1,128)S(1)}, u32[]{:S(2)}, u32[]{:S(2)}) collective-permute-start(f32[1,512]{1,0:T(1,128)S(1)} %get-tuple-element.48.a_ref), channel_id=1, source_target_pairs={{0,2},{1,3},{2,0},{3,1},{4,6},{5,7},{6,4},{7,5},{8,10},{9,11},{10,... | collective-permute-start | bytes 6152 | tf_op jit(solution)/shard_map/ppermute | solution.py:373
  47.0 1.0 %collective-permute-start.19 = (f32[1,512]{1,0:T(1,128)S(1)}, f32[1,512]{1,0:T(1,128)S(1)}, u32[]{:S(2)}, u32[]{:S(2)}) collective-permute-start(f32[1,512]{1,0:T(1,128)S(1)} %get-tuple-element.48.a_ref), channel_id=1, source_target_pairs={{0,1},{1,2},{2,3},{3,0},{4,5},{5,6},{6,7},{7,4},{8,9},{9,10},{10,1... | collective-permute-start | bytes 6152 | tf_op jit(solution)/shard_map/ppermute | solution.py:373
  48.0 0.3 shard_map.108.g_ref
  48.3 0.0 collective-permute-done.21.e_ref
  48.3 3.1 %collective-permute-done.20.c_ref = f32[1,512]{1,0:T(1,128)S(1)} collective-permute-done((f32[1,512]{1,0:T(1,128)S(1)}, f32[1,512]{1,0:T(1,128)S(1)}, u32[]{:S(2)}, u32[]{:S(2)}) %collective-permute-start.20) | collective-permute-done | bytes 2080 | tf_op jit(solution)/shard_map/ppermute | solution.py:373
  51.4 0.3 collective-permute-done.19.b_ref
  51.8 0.9 %shard_map.109 = bf16[512,512]{1,0:T(8,128)(2,1)} custom-call(f32[512,512]{1,0:T(8,128)S(1)} %shard_map.108.g_ref, f32[1,512]{1,0:T(1,128)S(1)} %get-tuple-element.48.a_ref, f32[1,512]{1,0:T(1,128)S(1)} %collective-permute-done.19.b_ref, f32[1,512]{1,0:T(1,128)S(1)} %collective-permute-done.20.c_ref, f32[1,512]{1,0:T(1,128)S(1)} %collective-permute-done.21.e_ref), custom_call_target="tpu_custom_call" | custom-call | flops 100000000 | bytes 1048576 | tf_op jit(solution)/shard_map/pallas_call | solution.py:324
  (21 shorter events, 0.3 us)
Async XLA Ops:
  0.0 2.3 %copy-start.2 = (bf16[512,512]{1,0:T(8,128)(2,1)S(1)}, bf16[512,512]{1,0:T(8,128)(2,1)}, u32[]{:S(2)}) copy-start(bf16[512,512]{1,0:T(8,128)(2,1)} %gate_ref.1) | copy-start | bytes 1572868
  0.0 2.3 %copy-start.3 = (bf16[512,128]{1,0:T(8,128)(2,1)S(1)}, bf16[512,128]{1,0:T(8,128)(2,1)}, u32[]{:S(2)}) copy-start(bf16[512,128]{1,0:T(8,128)(2,1)} %q_ref.1) | copy-start | bytes 393220
  1.7 1.3 %collective-permute-start = (f32[136,128]{1,0:T(8,128)S(1)}, f32[136,128]{1,0:T(8,128)S(1)}, u32[]{:S(2)}, u32[]{:S(2)}) collective-permute-start(f32[136,128]{1,0:T(8,128)S(1)} %get-tuple-element.29), channel_id=1, source_target_pairs={{0,4},{4,0},{8,12},{12,8},{16,20},{20,16},{24,28},{28,24},{32,36},... | collective-permute-start | bytes 208904 | tf_op jit(solution)/shard_map/ppermute | solution.py:343
  1.8 3.2 %collective-permute-start.1 = (f32[136,128]{1,0:T(8,128)S(1)}, f32[136,128]{1,0:T(8,128)S(1)}, u32[]{:S(2)}, u32[]{:S(2)}) collective-permute-start(f32[136,128]{1,0:T(8,128)S(1)} %get-tuple-element.30), channel_id=1, source_target_pairs={{0,4},{4,0},{8,12},{12,8},{16,20},{20,16},{24,28},{28,24},{32,36},... | collective-permute-start | bytes 208904 | tf_op jit(solution)/shard_map/ppermute | solution.py:343
  3.1 2.3 %copy-start = (f32[512,8,18]{0,1,2:T(8,128)S(1)}, f32[512,8,18]{0,1,2:T(8,128)}, u32[]{:S(2)}) copy-start(f32[512,8,18]{0,1,2:T(8,128)} %param.12) | copy-start | bytes 884740
  3.1 4.4 %collective-permute-start.3 = (f32[136,128]{1,0:T(8,128)S(1)}, f32[136,128]{1,0:T(8,128)S(1)}, u32[]{:S(2)}, u32[]{:S(2)}) collective-permute-start(f32[136,128]{1,0:T(8,128)S(1)} %shard_map.85.refs_0_.own_ref), channel_id=1, source_target_pairs={{0,8},{4,12},{8,0},{12,4},{16,24},{20,28},{24,16},{28,20},{32,40},... | collective-permute-start | bytes 208904 | tf_op jit(solution)/shard_map/ppermute | solution.py:362
  5.0 0.9 %copy-start.1 = (bf16[512,128]{1,0:T(8,128)(2,1)S(1)}, bf16[512,128]{1,0:T(8,128)(2,1)}, u32[]{:S(2)}) copy-start(bf16[512,128]{1,0:T(8,128)(2,1)} %k_ref.7) | copy-start | bytes 393220
  5.0 4.6 %collective-permute-start.4 = (f32[136,128]{1,0:T(8,128)S(1)}, f32[136,128]{1,0:T(8,128)S(1)}, u32[]{:S(2)}, u32[]{:S(2)}) collective-permute-start(f32[136,128]{1,0:T(8,128)S(1)} %shard_map.86.token_ref.own_ref), channel_id=1, source_target_pairs={{0,8},{4,12},{8,0},{12,4},{16,24},{20,28},{24,16},{28,20},{32,40},... | collective-permute-start | bytes 208904 | tf_op jit(solution)/shard_map/ppermute | solution.py:362
  5.3 6.3 %collective-permute-start.2 = (f32[256,128]{1,0:T(8,128)S(1)}, f32[256,128]{1,0:T(8,128)S(1)}, u32[]{:S(2)}, u32[]{:S(2)}) collective-permute-start(f32[256,128]{1,0:T(8,128)S(1)} %get-tuple-element.31), channel_id=1, source_target_pairs={{0,4},{4,0},{8,12},{12,8},{16,20},{20,16},{24,28},{28,24},{32,36},... | collective-permute-start | bytes 393224 | tf_op jit(solution)/shard_map/ppermute | solution.py:343
  5.3 0.7 %copy-start.4 = (f32[8]{0:T(128)S(1)}, f32[8]{0:T(128)}, u32[]{:S(2)}) copy-start(f32[8]{0:T(128)} %skip_ref.7) | copy-start | bytes 100
  7.5 5.9 %collective-permute-start.6 = (f32[136,128]{1,0:T(8,128)S(1)}, f32[136,128]{1,0:T(8,128)S(1)}, u32[]{:S(2)}, u32[]{:S(2)}) collective-permute-start(f32[136,128]{1,0:T(8,128)S(1)} %shard_map.88.refs_0_.own_ref), channel_id=1, source_target_pairs={{0,24},{4,28},{8,16},{12,20},{16,8},{20,12},{24,0},{28,4},{32,56},... | collective-permute-start | bytes 208904 | tf_op jit(solution)/shard_map/ppermute | solution.py:362
  9.7 11.5 %collective-permute-start.7 = (f32[136,128]{1,0:T(8,128)S(1)}, f32[136,128]{1,0:T(8,128)S(1)}, u32[]{:S(2)}, u32[]{:S(2)}) collective-permute-start(f32[136,128]{1,0:T(8,128)S(1)} %shard_map.89.refs_2_.token_ref.own_ref), channel_id=1, source_target_pairs={{0,24},{4,28},{8,16},{12,20},{16,8},{20,12},{24,0},{28,4},{32,56},... | collective-permute-start | bytes 208904 | tf_op jit(solution)/shard_map/ppermute | solution.py:362
  11.6 12.5 %collective-permute-start.5 = (f32[256,128]{1,0:T(8,128)S(1)}, f32[256,128]{1,0:T(8,128)S(1)}, u32[]{:S(2)}, u32[]{:S(2)}) collective-permute-start(f32[256,128]{1,0:T(8,128)S(1)} %shard_map.90), channel_id=1, source_target_pairs={{0,4},{4,0},{8,12},{12,8},{16,20},{20,16},{24,28},{28,24},{32,36},... | collective-permute-start | bytes 393224 | tf_op jit(solution)/shard_map/ppermute | solution.py:343
  13.4 11.1 %collective-permute-start.9 = (f32[136,128]{1,0:T(8,128)S(1)}, f32[136,128]{1,0:T(8,128)S(1)}, u32[]{:S(2)}, u32[]{:S(2)}) collective-permute-start(f32[136,128]{1,0:T(8,128)S(1)} %shard_map.93.refs_0_.own_ref), channel_id=1, source_target_pairs={{0,56},{4,60},{8,48},{12,52},{16,40},{20,44},{24,32},{28,36},{32,2... | collective-permute-start | bytes 208904 | tf_op jit(solution)/shard_map/ppermute | solution.py:362
  21.2 7.4 %collective-permute-start.10 = (f32[136,128]{1,0:T(8,128)S(1)}, f32[136,128]{1,0:T(8,128)S(1)}, u32[]{:S(2)}, u32[]{:S(2)}) collective-permute-start(f32[136,128]{1,0:T(8,128)S(1)} %shard_map.94.refs_2_.token_ref.own_ref), channel_id=1, source_target_pairs={{0,56},{4,60},{8,48},{12,52},{16,40},{20,44},{24,32},{28,36},{32,2... | collective-permute-start | bytes 208904 | tf_op jit(solution)/shard_map/ppermute | solution.py:362
  22.6 8.9 %collective-permute-start.8 = (f32[256,128]{1,0:T(8,128)S(1)}, f32[256,128]{1,0:T(8,128)S(1)}, u32[]{:S(2)}, u32[]{:S(2)}) collective-permute-start(f32[256,128]{1,0:T(8,128)S(1)} %shard_map.95), channel_id=1, source_target_pairs={{0,4},{4,0},{8,12},{12,8},{16,20},{20,16},{24,28},{28,24},{32,36},... | collective-permute-start | bytes 393224 | tf_op jit(solution)/shard_map/ppermute | solution.py:343
  24.5 7.4 %collective-permute-start.12 = (f32[136,128]{1,0:T(8,128)S(1)}, f32[136,128]{1,0:T(8,128)S(1)}, u32[]{:S(2)}, u32[]{:S(2)}) collective-permute-start(f32[136,128]{1,0:T(8,128)S(1)} %shard_map.98.refs_0_.own_ref), channel_id=1, source_target_pairs={{0,64},{4,68},{8,72},{12,76},{16,80},{20,84},{24,88},{28,92},{32,9... | collective-permute-start | bytes 208904 | tf_op jit(solution)/shard_map/ppermute | solution.py:362
  28.6 4.4 %collective-permute-start.13 = (f32[136,128]{1,0:T(8,128)S(1)}, f32[136,128]{1,0:T(8,128)S(1)}, u32[]{:S(2)}, u32[]{:S(2)}) collective-permute-start(f32[136,128]{1,0:T(8,128)S(1)} %shard_map.99.refs_2_.token_ref.own_ref), channel_id=1, source_target_pairs={{0,64},{4,68},{8,72},{12,76},{16,80},{20,84},{24,88},{28,92},{32,9... | collective-permute-start | bytes 208904 | tf_op jit(solution)/shard_map/ppermute | solution.py:362
  33.0 5.8 %collective-permute-start.16 = (f32[136,128]{1,0:T(8,128)S(1)}, f32[136,128]{1,0:T(8,128)S(1)}, u32[]{:S(2)}, u32[]{:S(2)}) collective-permute-start(f32[136,128]{1,0:T(8,128)S(1)} %shard_map.104.refs_2_), channel_id=1, source_target_pairs={{0,192},{4,196},{8,200},{12,204},{16,208},{20,212},{24,216},{28,22... | collective-permute-start | bytes 208904 | tf_op jit(solution)/shard_map/ppermute | solution.py:362
  36.0 5.5 %collective-permute-start.15 = (f32[136,128]{1,0:T(8,128)S(1)}, f32[136,128]{1,0:T(8,128)S(1)}, u32[]{:S(2)}, u32[]{:S(2)}) collective-permute-start(f32[136,128]{1,0:T(8,128)S(1)} %shard_map.103.refs_0_), channel_id=1, source_target_pairs={{0,192},{4,196},{8,200},{12,204},{16,208},{20,212},{24,216},{28,22... | collective-permute-start | bytes 208904 | tf_op jit(solution)/shard_map/ppermute | solution.py:362
  36.5 5.0 %collective-permute-start.11 = (f32[256,128]{1,0:T(8,128)S(1)}, f32[256,128]{1,0:T(8,128)S(1)}, u32[]{:S(2)}, u32[]{:S(2)}) collective-permute-start(f32[256,128]{1,0:T(8,128)S(1)} %shard_map.100), channel_id=1, source_target_pairs={{0,4},{4,0},{8,12},{12,8},{16,20},{20,16},{24,28},{28,24},{32,36},... | collective-permute-start | bytes 393224 | tf_op jit(solution)/shard_map/ppermute | solution.py:343
  36.6 5.3 %collective-permute-start.14 = (f32[256,128]{1,0:T(8,128)S(1)}, f32[256,128]{1,0:T(8,128)S(1)}, u32[]{:S(2)}, u32[]{:S(2)}) collective-permute-start(f32[256,128]{1,0:T(8,128)S(1)} %shard_map.105), channel_id=1, source_target_pairs={{0,4},{4,0},{8,12},{12,8},{16,20},{20,16},{24,28},{28,24},{32,36},... | collective-permute-start | bytes 393224 | tf_op jit(solution)/shard_map/ppermute | solution.py:343
  38.8 3.5 %collective-permute-start.18 = (f32[136,128]{1,0:T(8,128)S(1)}, f32[136,128]{1,0:T(8,128)S(1)}, u32[]{:S(2)}, u32[]{:S(2)}) collective-permute-start(f32[136,128]{1,0:T(8,128)S(1)} %collective-permute-done.16.rest_1_), channel_id=1, source_target_pairs={{0,4},{4,0},{8,12},{12,8},{16,20},{20,16},{24,28},{28,24},{32,36},... | collective-permute-start | bytes 208904 | tf_op jit(solution)/shard_map/ppermute | solution.py:343
  41.6 1.3 %collective-permute-start.17 = (f32[136,128]{1,0:T(8,128)S(1)}, f32[136,128]{1,0:T(8,128)S(1)}, u32[]{:S(2)}, u32[]{:S(2)}) collective-permute-start(f32[136,128]{1,0:T(8,128)S(1)} %collective-permute-done.15.rest_0_), channel_id=1, source_target_pairs={{0,4},{4,0},{8,12},{12,8},{16,20},{20,16},{24,28},{28,24},{32,36},... | collective-permute-start | bytes 208904 | tf_op jit(solution)/shard_map/ppermute | solution.py:343
  43.2 4.7 %copy-start.5 = (f32[512]{0:T(512)S(1)}, f32[512]{0:T(512)}, u32[]{:S(2)}) copy-start(f32[512]{0:T(512)} %param.15) | copy-start | bytes 6148
  43.3 5.0 %collective-permute-start.21 = (f32[1,512]{1,0:T(1,128)S(1)}, f32[1,512]{1,0:T(1,128)S(1)}, u32[]{:S(2)}, u32[]{:S(2)}) collective-permute-start(f32[1,512]{1,0:T(1,128)S(1)} %get-tuple-element.48.a_ref), channel_id=1, source_target_pairs={{0,3},{1,0},{2,1},{3,2},{4,7},{5,4},{6,5},{7,6},{8,11},{9,8},{10,9... | collective-permute-start | bytes 6152 | tf_op jit(solution)/shard_map/ppermute | solution.py:373
  46.3 5.1 %collective-permute-start.20 = (f32[1,512]{1,0:T(1,128)S(1)}, f32[1,512]{1,0:T(1,128)S(1)}, u32[]{:S(2)}, u32[]{:S(2)}) collective-permute-start(f32[1,512]{1,0:T(1,128)S(1)} %get-tuple-element.48.a_ref), channel_id=1, source_target_pairs={{0,2},{1,3},{2,0},{3,1},{4,6},{5,7},{6,4},{7,5},{8,10},{9,11},{10,... | collective-permute-start | bytes 6152 | tf_op jit(solution)/shard_map/ppermute | solution.py:373
  47.0 4.8 %collective-permute-start.19 = (f32[1,512]{1,0:T(1,128)S(1)}, f32[1,512]{1,0:T(1,128)S(1)}, u32[]{:S(2)}, u32[]{:S(2)}) collective-permute-start(f32[1,512]{1,0:T(1,128)S(1)} %get-tuple-element.48.a_ref), channel_id=1, source_target_pairs={{0,1},{1,2},{2,3},{3,0},{4,5},{5,6},{6,7},{7,4},{8,9},{9,10},{10,1... | collective-permute-start | bytes 6152 | tf_op jit(solution)/shard_map/ppermute | solution.py:373

commit v4 on v3

--- a/solution.py
+++ b/solution.py
@@ -13,13 +13,10 @@
 HEADS = 8
 WIDTH = 64
 STATE = 128
-CHUNKS = 2
-CHUNK_HEADS = HEADS // 2 // CHUNKS
-CHUNK_ROWS = CHUNK_HEADS * WIDTH
-BUF_ROWS = CHUNK_ROWS + HEADS
-HALF_ROWS = CHUNKS * CHUNK_ROWS
+HALF = HEADS // 2
+ROWS = HALF * WIDTH
+BUF_ROWS = ROWS + HEADS
 LOCAL_BITS = 9
-TREE_BITS = 6
 F32 = jnp.float32
 BF16 = jnp.bfloat16
 VM = pl.BlockSpec(memory_space=pltpu.VMEM)
@@ -56,9 +53,10 @@
     return hi, mid, rest - mid
 
 
-def prep_body(ld_hbm, v_hbm, k_hbm, d_ref, dcol_ref, vt_ref, *rest):
-    own_refs, send_refs = rest[:CHUNKS], rest[CHUNKS : 2 * CHUNKS]
-    pack_ref, state_ref, ld_ref, v_ref, k_ref, sems = rest[2 * CHUNKS :]
+def prep_body(
+    ld_hbm, v_hbm, k_hbm, d_ref, dcol_ref, vt_ref, own_ref, send_ref,
+    state_ref, ld_ref, v_ref, k_ref, sems,
+):
     pairs = ((ld_hbm, ld_ref), (v_hbm, v_ref), (k_hbm, k_ref))
     copies = [pltpu.make_async_copy(a, b, sems.at[i]) for i, (a, b) in enumerate(pairs)]
     for copy in copies:
@@ -86,22 +84,18 @@
     state_ref[...] = jnp.dot(
         jnp.concatenate(scaled, axis=0), k_ref[...], preferred_element_type=F32
     )
-    for k in range(CHUNKS):
-        mine = pl.multiple_of(core * (HEADS // 2 * WIDTH) + k * CHUNK_ROWS, CHUNK_ROWS)
-        other = pl.multiple_of((1 - core) * (HEADS // 2 * WIDTH) + k * CHUNK_ROWS, CHUNK_ROWS)
-        own_refs[k][0:CHUNK_ROWS] = state_ref[pl.ds(mine, CHUNK_ROWS), :]
-        own_refs[k][CHUNK_ROWS:BUF_ROWS] = total[:, 0:STATE]
-        send_refs[k][0:CHUNK_ROWS] = state_ref[pl.ds(other, CHUNK_ROWS), :]
-        send_refs[k][CHUNK_ROWS:BUF_ROWS] = total[:, 0:STATE]
-    pack_ref[...] = state_ref[pl.ds(pl.multiple_of(core * HALF_ROWS, HALF_ROWS), HALF_ROWS), :]
+    own_ref[0:ROWS] = state_ref[pl.ds(pl.multiple_of(core * ROWS, ROWS), ROWS), :]
+    own_ref[ROWS:BUF_ROWS] = total[:, 0:STATE]
+    send_ref[0:ROWS] = state_ref[pl.ds(pl.multiple_of((1 - core) * ROWS, ROWS), ROWS), :]
+    send_ref[ROWS:BUF_ROWS] = total[:, 0:STATE]
     dcol_ref[...] = d.T
 
 
 def prep(ld, v, k):
     buf = sds((BUF_ROWS, STATE))
     outs = [sds((HEADS, BLOCK)), sds((BLOCK, HEADS)), sds((BLOCK, BLOCK), BF16)]
-    outs += [buf] * (2 * CHUNKS) + [sds((HALF_ROWS, STATE))]
-    got = call(
+    outs += [buf, buf]
+    return call(
         prep_body, outs, [HB] * 3, 10**7,
         scratch=[
             pltpu.VMEM((HEADS * WIDTH, STATE), F32),
@@ -111,49 +105,31 @@
             pltpu.SemaphoreType.DMA((3,)),
         ],
     )(*(pltpu.with_memory_space_constraint(x, pltpu.HBM) for x in (ld, v, k)))
-    return got[0], got[1], got[2], got[3 : 3 + CHUNKS], got[3 + CHUNKS : -1], got[-1]
-
-
-def merge_body(level, chunk, own_ref, got_ref, *refs):
+
+
+def merge_body(level, own_ref, got_ref, *refs):
     out_ref, fac_ref = refs[-2:]
     upper = ((lax.axis_index("tok") >> level) & 1) == 1
-    own_ext = own_ref[CHUNK_ROWS:BUF_ROWS]
-    got_ext = got_ref[CHUNK_ROWS:BUF_ROWS]
+    own_ext = own_ref[ROWS:BUF_ROWS]
+    got_ext = got_ref[ROWS:BUF_ROWS]
     one = jnp.ones_like(own_ext)
     fac_ref[0:HEADS] = jnp.where(upper, one, jnp.exp(got_ext))
     fac_ref[HEADS : 2 * HEADS] = jnp.where(upper, jnp.exp(own_ext), one)
-    first = core_index() * (HEADS // 2) + chunk * CHUNK_HEADS
-    for j in range(CHUNK_HEADS):
+    first = core_index() * HALF
+    for j in range(HALF):
         rows = slice(j * WIDTH, (j + 1) * WIDTH)
         fa = fac_ref[pl.ds(first + j, 1), :]
         fb = fac_ref[pl.ds(first + (HEADS + j), 1), :]
         out_ref[rows] = own_ref[rows] * fa + got_ref[rows] * fb
-    out_ref[CHUNK_ROWS:BUF_ROWS] = own_ext + got_ext
-
-
-def merge(level, chunk, own, got, tokens):
-    return call(
-        functools.partial(merge_body, level, chunk), sds((BUF_ROWS, STATE)),
+    out_ref[ROWS:BUF_ROWS] = own_ext + got_ext
+
+
+def merge(level, own, got, *tokens):
+    return call(
+        functools.partial(merge_body, level), sds((BUF_ROWS, STATE)),
         [VM] * (2 + len(tokens)), 10**5,
         scratch=[pltpu.VMEM((2 * HEADS, STATE), F32)], vmem=4,
     )(own, got, *tokens)
-
-
-def merge_all(level, own, got, tokens):
-    out = []
-    for k in range(CHUNKS):
-        out.append(merge(level, k, own[k], got[k], tokens))
-        tokens = out[-1:]
-    return out
-
-
-def pack_body(*refs):
-    for k, ref in enumerate(refs[:CHUNKS]):
-        refs[-1][k * CHUNK_ROWS : (k + 1) * CHUNK_ROWS] = ref[0:CHUNK_ROWS]
-
-
-def pack(got, token):
-    return call(pack_body, sds((HALF_ROWS, STATE)), [VM] * (CHUNKS + 1), 10**5, vmem=4)(*got, token)
 
 
 def aux_body(q_ref, gate_ref, qt_ref, gt_ref):
@@ -226,52 +202,47 @@
     gain = jnp.where(upper, jnp.exp(lead), 0.0)[:, 0:1]
     coef_ref[...] = w_ref[LOCAL_BITS + 1 + level] * jnp.exp(d_ref[...]) * gain
     core = core_index()
-    places = [(core, k * CHUNK_HEADS, CHUNK_HEADS) for k in range(CHUNKS)]
-    if len(buf_refs) == 2 * CHUNKS:
-        places += [(1 - core, k * CHUNK_HEADS, CHUNK_HEADS) for k in range(CHUNKS)]
-    else:
-        places += [(1 - core, 0, HEADS // 2)]
-    for ref, (side, first, heads) in zip(buf_refs, places):
-        states = ref[0 : heads * WIDTH]
+    for side, ref in zip((core, 1 - core), buf_refs):
+        states = ref[0:ROWS]
         hi = states.astype(BF16)
         lo = (states - hi.astype(F32)).astype(BF16)
         read = jnp.dot(jnp.concatenate([hi, lo], axis=1), qt_ref[...], preferred_element_type=F32)
-        for j in range(heads):
-            head = side * (HEADS // 2) + (first + j)
+        for j in range(HALF):
+            head = side * HALF + j
             row = pl.multiple_of(head * WIDTH, WIDTH)
             term = read[j * WIDTH : (j + 1) * WIDTH] * coef_ref[pl.ds(head, 1), :]
             emit(row, acc_rows(row) + term)
-    got = buf_refs[0][CHUNK_ROWS:BUF_ROWS]
+    got = buf_refs[0][ROWS:BUF_ROWS]
     return lead + jnp.where(upper, got, 0.0)
 
 
 def far_body(level, qt_ref, d_ref, w_ref, lead_ref, *rest):
     coef_ref, next_ref, out_ref = rest[-1], rest[-2], rest[-3]
-    bufs = rest[: CHUNKS + 1]
+    bufs = rest[:2]
 
     def emit(row, value):
         out_ref[pl.ds(row, WIDTH), :] = value
 
     def start(row):
-        return rest[CHUNKS + 1][pl.ds(row, WIDTH), :] if level > 0 else 0.0
+        return rest[2][pl.ds(row, WIDTH), :] if level > 0 else 0.0
 
     next_ref[...] = readout(level, start, emit, qt_ref, d_ref, w_ref, lead_ref, bufs, coef_ref)
     if level > 0:
         rows = slice((level - 1) * 2 * WIDTH, level * 2 * WIDTH)
-        out_ref[rows] = out_ref[rows] + rest[CHUNKS + 2][...]
+        out_ref[rows] = out_ref[rows] + rest[3][...]
 
 
 def far(level, qt, d, w, lead, bufs, *more):
     return call(
         functools.partial(far_body, level), [sds((BLOCK, BLOCK)), sds((HEADS, STATE))],
-        [VM] * (5 + CHUNKS + len(more)), 10**7,
-        aliases={5 + CHUNKS: 0} if more else None,
+        [VM] * (6 + len(more)), 10**7,
+        aliases={6: 0} if more else None,
         scratch=[pltpu.VMEM((HEADS, BLOCK), F32)],
     )(qt, d, w, lead, *bufs, *more)
 
 
 def close_body(level, qt_ref, d_ref, w_ref, lead_ref, acc_ref, gt_ref, *rest):
-    bufs, out_ref, sq_ref, coef_ref = rest[: 2 * CHUNKS], rest[-3], rest[-2], rest[-1]
+    bufs, out_ref, sq_ref, coef_ref = rest[:2], rest[-3], rest[-2], rest[-1]
     sums = []
 
     def emit(row, value):
@@ -289,7 +260,7 @@
 def close(level, qt, d, w, lead, acc, gt, bufs):
     return call(
         functools.partial(close_body, level), [sds((BLOCK, BLOCK)), sds((1, BLOCK))],
-        [VM] * (6 + 2 * CHUNKS), 10**7,
+        [VM] * 8, 10**7,
         scratch=[pltpu.VMEM((HEADS, BLOCK), F32)],
     )(qt, d, w, lead, acc, gt, *bufs)
 
@@ -328,53 +299,54 @@
     )(g, *sums)
 
 
-def route_of(partner):
-    return [(i, partner(i)) for i in range(1 << TREE_BITS)]
-
-
-def partner_of(level):
-    flip = (1, 2, 6, 14, 16, 48)[level]
-    return route_of(lambda i: i ^ flip)
+def hop(x, axis, flip):
+    count = lax.axis_size(axis)
+    return lax.ppermute(x, axis, [(i, i ^ flip) for i in range(count)])
+
+
+CORE, Z1, Z2, Z3, Z7, X1, X2, X3 = 1, 2, 4, 6, 14, 16, 32, 48
 
 
 def work(head_inputs, state_keys, state_queries, log_decay, level_weight, skip_scale, gate_input, norm_gain):
     w = level_weight.transpose(2, 1, 0)
-    d, dcol, vt, own, send, packed = prep(log_decay.T, head_inputs, state_keys)
-    swap = lambda x: lax.ppermute(x, "tok", partner_of(0))
-    got = [swap(x) for x in send]
+    d, dcol, vt, own, send = prep(log_decay.T, head_inputs, state_keys)
+    swap = lambda x: hop(x, "tok", CORE)
+    close_by = lambda first, token: near(
+        first, state_keys, qt, vt, d, dcol, w, skip_scale, token
+    )
+    step = lambda level, lead, bufs, *more: far(level, qt, d, w, lead, bufs, *more)
+    got = swap(send)
     qt, gt = aux(state_queries, gate_input)
-    sums = merge_all(0, own, got, [gt])
-    levels = [(*got, swap(packed))]
-    acc, lead = None, jnp.zeros((HEADS, STATE), F32)
-    parts = []
-    for level in range(1, TREE_BITS):
-        before = []
-        if level < 5:
-            first = 2 * (level - 1)
-            parts.append(near(first, state_keys, qt, vt, d, dcol, w, skip_scale, sums[-1]))
-            before.append(parts[-1])
-        if level > 1:
-            more = () if acc is None else (acc, parts[level - 3])
-            acc, lead = far(level - 2, qt, d, w, lead, levels[level - 2], *more)
-            before.append(acc)
-        got = []
-        for x in sums:
-            got.append(lax.ppermute(x, "tok", partner_of(level)))
-        if level + 1 < TREE_BITS:
-            sums = merge_all(level, sums, got, before)
-            levels.append((*got, swap(pack(got, sums[-1]))))
-        else:
-            levels.append((*got, *[swap(x) for x in got]))
-    acc, lead = far(TREE_BITS - 2, qt, d, w, lead, levels[TREE_BITS - 2], acc, parts[-1])
-    last = TREE_BITS - 1
-    gated, squares = close(last, qt, d, w, lead, acc, gt, levels[last])
-    count = lax.axis_size("head")
-    shares = [
-        lax.ppermute(squares, "head", [(i, (i + s) % count) for i in range(count)])
-        for s in range(1, count)
-    ]
+    chip = merge(0, own, got, gt)
+    levels = [(got, swap(own))]
+    parts = [close_by(0, chip), close_by(2, chip)]
+    z2 = hop(chip, "tok", Z2)
+    z1 = hop(chip, "tok", Z1)
+    z3 = hop(chip, "tok", Z3)
+    pair = merge(1, chip, z1)
+    across = merge(1, z2, z3)
+    quad = merge(2, pair, across, *parts)
+    levels += [(z1, swap(z1)), (across, swap(across))]
+    parts.append(close_by(4, quad))
+    acc, lead = step(0, jnp.zeros((HEADS, STATE), F32), levels[0])
+    acc, lead = step(1, lead, levels[1], acc, parts[0])
+    z7 = hop(quad, "tok", Z7)
+    line = merge(3, quad, z7, parts[2], acc)
+    levels.append((z7, swap(z7)))
+    parts.append(close_by(6, line))
+    acc, lead = step(2, lead, levels[2], acc, parts[1])
+    x2 = hop(line, "tok", X2)
+    x1 = hop(line, "tok", X1)
+    x3 = hop(line, "tok", X3)
+    levels.append((x1, swap(x1)))
+    beyond = merge(4, x2, x3, parts[3], acc)
+    levels.append((beyond, swap(beyond)))
+    acc, lead = step(3, lead, levels[3], acc, parts[2])
+    acc, lead = step(4, lead, levels[4], acc, parts[3])
+    gated, squares = close(5, qt, d, w, lead, acc, gt, levels[5])
+    shares = [hop(squares, "head", 2), hop(squares, "head", 1), hop(squares, "head", 3)]
     turned = turn(gated, norm_gain[None])
-    return finish(HEADS * WIDTH * count, turned, [squares, *shares])
+    return finish(HEADS * WIDTH * lax.axis_size("head"), turned, [squares, *shares])
 
 
 def solution(mesh):

time: 53 us -> 53.9 us (1.017); the launches traced: 52.9 us -> 52.9 us
  waiting for transfers between devices: 12.3 us -> 21.3 us
  starting transfers between devices: 28.2 us -> 19.3 us
    ppermute x22 -> x17, waiting for transfers between devices: 12.3 us -> 21.3 us  [hop(): return lax.ppermute(x, axis, [(i, i ^ flip) for i in range(count)])]
    ppermute x22 -> x17, starting transfers between devices: 28.2 us -> 19.3 us  [hop(): return lax.ppermute(x, axis, [(i, i ^ flip) for i in range(count)])]
  transfers between devices with their start and end apart: 22 -> 17, of which waited for: 9 -> 11; matrix products, arithmetic and copies ran while one was open for 0% -> 0% of each run, Pallas kernels for 16% -> 15%
where the time goes in v4:
time: 53.9 us; the launch traced here: 52.9 us
  waiting for transfers between devices  21.3 us (40%)
  starting transfers between devices  19.3 us (36%)
  Pallas kernels  11.2 us (21%)
  local copies, waits for them, and re-layouts  0.67 us (1%)
    ppermute x17, waiting for transfers between devices, hop(): return lax.ppermute(x, axis, [(i, i ^ flip) for i in range(count)])  21.3 us
    ppermute x17, starting transfers between devices, hop(): return lax.ppermute(x, axis, [(i, i ^ flip) for i in range(count)])  19.3 us
    pallas_call x4, Pallas kernels, near(): call(functools.partial(near_body, first), sds((2 * WIDTH, BLOCK)), [VM] *...  5.51 us
    pallas_call x5, Pallas kernels, far(): call(functools.partial(far_body, level), [sds((BLOCK, BLOCK)), sds((HEADS...  1.73 us
    pallas_call x1, Pallas kernels, prep(): call(prep_body, outs, [HB] * 3, 10 ** 7, scratch=[pltpu.VMEM((HEADS * WID...  1.7 us
  transfers between devices with their start and end apart: 17, of which 11 were waited for; matrix products, arithmetic and copies ran while one was open for 0% of the time, Pallas kernels for 15%

profile of v4, /device:TPU:32, one launch (start us, length us, event | category | flops | bytes accessed | tf_op | source)
XLA Modules:
  0.0 52.9 jit_solution(8383391447762350557)
XLA Ops:
  0.0 0.0 copy-start.2
  0.0 0.0 copy-start.3
  0.0 1.7 %shard_map.83 = (f32[8,512]{1,0:T(8,128)S(1)}, f32[512,8]{1,0:T(8,128)S(1)}, bf16[512,512]{1,0:T(8,128)(2,1)S(1)}, f32[264,128]{1,0:T(8,128)S(1)}, f32[264,128]{1,0:T(8,128)S(1)}) custom-call(f32[8,512]{1,0:T(8,128)} %bitcast.14, bf16[512,512]{1,0:T(8,128)(2,1)} %v_hbm.1, bf16[512,128]{1,0:T(8,128)(2,1)} %k_ref.7), custom_call_target="tpu_custom_call" | custom-call | flops 10000000 | bytes 1048576 | tf_op jit(solution)/shard_map/pallas_call | solution.py:98
  1.7 0.1 collective-permute-start
  1.8 0.0 copy-done.2
  1.8 0.0 copy-done.3
  1.8 0.4 shard_map.82
  2.2 0.9 %collective-permute-done.rest_0_.got_ref = f32[264,128]{1,0:T(8,128)S(1)} collective-permute-done((f32[264,128]{1,0:T(8,128)S(1)}, f32[264,128]{1,0:T(8,128)S(1)}, u32[]{:S(2)}, u32[]{:S(2)}) %collective-permute-start) | collective-permute-done | bytes 135200 | tf_op jit(solution)/shard_map/ppermute | solution.py:304
  3.2 0.0 copy-start
  3.2 0.0 copy-start.1
  3.2 1.9 %collective-permute-start.2 = (f32[264,128]{1,0:T(8,128)S(1)}, f32[264,128]{1,0:T(8,128)S(1)}, u32[]{:S(2)}, u32[]{:S(2)}) collective-permute-start(f32[264,128]{1,0:T(8,128)S(1)} %shard_map.85.token_ref.own_ref), channel_id=1, source_target_pairs={{0,8},{4,12},{8,0},{12,4},{16,24},{20,28},{24,16},{28,20},{32,40},... | collective-permute-start | bytes 405512 | tf_op jit(solution)/shard_map/ppermute | solution.py:304
  5.1 1.6 %collective-permute-start.4 = (f32[264,128]{1,0:T(8,128)S(1)}, f32[264,128]{1,0:T(8,128)S(1)}, u32[]{:S(2)}, u32[]{:S(2)}) collective-permute-start(f32[264,128]{1,0:T(8,128)S(1)} %shard_map.85.token_ref.own_ref), channel_id=1, source_target_pairs={{0,16},{4,20},{8,24},{12,28},{16,0},{20,4},{24,8},{28,12},{32,48},... | collective-permute-start | bytes 405512 | tf_op jit(solution)/shard_map/ppermute | solution.py:304
  6.7 0.5 collective-permute-start.5
  7.1 0.0 collective-permute-start.1
  7.1 0.0 copy-start.4
  7.1 0.0 copy-done
  7.1 0.0 copy-done.1
  7.1 0.6 %copy-done.4 = f32[8]{0:T(128)S(1)} copy-done((f32[8]{0:T(128)S(1)}, f32[8]{0:T(128)}, u32[]{:S(2)}) %copy-start.4) | copy-done | bytes 56
  7.8 1.4 %shard_map.86.rest_3_.refs_0_ = f32[128,512]{1,0:T(8,128)S(1)} custom-call(bf16[512,128]{1,0:T(8,128)(2,1)S(1)} %copy-done.1, bf16[256,512]{1,0:T(8,128)(2,1)S(1)} %get-tuple-element.24.qt_ref, bf16[512,512]{1,0:T(8,128)(2,1)S(1)} %get-tuple-element.31.vt_ref, f32[8,512]{1,0:T(8,128)S(1)} %get-tuple-element.25.d_ref, ...), custom_call_target="tpu_custom_call" | custom-call | flops 10000000 | bytes 1048576 | tf_op jit(solution)/shard_map/pallas_call | solution.py:192
  9.2 1.5 %collective-permute-done.2.rest_0_.got_ref = f32[264,128]{1,0:T(8,128)S(1)} collective-permute-done((f32[264,128]{1,0:T(8,128)S(1)}, f32[264,128]{1,0:T(8,128)S(1)}, u32[]{:S(2)}, u32[]{:S(2)}) %collective-permute-start.2) | collective-permute-done | bytes 135200 | tf_op jit(solution)/shard_map/ppermute | solution.py:304
  10.7 0.0 collective-permute-start.3
  10.7 1.4 %shard_map.89.rest_3_.refs_1_ = f32[128,512]{1,0:T(8,128)S(1)} custom-call(bf16[512,128]{1,0:T(8,128)(2,1)S(1)} %copy-done.1, bf16[256,512]{1,0:T(8,128)(2,1)S(1)} %get-tuple-element.24.qt_ref, bf16[512,512]{1,0:T(8,128)(2,1)S(1)} %get-tuple-element.31.vt_ref, f32[8,512]{1,0:T(8,128)S(1)} %get-tuple-element.25.d_ref, ...), custom_call_target="tpu_custom_call" | custom-call | flops 10000000 | bytes 1048576 | tf_op jit(solution)/shard_map/pallas_call | solution.py:192
  12.1 4.4 %collective-permute-done.4.own_ref = f32[264,128]{1,0:T(8,128)S(1)} collective-permute-done((f32[264,128]{1,0:T(8,128)S(1)}, f32[264,128]{1,0:T(8,128)S(1)}, u32[]{:S(2)}, u32[]{:S(2)}) %collective-permute-start.4) | collective-permute-done | bytes 135200 | tf_op jit(solution)/shard_map/ppermute | solution.py:304
  16.5 3.0 %collective-permute-done.5.got_ref = f32[264,128]{1,0:T(8,128)S(1)} collective-permute-done((f32[264,128]{1,0:T(8,128)S(1)}, f32[264,128]{1,0:T(8,128)S(1)}, u32[]{:S(2)}, u32[]{:S(2)}) %collective-permute-start.5) | collective-permute-done | bytes 135200 | tf_op jit(solution)/shard_map/ppermute | solution.py:304
  19.5 5.3 %collective-permute-start.7 = (f32[264,128]{1,0:T(8,128)S(1)}, f32[264,128]{1,0:T(8,128)S(1)}, u32[]{:S(2)}, u32[]{:S(2)}) collective-permute-start(f32[264,128]{1,0:T(8,128)S(1)} %shard_map.92.token_ref.own_ref), channel_id=1, source_target_pairs={{0,56},{4,60},{8,48},{12,52},{16,40},{20,44},{24,32},{28,36},{32,2... | collective-permute-start | bytes 405512 | tf_op jit(solution)/shard_map/ppermute | solution.py:304
  24.9 0.0 collective-permute-done.1.rest_1_
  24.9 0.3 shard_map.84
  25.2 1.4 %shard_map.93.rest_3_.refs_0_ = f32[128,512]{1,0:T(8,128)S(1)} custom-call(bf16[512,128]{1,0:T(8,128)(2,1)S(1)} %copy-done.1, bf16[256,512]{1,0:T(8,128)(2,1)S(1)} %get-tuple-element.24.qt_ref, bf16[512,512]{1,0:T(8,128)(2,1)S(1)} %get-tuple-element.31.vt_ref, f32[8,512]{1,0:T(8,128)S(1)} %get-tuple-element.25.d_ref, ...), custom_call_target="tpu_custom_call" | custom-call | flops 10000000 | bytes 1048576 | tf_op jit(solution)/shard_map/pallas_call | solution.py:192
  26.6 0.0 collective-permute-done.3.rest_1_
  26.6 0.4 shard_map.87
  26.9 0.9 %collective-permute-done.7.rest_0_.got_ref = f32[264,128]{1,0:T(8,128)S(1)} collective-permute-done((f32[264,128]{1,0:T(8,128)S(1)}, f32[264,128]{1,0:T(8,128)S(1)}, u32[]{:S(2)}, u32[]{:S(2)}) %collective-permute-start.7) | collective-permute-done | bytes 135200 | tf_op jit(solution)/shard_map/ppermute | solution.py:304
  27.9 1.6 %collective-permute-start.9 = (f32[264,128]{1,0:T(8,128)S(1)}, f32[264,128]{1,0:T(8,128)S(1)}, u32[]{:S(2)}, u32[]{:S(2)}) collective-permute-start(f32[264,128]{1,0:T(8,128)S(1)} %shard_map.95.token_ref), channel_id=1, source_target_pairs={{0,64},{4,68},{8,72},{12,76},{16,80},{20,84},{24,88},{28,92},{32,9... | collective-permute-start | bytes 405512 | tf_op jit(solution)/shard_map/ppermute | solution.py:304
  29.5 0.0 collective-permute-start.6
  29.5 2.7 %collective-permute-start.11 = (f32[264,128]{1,0:T(8,128)S(1)}, f32[264,128]{1,0:T(8,128)S(1)}, u32[]{:S(2)}, u32[]{:S(2)}) collective-permute-start(f32[264,128]{1,0:T(8,128)S(1)} %shard_map.95.token_ref), channel_id=1, source_target_pairs={{0,128},{4,132},{8,136},{12,140},{16,144},{20,148},{24,152},{28,15... | collective-permute-start | bytes 405512 | tf_op jit(solution)/shard_map/ppermute | solution.py:304
  32.2 0.5 collective-permute-start.12
  32.7 0.0 collective-permute-start.8
  32.7 1.4 %shard_map.96.rest_3_.refs_0_ = f32[128,512]{1,0:T(8,128)S(1)} custom-call(bf16[512,128]{1,0:T(8,128)(2,1)S(1)} %copy-done.1, bf16[256,512]{1,0:T(8,128)(2,1)S(1)} %get-tuple-element.24.qt_ref, bf16[512,512]{1,0:T(8,128)(2,1)S(1)} %get-tuple-element.31.vt_ref, f32[8,512]{1,0:T(8,128)S(1)} %get-tuple-element.25.d_ref, ...), custom_call_target="tpu_custom_call" | custom-call | flops 10000000 | bytes 1048576 | tf_op jit(solution)/shard_map/pallas_call | solution.py:192
  34.1 0.0 collective-permute-done.9.rest_0_
  34.1 0.6 %collective-permute-start.10 = (f32[264,128]{1,0:T(8,128)S(1)}, f32[264,128]{1,0:T(8,128)S(1)}, u32[]{:S(2)}, u32[]{:S(2)}) collective-permute-start(f32[264,128]{1,0:T(8,128)S(1)} %collective-permute-done.9.rest_0_), channel_id=1, source_target_pairs={{0,4},{4,0},{8,12},{12,8},{16,20},{20,16},{24,28},{28,24},{32,36},... | collective-permute-start | bytes 405512 | tf_op jit(solution)/shard_map/ppermute | solution.py:304
  34.7 0.0 collective-permute-done.6.rest_1_
  34.7 0.3 shard_map.90
  35.0 3.1 %collective-permute-done.11.own_ref = f32[264,128]{1,0:T(8,128)S(1)} collective-permute-done((f32[264,128]{1,0:T(8,128)S(1)}, f32[264,128]{1,0:T(8,128)S(1)}, u32[]{:S(2)}, u32[]{:S(2)}) %collective-permute-start.11) | collective-permute-done | bytes 135200 | tf_op jit(solution)/shard_map/ppermute | solution.py:304
  38.2 2.8 %collective-permute-done.12.got_ref = f32[264,128]{1,0:T(8,128)S(1)} collective-permute-done((f32[264,128]{1,0:T(8,128)S(1)}, f32[264,128]{1,0:T(8,128)S(1)}, u32[]{:S(2)}, u32[]{:S(2)}) %collective-permute-start.12) | collective-permute-done | bytes 135200 | tf_op jit(solution)/shard_map/ppermute | solution.py:304
  41.0 0.3 collective-permute-start.13
  41.3 0.0 collective-permute-done.8.rest_1_
  41.3 0.4 shard_map.94
  41.6 0.0 collective-permute-done.10.rest_1_
  41.6 0.4 shard_map.97
  42.0 0.6 %collective-permute-done.13.rest_1_ = f32[264,128]{1,0:T(8,128)S(1)} collective-permute-done((f32[264,128]{1,0:T(8,128)S(1)}, f32[264,128]{1,0:T(8,128)S(1)}, u32[]{:S(2)}, u32[]{:S(2)}) %collective-permute-start.13) | collective-permute-done | bytes 135200 | tf_op jit(solution)/shard_map/ppermute | solution.py:304
  42.6 0.4 shard_map.99
  43.0 0.0 copy-start.5
  43.0 3.3 %collective-permute-start.14 = (f32[1,512]{1,0:T(1,128)S(1)}, f32[1,512]{1,0:T(1,128)S(1)}, u32[]{:S(2)}, u32[]{:S(2)}) collective-permute-start(f32[1,512]{1,0:T(1,128)S(1)} %get-tuple-element.42.a_ref), channel_id=1, source_target_pairs={{0,2},{1,3},{2,0},{3,1},{4,6},{5,7},{6,4},{7,5},{8,10},{9,11},{10,... | collective-permute-start | bytes 6152 | tf_op jit(solution)/shard_map/ppermute | solution.py:304
  46.3 0.7 %collective-permute-start.15 = (f32[1,512]{1,0:T(1,128)S(1)}, f32[1,512]{1,0:T(1,128)S(1)}, u32[]{:S(2)}, u32[]{:S(2)}) collective-permute-start(f32[1,512]{1,0:T(1,128)S(1)} %get-tuple-element.42.a_ref), channel_id=1, source_target_pairs={{0,1},{1,0},{2,3},{3,2},{4,5},{5,4},{6,7},{7,6},{8,9},{9,8},{10,11... | collective-permute-start | bytes 6152 | tf_op jit(solution)/shard_map/ppermute | solution.py:304
  47.0 0.4 collective-permute-start.16
  47.4 0.0 copy-done.5
  47.4 0.3 shard_map.100.g_ref
  47.7 0.5 collective-permute-done.14.b_ref
  48.2 1.7 %collective-permute-done.15.c_ref = f32[1,512]{1,0:T(1,128)S(1)} collective-permute-done((f32[1,512]{1,0:T(1,128)S(1)}, f32[1,512]{1,0:T(1,128)S(1)}, u32[]{:S(2)}, u32[]{:S(2)}) %collective-permute-start.15) | collective-permute-done | bytes 2080 | tf_op jit(solution)/shard_map/ppermute | solution.py:304
  49.9 1.9 %collective-permute-done.16.e_ref = f32[1,512]{1,0:T(1,128)S(1)} collective-permute-done((f32[1,512]{1,0:T(1,128)S(1)}, f32[1,512]{1,0:T(1,128)S(1)}, u32[]{:S(2)}, u32[]{:S(2)}) %collective-permute-start.16) | collective-permute-done | bytes 2080 | tf_op jit(solution)/shard_map/ppermute | solution.py:304
  51.8 0.9 %shard_map.101 = bf16[512,512]{1,0:T(8,128)(2,1)} custom-call(f32[512,512]{1,0:T(8,128)S(1)} %shard_map.100.g_ref, f32[1,512]{1,0:T(1,128)S(1)} %get-tuple-element.42.a_ref, f32[1,512]{1,0:T(1,128)S(1)} %collective-permute-done.14.b_ref, f32[1,512]{1,0:T(1,128)S(1)} %collective-permute-done.15.c_ref, f32[1,512]{1,0:T(1,128)S(1)} %collective-permute-done.16.e_ref), custom_call_target="tpu_custom_call" | custom-call | flops 100000000 | bytes 1048576 | tf_op jit(solution)/shard_map/pallas_call | solution.py:295
  (7 shorter events, 0.2 us)
Async XLA Ops:
  0.0 1.8 %copy-start.2 = (bf16[512,512]{1,0:T(8,128)(2,1)S(1)}, bf16[512,512]{1,0:T(8,128)(2,1)}, u32[]{:S(2)}) copy-start(bf16[512,512]{1,0:T(8,128)(2,1)} %gate_ref.1) | copy-start | bytes 1572868
  0.0 1.8 %copy-start.3 = (bf16[512,128]{1,0:T(8,128)(2,1)S(1)}, bf16[512,128]{1,0:T(8,128)(2,1)}, u32[]{:S(2)}) copy-start(bf16[512,128]{1,0:T(8,128)(2,1)} %q_ref.1) | copy-start | bytes 393220
  1.7 1.4 %collective-permute-start = (f32[264,128]{1,0:T(8,128)S(1)}, f32[264,128]{1,0:T(8,128)S(1)}, u32[]{:S(2)}, u32[]{:S(2)}) collective-permute-start(f32[264,128]{1,0:T(8,128)S(1)} %get-tuple-element.26), channel_id=1, source_target_pairs={{0,4},{4,0},{8,12},{12,8},{16,20},{20,16},{24,28},{28,24},{32,36},... | collective-permute-start | bytes 405512 | tf_op jit(solution)/shard_map/ppermute | solution.py:304
  3.2 4.0 %copy-start = (f32[512,8,18]{0,1,2:T(8,128)S(1)}, f32[512,8,18]{0,1,2:T(8,128)}, u32[]{:S(2)}) copy-start(f32[512,8,18]{0,1,2:T(8,128)} %param.12) | copy-start | bytes 884740
  3.2 4.0 %copy-start.1 = (bf16[512,128]{1,0:T(8,128)(2,1)S(1)}, bf16[512,128]{1,0:T(8,128)(2,1)}, u32[]{:S(2)}) copy-start(bf16[512,128]{1,0:T(8,128)(2,1)} %k_ref.7) | copy-start | bytes 393220
  3.2 7.5 %collective-permute-start.2 = (f32[264,128]{1,0:T(8,128)S(1)}, f32[264,128]{1,0:T(8,128)S(1)}, u32[]{:S(2)}, u32[]{:S(2)}) collective-permute-start(f32[264,128]{1,0:T(8,128)S(1)} %shard_map.85.token_ref.own_ref), channel_id=1, source_target_pairs={{0,8},{4,12},{8,0},{12,4},{16,24},{20,28},{24,16},{28,20},{32,40},... | collective-permute-start | bytes 405512 | tf_op jit(solution)/shard_map/ppermute | solution.py:304
  5.1 11.4 %collective-permute-start.4 = (f32[264,128]{1,0:T(8,128)S(1)}, f32[264,128]{1,0:T(8,128)S(1)}, u32[]{:S(2)}, u32[]{:S(2)}) collective-permute-start(f32[264,128]{1,0:T(8,128)S(1)} %shard_map.85.token_ref.own_ref), channel_id=1, source_target_pairs={{0,16},{4,20},{8,24},{12,28},{16,0},{20,4},{24,8},{28,12},{32,48},... | collective-permute-start | bytes 405512 | tf_op jit(solution)/shard_map/ppermute | solution.py:304
  6.7 12.8 %collective-permute-start.5 = (f32[264,128]{1,0:T(8,128)S(1)}, f32[264,128]{1,0:T(8,128)S(1)}, u32[]{:S(2)}, u32[]{:S(2)}) collective-permute-start(f32[264,128]{1,0:T(8,128)S(1)} %shard_map.85.token_ref.own_ref), channel_id=1, source_target_pairs={{0,24},{4,28},{8,16},{12,20},{16,8},{20,12},{24,0},{28,4},{32,56},... | collective-permute-start | bytes 405512 | tf_op jit(solution)/shard_map/ppermute | solution.py:304
  7.1 17.7 %collective-permute-start.1 = (f32[264,128]{1,0:T(8,128)S(1)}, f32[264,128]{1,0:T(8,128)S(1)}, u32[]{:S(2)}, u32[]{:S(2)}) collective-permute-start(f32[264,128]{1,0:T(8,128)S(1)} %get-tuple-element.27.own_ref), channel_id=1, source_target_pairs={{0,4},{4,0},{8,12},{12,8},{16,20},{20,16},{24,28},{28,24},{32,36},... | collective-permute-start | bytes 405512 | tf_op jit(solution)/shard_map/ppermute | solution.py:304
  7.1 0.7 %copy-start.4 = (f32[8]{0:T(128)S(1)}, f32[8]{0:T(128)}, u32[]{:S(2)}) copy-start(f32[8]{0:T(128)} %skip_ref.7) | copy-start | bytes 100
  10.7 15.9 %collective-permute-start.3 = (f32[264,128]{1,0:T(8,128)S(1)}, f32[264,128]{1,0:T(8,128)S(1)}, u32[]{:S(2)}, u32[]{:S(2)}) collective-permute-start(f32[264,128]{1,0:T(8,128)S(1)} %collective-permute-done.2.rest_0_.got_ref), channel_id=1, source_target_pairs={{0,4},{4,0},{8,12},{12,8},{16,20},{20,16},{24,28},{28,24},{32,36},... | collective-permute-start | bytes 405512 | tf_op jit(solution)/shard_map/ppermute | solution.py:304
  19.5 8.3 %collective-permute-start.7 = (f32[264,128]{1,0:T(8,128)S(1)}, f32[264,128]{1,0:T(8,128)S(1)}, u32[]{:S(2)}, u32[]{:S(2)}) collective-permute-start(f32[264,128]{1,0:T(8,128)S(1)} %shard_map.92.token_ref.own_ref), channel_id=1, source_target_pairs={{0,56},{4,60},{8,48},{12,52},{16,40},{20,44},{24,32},{28,36},{32,2... | collective-permute-start | bytes 405512 | tf_op jit(solution)/shard_map/ppermute | solution.py:304
  27.9 6.2 %collective-permute-start.9 = (f32[264,128]{1,0:T(8,128)S(1)}, f32[264,128]{1,0:T(8,128)S(1)}, u32[]{:S(2)}, u32[]{:S(2)}) collective-permute-start(f32[264,128]{1,0:T(8,128)S(1)} %shard_map.95.token_ref), channel_id=1, source_target_pairs={{0,64},{4,68},{8,72},{12,76},{16,80},{20,84},{24,88},{28,92},{32,9... | collective-permute-start | bytes 405512 | tf_op jit(solution)/shard_map/ppermute | solution.py:304
  29.5 5.2 %collective-permute-start.6 = (f32[264,128]{1,0:T(8,128)S(1)}, f32[264,128]{1,0:T(8,128)S(1)}, u32[]{:S(2)}, u32[]{:S(2)}) collective-permute-start(f32[264,128]{1,0:T(8,128)S(1)} %shard_map.88.rest_0_.got_ref), channel_id=1, source_target_pairs={{0,4},{4,0},{8,12},{12,8},{16,20},{20,16},{24,28},{28,24},{32,36},... | collective-permute-start | bytes 405512 | tf_op jit(solution)/shard_map/ppermute | solution.py:304
  29.5 8.7 %collective-permute-start.11 = (f32[264,128]{1,0:T(8,128)S(1)}, f32[264,128]{1,0:T(8,128)S(1)}, u32[]{:S(2)}, u32[]{:S(2)}) collective-permute-start(f32[264,128]{1,0:T(8,128)S(1)} %shard_map.95.token_ref), channel_id=1, source_target_pairs={{0,128},{4,132},{8,136},{12,140},{16,144},{20,148},{24,152},{28,15... | collective-permute-start | bytes 405512 | tf_op jit(solution)/shard_map/ppermute | solution.py:304
  32.2 8.7 %collective-permute-start.12 = (f32[264,128]{1,0:T(8,128)S(1)}, f32[264,128]{1,0:T(8,128)S(1)}, u32[]{:S(2)}, u32[]{:S(2)}) collective-permute-start(f32[264,128]{1,0:T(8,128)S(1)} %shard_map.95.token_ref), channel_id=1, source_target_pairs={{0,192},{4,196},{8,200},{12,204},{16,208},{20,212},{24,216},{28,22... | collective-permute-start | bytes 405512 | tf_op jit(solution)/shard_map/ppermute | solution.py:304
  32.7 8.6 %collective-permute-start.8 = (f32[264,128]{1,0:T(8,128)S(1)}, f32[264,128]{1,0:T(8,128)S(1)}, u32[]{:S(2)}, u32[]{:S(2)}) collective-permute-start(f32[264,128]{1,0:T(8,128)S(1)} %collective-permute-done.7.rest_0_.got_ref), channel_id=1, source_target_pairs={{0,4},{4,0},{8,12},{12,8},{16,20},{20,16},{24,28},{28,24},{32,36},... | collective-permute-start | bytes 405512 | tf_op jit(solution)/shard_map/ppermute | solution.py:304
  34.1 7.6 %collective-permute-start.10 = (f32[264,128]{1,0:T(8,128)S(1)}, f32[264,128]{1,0:T(8,128)S(1)}, u32[]{:S(2)}, u32[]{:S(2)}) collective-permute-start(f32[264,128]{1,0:T(8,128)S(1)} %collective-permute-done.9.rest_0_), channel_id=1, source_target_pairs={{0,4},{4,0},{8,12},{12,8},{16,20},{20,16},{24,28},{28,24},{32,36},... | collective-permute-start | bytes 405512 | tf_op jit(solution)/shard_map/ppermute | solution.py:304
  41.0 1.6 %collective-permute-start.13 = (f32[264,128]{1,0:T(8,128)S(1)}, f32[264,128]{1,0:T(8,128)S(1)}, u32[]{:S(2)}, u32[]{:S(2)}) collective-permute-start(f32[264,128]{1,0:T(8,128)S(1)} %shard_map.98.rest_0_), channel_id=1, source_target_pairs={{0,4},{4,0},{8,12},{12,8},{16,20},{20,16},{24,28},{28,24},{32,36},... | collective-permute-start | bytes 405512 | tf_op jit(solution)/shard_map/ppermute | solution.py:304
  43.0 4.4 %copy-start.5 = (f32[512]{0:T(512)S(1)}, f32[512]{0:T(512)}, u32[]{:S(2)}) copy-start(f32[512]{0:T(512)} %param.15) | copy-start | bytes 6148
  43.0 5.2 %collective-permute-start.14 = (f32[1,512]{1,0:T(1,128)S(1)}, f32[1,512]{1,0:T(1,128)S(1)}, u32[]{:S(2)}, u32[]{:S(2)}) collective-permute-start(f32[1,512]{1,0:T(1,128)S(1)} %get-tuple-element.42.a_ref), channel_id=1, source_target_pairs={{0,2},{1,3},{2,0},{3,1},{4,6},{5,7},{6,4},{7,5},{8,10},{9,11},{10,... | collective-permute-start | bytes 6152 | tf_op jit(solution)/shard_map/ppermute | solution.py:304
  46.3 3.6 %collective-permute-start.15 = (f32[1,512]{1,0:T(1,128)S(1)}, f32[1,512]{1,0:T(1,128)S(1)}, u32[]{:S(2)}, u32[]{:S(2)}) collective-permute-start(f32[1,512]{1,0:T(1,128)S(1)} %get-tuple-element.42.a_ref), channel_id=1, source_target_pairs={{0,1},{1,0},{2,3},{3,2},{4,5},{5,4},{6,7},{7,6},{8,9},{9,8},{10,11... | collective-permute-start | bytes 6152 | tf_op jit(solution)/shard_map/ppermute | solution.py:304
  47.0 4.8 %collective-permute-start.16 = (f32[1,512]{1,0:T(1,128)S(1)}, f32[1,512]{1,0:T(1,128)S(1)}, u32[]{:S(2)}, u32[]{:S(2)}) collective-permute-start(f32[1,512]{1,0:T(1,128)S(1)} %get-tuple-element.42.a_ref), channel_id=1, source_target_pairs={{0,3},{1,2},{2,1},{3,0},{4,7},{5,6},{6,5},{7,4},{8,11},{9,10},{10,... | collective-permute-start | bytes 6152 | tf_op jit(solution)/shard_map/ppermute | solution.py:304

commit v5 on v4

--- a/solution.py
+++ b/solution.py
@@ -54,54 +54,61 @@
 
 
 def prep_body(
-    ld_hbm, v_hbm, k_hbm, d_ref, dcol_ref, vt_ref, own_ref, send_ref,
-    state_ref, ld_ref, v_ref, k_ref, sems,
+    ld_hbm, v_hbm, k_hbm, d_ref, vt_ref, own_ref, send_ref, ld_ref, v_ref, k_ref, scaled_ref, sems
 ):
-    pairs = ((ld_hbm, ld_ref), (v_hbm, v_ref), (k_hbm, k_ref))
+    pairs = ((v_hbm, v_ref), (ld_hbm, ld_ref), (k_hbm, k_ref))
     copies = [pltpu.make_async_copy(a, b, sems.at[i]) for i, (a, b) in enumerate(pairs)]
     for copy in copies:
         copy.start()
     core = core_index()
+    row = lax.broadcasted_iota(jnp.int32, (128, 128), 0)
+    col = lax.broadcasted_iota(jnp.int32, (128, 128), 1)
+    upto = (row <= col).astype(F32).astype(BF16)
+    copies[1].wait()
+    terms = []
+    for j in range(4):
+        ld = ld_ref[:, j * 128 : (j + 1) * 128]
+        terms += [*split3(ld), jnp.zeros_like(ld)]
+    sums = jnp.dot(jnp.concatenate(terms, axis=0).astype(BF16), upto, preferred_element_type=F32)
+    inner, totals = [], []
+    for j in range(4):
+        base = j * 32
+        part = sums[base : base + 8] + sums[base + 8 : base + 16] + sums[base + 16 : base + 24]
+        inner.append(part)
+        totals.append(jnp.broadcast_to(part[:, 127:128], (HEADS, 128)))
+    ahead = jnp.zeros((HEADS, 128), F32)
+    d = []
+    for j in range(4):
+        d.append(inner[j] + ahead)
+        ahead = ahead + totals[j]
+    total = ahead
+    toend = jnp.concatenate([jnp.exp(total - x) for x in d], axis=1)
+    for j in range(4):
+        d_ref[:, j * 128 : (j + 1) * 128] = d[j]
     copies[0].wait()
-    ld = ld_ref[...]
-    parts = jnp.concatenate([*split3(ld), jnp.zeros_like(ld)], axis=0).astype(BF16)
-    row = lax.broadcasted_iota(jnp.int32, (BLOCK, BLOCK), 0)
-    col = lax.broadcasted_iota(jnp.int32, (BLOCK, BLOCK), 1)
-    upto = (row <= col).astype(F32).astype(BF16)
-    sums = jnp.dot(parts, upto, preferred_element_type=F32)
-    d = sums[0:8] + sums[8:16] + sums[16:24]
-    d_ref[...] = d
-    total = jnp.broadcast_to(d[:, BLOCK - 1 : BLOCK], (HEADS, BLOCK))
-    toend = jnp.exp(total - d)
-    copies[1].wait()
     vt = v_ref[...].T
+    for h in range(HEADS):
+        rows = slice(h * WIDTH, (h + 1) * WIDTH)
+        scaled_ref[rows] = (vt[rows].astype(F32) * toend[h : h + 1]).astype(BF16)
+    copies[2].wait()
+    keys = k_ref[...]
+    for ref, side in ((send_ref, 1 - core), (own_ref, core)):
+        rows = pl.ds(pl.multiple_of(side * ROWS, ROWS), ROWS)
+        ref[0:ROWS] = jnp.dot(scaled_ref[rows, :], keys, preferred_element_type=F32)
+        ref[ROWS:BUF_ROWS] = total
     vt_ref[...] = vt
-    scaled = [
-        (vt[h * WIDTH : (h + 1) * WIDTH].astype(F32) * toend[h : h + 1]).astype(BF16)
-        for h in range(HEADS)
-    ]
-    copies[2].wait()
-    state_ref[...] = jnp.dot(
-        jnp.concatenate(scaled, axis=0), k_ref[...], preferred_element_type=F32
-    )
-    own_ref[0:ROWS] = state_ref[pl.ds(pl.multiple_of(core * ROWS, ROWS), ROWS), :]
-    own_ref[ROWS:BUF_ROWS] = total[:, 0:STATE]
-    send_ref[0:ROWS] = state_ref[pl.ds(pl.multiple_of((1 - core) * ROWS, ROWS), ROWS), :]
-    send_ref[ROWS:BUF_ROWS] = total[:, 0:STATE]
-    dcol_ref[...] = d.T
 
 
 def prep(ld, v, k):
     buf = sds((BUF_ROWS, STATE))
-    outs = [sds((HEADS, BLOCK)), sds((BLOCK, HEADS)), sds((BLOCK, BLOCK), BF16)]
-    outs += [buf, buf]
+    outs = [sds((HEADS, BLOCK)), sds((BLOCK, BLOCK), BF16), buf, buf]
     return call(
         prep_body, outs, [HB] * 3, 10**7,
         scratch=[
-            pltpu.VMEM((HEADS * WIDTH, STATE), F32),
             pltpu.VMEM((HEADS, BLOCK), F32),
             pltpu.VMEM((BLOCK, HEADS * WIDTH), BF16),
             pltpu.VMEM((BLOCK, STATE), BF16),
+            pltpu.VMEM((HEADS * WIDTH, BLOCK), BF16),
             pltpu.SemaphoreType.DMA((3,)),
         ],
     )(*(pltpu.with_memory_space_constraint(x, pltpu.HBM) for x in (ld, v, k)))
@@ -132,7 +139,7 @@
     )(own, got, *tokens)
 
 
-def aux_body(q_ref, gate_ref, qt_ref, gt_ref):
+def aux_body(q_ref, gate_ref, d_ref, qt_ref, gt_ref, dcol_ref):
     qt = q_ref[...].T
     qt_ref[0:STATE] = qt
     qt_ref[STATE : 2 * STATE] = qt
@@ -140,12 +147,12 @@
         cols = slice(j * 128, (j + 1) * 128)
         v = gate_ref[:, cols].T.astype(F32)
         gt_ref[cols] = v / (1.0 + jnp.exp(-v))
-
-
-def aux(q, gate):
-    return call(
-        aux_body, [sds((2 * STATE, BLOCK), BF16), sds((BLOCK, BLOCK))], [VM] * 2, 10**7
-    )(q, gate)
+    dcol_ref[...] = d_ref[...].T
+
+
+def aux(q, gate, d):
+    outs = [sds((2 * STATE, BLOCK), BF16), sds((BLOCK, BLOCK)), sds((BLOCK, HEADS))]
+    return call(aux_body, outs, [VM] * 3, 10**7)(q, gate, d)
 
 
 def near_body(first, k_ref, qt_ref, vt_ref, d_ref, dcol_ref, w_ref, skip_ref, token_ref, out_ref, sc_ref, mix_ref):
@@ -196,13 +203,13 @@
     )(k, qt, vt, d, dcol, w, skip, token)
 
 
-def readout(level, acc_rows, emit, qt_ref, d_ref, w_ref, lead_ref, buf_refs, coef_ref):
+def readout(level, sides, acc_rows, emit, qt_ref, d_ref, w_ref, lead, buf_refs, coef_ref):
     upper = ((lax.axis_index("tok") >> level) & 1) == 1
-    lead = lead_ref[...]
     gain = jnp.where(upper, jnp.exp(lead), 0.0)[:, 0:1]
     coef_ref[...] = w_ref[LOCAL_BITS + 1 + level] * jnp.exp(d_ref[...]) * gain
     core = core_index()
-    for side, ref in zip((core, 1 - core), buf_refs):
+    for n, ref in zip(sides, buf_refs):
+        side = core if n == 0 else 1 - core
         states = ref[0:ROWS]
         hi = states.astype(BF16)
         lo = (states - hi.astype(F32)).astype(BF16)
@@ -212,8 +219,6 @@
             row = pl.multiple_of(head * WIDTH, WIDTH)
             term = read[j * WIDTH : (j + 1) * WIDTH] * coef_ref[pl.ds(head, 1), :]
             emit(row, acc_rows(row) + term)
-    got = buf_refs[0][ROWS:BUF_ROWS]
-    return lead + jnp.where(upper, got, 0.0)
 
 
 def far_body(level, qt_ref, d_ref, w_ref, lead_ref, *rest):
@@ -226,7 +231,10 @@
     def start(row):
         return rest[2][pl.ds(row, WIDTH), :] if level > 0 else 0.0
 
-    next_ref[...] = readout(level, start, emit, qt_ref, d_ref, w_ref, lead_ref, bufs, coef_ref)
+    lead = lead_ref[...]
+    readout(level, (0, 1), start, emit, qt_ref, d_ref, w_ref, lead, bufs, coef_ref)
+    upper = ((lax.axis_index("tok") >> level) & 1) == 1
+    next_ref[...] = lead + jnp.where(upper, bufs[0][ROWS:BUF_ROWS], 0.0)
     if level > 0:
         rows = slice((level - 1) * 2 * WIDTH, level * 2 * WIDTH)
         out_ref[rows] = out_ref[rows] + rest[3][...]
@@ -241,38 +249,43 @@
     )(qt, d, w, lead, *bufs, *more)
 
 
-def close_body(level, qt_ref, d_ref, w_ref, lead_ref, acc_ref, gt_ref, *rest):
-    bufs, out_ref, sq_ref, coef_ref = rest[:2], rest[-3], rest[-2], rest[-1]
-    sums = []
+def close_body(level, side, qt_ref, d_ref, w_ref, lead_ref, acc_ref, gt_ref, buf_ref, *rest):
+    out_ref, sq_ref, coef_ref = rest[-3:]
+    sums = [] if side == 0 else [rest[0][...]]
+    half = core_index() if side == 0 else 1 - core_index()
 
     def emit(row, value):
         gated = value * gt_ref[pl.ds(row, WIDTH), :]
-        out_ref[pl.ds(row, WIDTH), :] = gated
+        out_ref[pl.ds(pl.multiple_of(row - half * ROWS, WIDTH), WIDTH), :] = gated
         sums.append(jnp.sum(gated * gated, axis=0, keepdims=True))
 
     readout(
-        level, lambda row: acc_ref[pl.ds(row, WIDTH), :], emit,
-        qt_ref, d_ref, w_ref, lead_ref, bufs, coef_ref,
+        level, (side,), lambda row: acc_ref[pl.ds(row, WIDTH), :], emit,
+        qt_ref, d_ref, w_ref, lead_ref[...], (buf_ref,), coef_ref,
     )
     sq_ref[...] = sum(sums[1:], sums[0])
 
 
-def close(level, qt, d, w, lead, acc, gt, bufs):
-    return call(
-        functools.partial(close_body, level), [sds((BLOCK, BLOCK)), sds((1, BLOCK))],
-        [VM] * 8, 10**7,
+def close(level, side, qt, d, w, lead, acc, gt, buf, *more):
+    return call(
+        functools.partial(close_body, level, side), [sds((ROWS, BLOCK)), sds((1, BLOCK))],
+        [VM] * (7 + len(more)), 10**7,
         scratch=[pltpu.VMEM((HEADS, BLOCK), F32)],
-    )(qt, d, w, lead, acc, gt, *bufs)
-
-
-def turn_body(g_ref, gain_ref, out_ref):
-    for j in range(4):
-        rows = slice(j * 128, (j + 1) * 128)
-        out_ref[rows] = g_ref[:, rows].T * gain_ref[...]
-
-
-def turn(g, gain):
-    return call(turn_body, sds((BLOCK, BLOCK)), [VM] * 2, 10**7)(g, gain)
+    )(qt, d, w, lead, acc, gt, buf, *more)
+
+
+def turn_body(own_ref, other_ref, gain_ref, out_ref):
+    core = core_index()
+    for ref, side in ((own_ref, core), (other_ref, 1 - core)):
+        cols = pl.ds(pl.multiple_of(side * ROWS, ROWS), ROWS)
+        gain = gain_ref[:, cols]
+        for j in range(4):
+            rows = slice(j * 128, (j + 1) * 128)
+            out_ref[rows, cols] = ref[:, rows].T * gain
+
+
+def turn(own, other, gain):
+    return call(turn_body, sds((BLOCK, BLOCK)), [VM] * 3, 10**7)(own, other, gain)
 
 
 def finish_body(width, g_ref, a_ref, b_ref, c_ref, e_ref, out_hbm, out_ref, sems):
@@ -304,48 +317,53 @@
     return lax.ppermute(x, axis, [(i, i ^ flip) for i in range(count)])
 
 
-CORE, Z1, Z2, Z3, Z7, X1, X2, X3 = 1, 2, 4, 6, 14, 16, 32, 48
+CORE, Z1, Z3, Z7, X1, X2, X3 = 1, 2, 6, 14, 16, 32, 48
 
 
 def work(head_inputs, state_keys, state_queries, log_decay, level_weight, skip_scale, gate_input, norm_gain):
     w = level_weight.transpose(2, 1, 0)
-    d, dcol, vt, own, send = prep(log_decay.T, head_inputs, state_keys)
+    d, vt, own, send = prep(log_decay.T, head_inputs, state_keys)
     swap = lambda x: hop(x, "tok", CORE)
-    close_by = lambda first, token: near(
-        first, state_keys, qt, vt, d, dcol, w, skip_scale, token
-    )
-    step = lambda level, lead, bufs, *more: far(level, qt, d, w, lead, bufs, *more)
+
+    def close_by(first, token):
+        return near(first, state_keys, qt, vt, d, dcol, w, skip_scale, token)
+
+    def step(level, lead, bufs, *more):
+        return far(level, qt, d, w, lead, bufs, *more)
+
     got = swap(send)
-    qt, gt = aux(state_queries, gate_input)
+    qt, gt, dcol = aux(state_queries, gate_input, d)
     chip = merge(0, own, got, gt)
     levels = [(got, swap(own))]
-    parts = [close_by(0, chip), close_by(2, chip)]
-    z2 = hop(chip, "tok", Z2)
+    parts = [close_by(0, chip)]
     z1 = hop(chip, "tok", Z1)
-    z3 = hop(chip, "tok", Z3)
-    pair = merge(1, chip, z1)
-    across = merge(1, z2, z3)
-    quad = merge(2, pair, across, *parts)
-    levels += [(z1, swap(z1)), (across, swap(across))]
+    pair = merge(1, chip, z1, parts[0])
+    levels.append((z1, swap(z1)))
+    parts.append(close_by(2, pair))
+    acc, lead = step(0, jnp.zeros((HEADS, STATE), F32), levels[0])
+    z3 = hop(pair, "tok", Z3)
+    quad = merge(2, pair, z3, parts[1], acc)
+    levels.append((z3, swap(z3)))
     parts.append(close_by(4, quad))
-    acc, lead = step(0, jnp.zeros((HEADS, STATE), F32), levels[0])
     acc, lead = step(1, lead, levels[1], acc, parts[0])
     z7 = hop(quad, "tok", Z7)
+    acc, lead = step(2, lead, levels[2], acc, parts[1])
     line = merge(3, quad, z7, parts[2], acc)
     levels.append((z7, swap(z7)))
     parts.append(close_by(6, line))
-    acc, lead = step(2, lead, levels[2], acc, parts[1])
+    acc, lead = step(3, lead, levels[3], acc, parts[2])
     x2 = hop(line, "tok", X2)
     x1 = hop(line, "tok", X1)
     x3 = hop(line, "tok", X3)
     levels.append((x1, swap(x1)))
     beyond = merge(4, x2, x3, parts[3], acc)
-    levels.append((beyond, swap(beyond)))
-    acc, lead = step(3, lead, levels[3], acc, parts[2])
+    other = swap(beyond)
     acc, lead = step(4, lead, levels[4], acc, parts[3])
-    gated, squares = close(5, qt, d, w, lead, acc, gt, levels[5])
+    last = (qt, d, w, lead, acc, gt)
+    mine, part = close(5, 0, *last, beyond)
+    rest, squares = close(5, 1, *last, other, part)
     shares = [hop(squares, "head", 2), hop(squares, "head", 1), hop(squares, "head", 3)]
-    turned = turn(gated, norm_gain[None])
+    turned = turn(mine, rest, norm_gain[None])
     return finish(HEADS * WIDTH * lax.axis_size("head"), turned, [squares, *shares])
 
 

time: 53.9 us -> 55.1 us (1.022)
  the two profiles are of different devices: /device:TPU:32 before, /device:TPU:1 now
where the time goes in v5:
time: 55.1 us; the launch traced here: 54.9 us
  starting transfers between devices  25.2 us (46%)
  waiting for transfers between devices  16.7 us (30%)
  Pallas kernels  11.3 us (21%)
  local copies, waits for them, and re-layouts  1.38 us (3%)
    ppermute x16, starting transfers between devices, hop(): return lax.ppermute(x, axis, [(i, i ^ flip) for i in range(count)])  25.2 us
    ppermute x16, waiting for transfers between devices, hop(): return lax.ppermute(x, axis, [(i, i ^ flip) for i in range(count)])  16.7 us
    pallas_call x4, Pallas kernels, near(): call(functools.partial(near_body, first), sds((2 * WIDTH, BLOCK)), [VM] *...  5.49 us
    pallas_call x5, Pallas kernels, far(): call(functools.partial(far_body, level), [sds((BLOCK, BLOCK)), sds((HEADS...  1.74 us
    pallas_call x1, Pallas kernels, prep(): call(prep_body, outs, [HB] * 3, 10 ** 7, scratch=[pltpu.VMEM((HEADS, BLOC...  1.7 us
    unnamed x12, local copies, waits for them, and re-layouts  1.38 us
  transfers between devices with their start and end apart: 16, of which 9 were waited for; matrix products, arithmetic and copies ran while one was open for 0% of the time, Pallas kernels for 15%

profile of v5, /device:TPU:1, one launch (start us, length us, event | category | flops | bytes accessed | tf_op | source)
XLA Modules:
  0.0 54.9 jit_solution(6646281778695035746)
XLA Ops:
  0.0 0.0 copy-start.2
  0.0 0.0 copy-start.3
  0.0 1.7 %shard_map.82 = (f32[8,512]{1,0:T(8,128)S(1)}, bf16[512,512]{1,0:T(8,128)(2,1)S(1)}, f32[264,128]{1,0:T(8,128)S(1)}, f32[264,128]{1,0:T(8,128)S(1)}) custom-call(f32[8,512]{1,0:T(8,128)} %bitcast.15, bf16[512,512]{1,0:T(8,128)(2,1)} %v_hbm.1, bf16[512,128]{1,0:T(8,128)(2,1)} %k_ref.7), custom_call_target="tpu_custom_call" | custom-call | flops 10000000 | bytes 1048576 | tf_op jit(solution)/shard_map/pallas_call | solution.py:105
  1.7 3.3 %collective-permute-start = (f32[264,128]{1,0:T(8,128)S(1)}, f32[264,128]{1,0:T(8,128)S(1)}, u32[]{:S(2)}, u32[]{:S(2)}) collective-permute-start(f32[264,128]{1,0:T(8,128)S(1)} %get-tuple-element.28), channel_id=1, source_target_pairs={{0,4},{4,0},{8,12},{12,8},{16,20},{20,16},{24,28},{28,24},{32,36},... | collective-permute-start | bytes 405512 | tf_op jit(solution)/shard_map/ppermute | solution.py:317
  5.0 0.0 copy-done.2
  5.0 0.0 copy-done.3
  5.0 0.4 shard_map.83
  5.4 0.6 %collective-permute-done.rest_0_.got_ref = f32[264,128]{1,0:T(8,128)S(1)} collective-permute-done((f32[264,128]{1,0:T(8,128)S(1)}, f32[264,128]{1,0:T(8,128)S(1)}, u32[]{:S(2)}, u32[]{:S(2)}) %collective-permute-start) | collective-permute-done | bytes 135200 | tf_op jit(solution)/shard_map/ppermute | solution.py:317
  6.0 0.0 copy-start
  6.0 0.0 copy-start.1
  6.0 0.1 collective-permute-start.2
  6.1 0.6 %collective-permute-start.1 = (f32[264,128]{1,0:T(8,128)S(1)}, f32[264,128]{1,0:T(8,128)S(1)}, u32[]{:S(2)}, u32[]{:S(2)}) collective-permute-start(f32[264,128]{1,0:T(8,128)S(1)} %get-tuple-element.29.own_ref), channel_id=1, source_target_pairs={{0,4},{4,0},{8,12},{12,8},{16,20},{20,16},{24,28},{28,24},{32,36},... | collective-permute-start | bytes 405512 | tf_op jit(solution)/shard_map/ppermute | solution.py:317
  6.7 0.0 copy-start.4
  6.7 0.3 copy-done
  7.0 0.0 copy-done.1
  7.0 0.4 copy-done.4
  7.4 1.4 %shard_map.86.rest_3_.refs_0_ = f32[128,512]{1,0:T(8,128)S(1)} custom-call(bf16[512,128]{1,0:T(8,128)(2,1)S(1)} %copy-done.1, bf16[256,512]{1,0:T(8,128)(2,1)S(1)} %get-tuple-element.27.qt_ref, bf16[512,512]{1,0:T(8,128)(2,1)S(1)} %get-tuple-element.33.vt_ref, f32[8,512]{1,0:T(8,128)S(1)} %get-tuple-element.26.d_ref, ...), custom_call_target="tpu_custom_call" | custom-call | flops 10000000 | bytes 1048576 | tf_op jit(solution)/shard_map/pallas_call | solution.py:199
  8.8 2.1 %collective-permute-done.2.rest_0_.got_ref = f32[264,128]{1,0:T(8,128)S(1)} collective-permute-done((f32[264,128]{1,0:T(8,128)S(1)}, f32[264,128]{1,0:T(8,128)S(1)}, u32[]{:S(2)}, u32[]{:S(2)}) %collective-permute-start.2) | collective-permute-done | bytes 135200 | tf_op jit(solution)/shard_map/ppermute | solution.py:317
  10.9 2.7 %collective-permute-start.4 = (f32[264,128]{1,0:T(8,128)S(1)}, f32[264,128]{1,0:T(8,128)S(1)}, u32[]{:S(2)}, u32[]{:S(2)}) collective-permute-start(f32[264,128]{1,0:T(8,128)S(1)} %shard_map.88.token_ref.own_ref), channel_id=1, source_target_pairs={{0,24},{4,28},{8,16},{12,20},{16,8},{20,12},{24,0},{28,4},{32,56},... | collective-permute-start | bytes 405512 | tf_op jit(solution)/shard_map/ppermute | solution.py:317
  13.7 1.5 %collective-permute-start.3 = (f32[264,128]{1,0:T(8,128)S(1)}, f32[264,128]{1,0:T(8,128)S(1)}, u32[]{:S(2)}, u32[]{:S(2)}) collective-permute-start(f32[264,128]{1,0:T(8,128)S(1)} %collective-permute-done.2.rest_0_.got_ref), channel_id=1, source_target_pairs={{0,4},{4,0},{8,12},{12,8},{16,20},{20,16},{24,28},{28,24},{32,36},... | collective-permute-start | bytes 405512 | tf_op jit(solution)/shard_map/ppermute | solution.py:317
  15.2 0.0 collective-permute-done.1.rest_1_
  15.2 0.3 shard_map.84
  15.5 1.3 %collective-permute-done.4.rest_0_.got_ref = f32[264,128]{1,0:T(8,128)S(1)} collective-permute-done((f32[264,128]{1,0:T(8,128)S(1)}, f32[264,128]{1,0:T(8,128)S(1)}, u32[]{:S(2)}, u32[]{:S(2)}) %collective-permute-start.4) | collective-permute-done | bytes 135200 | tf_op jit(solution)/shard_map/ppermute | solution.py:317
  16.8 2.3 %collective-permute-start.5 = (f32[264,128]{1,0:T(8,128)S(1)}, f32[264,128]{1,0:T(8,128)S(1)}, u32[]{:S(2)}, u32[]{:S(2)}) collective-permute-start(f32[264,128]{1,0:T(8,128)S(1)} %collective-permute-done.4.rest_0_.got_ref), channel_id=1, source_target_pairs={{0,4},{4,0},{8,12},{12,8},{16,20},{20,16},{24,28},{28,24},{32,36},... | collective-permute-start | bytes 405512 | tf_op jit(solution)/shard_map/ppermute | solution.py:317
  19.1 1.4 %shard_map.89.rest_3_.refs_0_ = f32[128,512]{1,0:T(8,128)S(1)} custom-call(bf16[512,128]{1,0:T(8,128)(2,1)S(1)} %copy-done.1, bf16[256,512]{1,0:T(8,128)(2,1)S(1)} %get-tuple-element.27.qt_ref, bf16[512,512]{1,0:T(8,128)(2,1)S(1)} %get-tuple-element.33.vt_ref, f32[8,512]{1,0:T(8,128)S(1)} %get-tuple-element.26.d_ref, ...), custom_call_target="tpu_custom_call" | custom-call | flops 10000000 | bytes 1048576 | tf_op jit(solution)/shard_map/pallas_call | solution.py:199
  20.5 4.0 %collective-permute-start.6 = (f32[264,128]{1,0:T(8,128)S(1)}, f32[264,128]{1,0:T(8,128)S(1)}, u32[]{:S(2)}, u32[]{:S(2)}) collective-permute-start(f32[264,128]{1,0:T(8,128)S(1)} %shard_map.91.token_ref.own_ref), channel_id=1, source_target_pairs={{0,56},{4,60},{8,48},{12,52},{16,40},{20,44},{24,32},{28,36},{32,2... | collective-permute-start | bytes 405512 | tf_op jit(solution)/shard_map/ppermute | solution.py:317
  24.4 1.4 %shard_map.92.rest_3_.refs_0_ = f32[128,512]{1,0:T(8,128)S(1)} custom-call(bf16[512,128]{1,0:T(8,128)(2,1)S(1)} %copy-done.1, bf16[256,512]{1,0:T(8,128)(2,1)S(1)} %get-tuple-element.27.qt_ref, bf16[512,512]{1,0:T(8,128)(2,1)S(1)} %get-tuple-element.33.vt_ref, f32[8,512]{1,0:T(8,128)S(1)} %get-tuple-element.26.d_ref, ...), custom_call_target="tpu_custom_call" | custom-call | flops 10000000 | bytes 1048576 | tf_op jit(solution)/shard_map/pallas_call | solution.py:199
  25.8 0.0 collective-permute-done.3.rest_1_
  25.8 0.4 shard_map.87
  26.2 0.0 collective-permute-done.5.rest_1_
  26.2 0.4 shard_map.90
  26.6 4.7 %collective-permute-done.6.rest_0_.got_ref = f32[264,128]{1,0:T(8,128)S(1)} collective-permute-done((f32[264,128]{1,0:T(8,128)S(1)}, f32[264,128]{1,0:T(8,128)S(1)}, u32[]{:S(2)}, u32[]{:S(2)}) %collective-permute-start.6) | collective-permute-done | bytes 135200 | tf_op jit(solution)/shard_map/ppermute | solution.py:317
  31.3 1.3 %collective-permute-start.8 = (f32[264,128]{1,0:T(8,128)S(1)}, f32[264,128]{1,0:T(8,128)S(1)}, u32[]{:S(2)}, u32[]{:S(2)}) collective-permute-start(f32[264,128]{1,0:T(8,128)S(1)} %shard_map.94.token_ref), channel_id=1, source_target_pairs={{0,64},{4,68},{8,72},{12,76},{16,80},{20,84},{24,88},{28,92},{32,9... | collective-permute-start | bytes 405512 | tf_op jit(solution)/shard_map/ppermute | solution.py:317
  32.6 0.9 %collective-permute-start.7 = (f32[264,128]{1,0:T(8,128)S(1)}, f32[264,128]{1,0:T(8,128)S(1)}, u32[]{:S(2)}, u32[]{:S(2)}) collective-permute-start(f32[264,128]{1,0:T(8,128)S(1)} %collective-permute-done.6.rest_0_.got_ref), channel_id=1, source_target_pairs={{0,4},{4,0},{8,12},{12,8},{16,20},{20,16},{24,28},{28,24},{32,36},... | collective-permute-start | bytes 405512 | tf_op jit(solution)/shard_map/ppermute | solution.py:317
  33.5 2.5 %collective-permute-start.10 = (f32[264,128]{1,0:T(8,128)S(1)}, f32[264,128]{1,0:T(8,128)S(1)}, u32[]{:S(2)}, u32[]{:S(2)}) collective-permute-start(f32[264,128]{1,0:T(8,128)S(1)} %shard_map.94.token_ref), channel_id=1, source_target_pairs={{0,128},{4,132},{8,136},{12,140},{16,144},{20,148},{24,152},{28,15... | collective-permute-start | bytes 405512 | tf_op jit(solution)/shard_map/ppermute | solution.py:317
  35.9 0.2 collective-permute-start.11
  36.1 0.0 collective-permute-done.8.rest_0_
  36.1 1.3 %collective-permute-start.9 = (f32[264,128]{1,0:T(8,128)S(1)}, f32[264,128]{1,0:T(8,128)S(1)}, u32[]{:S(2)}, u32[]{:S(2)}) collective-permute-start(f32[264,128]{1,0:T(8,128)S(1)} %collective-permute-done.8.rest_0_), channel_id=1, source_target_pairs={{0,4},{4,0},{8,12},{12,8},{16,20},{20,16},{24,28},{28,24},{32,36},... | collective-permute-start | bytes 405512 | tf_op jit(solution)/shard_map/ppermute | solution.py:317
  37.4 1.4 %shard_map.95.rest_3_.refs_0_ = f32[128,512]{1,0:T(8,128)S(1)} custom-call(bf16[512,128]{1,0:T(8,128)(2,1)S(1)} %copy-done.1, bf16[256,512]{1,0:T(8,128)(2,1)S(1)} %get-tuple-element.27.qt_ref, bf16[512,512]{1,0:T(8,128)(2,1)S(1)} %get-tuple-element.33.vt_ref, f32[8,512]{1,0:T(8,128)S(1)} %get-tuple-element.26.d_ref, ...), custom_call_target="tpu_custom_call" | custom-call | flops 10000000 | bytes 1048576 | tf_op jit(solution)/shard_map/pallas_call | solution.py:199
  38.8 0.0 collective-permute-done.7.rest_1_
  38.8 0.3 shard_map.93
  39.2 1.9 %collective-permute-done.10.own_ref = f32[264,128]{1,0:T(8,128)S(1)} collective-permute-done((f32[264,128]{1,0:T(8,128)S(1)}, f32[264,128]{1,0:T(8,128)S(1)}, u32[]{:S(2)}, u32[]{:S(2)}) %collective-permute-start.10) | collective-permute-done | bytes 135200 | tf_op jit(solution)/shard_map/ppermute | solution.py:317
  41.1 3.4 %collective-permute-done.11.got_ref = f32[264,128]{1,0:T(8,128)S(1)} collective-permute-done((f32[264,128]{1,0:T(8,128)S(1)}, f32[264,128]{1,0:T(8,128)S(1)}, u32[]{:S(2)}, u32[]{:S(2)}) %collective-permute-start.11) | collective-permute-done | bytes 135200 | tf_op jit(solution)/shard_map/ppermute | solution.py:317
  44.5 1.0 %collective-permute-start.12 = (f32[264,128]{1,0:T(8,128)S(1)}, f32[264,128]{1,0:T(8,128)S(1)}, u32[]{:S(2)}, u32[]{:S(2)}) collective-permute-start(f32[264,128]{1,0:T(8,128)S(1)} %shard_map.97.buf_ref), channel_id=1, source_target_pairs={{0,4},{4,0},{8,12},{12,8},{16,20},{20,16},{24,28},{28,24},{32,36},... | collective-permute-start | bytes 405512 | tf_op jit(solution)/shard_map/ppermute | solution.py:317
  45.5 0.0 collective-permute-done.9.rest_1_
  45.5 0.3 shard_map.96
  45.9 0.3 shard_map.98
  46.2 0.3 collective-permute-done.12.buf_ref
  46.5 0.3 shard_map.99
  46.8 3.0 %collective-permute-start.13 = (f32[1,512]{1,0:T(1,128)S(1)}, f32[1,512]{1,0:T(1,128)S(1)}, u32[]{:S(2)}, u32[]{:S(2)}) collective-permute-start(f32[1,512]{1,0:T(1,128)S(1)} %get-tuple-element.46.a_ref), channel_id=1, source_target_pairs={{0,2},{1,3},{2,0},{3,1},{4,6},{5,7},{6,4},{7,5},{8,10},{9,11},{10,... | collective-permute-start | bytes 6152 | tf_op jit(solution)/shard_map/ppermute | solution.py:317
  49.8 0.4 collective-permute-start.14
  50.2 0.4 collective-permute-start.15
  50.6 0.0 copy-start.5
  50.6 0.7 %copy-done.5 = f32[512]{0:T(512)S(1)} copy-done((f32[512]{0:T(512)S(1)}, f32[512]{0:T(512)}, u32[]{:S(2)}) %copy-start.5) | copy-done | bytes 2072
  51.2 0.3 shard_map.100.g_ref
  51.6 0.0 collective-permute-done.13.b_ref
  51.6 0.6 %collective-permute-done.14.c_ref = f32[1,512]{1,0:T(1,128)S(1)} collective-permute-done((f32[1,512]{1,0:T(1,128)S(1)}, f32[1,512]{1,0:T(1,128)S(1)}, u32[]{:S(2)}, u32[]{:S(2)}) %collective-permute-start.14) | collective-permute-done | bytes 2080 | tf_op jit(solution)/shard_map/ppermute | solution.py:317
  52.2 1.6 %collective-permute-done.15.e_ref = f32[1,512]{1,0:T(1,128)S(1)} collective-permute-done((f32[1,512]{1,0:T(1,128)S(1)}, f32[1,512]{1,0:T(1,128)S(1)}, u32[]{:S(2)}, u32[]{:S(2)}) %collective-permute-start.15) | collective-permute-done | bytes 2080 | tf_op jit(solution)/shard_map/ppermute | solution.py:317
  53.8 0.9 %shard_map.101 = bf16[512,512]{1,0:T(8,128)(2,1)} custom-call(f32[512,512]{1,0:T(8,128)S(1)} %shard_map.100.g_ref, f32[1,512]{1,0:T(1,128)S(1)} %get-tuple-element.46.a_ref, f32[1,512]{1,0:T(1,128)S(1)} %collective-permute-done.13.b_ref, f32[1,512]{1,0:T(1,128)S(1)} %collective-permute-done.14.c_ref, f32[1,512]{1,0:T(1,128)S(1)} %collective-permute-done.15.e_ref), custom_call_target="tpu_custom_call" | custom-call | flops 100000000 | bytes 1048576 | tf_op jit(solution)/shard_map/pallas_call | solution.py:308
  (6 shorter events, 0.2 us)
Async XLA Ops:
  0.0 5.0 %copy-start.2 = (bf16[512,512]{1,0:T(8,128)(2,1)S(1)}, bf16[512,512]{1,0:T(8,128)(2,1)}, u32[]{:S(2)}) copy-start(bf16[512,512]{1,0:T(8,128)(2,1)} %gate_ref.1) | copy-start | bytes 1572868
  0.0 5.0 %copy-start.3 = (bf16[512,128]{1,0:T(8,128)(2,1)S(1)}, bf16[512,128]{1,0:T(8,128)(2,1)}, u32[]{:S(2)}) copy-start(bf16[512,128]{1,0:T(8,128)(2,1)} %q_ref.1) | copy-start | bytes 393220
  1.7 4.3 %collective-permute-start = (f32[264,128]{1,0:T(8,128)S(1)}, f32[264,128]{1,0:T(8,128)S(1)}, u32[]{:S(2)}, u32[]{:S(2)}) collective-permute-start(f32[264,128]{1,0:T(8,128)S(1)} %get-tuple-element.28), channel_id=1, source_target_pairs={{0,4},{4,0},{8,12},{12,8},{16,20},{20,16},{24,28},{28,24},{32,36},... | collective-permute-start | bytes 405512 | tf_op jit(solution)/shard_map/ppermute | solution.py:317
  6.0 1.0 %copy-start = (f32[512,8,18]{0,1,2:T(8,128)S(1)}, f32[512,8,18]{0,1,2:T(8,128)}, u32[]{:S(2)}) copy-start(f32[512,8,18]{0,1,2:T(8,128)} %param.12) | copy-start | bytes 884740
  6.0 1.0 %copy-start.1 = (bf16[512,128]{1,0:T(8,128)(2,1)S(1)}, bf16[512,128]{1,0:T(8,128)(2,1)}, u32[]{:S(2)}) copy-start(bf16[512,128]{1,0:T(8,128)(2,1)} %k_ref.7) | copy-start | bytes 393220
  6.0 4.9 %collective-permute-start.2 = (f32[264,128]{1,0:T(8,128)S(1)}, f32[264,128]{1,0:T(8,128)S(1)}, u32[]{:S(2)}, u32[]{:S(2)}) collective-permute-start(f32[264,128]{1,0:T(8,128)S(1)} %shard_map.85.token_ref.own_ref), channel_id=1, source_target_pairs={{0,8},{4,12},{8,0},{12,4},{16,24},{20,28},{24,16},{28,20},{32,40},... | collective-permute-start | bytes 405512 | tf_op jit(solution)/shard_map/ppermute | solution.py:317
  6.1 9.0 %collective-permute-start.1 = (f32[264,128]{1,0:T(8,128)S(1)}, f32[264,128]{1,0:T(8,128)S(1)}, u32[]{:S(2)}, u32[]{:S(2)}) collective-permute-start(f32[264,128]{1,0:T(8,128)S(1)} %get-tuple-element.29.own_ref), channel_id=1, source_target_pairs={{0,4},{4,0},{8,12},{12,8},{16,20},{20,16},{24,28},{28,24},{32,36},... | collective-permute-start | bytes 405512 | tf_op jit(solution)/shard_map/ppermute | solution.py:317
  6.7 0.7 %copy-start.4 = (f32[8]{0:T(128)S(1)}, f32[8]{0:T(128)}, u32[]{:S(2)}) copy-start(f32[8]{0:T(128)} %skip_ref.7) | copy-start | bytes 100
  10.9 5.8 %collective-permute-start.4 = (f32[264,128]{1,0:T(8,128)S(1)}, f32[264,128]{1,0:T(8,128)S(1)}, u32[]{:S(2)}, u32[]{:S(2)}) collective-permute-start(f32[264,128]{1,0:T(8,128)S(1)} %shard_map.88.token_ref.own_ref), channel_id=1, source_target_pairs={{0,24},{4,28},{8,16},{12,20},{16,8},{20,12},{24,0},{28,4},{32,56},... | collective-permute-start | bytes 405512 | tf_op jit(solution)/shard_map/ppermute | solution.py:317
  13.7 12.1 %collective-permute-start.3 = (f32[264,128]{1,0:T(8,128)S(1)}, f32[264,128]{1,0:T(8,128)S(1)}, u32[]{:S(2)}, u32[]{:S(2)}) collective-permute-start(f32[264,128]{1,0:T(8,128)S(1)} %collective-permute-done.2.rest_0_.got_ref), channel_id=1, source_target_pairs={{0,4},{4,0},{8,12},{12,8},{16,20},{20,16},{24,28},{28,24},{32,36},... | collective-permute-start | bytes 405512 | tf_op jit(solution)/shard_map/ppermute | solution.py:317
  16.8 9.4 %collective-permute-start.5 = (f32[264,128]{1,0:T(8,128)S(1)}, f32[264,128]{1,0:T(8,128)S(1)}, u32[]{:S(2)}, u32[]{:S(2)}) collective-permute-start(f32[264,128]{1,0:T(8,128)S(1)} %collective-permute-done.4.rest_0_.got_ref), channel_id=1, source_target_pairs={{0,4},{4,0},{8,12},{12,8},{16,20},{20,16},{24,28},{28,24},{32,36},... | collective-permute-start | bytes 405512 | tf_op jit(solution)/shard_map/ppermute | solution.py:317
  20.5 10.8 %collective-permute-start.6 = (f32[264,128]{1,0:T(8,128)S(1)}, f32[264,128]{1,0:T(8,128)S(1)}, u32[]{:S(2)}, u32[]{:S(2)}) collective-permute-start(f32[264,128]{1,0:T(8,128)S(1)} %shard_map.91.token_ref.own_ref), channel_id=1, source_target_pairs={{0,56},{4,60},{8,48},{12,52},{16,40},{20,44},{24,32},{28,36},{32,2... | collective-permute-start | bytes 405512 | tf_op jit(solution)/shard_map/ppermute | solution.py:317
  31.3 4.8 %collective-permute-start.8 = (f32[264,128]{1,0:T(8,128)S(1)}, f32[264,128]{1,0:T(8,128)S(1)}, u32[]{:S(2)}, u32[]{:S(2)}) collective-permute-start(f32[264,128]{1,0:T(8,128)S(1)} %shard_map.94.token_ref), channel_id=1, source_target_pairs={{0,64},{4,68},{8,72},{12,76},{16,80},{20,84},{24,88},{28,92},{32,9... | collective-permute-start | bytes 405512 | tf_op jit(solution)/shard_map/ppermute | solution.py:317
  32.6 6.2 %collective-permute-start.7 = (f32[264,128]{1,0:T(8,128)S(1)}, f32[264,128]{1,0:T(8,128)S(1)}, u32[]{:S(2)}, u32[]{:S(2)}) collective-permute-start(f32[264,128]{1,0:T(8,128)S(1)} %collective-permute-done.6.rest_0_.got_ref), channel_id=1, source_target_pairs={{0,4},{4,0},{8,12},{12,8},{16,20},{20,16},{24,28},{28,24},{32,36},... | collective-permute-start | bytes 405512 | tf_op jit(solution)/shard_map/ppermute | solution.py:317
  33.5 7.6 %collective-permute-start.10 = (f32[264,128]{1,0:T(8,128)S(1)}, f32[264,128]{1,0:T(8,128)S(1)}, u32[]{:S(2)}, u32[]{:S(2)}) collective-permute-start(f32[264,128]{1,0:T(8,128)S(1)} %shard_map.94.token_ref), channel_id=1, source_target_pairs={{0,128},{4,132},{8,136},{12,140},{16,144},{20,148},{24,152},{28,15... | collective-permute-start | bytes 405512 | tf_op jit(solution)/shard_map/ppermute | solution.py:317
  35.9 8.6 %collective-permute-start.11 = (f32[264,128]{1,0:T(8,128)S(1)}, f32[264,128]{1,0:T(8,128)S(1)}, u32[]{:S(2)}, u32[]{:S(2)}) collective-permute-start(f32[264,128]{1,0:T(8,128)S(1)} %shard_map.94.token_ref), channel_id=1, source_target_pairs={{0,192},{4,196},{8,200},{12,204},{16,208},{20,212},{24,216},{28,22... | collective-permute-start | bytes 405512 | tf_op jit(solution)/shard_map/ppermute | solution.py:317
  36.1 9.4 %collective-permute-start.9 = (f32[264,128]{1,0:T(8,128)S(1)}, f32[264,128]{1,0:T(8,128)S(1)}, u32[]{:S(2)}, u32[]{:S(2)}) collective-permute-start(f32[264,128]{1,0:T(8,128)S(1)} %collective-permute-done.8.rest_0_), channel_id=1, source_target_pairs={{0,4},{4,0},{8,12},{12,8},{16,20},{20,16},{24,28},{28,24},{32,36},... | collective-permute-start | bytes 405512 | tf_op jit(solution)/shard_map/ppermute | solution.py:317
  44.5 2.0 %collective-permute-start.12 = (f32[264,128]{1,0:T(8,128)S(1)}, f32[264,128]{1,0:T(8,128)S(1)}, u32[]{:S(2)}, u32[]{:S(2)}) collective-permute-start(f32[264,128]{1,0:T(8,128)S(1)} %shard_map.97.buf_ref), channel_id=1, source_target_pairs={{0,4},{4,0},{8,12},{12,8},{16,20},{20,16},{24,28},{28,24},{32,36},... | collective-permute-start | bytes 405512 | tf_op jit(solution)/shard_map/ppermute | solution.py:317
  46.8 4.8 %collective-permute-start.13 = (f32[1,512]{1,0:T(1,128)S(1)}, f32[1,512]{1,0:T(1,128)S(1)}, u32[]{:S(2)}, u32[]{:S(2)}) collective-permute-start(f32[1,512]{1,0:T(1,128)S(1)} %get-tuple-element.46.a_ref), channel_id=1, source_target_pairs={{0,2},{1,3},{2,0},{3,1},{4,6},{5,7},{6,4},{7,5},{8,10},{9,11},{10,... | collective-permute-start | bytes 6152 | tf_op jit(solution)/shard_map/ppermute | solution.py:317
  49.8 2.4 %collective-permute-start.14 = (f32[1,512]{1,0:T(1,128)S(1)}, f32[1,512]{1,0:T(1,128)S(1)}, u32[]{:S(2)}, u32[]{:S(2)}) collective-permute-start(f32[1,512]{1,0:T(1,128)S(1)} %get-tuple-element.46.a_ref), channel_id=1, source_target_pairs={{0,1},{1,0},{2,3},{3,2},{4,5},{5,4},{6,7},{7,6},{8,9},{9,8},{10,11... | collective-permute-start | bytes 6152 | tf_op jit(solution)/shard_map/ppermute | solution.py:317
  50.2 3.6 %collective-permute-start.15 = (f32[1,512]{1,0:T(1,128)S(1)}, f32[1,512]{1,0:T(1,128)S(1)}, u32[]{:S(2)}, u32[]{:S(2)}) collective-permute-start(f32[1,512]{1,0:T(1,128)S(1)} %get-tuple-element.46.a_ref), channel_id=1, source_target_pairs={{0,3},{1,2},{2,1},{3,0},{4,7},{5,6},{6,5},{7,4},{8,11},{9,10},{10,... | collective-permute-start | bytes 6152 | tf_op jit(solution)/shard_map/ppermute | solution.py:317
  50.6 0.7 %copy-start.5 = (f32[512]{0:T(512)S(1)}, f32[512]{0:T(512)}, u32[]{:S(2)}) copy-start(f32[512]{0:T(512)} %param.15) | copy-start | bytes 6148

commit v6 on v5

--- a/solution.py
+++ b/solution.py
@@ -53,14 +53,32 @@
     return hi, mid, rest - mid
 
 
+def product(v, toend_ref, total, side, keys, out_ref):
+    vt = v.T
+    scaled = [
+        (vt[j * WIDTH : (j + 1) * WIDTH].astype(F32) * toend_ref[pl.ds(side * HALF + j, 1), :])
+        .astype(BF16)
+        for j in range(HALF)
+    ]
+    out_ref[0:ROWS] = jnp.dot(
+        jnp.concatenate(scaled, axis=0), keys, preferred_element_type=F32
+    )
+    out_ref[ROWS:BUF_ROWS] = total
+
+
 def prep_body(
-    ld_hbm, v_hbm, k_hbm, d_ref, vt_ref, own_ref, send_ref, ld_ref, v_ref, k_ref, scaled_ref, sems
+    ld_hbm, v_hbm, k_hbm, d_ref, toend_ref, total_ref, send_ref, mine_ref, k_ref,
+    ld_ref, theirs_ref, sems,
 ):
-    pairs = ((v_hbm, v_ref), (ld_hbm, ld_ref), (k_hbm, k_ref))
+    me = core_index()
+    columns = lambda side: pl.ds(pl.multiple_of(side * ROWS, ROWS), ROWS)
+    pairs = (
+        (v_hbm.at[:, columns(1 - me)], theirs_ref), (ld_hbm, ld_ref), (k_hbm, k_ref),
+        (v_hbm.at[:, columns(me)], mine_ref),
+    )
     copies = [pltpu.make_async_copy(a, b, sems.at[i]) for i, (a, b) in enumerate(pairs)]
     for copy in copies:
         copy.start()
-    core = core_index()
     row = lax.broadcasted_iota(jnp.int32, (128, 128), 0)
     col = lax.broadcasted_iota(jnp.int32, (128, 128), 1)
     upto = (row <= col).astype(F32).astype(BF16)
@@ -82,36 +100,36 @@
         d.append(inner[j] + ahead)
         ahead = ahead + totals[j]
     total = ahead
-    toend = jnp.concatenate([jnp.exp(total - x) for x in d], axis=1)
-    for j in range(4):
-        d_ref[:, j * 128 : (j + 1) * 128] = d[j]
+    total_ref[...] = total
+    for j in range(4):
+        cols = slice(j * 128, (j + 1) * 128)
+        d_ref[:, cols] = d[j]
+        toend_ref[:, cols] = jnp.exp(total - d[j])
     copies[0].wait()
-    vt = v_ref[...].T
-    for h in range(HEADS):
-        rows = slice(h * WIDTH, (h + 1) * WIDTH)
-        scaled_ref[rows] = (vt[rows].astype(F32) * toend[h : h + 1]).astype(BF16)
     copies[2].wait()
-    keys = k_ref[...]
-    for ref, side in ((send_ref, 1 - core), (own_ref, core)):
-        rows = pl.ds(pl.multiple_of(side * ROWS, ROWS), ROWS)
-        ref[0:ROWS] = jnp.dot(scaled_ref[rows, :], keys, preferred_element_type=F32)
-        ref[ROWS:BUF_ROWS] = total
-    vt_ref[...] = vt
+    product(theirs_ref[...], toend_ref, total, 1 - me, k_ref[...], send_ref)
+    copies[3].wait()
 
 
 def prep(ld, v, k):
-    buf = sds((BUF_ROWS, STATE))
-    outs = [sds((HEADS, BLOCK)), sds((BLOCK, BLOCK), BF16), buf, buf]
+    outs = [sds((HEADS, BLOCK)), sds((HEADS, BLOCK)), sds((HEADS, 128)), sds((BUF_ROWS, STATE))]
+    outs += [sds((BLOCK, ROWS), BF16), sds((BLOCK, STATE), BF16)]
     return call(
         prep_body, outs, [HB] * 3, 10**7,
         scratch=[
             pltpu.VMEM((HEADS, BLOCK), F32),
-            pltpu.VMEM((BLOCK, HEADS * WIDTH), BF16),
-            pltpu.VMEM((BLOCK, STATE), BF16),
-            pltpu.VMEM((HEADS * WIDTH, BLOCK), BF16),
-            pltpu.SemaphoreType.DMA((3,)),
+            pltpu.VMEM((BLOCK, ROWS), BF16),
+            pltpu.SemaphoreType.DMA((4,)),
         ],
     )(*(pltpu.with_memory_space_constraint(x, pltpu.HBM) for x in (ld, v, k)))
+
+
+def own_body(v_ref, k_ref, toend_ref, total_ref, out_ref):
+    product(v_ref[...], toend_ref, total_ref[...], core_index(), k_ref[...], out_ref)
+
+
+def own_state(v, k, toend, total):
+    return call(own_body, sds((BUF_ROWS, STATE)), [VM] * 4, 10**6)(v, k, toend, total)
 
 
 def merge_body(level, own_ref, got_ref, *refs):
@@ -139,20 +157,22 @@
     )(own, got, *tokens)
 
 
-def aux_body(q_ref, gate_ref, d_ref, qt_ref, gt_ref, dcol_ref):
+def aux_body(q_ref, gate_ref, d_ref, v_ref, qt_ref, gt_ref, dcol_ref, vt_ref):
     qt = q_ref[...].T
     qt_ref[0:STATE] = qt
     qt_ref[STATE : 2 * STATE] = qt
+    vt_ref[...] = v_ref[...].T
+    dcol_ref[...] = d_ref[...].T
     for j in range(4):
         cols = slice(j * 128, (j + 1) * 128)
         v = gate_ref[:, cols].T.astype(F32)
         gt_ref[cols] = v / (1.0 + jnp.exp(-v))
-    dcol_ref[...] = d_ref[...].T
-
-
-def aux(q, gate, d):
+
+
+def aux(q, gate, d, v):
     outs = [sds((2 * STATE, BLOCK), BF16), sds((BLOCK, BLOCK)), sds((BLOCK, HEADS))]
-    return call(aux_body, outs, [VM] * 3, 10**7)(q, gate, d)
+    outs += [sds((BLOCK, BLOCK), BF16)]
+    return call(aux_body, outs, [VM] * 4, 10**7)(q, gate, d, v)
 
 
 def near_body(first, k_ref, qt_ref, vt_ref, d_ref, dcol_ref, w_ref, skip_ref, token_ref, out_ref, sc_ref, mix_ref):
@@ -322,18 +342,19 @@
 
 def work(head_inputs, state_keys, state_queries, log_decay, level_weight, skip_scale, gate_input, norm_gain):
     w = level_weight.transpose(2, 1, 0)
-    d, vt, own, send = prep(log_decay.T, head_inputs, state_keys)
+    d, toend, total, send, mine, keys = prep(log_decay.T, head_inputs, state_keys)
     swap = lambda x: hop(x, "tok", CORE)
 
     def close_by(first, token):
-        return near(first, state_keys, qt, vt, d, dcol, w, skip_scale, token)
+        return near(first, keys, qt, vt, d, dcol, w, skip_scale, token)
 
     def step(level, lead, bufs, *more):
         return far(level, qt, d, w, lead, bufs, *more)
 
     got = swap(send)
-    qt, gt, dcol = aux(state_queries, gate_input, d)
-    chip = merge(0, own, got, gt)
+    own = own_state(mine, keys, toend, total)
+    chip = merge(0, own, got)
+    qt, gt, dcol, vt = aux(state_queries, gate_input, d, head_inputs)
     levels = [(got, swap(own))]
     parts = [close_by(0, chip)]
     z1 = hop(chip, "tok", Z1)
@@ -360,10 +381,10 @@
     other = swap(beyond)
     acc, lead = step(4, lead, levels[4], acc, parts[3])
     last = (qt, d, w, lead, acc, gt)
-    mine, part = close(5, 0, *last, beyond)
+    near_half, part = close(5, 0, *last, beyond)
     rest, squares = close(5, 1, *last, other, part)
     shares = [hop(squares, "head", 2), hop(squares, "head", 1), hop(squares, "head", 3)]
-    turned = turn(mine, rest, norm_gain[None])
+    turned = turn(near_half, rest, norm_gain[None])
     return finish(HEADS * WIDTH * lax.axis_size("head"), turned, [squares, *shares])
 
 

time: 55.1 us -> 54.8 us (level)
  transfers between devices with their start and end apart: 16 -> 16, of which waited for: 9 -> 9; matrix products, arithmetic and copies ran while one was open for 0% -> 0% of each run, Pallas kernels for 15% -> 16%
where the time goes in v6:
time: 54.8 us; the launch traced here: 54.6 us
  starting transfers between devices  25.2 us (46%)
  waiting for transfers between devices  16.2 us (30%)
  Pallas kernels  11.5 us (21%)
  local copies, waits for them, and re-layouts  1.37 us (2%)
    ppermute x16, starting transfers between devices, hop(): return lax.ppermute(x, axis, [(i, i ^ flip) for i in range(count)])  25.2 us
    ppermute x16, waiting for transfers between devices, hop(): return lax.ppermute(x, axis, [(i, i ^ flip) for i in range(count)])  16.2 us
    pallas_call x4, Pallas kernels, near(): call(functools.partial(near_body, first), sds((2 * WIDTH, BLOCK)), [VM] *...  5.51 us
    pallas_call x5, Pallas kernels, far(): call(functools.partial(far_body, level), [sds((BLOCK, BLOCK)), sds((HEADS...  1.74 us
    pallas_call x1, Pallas kernels, prep(): call(prep_body, outs, [HB] * 3, 10 ** 7, scratch=[pltpu.VMEM((HEADS, BLOC...  1.39 us
    unnamed x12, local copies, waits for them, and re-layouts  1.37 us
  transfers between devices with their start and end apart: 16, of which 9 were waited for; matrix products, arithmetic and copies ran while one was open for 0% of the time, Pallas kernels for 16%

profile of v6, /device:TPU:1, one launch (start us, length us, event | category | flops | bytes accessed | tf_op | source)
XLA Modules:
  0.0 54.6 jit_solution(6352890180384970970)
XLA Ops:
  0.0 0.0 copy-start.2
  0.0 1.4 %shard_map.82 = (f32[8,512]{1,0:T(8,128)S(1)}, f32[8,512]{1,0:T(8,128)S(1)}, f32[8,128]{1,0:T(8,128)S(1)}, f32[264,128]{1,0:T(8,128)S(1)}, bf16[512,256]{1,0:T(8,128)(2,1)S(1)}, /*index=5*/bf16[512,128]{1,0:T(8,128)(2,1)S(1)}) custom-call(f32[8,512]{1,0:T(8,128)} %bitcast.15, bf16[512,512]{1,0:T(8,128)(2,1)} %v_ref.1, bf16[512,128]{1,0:T(8,128)(2,1)} %k_hbm.1), custom_call_target="tpu_custom_call" | custom-call | flops 10000000 | bytes 1048576 | tf_op jit(solution)/shard_map/pallas_call | solution.py:117
  1.4 0.0 copy-start.1
  1.4 3.3 %collective-permute-start = (f32[264,128]{1,0:T(8,128)S(1)}, f32[264,128]{1,0:T(8,128)S(1)}, u32[]{:S(2)}, u32[]{:S(2)}) collective-permute-start(f32[264,128]{1,0:T(8,128)S(1)} %get-tuple-element.31), channel_id=1, source_target_pairs={{0,4},{4,0},{8,12},{12,8},{16,20},{20,16},{24,28},{28,24},{32,36},... | collective-permute-start | bytes 405512 | tf_op jit(solution)/shard_map/ppermute | solution.py:337
  4.7 0.3 shard_map.84.own_ref
  5.0 0.0 copy-start.3
  5.0 0.7 %collective-permute-done.rest_0_.got_ref = f32[264,128]{1,0:T(8,128)S(1)} collective-permute-done((f32[264,128]{1,0:T(8,128)S(1)}, f32[264,128]{1,0:T(8,128)S(1)}, u32[]{:S(2)}, u32[]{:S(2)}) %collective-permute-start) | collective-permute-done | bytes 135200 | tf_op jit(solution)/shard_map/ppermute | solution.py:337
  5.7 0.1 collective-permute-start.2
  5.8 0.6 %collective-permute-start.1 = (f32[264,128]{1,0:T(8,128)S(1)}, f32[264,128]{1,0:T(8,128)S(1)}, u32[]{:S(2)}, u32[]{:S(2)}) collective-permute-start(f32[264,128]{1,0:T(8,128)S(1)} %shard_map.84.own_ref), channel_id=1, source_target_pairs={{0,4},{4,0},{8,12},{12,8},{16,20},{20,16},{24,28},{28,24},{32,36},... | collective-permute-start | bytes 405512 | tf_op jit(solution)/shard_map/ppermute | solution.py:337
  6.4 0.0 copy-done.2
  6.4 0.0 copy-done.1
  6.4 0.0 copy-done.3
  6.4 0.0 copy-start
  6.4 0.6 %shard_map.83 = (bf16[256,512]{1,0:T(8,128)(2,1)S(1)}, f32[512,512]{1,0:T(8,128)S(1)}, f32[512,8]{1,0:T(8,128)S(1)}, bf16[512,512]{1,0:T(8,128)(2,1)S(1)}) custom-call(bf16[512,128]{1,0:T(8,128)(2,1)S(1)} %copy-done.3, bf16[512,512]{1,0:T(8,128)(2,1)S(1)} %copy-done.2, f32[8,512]{1,0:T(8,128)S(1)} %get-tuple-element.29.d_ref, bf16[512,512]{1,0:T(8,128)(2,1)S(1)} %copy-done.1), custom_call_target="tpu_custom_call" | custom-call | flops 10000000 | bytes 1048576 | tf_op jit(solution)/shard_map/pallas_call | solution.py:175
  7.0 0.0 copy-start.4
  7.0 0.3 copy-done
  7.4 0.3 copy-done.4
  7.7 1.4 %shard_map.87.rest_3_.refs_0_ = f32[128,512]{1,0:T(8,128)S(1)} custom-call(bf16[512,128]{1,0:T(8,128)(2,1)S(1)} %get-tuple-element.33.k_ref, bf16[256,512]{1,0:T(8,128)(2,1)S(1)} %get-tuple-element.30.qt_ref, bf16[512,512]{1,0:T(8,128)(2,1)S(1)} %get-tuple-element.38.vt_ref, f32[8,512]{1,0:T(8,128)S(1)} %get-tuple-element.29.d_ref, ...), custom_call_target="tpu_custom_call" | custom-call | flops 10000000 | bytes 1048576 | tf_op jit(solution)/shard_map/pallas_call | solution.py:219
  9.1 1.5 %collective-permute-done.2.rest_0_.got_ref = f32[264,128]{1,0:T(8,128)S(1)} collective-permute-done((f32[264,128]{1,0:T(8,128)S(1)}, f32[264,128]{1,0:T(8,128)S(1)}, u32[]{:S(2)}, u32[]{:S(2)}) %collective-permute-start.2) | collective-permute-done | bytes 135200 | tf_op jit(solution)/shard_map/ppermute | solution.py:337
  10.6 2.7 %collective-permute-start.4 = (f32[264,128]{1,0:T(8,128)S(1)}, f32[264,128]{1,0:T(8,128)S(1)}, u32[]{:S(2)}, u32[]{:S(2)}) collective-permute-start(f32[264,128]{1,0:T(8,128)S(1)} %shard_map.89.token_ref.own_ref), channel_id=1, source_target_pairs={{0,24},{4,28},{8,16},{12,20},{16,8},{20,12},{24,0},{28,4},{32,56},... | collective-permute-start | bytes 405512 | tf_op jit(solution)/shard_map/ppermute | solution.py:337
  13.4 1.5 %collective-permute-start.3 = (f32[264,128]{1,0:T(8,128)S(1)}, f32[264,128]{1,0:T(8,128)S(1)}, u32[]{:S(2)}, u32[]{:S(2)}) collective-permute-start(f32[264,128]{1,0:T(8,128)S(1)} %collective-permute-done.2.rest_0_.got_ref), channel_id=1, source_target_pairs={{0,4},{4,0},{8,12},{12,8},{16,20},{20,16},{24,28},{28,24},{32,36},... | collective-permute-start | bytes 405512 | tf_op jit(solution)/shard_map/ppermute | solution.py:337
  14.9 0.0 collective-permute-done.1.rest_1_
  14.9 0.3 shard_map.85
  15.2 1.3 %collective-permute-done.4.rest_0_.got_ref = f32[264,128]{1,0:T(8,128)S(1)} collective-permute-done((f32[264,128]{1,0:T(8,128)S(1)}, f32[264,128]{1,0:T(8,128)S(1)}, u32[]{:S(2)}, u32[]{:S(2)}) %collective-permute-start.4) | collective-permute-done | bytes 135200 | tf_op jit(solution)/shard_map/ppermute | solution.py:337
  16.5 2.3 %collective-permute-start.5 = (f32[264,128]{1,0:T(8,128)S(1)}, f32[264,128]{1,0:T(8,128)S(1)}, u32[]{:S(2)}, u32[]{:S(2)}) collective-permute-start(f32[264,128]{1,0:T(8,128)S(1)} %collective-permute-done.4.rest_0_.got_ref), channel_id=1, source_target_pairs={{0,4},{4,0},{8,12},{12,8},{16,20},{20,16},{24,28},{28,24},{32,36},... | collective-permute-start | bytes 405512 | tf_op jit(solution)/shard_map/ppermute | solution.py:337
  18.8 1.4 %shard_map.90.rest_3_.refs_0_ = f32[128,512]{1,0:T(8,128)S(1)} custom-call(bf16[512,128]{1,0:T(8,128)(2,1)S(1)} %get-tuple-element.33.k_ref, bf16[256,512]{1,0:T(8,128)(2,1)S(1)} %get-tuple-element.30.qt_ref, bf16[512,512]{1,0:T(8,128)(2,1)S(1)} %get-tuple-element.38.vt_ref, f32[8,512]{1,0:T(8,128)S(1)} %get-tuple-element.29.d_ref, ...), custom_call_target="tpu_custom_call" | custom-call | flops 10000000 | bytes 1048576 | tf_op jit(solution)/shard_map/pallas_call | solution.py:219
  20.2 4.0 %collective-permute-start.6 = (f32[264,128]{1,0:T(8,128)S(1)}, f32[264,128]{1,0:T(8,128)S(1)}, u32[]{:S(2)}, u32[]{:S(2)}) collective-permute-start(f32[264,128]{1,0:T(8,128)S(1)} %shard_map.92.token_ref.own_ref), channel_id=1, source_target_pairs={{0,56},{4,60},{8,48},{12,52},{16,40},{20,44},{24,32},{28,36},{32,2... | collective-permute-start | bytes 405512 | tf_op jit(solution)/shard_map/ppermute | solution.py:337
  24.1 1.4 %shard_map.93.rest_3_.refs_0_ = f32[128,512]{1,0:T(8,128)S(1)} custom-call(bf16[512,128]{1,0:T(8,128)(2,1)S(1)} %get-tuple-element.33.k_ref, bf16[256,512]{1,0:T(8,128)(2,1)S(1)} %get-tuple-element.30.qt_ref, bf16[512,512]{1,0:T(8,128)(2,1)S(1)} %get-tuple-element.38.vt_ref, f32[8,512]{1,0:T(8,128)S(1)} %get-tuple-element.29.d_ref, ...), custom_call_target="tpu_custom_call" | custom-call | flops 10000000 | bytes 1048576 | tf_op jit(solution)/shard_map/pallas_call | solution.py:219
  25.5 0.0 collective-permute-done.3.rest_1_
  25.5 0.4 shard_map.88
  25.9 0.0 collective-permute-done.5.rest_1_
  25.9 0.4 shard_map.91
  26.3 4.7 %collective-permute-done.6.rest_0_.got_ref = f32[264,128]{1,0:T(8,128)S(1)} collective-permute-done((f32[264,128]{1,0:T(8,128)S(1)}, f32[264,128]{1,0:T(8,128)S(1)}, u32[]{:S(2)}, u32[]{:S(2)}) %collective-permute-start.6) | collective-permute-done | bytes 135200 | tf_op jit(solution)/shard_map/ppermute | solution.py:337
  31.0 1.3 %collective-permute-start.8 = (f32[264,128]{1,0:T(8,128)S(1)}, f32[264,128]{1,0:T(8,128)S(1)}, u32[]{:S(2)}, u32[]{:S(2)}) collective-permute-start(f32[264,128]{1,0:T(8,128)S(1)} %shard_map.95.token_ref), channel_id=1, source_target_pairs={{0,64},{4,68},{8,72},{12,76},{16,80},{20,84},{24,88},{28,92},{32,9... | collective-permute-start | bytes 405512 | tf_op jit(solution)/shard_map/ppermute | solution.py:337
  32.3 0.9 %collective-permute-start.7 = (f32[264,128]{1,0:T(8,128)S(1)}, f32[264,128]{1,0:T(8,128)S(1)}, u32[]{:S(2)}, u32[]{:S(2)}) collective-permute-start(f32[264,128]{1,0:T(8,128)S(1)} %collective-permute-done.6.rest_0_.got_ref), channel_id=1, source_target_pairs={{0,4},{4,0},{8,12},{12,8},{16,20},{20,16},{24,28},{28,24},{32,36},... | collective-permute-start | bytes 405512 | tf_op jit(solution)/shard_map/ppermute | solution.py:337
  33.2 2.4 %collective-permute-start.10 = (f32[264,128]{1,0:T(8,128)S(1)}, f32[264,128]{1,0:T(8,128)S(1)}, u32[]{:S(2)}, u32[]{:S(2)}) collective-permute-start(f32[264,128]{1,0:T(8,128)S(1)} %shard_map.95.token_ref), channel_id=1, source_target_pairs={{0,128},{4,132},{8,136},{12,140},{16,144},{20,148},{24,152},{28,15... | collective-permute-start | bytes 405512 | tf_op jit(solution)/shard_map/ppermute | solution.py:337
  35.6 0.2 collective-permute-start.11
  35.8 0.0 collective-permute-done.8.rest_0_
  35.8 1.3 %collective-permute-start.9 = (f32[264,128]{1,0:T(8,128)S(1)}, f32[264,128]{1,0:T(8,128)S(1)}, u32[]{:S(2)}, u32[]{:S(2)}) collective-permute-start(f32[264,128]{1,0:T(8,128)S(1)} %collective-permute-done.8.rest_0_), channel_id=1, source_target_pairs={{0,4},{4,0},{8,12},{12,8},{16,20},{20,16},{24,28},{28,24},{32,36},... | collective-permute-start | bytes 405512 | tf_op jit(solution)/shard_map/ppermute | solution.py:337
  37.1 1.4 %shard_map.96.rest_3_.refs_0_ = f32[128,512]{1,0:T(8,128)S(1)} custom-call(bf16[512,128]{1,0:T(8,128)(2,1)S(1)} %get-tuple-element.33.k_ref, bf16[256,512]{1,0:T(8,128)(2,1)S(1)} %get-tuple-element.30.qt_ref, bf16[512,512]{1,0:T(8,128)(2,1)S(1)} %get-tuple-element.38.vt_ref, f32[8,512]{1,0:T(8,128)S(1)} %get-tuple-element.29.d_ref, ...), custom_call_target="tpu_custom_call" | custom-call | flops 10000000 | bytes 1048576 | tf_op jit(solution)/shard_map/pallas_call | solution.py:219
  38.5 0.0 collective-permute-done.7.rest_1_
  38.5 0.4 shard_map.94
  38.9 1.9 %collective-permute-done.10.own_ref = f32[264,128]{1,0:T(8,128)S(1)} collective-permute-done((f32[264,128]{1,0:T(8,128)S(1)}, f32[264,128]{1,0:T(8,128)S(1)}, u32[]{:S(2)}, u32[]{:S(2)}) %collective-permute-start.10) | collective-permute-done | bytes 135200 | tf_op jit(solution)/shard_map/ppermute | solution.py:337
  40.8 3.4 %collective-permute-done.11.got_ref = f32[264,128]{1,0:T(8,128)S(1)} collective-permute-done((f32[264,128]{1,0:T(8,128)S(1)}, f32[264,128]{1,0:T(8,128)S(1)}, u32[]{:S(2)}, u32[]{:S(2)}) %collective-permute-start.11) | collective-permute-done | bytes 135200 | tf_op jit(solution)/shard_map/ppermute | solution.py:337
  44.3 1.0 %collective-permute-start.12 = (f32[264,128]{1,0:T(8,128)S(1)}, f32[264,128]{1,0:T(8,128)S(1)}, u32[]{:S(2)}, u32[]{:S(2)}) collective-permute-start(f32[264,128]{1,0:T(8,128)S(1)} %shard_map.98.buf_ref), channel_id=1, source_target_pairs={{0,4},{4,0},{8,12},{12,8},{16,20},{20,16},{24,28},{28,24},{32,36},... | collective-permute-start | bytes 405512 | tf_op jit(solution)/shard_map/ppermute | solution.py:337
  45.2 0.0 collective-permute-done.9.rest_1_
  45.2 0.4 shard_map.97
  45.6 0.3 shard_map.99
  45.9 0.3 collective-permute-done.12.buf_ref
  46.2 0.3 shard_map.100
  46.5 3.0 %collective-permute-start.13 = (f32[1,512]{1,0:T(1,128)S(1)}, f32[1,512]{1,0:T(1,128)S(1)}, u32[]{:S(2)}, u32[]{:S(2)}) collective-permute-start(f32[1,512]{1,0:T(1,128)S(1)} %get-tuple-element.52.a_ref), channel_id=1, source_target_pairs={{0,2},{1,3},{2,0},{3,1},{4,6},{5,7},{6,4},{7,5},{8,10},{9,11},{10,... | collective-permute-start | bytes 6152 | tf_op jit(solution)/shard_map/ppermute | solution.py:337
  49.5 0.4 collective-permute-start.14
  49.9 0.4 collective-permute-start.15
  50.3 0.0 copy-start.5
  50.3 0.7 %copy-done.5 = f32[512]{0:T(512)S(1)} copy-done((f32[512]{0:T(512)S(1)}, f32[512]{0:T(512)}, u32[]{:S(2)}) %copy-start.5) | copy-done | bytes 2072
  50.9 0.3 shard_map.101.g_ref
  51.3 0.0 collective-permute-done.13.b_ref
  51.3 0.6 %collective-permute-done.14.c_ref = f32[1,512]{1,0:T(1,128)S(1)} collective-permute-done((f32[1,512]{1,0:T(1,128)S(1)}, f32[1,512]{1,0:T(1,128)S(1)}, u32[]{:S(2)}, u32[]{:S(2)}) %collective-permute-start.14) | collective-permute-done | bytes 2080 | tf_op jit(solution)/shard_map/ppermute | solution.py:337
  51.9 1.6 %collective-permute-done.15.e_ref = f32[1,512]{1,0:T(1,128)S(1)} collective-permute-done((f32[1,512]{1,0:T(1,128)S(1)}, f32[1,512]{1,0:T(1,128)S(1)}, u32[]{:S(2)}, u32[]{:S(2)}) %collective-permute-start.15) | collective-permute-done | bytes 2080 | tf_op jit(solution)/shard_map/ppermute | solution.py:337
  53.5 0.9 %shard_map.102 = bf16[512,512]{1,0:T(8,128)(2,1)} custom-call(f32[512,512]{1,0:T(8,128)S(1)} %shard_map.101.g_ref, f32[1,512]{1,0:T(1,128)S(1)} %get-tuple-element.52.a_ref, f32[1,512]{1,0:T(1,128)S(1)} %collective-permute-done.13.b_ref, f32[1,512]{1,0:T(1,128)S(1)} %collective-permute-done.14.c_ref, f32[1,512]{1,0:T(1,128)S(1)} %collective-permute-done.15.e_ref), custom_call_target="tpu_custom_call" | custom-call | flops 100000000 | bytes 1048576 | tf_op jit(solution)/shard_map/pallas_call | solution.py:328
  (6 shorter events, 0.2 us)
Async XLA Ops:
  0.0 6.4 %copy-start.2 = (bf16[512,512]{1,0:T(8,128)(2,1)S(1)}, bf16[512,512]{1,0:T(8,128)(2,1)}, u32[]{:S(2)}) copy-start(bf16[512,512]{1,0:T(8,128)(2,1)} %gate_ref.1) | copy-start | bytes 1572868
  1.4 5.0 %copy-start.1 = (bf16[512,512]{1,0:T(8,128)(2,1)S(1)}, bf16[512,512]{1,0:T(8,128)(2,1)}, u32[]{:S(2)}) copy-start(bf16[512,512]{1,0:T(8,128)(2,1)} %v_ref.1) | copy-start | bytes 1572868
  1.4 4.3 %collective-permute-start = (f32[264,128]{1,0:T(8,128)S(1)}, f32[264,128]{1,0:T(8,128)S(1)}, u32[]{:S(2)}, u32[]{:S(2)}) collective-permute-start(f32[264,128]{1,0:T(8,128)S(1)} %get-tuple-element.31), channel_id=1, source_target_pairs={{0,4},{4,0},{8,12},{12,8},{16,20},{20,16},{24,28},{28,24},{32,36},... | collective-permute-start | bytes 405512 | tf_op jit(solution)/shard_map/ppermute | solution.py:337
  5.0 1.4 %copy-start.3 = (bf16[512,128]{1,0:T(8,128)(2,1)S(1)}, bf16[512,128]{1,0:T(8,128)(2,1)}, u32[]{:S(2)}) copy-start(bf16[512,128]{1,0:T(8,128)(2,1)} %q_ref.1) | copy-start | bytes 393220
  5.7 4.9 %collective-permute-start.2 = (f32[264,128]{1,0:T(8,128)S(1)}, f32[264,128]{1,0:T(8,128)S(1)}, u32[]{:S(2)}, u32[]{:S(2)}) collective-permute-start(f32[264,128]{1,0:T(8,128)S(1)} %shard_map.86.token_ref.own_ref), channel_id=1, source_target_pairs={{0,8},{4,12},{8,0},{12,4},{16,24},{20,28},{24,16},{28,20},{32,40},... | collective-permute-start | bytes 405512 | tf_op jit(solution)/shard_map/ppermute | solution.py:337
  5.8 9.0 %collective-permute-start.1 = (f32[264,128]{1,0:T(8,128)S(1)}, f32[264,128]{1,0:T(8,128)S(1)}, u32[]{:S(2)}, u32[]{:S(2)}) collective-permute-start(f32[264,128]{1,0:T(8,128)S(1)} %shard_map.84.own_ref), channel_id=1, source_target_pairs={{0,4},{4,0},{8,12},{12,8},{16,20},{20,16},{24,28},{28,24},{32,36},... | collective-permute-start | bytes 405512 | tf_op jit(solution)/shard_map/ppermute | solution.py:337
  6.4 1.0 %copy-start = (f32[512,8,18]{0,1,2:T(8,128)S(1)}, f32[512,8,18]{0,1,2:T(8,128)}, u32[]{:S(2)}) copy-start(f32[512,8,18]{0,1,2:T(8,128)} %param.12) | copy-start | bytes 884740
  7.0 0.7 %copy-start.4 = (f32[8]{0:T(128)S(1)}, f32[8]{0:T(128)}, u32[]{:S(2)}) copy-start(f32[8]{0:T(128)} %skip_ref.7) | copy-start | bytes 100
  10.6 5.8 %collective-permute-start.4 = (f32[264,128]{1,0:T(8,128)S(1)}, f32[264,128]{1,0:T(8,128)S(1)}, u32[]{:S(2)}, u32[]{:S(2)}) collective-permute-start(f32[264,128]{1,0:T(8,128)S(1)} %shard_map.89.token_ref.own_ref), channel_id=1, source_target_pairs={{0,24},{4,28},{8,16},{12,20},{16,8},{20,12},{24,0},{28,4},{32,56},... | collective-permute-start | bytes 405512 | tf_op jit(solution)/shard_map/ppermute | solution.py:337
  13.4 12.2 %collective-permute-start.3 = (f32[264,128]{1,0:T(8,128)S(1)}, f32[264,128]{1,0:T(8,128)S(1)}, u32[]{:S(2)}, u32[]{:S(2)}) collective-permute-start(f32[264,128]{1,0:T(8,128)S(1)} %collective-permute-done.2.rest_0_.got_ref), channel_id=1, source_target_pairs={{0,4},{4,0},{8,12},{12,8},{16,20},{20,16},{24,28},{28,24},{32,36},... | collective-permute-start | bytes 405512 | tf_op jit(solution)/shard_map/ppermute | solution.py:337
  16.5 9.4 %collective-permute-start.5 = (f32[264,128]{1,0:T(8,128)S(1)}, f32[264,128]{1,0:T(8,128)S(1)}, u32[]{:S(2)}, u32[]{:S(2)}) collective-permute-start(f32[264,128]{1,0:T(8,128)S(1)} %collective-permute-done.4.rest_0_.got_ref), channel_id=1, source_target_pairs={{0,4},{4,0},{8,12},{12,8},{16,20},{20,16},{24,28},{28,24},{32,36},... | collective-permute-start | bytes 405512 | tf_op jit(solution)/shard_map/ppermute | solution.py:337
  20.2 10.8 %collective-permute-start.6 = (f32[264,128]{1,0:T(8,128)S(1)}, f32[264,128]{1,0:T(8,128)S(1)}, u32[]{:S(2)}, u32[]{:S(2)}) collective-permute-start(f32[264,128]{1,0:T(8,128)S(1)} %shard_map.92.token_ref.own_ref), channel_id=1, source_target_pairs={{0,56},{4,60},{8,48},{12,52},{16,40},{20,44},{24,32},{28,36},{32,2... | collective-permute-start | bytes 405512 | tf_op jit(solution)/shard_map/ppermute | solution.py:337
  31.0 4.8 %collective-permute-start.8 = (f32[264,128]{1,0:T(8,128)S(1)}, f32[264,128]{1,0:T(8,128)S(1)}, u32[]{:S(2)}, u32[]{:S(2)}) collective-permute-start(f32[264,128]{1,0:T(8,128)S(1)} %shard_map.95.token_ref), channel_id=1, source_target_pairs={{0,64},{4,68},{8,72},{12,76},{16,80},{20,84},{24,88},{28,92},{32,9... | collective-permute-start | bytes 405512 | tf_op jit(solution)/shard_map/ppermute | solution.py:337
  32.3 6.2 %collective-permute-start.7 = (f32[264,128]{1,0:T(8,128)S(1)}, f32[264,128]{1,0:T(8,128)S(1)}, u32[]{:S(2)}, u32[]{:S(2)}) collective-permute-start(f32[264,128]{1,0:T(8,128)S(1)} %collective-permute-done.6.rest_0_.got_ref), channel_id=1, source_target_pairs={{0,4},{4,0},{8,12},{12,8},{16,20},{20,16},{24,28},{28,24},{32,36},... | collective-permute-start | bytes 405512 | tf_op jit(solution)/shard_map/ppermute | solution.py:337
  33.2 7.6 %collective-permute-start.10 = (f32[264,128]{1,0:T(8,128)S(1)}, f32[264,128]{1,0:T(8,128)S(1)}, u32[]{:S(2)}, u32[]{:S(2)}) collective-permute-start(f32[264,128]{1,0:T(8,128)S(1)} %shard_map.95.token_ref), channel_id=1, source_target_pairs={{0,128},{4,132},{8,136},{12,140},{16,144},{20,148},{24,152},{28,15... | collective-permute-start | bytes 405512 | tf_op jit(solution)/shard_map/ppermute | solution.py:337
  35.6 8.6 %collective-permute-start.11 = (f32[264,128]{1,0:T(8,128)S(1)}, f32[264,128]{1,0:T(8,128)S(1)}, u32[]{:S(2)}, u32[]{:S(2)}) collective-permute-start(f32[264,128]{1,0:T(8,128)S(1)} %shard_map.95.token_ref), channel_id=1, source_target_pairs={{0,192},{4,196},{8,200},{12,204},{16,208},{20,212},{24,216},{28,22... | collective-permute-start | bytes 405512 | tf_op jit(solution)/shard_map/ppermute | solution.py:337
  35.8 9.4 %collective-permute-start.9 = (f32[264,128]{1,0:T(8,128)S(1)}, f32[264,128]{1,0:T(8,128)S(1)}, u32[]{:S(2)}, u32[]{:S(2)}) collective-permute-start(f32[264,128]{1,0:T(8,128)S(1)} %collective-permute-done.8.rest_0_), channel_id=1, source_target_pairs={{0,4},{4,0},{8,12},{12,8},{16,20},{20,16},{24,28},{28,24},{32,36},... | collective-permute-start | bytes 405512 | tf_op jit(solution)/shard_map/ppermute | solution.py:337
  44.3 2.0 %collective-permute-start.12 = (f32[264,128]{1,0:T(8,128)S(1)}, f32[264,128]{1,0:T(8,128)S(1)}, u32[]{:S(2)}, u32[]{:S(2)}) collective-permute-start(f32[264,128]{1,0:T(8,128)S(1)} %shard_map.98.buf_ref), channel_id=1, source_target_pairs={{0,4},{4,0},{8,12},{12,8},{16,20},{20,16},{24,28},{28,24},{32,36},... | collective-permute-start | bytes 405512 | tf_op jit(solution)/shard_map/ppermute | solution.py:337
  46.5 4.8 %collective-permute-start.13 = (f32[1,512]{1,0:T(1,128)S(1)}, f32[1,512]{1,0:T(1,128)S(1)}, u32[]{:S(2)}, u32[]{:S(2)}) collective-permute-start(f32[1,512]{1,0:T(1,128)S(1)} %get-tuple-element.52.a_ref), channel_id=1, source_target_pairs={{0,2},{1,3},{2,0},{3,1},{4,6},{5,7},{6,4},{7,5},{8,10},{9,11},{10,... | collective-permute-start | bytes 6152 | tf_op jit(solution)/shard_map/ppermute | solution.py:337
  49.5 2.4 %collective-permute-start.14 = (f32[1,512]{1,0:T(1,128)S(1)}, f32[1,512]{1,0:T(1,128)S(1)}, u32[]{:S(2)}, u32[]{:S(2)}) collective-permute-start(f32[1,512]{1,0:T(1,128)S(1)} %get-tuple-element.52.a_ref), channel_id=1, source_target_pairs={{0,1},{1,0},{2,3},{3,2},{4,5},{5,4},{6,7},{7,6},{8,9},{9,8},{10,11... | collective-permute-start | bytes 6152 | tf_op jit(solution)/shard_map/ppermute | solution.py:337
  49.9 3.6 %collective-permute-start.15 = (f32[1,512]{1,0:T(1,128)S(1)}, f32[1,512]{1,0:T(1,128)S(1)}, u32[]{:S(2)}, u32[]{:S(2)}) collective-permute-start(f32[1,512]{1,0:T(1,128)S(1)} %get-tuple-element.52.a_ref), channel_id=1, source_target_pairs={{0,3},{1,2},{2,1},{3,0},{4,7},{5,6},{6,5},{7,4},{8,11},{9,10},{10,... | collective-permute-start | bytes 6152 | tf_op jit(solution)/shard_map/ppermute | solution.py:337
  50.3 0.7 %copy-start.5 = (f32[512]{0:T(512)S(1)}, f32[512]{0:T(512)}, u32[]{:S(2)}) copy-start(f32[512]{0:T(512)} %param.15) | copy-start | bytes 6148

commit v7 on v6

--- a/solution.py
+++ b/solution.py
@@ -256,8 +256,9 @@
     upper = ((lax.axis_index("tok") >> level) & 1) == 1
     next_ref[...] = lead + jnp.where(upper, bufs[0][ROWS:BUF_ROWS], 0.0)
     if level > 0:
-        rows = slice((level - 1) * 2 * WIDTH, level * 2 * WIDTH)
-        out_ref[rows] = out_ref[rows] + rest[3][...]
+        for n, ref in enumerate(rest[3:-3]):
+            rows = slice((level - 1 + n) * 2 * WIDTH, (level + n) * 2 * WIDTH)
+            out_ref[rows] = out_ref[rows] + ref[...]
 
 
 def far(level, qt, d, w, lead, bufs, *more):
@@ -269,29 +270,42 @@
     )(qt, d, w, lead, *bufs, *more)
 
 
-def close_body(level, side, qt_ref, d_ref, w_ref, lead_ref, acc_ref, gt_ref, buf_ref, *rest):
+def close_body(
+    level, side, qt_ref, d_ref, w_ref, lead_ref, acc_ref, gt_ref, near_ref, far_ref, *rest
+):
     out_ref, sq_ref, coef_ref = rest[-3:]
     sums = [] if side == 0 else [rest[0][...]]
     half = core_index() if side == 0 else 1 - core_index()
+    place = lambda row: pl.ds(pl.multiple_of(row - half * ROWS, WIDTH), WIDTH)
+
+    def keep(row, value):
+        out_ref[place(row), :] = value
 
     def emit(row, value):
         gated = value * gt_ref[pl.ds(row, WIDTH), :]
-        out_ref[pl.ds(pl.multiple_of(row - half * ROWS, WIDTH), WIDTH), :] = gated
+        out_ref[place(row), :] = gated
         sums.append(jnp.sum(gated * gated, axis=0, keepdims=True))
 
+    lead = lead_ref[...]
     readout(
-        level, (side,), lambda row: acc_ref[pl.ds(row, WIDTH), :], emit,
-        qt_ref, d_ref, w_ref, lead_ref[...], (buf_ref,), coef_ref,
+        level, (side,), lambda row: acc_ref[pl.ds(row, WIDTH), :], keep,
+        qt_ref, d_ref, w_ref, lead, (near_ref,), coef_ref,
+    )
+    upper = ((lax.axis_index("tok") >> level) & 1) == 1
+    lead = lead + jnp.where(upper, near_ref[ROWS:BUF_ROWS], 0.0)
+    readout(
+        level + 1, (side,), lambda row: out_ref[place(row), :], emit,
+        qt_ref, d_ref, w_ref, lead, (far_ref,), coef_ref,
     )
     sq_ref[...] = sum(sums[1:], sums[0])
 
 
-def close(level, side, qt, d, w, lead, acc, gt, buf, *more):
+def close(level, side, qt, d, w, lead, acc, gt, *bufs):
     return call(
         functools.partial(close_body, level, side), [sds((ROWS, BLOCK)), sds((1, BLOCK))],
-        [VM] * (7 + len(more)), 10**7,
+        [VM] * (6 + len(bufs)), 10**7,
         scratch=[pltpu.VMEM((HEADS, BLOCK), F32)],
-    )(qt, d, w, lead, acc, gt, buf, *more)
+    )(qt, d, w, lead, acc, gt, *bufs)
 
 
 def turn_body(own_ref, other_ref, gain_ref, out_ref):
@@ -372,17 +386,15 @@
     line = merge(3, quad, z7, parts[2], acc)
     levels.append((z7, swap(z7)))
     parts.append(close_by(6, line))
-    acc, lead = step(3, lead, levels[3], acc, parts[2])
+    acc, lead = step(3, lead, levels[3], acc, parts[2], parts[3])
     x2 = hop(line, "tok", X2)
     x1 = hop(line, "tok", X1)
     x3 = hop(line, "tok", X3)
-    levels.append((x1, swap(x1)))
-    beyond = merge(4, x2, x3, parts[3], acc)
+    beyond = merge(4, x2, x3, acc)
     other = swap(beyond)
-    acc, lead = step(4, lead, levels[4], acc, parts[3])
     last = (qt, d, w, lead, acc, gt)
-    near_half, part = close(5, 0, *last, beyond)
-    rest, squares = close(5, 1, *last, other, part)
+    near_half, part = close(4, 0, *last, x1, beyond)
+    rest, squares = close(4, 1, *last, swap(x1), other, part)
     shares = [hop(squares, "head", 2), hop(squares, "head", 1), hop(squares, "head", 3)]
     turned = turn(near_half, rest, norm_gain[None])
     return finish(HEADS * WIDTH * lax.axis_size("head"), turned, [squares, *shares])

time: 54.8 us -> 54.9 us (level)
  waiting for transfers between devices: 16.2 us -> 17 us
  starting transfers between devices: 25.2 us -> 24.6 us
    ppermute x16, waiting for transfers between devices: 16.2 us -> 17 us  [hop(): return lax.ppermute(x, axis, [(i, i ^ flip) for i in range(count)])]
    ppermute x16, starting transfers between devices: 25.2 us -> 24.6 us  [hop(): return lax.ppermute(x, axis, [(i, i ^ flip) for i in range(count)])]
    pallas_call x5 -> x4, Pallas kernels: 1.74 us -> 1.42 us  [far(): call(functools.partial(far_body, level), [sds((BLOCK, BLOCK)), sds((HEADS...]
where the time goes in v7:
time: 54.9 us; the launch traced here: 54.7 us
  starting transfers between devices  24.6 us (45%)
  waiting for transfers between devices  17 us (31%)
  Pallas kernels  11.4 us (21%)
  local copies, waits for them, and re-layouts  1.37 us (2%)
    ppermute x16, starting transfers between devices, hop(): return lax.ppermute(x, axis, [(i, i ^ flip) for i in range(count)])  24.6 us
    ppermute x16, waiting for transfers between devices, hop(): return lax.ppermute(x, axis, [(i, i ^ flip) for i in range(count)])  17 us
    pallas_call x4, Pallas kernels, near(): call(functools.partial(near_body, first), sds((2 * WIDTH, BLOCK)), [VM] *...  5.55 us
    pallas_call x4, Pallas kernels, far(): call(functools.partial(far_body, level), [sds((BLOCK, BLOCK)), sds((HEADS...  1.42 us
    pallas_call x1, Pallas kernels, prep(): call(prep_body, outs, [HB] * 3, 10 ** 7, scratch=[pltpu.VMEM((HEADS, BLOC...  1.39 us
    unnamed x12, local copies, waits for them, and re-layouts  1.37 us
  transfers between devices with their start and end apart: 16, of which 9 were waited for; matrix products, arithmetic and copies ran while one was open for 0% of the time, Pallas kernels for 16%

profile of v7, /device:TPU:1, one launch (start us, length us, event | category | flops | bytes accessed | tf_op | source)
XLA Modules:
  0.0 54.7 jit_solution(14941745714822297546)
XLA Ops:
  0.0 0.0 copy-start.2
  0.0 1.4 %shard_map.82 = (f32[8,512]{1,0:T(8,128)S(1)}, f32[8,512]{1,0:T(8,128)S(1)}, f32[8,128]{1,0:T(8,128)S(1)}, f32[264,128]{1,0:T(8,128)S(1)}, bf16[512,256]{1,0:T(8,128)(2,1)S(1)}, /*index=5*/bf16[512,128]{1,0:T(8,128)(2,1)S(1)}) custom-call(f32[8,512]{1,0:T(8,128)} %bitcast.14, bf16[512,512]{1,0:T(8,128)(2,1)} %v_ref.1, bf16[512,128]{1,0:T(8,128)(2,1)} %k_hbm.1), custom_call_target="tpu_custom_call" | custom-call | flops 10000000 | bytes 1048576 | tf_op jit(solution)/shard_map/pallas_call | solution.py:117
  1.4 0.0 copy-start.1
  1.4 3.3 %collective-permute-start = (f32[264,128]{1,0:T(8,128)S(1)}, f32[264,128]{1,0:T(8,128)S(1)}, u32[]{:S(2)}, u32[]{:S(2)}) collective-permute-start(f32[264,128]{1,0:T(8,128)S(1)} %get-tuple-element.29), channel_id=1, source_target_pairs={{0,4},{4,0},{8,12},{12,8},{16,20},{20,16},{24,28},{28,24},{32,36},... | collective-permute-start | bytes 405512 | tf_op jit(solution)/shard_map/ppermute | solution.py:351
  4.7 0.3 shard_map.84.own_ref
  5.0 0.0 copy-start.3
  5.0 0.7 %collective-permute-done.rest_0_.got_ref = f32[264,128]{1,0:T(8,128)S(1)} collective-permute-done((f32[264,128]{1,0:T(8,128)S(1)}, f32[264,128]{1,0:T(8,128)S(1)}, u32[]{:S(2)}, u32[]{:S(2)}) %collective-permute-start) | collective-permute-done | bytes 135200 | tf_op jit(solution)/shard_map/ppermute | solution.py:351
  5.7 0.1 collective-permute-start.2
  5.8 0.6 %collective-permute-start.1 = (f32[264,128]{1,0:T(8,128)S(1)}, f32[264,128]{1,0:T(8,128)S(1)}, u32[]{:S(2)}, u32[]{:S(2)}) collective-permute-start(f32[264,128]{1,0:T(8,128)S(1)} %shard_map.84.own_ref), channel_id=1, source_target_pairs={{0,4},{4,0},{8,12},{12,8},{16,20},{20,16},{24,28},{28,24},{32,36},... | collective-permute-start | bytes 405512 | tf_op jit(solution)/shard_map/ppermute | solution.py:351
  6.4 0.0 copy-done.2
  6.4 0.0 copy-done.1
  6.4 0.0 copy-done.3
  6.4 0.0 copy-start
  6.4 0.6 %shard_map.83 = (bf16[256,512]{1,0:T(8,128)(2,1)S(1)}, f32[512,512]{1,0:T(8,128)S(1)}, f32[512,8]{1,0:T(8,128)S(1)}, bf16[512,512]{1,0:T(8,128)(2,1)S(1)}) custom-call(bf16[512,128]{1,0:T(8,128)(2,1)S(1)} %copy-done.3, bf16[512,512]{1,0:T(8,128)(2,1)S(1)} %copy-done.2, f32[8,512]{1,0:T(8,128)S(1)} %get-tuple-element.27.d_ref, bf16[512,512]{1,0:T(8,128)(2,1)S(1)} %copy-done.1), custom_call_target="tpu_custom_call" | custom-call | flops 10000000 | bytes 1048576 | tf_op jit(solution)/shard_map/pallas_call | solution.py:175
  7.0 0.0 copy-start.4
  7.0 0.3 copy-done
  7.4 0.3 copy-done.4
  7.7 1.4 %shard_map.87.rest_3_.refs_0_ = f32[128,512]{1,0:T(8,128)S(1)} custom-call(bf16[512,128]{1,0:T(8,128)(2,1)S(1)} %get-tuple-element.31.k_ref, bf16[256,512]{1,0:T(8,128)(2,1)S(1)} %get-tuple-element.28.qt_ref, bf16[512,512]{1,0:T(8,128)(2,1)S(1)} %get-tuple-element.36.vt_ref, f32[8,512]{1,0:T(8,128)S(1)} %get-tuple-element.27.d_ref, ...), custom_call_target="tpu_custom_call" | custom-call | flops 10000000 | bytes 1048576 | tf_op jit(solution)/shard_map/pallas_call | solution.py:219
  9.1 1.5 %collective-permute-done.2.rest_0_.got_ref = f32[264,128]{1,0:T(8,128)S(1)} collective-permute-done((f32[264,128]{1,0:T(8,128)S(1)}, f32[264,128]{1,0:T(8,128)S(1)}, u32[]{:S(2)}, u32[]{:S(2)}) %collective-permute-start.2) | collective-permute-done | bytes 135200 | tf_op jit(solution)/shard_map/ppermute | solution.py:351
  10.6 2.7 %collective-permute-start.4 = (f32[264,128]{1,0:T(8,128)S(1)}, f32[264,128]{1,0:T(8,128)S(1)}, u32[]{:S(2)}, u32[]{:S(2)}) collective-permute-start(f32[264,128]{1,0:T(8,128)S(1)} %shard_map.89.token_ref.own_ref), channel_id=1, source_target_pairs={{0,24},{4,28},{8,16},{12,20},{16,8},{20,12},{24,0},{28,4},{32,56},... | collective-permute-start | bytes 405512 | tf_op jit(solution)/shard_map/ppermute | solution.py:351
  13.4 1.5 %collective-permute-start.3 = (f32[264,128]{1,0:T(8,128)S(1)}, f32[264,128]{1,0:T(8,128)S(1)}, u32[]{:S(2)}, u32[]{:S(2)}) collective-permute-start(f32[264,128]{1,0:T(8,128)S(1)} %collective-permute-done.2.rest_0_.got_ref), channel_id=1, source_target_pairs={{0,4},{4,0},{8,12},{12,8},{16,20},{20,16},{24,28},{28,24},{32,36},... | collective-permute-start | bytes 405512 | tf_op jit(solution)/shard_map/ppermute | solution.py:351
  14.9 0.0 collective-permute-done.1.rest_1_
  14.9 0.3 shard_map.85
  15.2 1.3 %collective-permute-done.4.rest_0_.got_ref = f32[264,128]{1,0:T(8,128)S(1)} collective-permute-done((f32[264,128]{1,0:T(8,128)S(1)}, f32[264,128]{1,0:T(8,128)S(1)}, u32[]{:S(2)}, u32[]{:S(2)}) %collective-permute-start.4) | collective-permute-done | bytes 135200 | tf_op jit(solution)/shard_map/ppermute | solution.py:351
  16.5 2.3 %collective-permute-start.5 = (f32[264,128]{1,0:T(8,128)S(1)}, f32[264,128]{1,0:T(8,128)S(1)}, u32[]{:S(2)}, u32[]{:S(2)}) collective-permute-start(f32[264,128]{1,0:T(8,128)S(1)} %collective-permute-done.4.rest_0_.got_ref), channel_id=1, source_target_pairs={{0,4},{4,0},{8,12},{12,8},{16,20},{20,16},{24,28},{28,24},{32,36},... | collective-permute-start | bytes 405512 | tf_op jit(solution)/shard_map/ppermute | solution.py:351
  18.8 1.4 %shard_map.90.rest_3_.refs_0_ = f32[128,512]{1,0:T(8,128)S(1)} custom-call(bf16[512,128]{1,0:T(8,128)(2,1)S(1)} %get-tuple-element.31.k_ref, bf16[256,512]{1,0:T(8,128)(2,1)S(1)} %get-tuple-element.28.qt_ref, bf16[512,512]{1,0:T(8,128)(2,1)S(1)} %get-tuple-element.36.vt_ref, f32[8,512]{1,0:T(8,128)S(1)} %get-tuple-element.27.d_ref, ...), custom_call_target="tpu_custom_call" | custom-call | flops 10000000 | bytes 1048576 | tf_op jit(solution)/shard_map/pallas_call | solution.py:219
  20.2 4.0 %collective-permute-start.6 = (f32[264,128]{1,0:T(8,128)S(1)}, f32[264,128]{1,0:T(8,128)S(1)}, u32[]{:S(2)}, u32[]{:S(2)}) collective-permute-start(f32[264,128]{1,0:T(8,128)S(1)} %shard_map.92.token_ref.own_ref), channel_id=1, source_target_pairs={{0,56},{4,60},{8,48},{12,52},{16,40},{20,44},{24,32},{28,36},{32,2... | collective-permute-start | bytes 405512 | tf_op jit(solution)/shard_map/ppermute | solution.py:351
  24.1 1.4 %shard_map.93.refs_0_.rest_3_ = f32[128,512]{1,0:T(8,128)S(1)} custom-call(bf16[512,128]{1,0:T(8,128)(2,1)S(1)} %get-tuple-element.31.k_ref, bf16[256,512]{1,0:T(8,128)(2,1)S(1)} %get-tuple-element.28.qt_ref, bf16[512,512]{1,0:T(8,128)(2,1)S(1)} %get-tuple-element.36.vt_ref, f32[8,512]{1,0:T(8,128)S(1)} %get-tuple-element.27.d_ref, ...), custom_call_target="tpu_custom_call" | custom-call | flops 10000000 | bytes 1048576 | tf_op jit(solution)/shard_map/pallas_call | solution.py:219
  25.5 0.0 collective-permute-done.3.rest_1_
  25.5 0.4 shard_map.88
  25.9 0.0 collective-permute-done.5.rest_1_
  25.9 0.4 shard_map.91
  26.3 4.7 %collective-permute-done.6.got_ref.rest_0_ = f32[264,128]{1,0:T(8,128)S(1)} collective-permute-done((f32[264,128]{1,0:T(8,128)S(1)}, f32[264,128]{1,0:T(8,128)S(1)}, u32[]{:S(2)}, u32[]{:S(2)}) %collective-permute-start.6) | collective-permute-done | bytes 135200 | tf_op jit(solution)/shard_map/ppermute | solution.py:351
  31.0 1.3 %collective-permute-start.8 = (f32[264,128]{1,0:T(8,128)S(1)}, f32[264,128]{1,0:T(8,128)S(1)}, u32[]{:S(2)}, u32[]{:S(2)}) collective-permute-start(f32[264,128]{1,0:T(8,128)S(1)} %shard_map.94.token_ref), channel_id=1, source_target_pairs={{0,64},{4,68},{8,72},{12,76},{16,80},{20,84},{24,88},{28,92},{32,9... | collective-permute-start | bytes 405512 | tf_op jit(solution)/shard_map/ppermute | solution.py:351
  32.3 0.9 %collective-permute-start.7 = (f32[264,128]{1,0:T(8,128)S(1)}, f32[264,128]{1,0:T(8,128)S(1)}, u32[]{:S(2)}, u32[]{:S(2)}) collective-permute-start(f32[264,128]{1,0:T(8,128)S(1)} %collective-permute-done.6.got_ref.rest_0_), channel_id=1, source_target_pairs={{0,4},{4,0},{8,12},{12,8},{16,20},{20,16},{24,28},{28,24},{32,36},... | collective-permute-start | bytes 405512 | tf_op jit(solution)/shard_map/ppermute | solution.py:351
  33.2 2.5 %collective-permute-start.9 = (f32[264,128]{1,0:T(8,128)S(1)}, f32[264,128]{1,0:T(8,128)S(1)}, u32[]{:S(2)}, u32[]{:S(2)}) collective-permute-start(f32[264,128]{1,0:T(8,128)S(1)} %shard_map.94.token_ref), channel_id=1, source_target_pairs={{0,128},{4,132},{8,136},{12,140},{16,144},{20,148},{24,152},{28,15... | collective-permute-start | bytes 405512 | tf_op jit(solution)/shard_map/ppermute | solution.py:351
  35.6 0.2 collective-permute-start.10
  35.8 1.4 %shard_map.95.rest_4_ = f32[128,512]{1,0:T(8,128)S(1)} custom-call(bf16[512,128]{1,0:T(8,128)(2,1)S(1)} %get-tuple-element.31.k_ref, bf16[256,512]{1,0:T(8,128)(2,1)S(1)} %get-tuple-element.28.qt_ref, bf16[512,512]{1,0:T(8,128)(2,1)S(1)} %get-tuple-element.36.vt_ref, f32[8,512]{1,0:T(8,128)S(1)} %get-tuple-element.27.d_ref, ...), custom_call_target="tpu_custom_call" | custom-call | flops 10000000 | bytes 1048576 | tf_op jit(solution)/shard_map/pallas_call | solution.py:219
  37.2 0.0 collective-permute-done.8.near_ref
  37.2 0.6 %collective-permute-start.11 = (f32[264,128]{1,0:T(8,128)S(1)}, f32[264,128]{1,0:T(8,128)S(1)}, u32[]{:S(2)}, u32[]{:S(2)}) collective-permute-start(f32[264,128]{1,0:T(8,128)S(1)} %collective-permute-done.8.near_ref), channel_id=1, source_target_pairs={{0,4},{4,0},{8,12},{12,8},{16,20},{20,16},{24,28},{28,24},{32,36},... | collective-permute-start | bytes 405512 | tf_op jit(solution)/shard_map/ppermute | solution.py:351
  37.9 0.0 collective-permute-done.7.rest_1_
  37.9 0.4 shard_map.96
  38.3 2.5 %collective-permute-done.9.own_ref = f32[264,128]{1,0:T(8,128)S(1)} collective-permute-done((f32[264,128]{1,0:T(8,128)S(1)}, f32[264,128]{1,0:T(8,128)S(1)}, u32[]{:S(2)}, u32[]{:S(2)}) %collective-permute-start.9) | collective-permute-done | bytes 135200 | tf_op jit(solution)/shard_map/ppermute | solution.py:351
  40.8 3.4 %collective-permute-done.10.got_ref = f32[264,128]{1,0:T(8,128)S(1)} collective-permute-done((f32[264,128]{1,0:T(8,128)S(1)}, f32[264,128]{1,0:T(8,128)S(1)}, u32[]{:S(2)}, u32[]{:S(2)}) %collective-permute-start.10) | collective-permute-done | bytes 135200 | tf_op jit(solution)/shard_map/ppermute | solution.py:351
  44.3 1.0 %collective-permute-start.12 = (f32[264,128]{1,0:T(8,128)S(1)}, f32[264,128]{1,0:T(8,128)S(1)}, u32[]{:S(2)}, u32[]{:S(2)}) collective-permute-start(f32[264,128]{1,0:T(8,128)S(1)} %shard_map.97.far_ref), channel_id=1, source_target_pairs={{0,4},{4,0},{8,12},{12,8},{16,20},{20,16},{24,28},{28,24},{32,36},... | collective-permute-start | bytes 405512 | tf_op jit(solution)/shard_map/ppermute | solution.py:351
  45.2 0.4 shard_map.98
  45.6 0.0 collective-permute-done.11.near_ref
  45.6 0.6 %collective-permute-done.12.far_ref = f32[264,128]{1,0:T(8,128)S(1)} collective-permute-done((f32[264,128]{1,0:T(8,128)S(1)}, f32[264,128]{1,0:T(8,128)S(1)}, u32[]{:S(2)}, u32[]{:S(2)}) %collective-permute-start.12) | collective-permute-done | bytes 135200 | tf_op jit(solution)/shard_map/ppermute | solution.py:351
  46.2 0.4 shard_map.99
  46.6 3.0 %collective-permute-start.13 = (f32[1,512]{1,0:T(1,128)S(1)}, f32[1,512]{1,0:T(1,128)S(1)}, u32[]{:S(2)}, u32[]{:S(2)}) collective-permute-start(f32[1,512]{1,0:T(1,128)S(1)} %get-tuple-element.48.a_ref), channel_id=1, source_target_pairs={{0,2},{1,3},{2,0},{3,1},{4,6},{5,7},{6,4},{7,5},{8,10},{9,11},{10,... | collective-permute-start | bytes 6152 | tf_op jit(solution)/shard_map/ppermute | solution.py:351
  49.6 0.4 collective-permute-start.14
  50.0 0.4 collective-permute-start.15
  50.4 0.0 copy-start.5
  50.4 0.7 %copy-done.5 = f32[512]{0:T(512)S(1)} copy-done((f32[512]{0:T(512)S(1)}, f32[512]{0:T(512)}, u32[]{:S(2)}) %copy-start.5) | copy-done | bytes 2072
  51.0 0.3 shard_map.100.g_ref
  51.4 0.0 collective-permute-done.13.b_ref
  51.4 0.6 %collective-permute-done.14.c_ref = f32[1,512]{1,0:T(1,128)S(1)} collective-permute-done((f32[1,512]{1,0:T(1,128)S(1)}, f32[1,512]{1,0:T(1,128)S(1)}, u32[]{:S(2)}, u32[]{:S(2)}) %collective-permute-start.14) | collective-permute-done | bytes 2080 | tf_op jit(solution)/shard_map/ppermute | solution.py:351
  52.0 1.6 %collective-permute-done.15.e_ref = f32[1,512]{1,0:T(1,128)S(1)} collective-permute-done((f32[1,512]{1,0:T(1,128)S(1)}, f32[1,512]{1,0:T(1,128)S(1)}, u32[]{:S(2)}, u32[]{:S(2)}) %collective-permute-start.15) | collective-permute-done | bytes 2080 | tf_op jit(solution)/shard_map/ppermute | solution.py:351
  53.6 0.9 %shard_map.101 = bf16[512,512]{1,0:T(8,128)(2,1)} custom-call(f32[512,512]{1,0:T(8,128)S(1)} %shard_map.100.g_ref, f32[1,512]{1,0:T(1,128)S(1)} %get-tuple-element.48.a_ref, f32[1,512]{1,0:T(1,128)S(1)} %collective-permute-done.13.b_ref, f32[1,512]{1,0:T(1,128)S(1)} %collective-permute-done.14.c_ref, f32[1,512]{1,0:T(1,128)S(1)} %collective-permute-done.15.e_ref), custom_call_target="tpu_custom_call" | custom-call | flops 100000000 | bytes 1048576 | tf_op jit(solution)/shard_map/pallas_call | solution.py:342
  (6 shorter events, 0.2 us)
Async XLA Ops:
  0.0 6.4 %copy-start.2 = (bf16[512,512]{1,0:T(8,128)(2,1)S(1)}, bf16[512,512]{1,0:T(8,128)(2,1)}, u32[]{:S(2)}) copy-start(bf16[512,512]{1,0:T(8,128)(2,1)} %gate_ref.1) | copy-start | bytes 1572868
  1.4 5.0 %copy-start.1 = (bf16[512,512]{1,0:T(8,128)(2,1)S(1)}, bf16[512,512]{1,0:T(8,128)(2,1)}, u32[]{:S(2)}) copy-start(bf16[512,512]{1,0:T(8,128)(2,1)} %v_ref.1) | copy-start | bytes 1572868
  1.4 4.3 %collective-permute-start = (f32[264,128]{1,0:T(8,128)S(1)}, f32[264,128]{1,0:T(8,128)S(1)}, u32[]{:S(2)}, u32[]{:S(2)}) collective-permute-start(f32[264,128]{1,0:T(8,128)S(1)} %get-tuple-element.29), channel_id=1, source_target_pairs={{0,4},{4,0},{8,12},{12,8},{16,20},{20,16},{24,28},{28,24},{32,36},... | collective-permute-start | bytes 405512 | tf_op jit(solution)/shard_map/ppermute | solution.py:351
  5.0 1.4 %copy-start.3 = (bf16[512,128]{1,0:T(8,128)(2,1)S(1)}, bf16[512,128]{1,0:T(8,128)(2,1)}, u32[]{:S(2)}) copy-start(bf16[512,128]{1,0:T(8,128)(2,1)} %q_ref.1) | copy-start | bytes 393220
  5.7 4.9 %collective-permute-start.2 = (f32[264,128]{1,0:T(8,128)S(1)}, f32[264,128]{1,0:T(8,128)S(1)}, u32[]{:S(2)}, u32[]{:S(2)}) collective-permute-start(f32[264,128]{1,0:T(8,128)S(1)} %shard_map.86.token_ref.own_ref), channel_id=1, source_target_pairs={{0,8},{4,12},{8,0},{12,4},{16,24},{20,28},{24,16},{28,20},{32,40},... | collective-permute-start | bytes 405512 | tf_op jit(solution)/shard_map/ppermute | solution.py:351
  5.8 9.0 %collective-permute-start.1 = (f32[264,128]{1,0:T(8,128)S(1)}, f32[264,128]{1,0:T(8,128)S(1)}, u32[]{:S(2)}, u32[]{:S(2)}) collective-permute-start(f32[264,128]{1,0:T(8,128)S(1)} %shard_map.84.own_ref), channel_id=1, source_target_pairs={{0,4},{4,0},{8,12},{12,8},{16,20},{20,16},{24,28},{28,24},{32,36},... | collective-permute-start | bytes 405512 | tf_op jit(solution)/shard_map/ppermute | solution.py:351
  6.4 1.0 %copy-start = (f32[512,8,18]{0,1,2:T(8,128)S(1)}, f32[512,8,18]{0,1,2:T(8,128)}, u32[]{:S(2)}) copy-start(f32[512,8,18]{0,1,2:T(8,128)} %param.12) | copy-start | bytes 884740
  7.0 0.7 %copy-start.4 = (f32[8]{0:T(128)S(1)}, f32[8]{0:T(128)}, u32[]{:S(2)}) copy-start(f32[8]{0:T(128)} %skip_ref.7) | copy-start | bytes 100
  10.6 5.8 %collective-permute-start.4 = (f32[264,128]{1,0:T(8,128)S(1)}, f32[264,128]{1,0:T(8,128)S(1)}, u32[]{:S(2)}, u32[]{:S(2)}) collective-permute-start(f32[264,128]{1,0:T(8,128)S(1)} %shard_map.89.token_ref.own_ref), channel_id=1, source_target_pairs={{0,24},{4,28},{8,16},{12,20},{16,8},{20,12},{24,0},{28,4},{32,56},... | collective-permute-start | bytes 405512 | tf_op jit(solution)/shard_map/ppermute | solution.py:351
  13.4 12.2 %collective-permute-start.3 = (f32[264,128]{1,0:T(8,128)S(1)}, f32[264,128]{1,0:T(8,128)S(1)}, u32[]{:S(2)}, u32[]{:S(2)}) collective-permute-start(f32[264,128]{1,0:T(8,128)S(1)} %collective-permute-done.2.rest_0_.got_ref), channel_id=1, source_target_pairs={{0,4},{4,0},{8,12},{12,8},{16,20},{20,16},{24,28},{28,24},{32,36},... | collective-permute-start | bytes 405512 | tf_op jit(solution)/shard_map/ppermute | solution.py:351
  16.5 9.4 %collective-permute-start.5 = (f32[264,128]{1,0:T(8,128)S(1)}, f32[264,128]{1,0:T(8,128)S(1)}, u32[]{:S(2)}, u32[]{:S(2)}) collective-permute-start(f32[264,128]{1,0:T(8,128)S(1)} %collective-permute-done.4.rest_0_.got_ref), channel_id=1, source_target_pairs={{0,4},{4,0},{8,12},{12,8},{16,20},{20,16},{24,28},{28,24},{32,36},... | collective-permute-start | bytes 405512 | tf_op jit(solution)/shard_map/ppermute | solution.py:351
  20.2 10.8 %collective-permute-start.6 = (f32[264,128]{1,0:T(8,128)S(1)}, f32[264,128]{1,0:T(8,128)S(1)}, u32[]{:S(2)}, u32[]{:S(2)}) collective-permute-start(f32[264,128]{1,0:T(8,128)S(1)} %shard_map.92.token_ref.own_ref), channel_id=1, source_target_pairs={{0,56},{4,60},{8,48},{12,52},{16,40},{20,44},{24,32},{28,36},{32,2... | collective-permute-start | bytes 405512 | tf_op jit(solution)/shard_map/ppermute | solution.py:351
  31.0 6.2 %collective-permute-start.8 = (f32[264,128]{1,0:T(8,128)S(1)}, f32[264,128]{1,0:T(8,128)S(1)}, u32[]{:S(2)}, u32[]{:S(2)}) collective-permute-start(f32[264,128]{1,0:T(8,128)S(1)} %shard_map.94.token_ref), channel_id=1, source_target_pairs={{0,64},{4,68},{8,72},{12,76},{16,80},{20,84},{24,88},{28,92},{32,9... | collective-permute-start | bytes 405512 | tf_op jit(solution)/shard_map/ppermute | solution.py:351
  32.3 5.6 %collective-permute-start.7 = (f32[264,128]{1,0:T(8,128)S(1)}, f32[264,128]{1,0:T(8,128)S(1)}, u32[]{:S(2)}, u32[]{:S(2)}) collective-permute-start(f32[264,128]{1,0:T(8,128)S(1)} %collective-permute-done.6.got_ref.rest_0_), channel_id=1, source_target_pairs={{0,4},{4,0},{8,12},{12,8},{16,20},{20,16},{24,28},{28,24},{32,36},... | collective-permute-start | bytes 405512 | tf_op jit(solution)/shard_map/ppermute | solution.py:351
  33.2 7.6 %collective-permute-start.9 = (f32[264,128]{1,0:T(8,128)S(1)}, f32[264,128]{1,0:T(8,128)S(1)}, u32[]{:S(2)}, u32[]{:S(2)}) collective-permute-start(f32[264,128]{1,0:T(8,128)S(1)} %shard_map.94.token_ref), channel_id=1, source_target_pairs={{0,128},{4,132},{8,136},{12,140},{16,144},{20,148},{24,152},{28,15... | collective-permute-start | bytes 405512 | tf_op jit(solution)/shard_map/ppermute | solution.py:351
  35.6 8.6 %collective-permute-start.10 = (f32[264,128]{1,0:T(8,128)S(1)}, f32[264,128]{1,0:T(8,128)S(1)}, u32[]{:S(2)}, u32[]{:S(2)}) collective-permute-start(f32[264,128]{1,0:T(8,128)S(1)} %shard_map.94.token_ref), channel_id=1, source_target_pairs={{0,192},{4,196},{8,200},{12,204},{16,208},{20,212},{24,216},{28,22... | collective-permute-start | bytes 405512 | tf_op jit(solution)/shard_map/ppermute | solution.py:351
  37.2 8.4 %collective-permute-start.11 = (f32[264,128]{1,0:T(8,128)S(1)}, f32[264,128]{1,0:T(8,128)S(1)}, u32[]{:S(2)}, u32[]{:S(2)}) collective-permute-start(f32[264,128]{1,0:T(8,128)S(1)} %collective-permute-done.8.near_ref), channel_id=1, source_target_pairs={{0,4},{4,0},{8,12},{12,8},{16,20},{20,16},{24,28},{28,24},{32,36},... | collective-permute-start | bytes 405512 | tf_op jit(solution)/shard_map/ppermute | solution.py:351
  44.3 2.0 %collective-permute-start.12 = (f32[264,128]{1,0:T(8,128)S(1)}, f32[264,128]{1,0:T(8,128)S(1)}, u32[]{:S(2)}, u32[]{:S(2)}) collective-permute-start(f32[264,128]{1,0:T(8,128)S(1)} %shard_map.97.far_ref), channel_id=1, source_target_pairs={{0,4},{4,0},{8,12},{12,8},{16,20},{20,16},{24,28},{28,24},{32,36},... | collective-permute-start | bytes 405512 | tf_op jit(solution)/shard_map/ppermute | solution.py:351
  46.6 4.8 %collective-permute-start.13 = (f32[1,512]{1,0:T(1,128)S(1)}, f32[1,512]{1,0:T(1,128)S(1)}, u32[]{:S(2)}, u32[]{:S(2)}) collective-permute-start(f32[1,512]{1,0:T(1,128)S(1)} %get-tuple-element.48.a_ref), channel_id=1, source_target_pairs={{0,2},{1,3},{2,0},{3,1},{4,6},{5,7},{6,4},{7,5},{8,10},{9,11},{10,... | collective-permute-start | bytes 6152 | tf_op jit(solution)/shard_map/ppermute | solution.py:351
  49.6 2.4 %collective-permute-start.14 = (f32[1,512]{1,0:T(1,128)S(1)}, f32[1,512]{1,0:T(1,128)S(1)}, u32[]{:S(2)}, u32[]{:S(2)}) collective-permute-start(f32[1,512]{1,0:T(1,128)S(1)} %get-tuple-element.48.a_ref), channel_id=1, source_target_pairs={{0,1},{1,0},{2,3},{3,2},{4,5},{5,4},{6,7},{7,6},{8,9},{9,8},{10,11... | collective-permute-start | bytes 6152 | tf_op jit(solution)/shard_map/ppermute | solution.py:351
  50.0 3.6 %collective-permute-start.15 = (f32[1,512]{1,0:T(1,128)S(1)}, f32[1,512]{1,0:T(1,128)S(1)}, u32[]{:S(2)}, u32[]{:S(2)}) collective-permute-start(f32[1,512]{1,0:T(1,128)S(1)} %get-tuple-element.48.a_ref), channel_id=1, source_target_pairs={{0,3},{1,2},{2,1},{3,0},{4,7},{5,6},{6,5},{7,4},{8,11},{9,10},{10,... | collective-permute-start | bytes 6152 | tf_op jit(solution)/shard_map/ppermute | solution.py:351
  50.4 0.7 %copy-start.5 = (f32[512]{0:T(512)S(1)}, f32[512]{0:T(512)}, u32[]{:S(2)}) copy-start(f32[512]{0:T(512)} %param.15) | copy-start | bytes 6148

commit v8 on v7

--- a/solution.py
+++ b/solution.py
@@ -42,8 +42,9 @@
     return jax.ShapeDtypeStruct(shape, dtype)
 
 
-def core_index():
-    return lax.axis_index("tok") & 1
+def half_index():
+    position = lax.axis_index("tok")
+    return (position ^ (position >> 1) ^ (position >> 5)) & 1
 
 
 def split3(x):
@@ -70,10 +71,10 @@
     ld_hbm, v_hbm, k_hbm, d_ref, toend_ref, total_ref, send_ref, mine_ref, k_ref,
     ld_ref, theirs_ref, sems,
 ):
-    me = core_index()
+    me = half_index()
     columns = lambda side: pl.ds(pl.multiple_of(side * ROWS, ROWS), ROWS)
     pairs = (
-        (v_hbm.at[:, columns(1 - me)], theirs_ref), (ld_hbm, ld_ref), (k_hbm, k_ref),
+        (ld_hbm, ld_ref), (v_hbm.at[:, columns(1 - me)], theirs_ref), (k_hbm, k_ref),
         (v_hbm.at[:, columns(me)], mine_ref),
     )
     copies = [pltpu.make_async_copy(a, b, sems.at[i]) for i, (a, b) in enumerate(pairs)]
@@ -82,7 +83,7 @@
     row = lax.broadcasted_iota(jnp.int32, (128, 128), 0)
     col = lax.broadcasted_iota(jnp.int32, (128, 128), 1)
     upto = (row <= col).astype(F32).astype(BF16)
-    copies[1].wait()
+    copies[0].wait()
     terms = []
     for j in range(4):
         ld = ld_ref[:, j * 128 : (j + 1) * 128]
@@ -105,7 +106,7 @@
         cols = slice(j * 128, (j + 1) * 128)
         d_ref[:, cols] = d[j]
         toend_ref[:, cols] = jnp.exp(total - d[j])
-    copies[0].wait()
+    copies[1].wait()
     copies[2].wait()
     product(theirs_ref[...], toend_ref, total, 1 - me, k_ref[...], send_ref)
     copies[3].wait()
@@ -125,7 +126,7 @@
 
 
 def own_body(v_ref, k_ref, toend_ref, total_ref, out_ref):
-    product(v_ref[...], toend_ref, total_ref[...], core_index(), k_ref[...], out_ref)
+    product(v_ref[...], toend_ref, total_ref[...], half_index(), k_ref[...], out_ref)
 
 
 def own_state(v, k, toend, total):
@@ -140,7 +141,7 @@
     one = jnp.ones_like(own_ext)
     fac_ref[0:HEADS] = jnp.where(upper, one, jnp.exp(got_ext))
     fac_ref[HEADS : 2 * HEADS] = jnp.where(upper, jnp.exp(own_ext), one)
-    first = core_index() * HALF
+    first = half_index() * HALF
     for j in range(HALF):
         rows = slice(j * WIDTH, (j + 1) * WIDTH)
         fa = fac_ref[pl.ds(first + j, 1), :]
@@ -227,7 +228,7 @@
     upper = ((lax.axis_index("tok") >> level) & 1) == 1
     gain = jnp.where(upper, jnp.exp(lead), 0.0)[:, 0:1]
     coef_ref[...] = w_ref[LOCAL_BITS + 1 + level] * jnp.exp(d_ref[...]) * gain
-    core = core_index()
+    core = half_index()
     for n, ref in zip(sides, buf_refs):
         side = core if n == 0 else 1 - core
         states = ref[0:ROWS]
@@ -275,7 +276,7 @@
 ):
     out_ref, sq_ref, coef_ref = rest[-3:]
     sums = [] if side == 0 else [rest[0][...]]
-    half = core_index() if side == 0 else 1 - core_index()
+    half = half_index() if side == 0 else 1 - half_index()
     place = lambda row: pl.ds(pl.multiple_of(row - half * ROWS, WIDTH), WIDTH)
 
     def keep(row, value):
@@ -309,7 +310,7 @@
 
 
 def turn_body(own_ref, other_ref, gain_ref, out_ref):
-    core = core_index()
+    core = half_index()
     for ref, side in ((own_ref, core), (other_ref, 1 - core)):
         cols = pl.ds(pl.multiple_of(side * ROWS, ROWS), ROWS)
         gain = gain_ref[:, cols]
@@ -351,7 +352,7 @@
     return lax.ppermute(x, axis, [(i, i ^ flip) for i in range(count)])
 
 
-CORE, Z1, Z3, Z7, X1, X2, X3 = 1, 2, 6, 14, 16, 32, 48
+CORE, Z1, Z3, Z7, X1, X2, X3 = 1, 3, 7, 15, 16, 33, 49
 
 
 def work(head_inputs, state_keys, state_queries, log_decay, level_weight, skip_scale, gate_input, norm_gain):
@@ -390,11 +391,12 @@
     x2 = hop(line, "tok", X2)
     x1 = hop(line, "tok", X1)
     x3 = hop(line, "tok", X3)
+    fourth = swap(x1)
     beyond = merge(4, x2, x3, acc)
     other = swap(beyond)
     last = (qt, d, w, lead, acc, gt)
     near_half, part = close(4, 0, *last, x1, beyond)
-    rest, squares = close(4, 1, *last, swap(x1), other, part)
+    rest, squares = close(4, 1, *last, fourth, other, part)
     shares = [hop(squares, "head", 2), hop(squares, "head", 1), hop(squares, "head", 3)]
     turned = turn(near_half, rest, norm_gain[None])
     return finish(HEADS * WIDTH * lax.axis_size("head"), turned, [squares, *shares])

time: 54.9 us -> 55.3 us (level)
  waiting for transfers between devices: 17 us -> 21.4 us
  starting transfers between devices: 24.6 us -> 20.7 us
    ppermute x16, waiting for transfers between devices: 17 us -> 21.4 us  [hop(): return lax.ppermute(x, axis, [(i, i ^ flip) for i in range(count)])]
    ppermute x16, starting transfers between devices: 24.6 us -> 20.7 us  [hop(): return lax.ppermute(x, axis, [(i, i ^ flip) for i in range(count)])]
where the time goes in v8:
time: 55.3 us; the launch traced here: 55.2 us
  waiting for transfers between devices  21.4 us (39%)
  starting transfers between devices  20.7 us (37%)
  Pallas kernels  11.4 us (21%)
  local copies, waits for them, and re-layouts  1.37 us (2%)
    ppermute x16, waiting for transfers between devices, hop(): return lax.ppermute(x, axis, [(i, i ^ flip) for i in range(count)])  21.4 us
    ppermute x16, starting transfers between devices, hop(): return lax.ppermute(x, axis, [(i, i ^ flip) for i in range(count)])  20.7 us
    pallas_call x4, Pallas kernels, near(): call(functools.partial(near_body, first), sds((2 * WIDTH, BLOCK)), [VM] *...  5.55 us
    pallas_call x4, Pallas kernels, far(): call(functools.partial(far_body, level), [sds((BLOCK, BLOCK)), sds((HEADS...  1.43 us
    unnamed x12, local copies, waits for them, and re-layouts  1.37 us
    pallas_call x1, Pallas kernels, prep(): call(prep_body, outs, [HB] * 3, 10 ** 7, scratch=[pltpu.VMEM((HEADS, BLOC...  1.36 us
  transfers between devices with their start and end apart: 16, of which 9 were waited for; matrix products, arithmetic and copies ran while one was open for 0% of the time, Pallas kernels for 16%

profile of v8, /device:TPU:1, one launch (start us, length us, event | category | flops | bytes accessed | tf_op | source)
XLA Modules:
  0.0 55.2 jit_solution(423953526145624247)
XLA Ops:
  0.0 0.0 copy-start.2
  0.0 1.4 %shard_map.82 = (f32[8,512]{1,0:T(8,128)S(1)}, f32[8,512]{1,0:T(8,128)S(1)}, f32[8,128]{1,0:T(8,128)S(1)}, f32[264,128]{1,0:T(8,128)S(1)}, bf16[512,256]{1,0:T(8,128)(2,1)S(1)}, /*index=5*/bf16[512,128]{1,0:T(8,128)(2,1)S(1)}) custom-call(f32[8,512]{1,0:T(8,128)} %bitcast.14, bf16[512,512]{1,0:T(8,128)(2,1)} %v_ref.1, bf16[512,128]{1,0:T(8,128)(2,1)} %k_hbm.1), custom_call_target="tpu_custom_call" | custom-call | flops 10000000 | bytes 1048576 | tf_op jit(solution)/shard_map/pallas_call | solution.py:118
  1.4 0.0 copy-start.1
  1.4 3.3 %collective-permute-start = (f32[264,128]{1,0:T(8,128)S(1)}, f32[264,128]{1,0:T(8,128)S(1)}, u32[]{:S(2)}, u32[]{:S(2)}) collective-permute-start(f32[264,128]{1,0:T(8,128)S(1)} %get-tuple-element.29), channel_id=1, source_target_pairs={{0,4},{4,0},{8,12},{12,8},{16,20},{20,16},{24,28},{28,24},{32,36},... | collective-permute-start | bytes 405512 | tf_op jit(solution)/shard_map/ppermute | solution.py:352
  4.7 0.3 shard_map.84.own_ref
  5.0 0.0 copy-start.3
  5.0 0.7 %collective-permute-done.rest_0_.got_ref = f32[264,128]{1,0:T(8,128)S(1)} collective-permute-done((f32[264,128]{1,0:T(8,128)S(1)}, f32[264,128]{1,0:T(8,128)S(1)}, u32[]{:S(2)}, u32[]{:S(2)}) %collective-permute-start) | collective-permute-done | bytes 135200 | tf_op jit(solution)/shard_map/ppermute | solution.py:352
  5.7 0.3 collective-permute-start.2
  6.0 0.3 collective-permute-start.1
  6.3 0.0 copy-done.2
  6.3 0.0 copy-done.1
  6.3 0.0 copy-done.3
  6.3 0.0 copy-start
  6.3 0.6 %shard_map.83 = (bf16[256,512]{1,0:T(8,128)(2,1)S(1)}, f32[512,512]{1,0:T(8,128)S(1)}, f32[512,8]{1,0:T(8,128)S(1)}, bf16[512,512]{1,0:T(8,128)(2,1)S(1)}) custom-call(bf16[512,128]{1,0:T(8,128)(2,1)S(1)} %copy-done.3, bf16[512,512]{1,0:T(8,128)(2,1)S(1)} %copy-done.2, f32[8,512]{1,0:T(8,128)S(1)} %get-tuple-element.27.d_ref, bf16[512,512]{1,0:T(8,128)(2,1)S(1)} %copy-done.1), custom_call_target="tpu_custom_call" | custom-call | flops 10000000 | bytes 1048576 | tf_op jit(solution)/shard_map/pallas_call | solution.py:176
  6.9 0.0 copy-start.4
  6.9 0.3 copy-done
  7.2 0.3 copy-done.4
  7.5 1.4 %shard_map.87.rest_3_.refs_0_ = f32[128,512]{1,0:T(8,128)S(1)} custom-call(bf16[512,128]{1,0:T(8,128)(2,1)S(1)} %get-tuple-element.31.k_ref, bf16[256,512]{1,0:T(8,128)(2,1)S(1)} %get-tuple-element.28.qt_ref, bf16[512,512]{1,0:T(8,128)(2,1)S(1)} %get-tuple-element.36.vt_ref, f32[8,512]{1,0:T(8,128)S(1)} %get-tuple-element.27.d_ref, ...), custom_call_target="tpu_custom_call" | custom-call | flops 10000000 | bytes 1048576 | tf_op jit(solution)/shard_map/pallas_call | solution.py:220
  8.9 2.4 %collective-permute-done.2.rest_0_.got_ref = f32[264,128]{1,0:T(8,128)S(1)} collective-permute-done((f32[264,128]{1,0:T(8,128)S(1)}, f32[264,128]{1,0:T(8,128)S(1)}, u32[]{:S(2)}, u32[]{:S(2)}) %collective-permute-start.2) | collective-permute-done | bytes 135200 | tf_op jit(solution)/shard_map/ppermute | solution.py:352
  11.4 3.0 %collective-permute-start.4 = (f32[264,128]{1,0:T(8,128)S(1)}, f32[264,128]{1,0:T(8,128)S(1)}, u32[]{:S(2)}, u32[]{:S(2)}) collective-permute-start(f32[264,128]{1,0:T(8,128)S(1)} %shard_map.89.token_ref.own_ref), channel_id=1, source_target_pairs={{0,28},{4,24},{8,20},{12,16},{16,12},{20,8},{24,4},{28,0},{32,60},... | collective-permute-start | bytes 405512 | tf_op jit(solution)/shard_map/ppermute | solution.py:352
  14.4 0.1 collective-permute-start.3
  14.5 0.0 collective-permute-done.1.rest_1_
  14.5 0.3 shard_map.85
  14.8 4.1 %collective-permute-done.4.rest_0_.got_ref = f32[264,128]{1,0:T(8,128)S(1)} collective-permute-done((f32[264,128]{1,0:T(8,128)S(1)}, f32[264,128]{1,0:T(8,128)S(1)}, u32[]{:S(2)}, u32[]{:S(2)}) %collective-permute-start.4) | collective-permute-done | bytes 135200 | tf_op jit(solution)/shard_map/ppermute | solution.py:352
  18.9 0.4 collective-permute-start.5
  19.3 1.4 %shard_map.90.rest_3_.refs_0_ = f32[128,512]{1,0:T(8,128)S(1)} custom-call(bf16[512,128]{1,0:T(8,128)(2,1)S(1)} %get-tuple-element.31.k_ref, bf16[256,512]{1,0:T(8,128)(2,1)S(1)} %get-tuple-element.28.qt_ref, bf16[512,512]{1,0:T(8,128)(2,1)S(1)} %get-tuple-element.36.vt_ref, f32[8,512]{1,0:T(8,128)S(1)} %get-tuple-element.27.d_ref, ...), custom_call_target="tpu_custom_call" | custom-call | flops 10000000 | bytes 1048576 | tf_op jit(solution)/shard_map/pallas_call | solution.py:220
  20.7 4.0 %collective-permute-start.6 = (f32[264,128]{1,0:T(8,128)S(1)}, f32[264,128]{1,0:T(8,128)S(1)}, u32[]{:S(2)}, u32[]{:S(2)}) collective-permute-start(f32[264,128]{1,0:T(8,128)S(1)} %shard_map.92.token_ref.own_ref), channel_id=1, source_target_pairs={{0,60},{4,56},{8,52},{12,48},{16,44},{20,40},{24,36},{28,32},{32,2... | collective-permute-start | bytes 405512 | tf_op jit(solution)/shard_map/ppermute | solution.py:352
  24.7 1.4 %shard_map.93.refs_0_.rest_3_ = f32[128,512]{1,0:T(8,128)S(1)} custom-call(bf16[512,128]{1,0:T(8,128)(2,1)S(1)} %get-tuple-element.31.k_ref, bf16[256,512]{1,0:T(8,128)(2,1)S(1)} %get-tuple-element.28.qt_ref, bf16[512,512]{1,0:T(8,128)(2,1)S(1)} %get-tuple-element.36.vt_ref, f32[8,512]{1,0:T(8,128)S(1)} %get-tuple-element.27.d_ref, ...), custom_call_target="tpu_custom_call" | custom-call | flops 10000000 | bytes 1048576 | tf_op jit(solution)/shard_map/pallas_call | solution.py:220
  26.1 0.0 collective-permute-done.3.rest_1_
  26.1 0.4 shard_map.88
  26.5 0.0 collective-permute-done.5.rest_1_
  26.5 0.4 shard_map.91
  26.9 4.6 %collective-permute-done.6.got_ref.rest_0_ = f32[264,128]{1,0:T(8,128)S(1)} collective-permute-done((f32[264,128]{1,0:T(8,128)S(1)}, f32[264,128]{1,0:T(8,128)S(1)}, u32[]{:S(2)}, u32[]{:S(2)}) %collective-permute-start.6) | collective-permute-done | bytes 135200 | tf_op jit(solution)/shard_map/ppermute | solution.py:352
  31.5 1.3 %collective-permute-start.8 = (f32[264,128]{1,0:T(8,128)S(1)}, f32[264,128]{1,0:T(8,128)S(1)}, u32[]{:S(2)}, u32[]{:S(2)}) collective-permute-start(f32[264,128]{1,0:T(8,128)S(1)} %shard_map.94.token_ref), channel_id=1, source_target_pairs={{0,64},{4,68},{8,72},{12,76},{16,80},{20,84},{24,88},{28,92},{32,9... | collective-permute-start | bytes 405512 | tf_op jit(solution)/shard_map/ppermute | solution.py:352
  32.8 0.6 %collective-permute-start.7 = (f32[264,128]{1,0:T(8,128)S(1)}, f32[264,128]{1,0:T(8,128)S(1)}, u32[]{:S(2)}, u32[]{:S(2)}) collective-permute-start(f32[264,128]{1,0:T(8,128)S(1)} %collective-permute-done.6.got_ref.rest_0_), channel_id=1, source_target_pairs={{0,4},{4,0},{8,12},{12,8},{16,20},{20,16},{24,28},{28,24},{32,36},... | collective-permute-start | bytes 405512 | tf_op jit(solution)/shard_map/ppermute | solution.py:352
  33.4 2.3 %collective-permute-start.9 = (f32[264,128]{1,0:T(8,128)S(1)}, f32[264,128]{1,0:T(8,128)S(1)}, u32[]{:S(2)}, u32[]{:S(2)}) collective-permute-start(f32[264,128]{1,0:T(8,128)S(1)} %shard_map.94.token_ref), channel_id=1, source_target_pairs={{0,132},{4,128},{8,140},{12,136},{16,148},{20,144},{24,156},{28,15... | collective-permute-start | bytes 405512 | tf_op jit(solution)/shard_map/ppermute | solution.py:352
  35.7 0.6 %collective-permute-start.10 = (f32[264,128]{1,0:T(8,128)S(1)}, f32[264,128]{1,0:T(8,128)S(1)}, u32[]{:S(2)}, u32[]{:S(2)}) collective-permute-start(f32[264,128]{1,0:T(8,128)S(1)} %shard_map.94.token_ref), channel_id=1, source_target_pairs={{0,196},{4,192},{8,204},{12,200},{16,212},{20,208},{24,220},{28,21... | collective-permute-start | bytes 405512 | tf_op jit(solution)/shard_map/ppermute | solution.py:352
  36.3 1.4 %shard_map.95.rest_4_ = f32[128,512]{1,0:T(8,128)S(1)} custom-call(bf16[512,128]{1,0:T(8,128)(2,1)S(1)} %get-tuple-element.31.k_ref, bf16[256,512]{1,0:T(8,128)(2,1)S(1)} %get-tuple-element.28.qt_ref, bf16[512,512]{1,0:T(8,128)(2,1)S(1)} %get-tuple-element.36.vt_ref, f32[8,512]{1,0:T(8,128)S(1)} %get-tuple-element.27.d_ref, ...), custom_call_target="tpu_custom_call" | custom-call | flops 10000000 | bytes 1048576 | tf_op jit(solution)/shard_map/pallas_call | solution.py:220
  37.7 0.0 collective-permute-done.8.near_ref
  37.7 0.1 collective-permute-start.11
  37.8 0.0 collective-permute-done.7.rest_1_
  37.8 0.4 shard_map.96
  38.2 3.8 %collective-permute-done.9.own_ref = f32[264,128]{1,0:T(8,128)S(1)} collective-permute-done((f32[264,128]{1,0:T(8,128)S(1)}, f32[264,128]{1,0:T(8,128)S(1)}, u32[]{:S(2)}, u32[]{:S(2)}) %collective-permute-start.9) | collective-permute-done | bytes 135200 | tf_op jit(solution)/shard_map/ppermute | solution.py:352
  42.1 2.9 %collective-permute-done.10.got_ref = f32[264,128]{1,0:T(8,128)S(1)} collective-permute-done((f32[264,128]{1,0:T(8,128)S(1)}, f32[264,128]{1,0:T(8,128)S(1)}, u32[]{:S(2)}, u32[]{:S(2)}) %collective-permute-start.10) | collective-permute-done | bytes 135200 | tf_op jit(solution)/shard_map/ppermute | solution.py:352
  45.0 0.7 %collective-permute-start.12 = (f32[264,128]{1,0:T(8,128)S(1)}, f32[264,128]{1,0:T(8,128)S(1)}, u32[]{:S(2)}, u32[]{:S(2)}) collective-permute-start(f32[264,128]{1,0:T(8,128)S(1)} %shard_map.97.far_ref), channel_id=1, source_target_pairs={{0,4},{4,0},{8,12},{12,8},{16,20},{20,16},{24,28},{28,24},{32,36},... | collective-permute-start | bytes 405512 | tf_op jit(solution)/shard_map/ppermute | solution.py:352
  45.7 0.4 shard_map.98
  46.0 0.0 collective-permute-done.11.near_ref
  46.0 0.6 %collective-permute-done.12.far_ref = f32[264,128]{1,0:T(8,128)S(1)} collective-permute-done((f32[264,128]{1,0:T(8,128)S(1)}, f32[264,128]{1,0:T(8,128)S(1)}, u32[]{:S(2)}, u32[]{:S(2)}) %collective-permute-start.12) | collective-permute-done | bytes 135200 | tf_op jit(solution)/shard_map/ppermute | solution.py:352
  46.7 0.4 shard_map.99
  47.0 3.0 %collective-permute-start.13 = (f32[1,512]{1,0:T(1,128)S(1)}, f32[1,512]{1,0:T(1,128)S(1)}, u32[]{:S(2)}, u32[]{:S(2)}) collective-permute-start(f32[1,512]{1,0:T(1,128)S(1)} %get-tuple-element.48.a_ref), channel_id=1, source_target_pairs={{0,2},{1,3},{2,0},{3,1},{4,6},{5,7},{6,4},{7,5},{8,10},{9,11},{10,... | collective-permute-start | bytes 6152 | tf_op jit(solution)/shard_map/ppermute | solution.py:352
  50.0 0.4 collective-permute-start.14
  50.4 0.4 collective-permute-start.15
  50.8 0.0 copy-start.5
  50.8 0.7 %copy-done.5 = f32[512]{0:T(512)S(1)} copy-done((f32[512]{0:T(512)S(1)}, f32[512]{0:T(512)}, u32[]{:S(2)}) %copy-start.5) | copy-done | bytes 2072
  51.5 0.3 shard_map.100.g_ref
  51.8 0.0 collective-permute-done.13.b_ref
  51.8 0.6 %collective-permute-done.14.c_ref = f32[1,512]{1,0:T(1,128)S(1)} collective-permute-done((f32[1,512]{1,0:T(1,128)S(1)}, f32[1,512]{1,0:T(1,128)S(1)}, u32[]{:S(2)}, u32[]{:S(2)}) %collective-permute-start.14) | collective-permute-done | bytes 2080 | tf_op jit(solution)/shard_map/ppermute | solution.py:352
  52.5 1.6 %collective-permute-done.15.e_ref = f32[1,512]{1,0:T(1,128)S(1)} collective-permute-done((f32[1,512]{1,0:T(1,128)S(1)}, f32[1,512]{1,0:T(1,128)S(1)}, u32[]{:S(2)}, u32[]{:S(2)}) %collective-permute-start.15) | collective-permute-done | bytes 2080 | tf_op jit(solution)/shard_map/ppermute | solution.py:352
  54.1 0.9 %shard_map.101 = bf16[512,512]{1,0:T(8,128)(2,1)} custom-call(f32[512,512]{1,0:T(8,128)S(1)} %shard_map.100.g_ref, f32[1,512]{1,0:T(1,128)S(1)} %get-tuple-element.48.a_ref, f32[1,512]{1,0:T(1,128)S(1)} %collective-permute-done.13.b_ref, f32[1,512]{1,0:T(1,128)S(1)} %collective-permute-done.14.c_ref, f32[1,512]{1,0:T(1,128)S(1)} %collective-permute-done.15.e_ref), custom_call_target="tpu_custom_call" | custom-call | flops 100000000 | bytes 1048576 | tf_op jit(solution)/shard_map/pallas_call | solution.py:343
  (6 shorter events, 0.2 us)
Async XLA Ops:
  0.0 6.3 %copy-start.2 = (bf16[512,512]{1,0:T(8,128)(2,1)S(1)}, bf16[512,512]{1,0:T(8,128)(2,1)}, u32[]{:S(2)}) copy-start(bf16[512,512]{1,0:T(8,128)(2,1)} %gate_ref.1) | copy-start | bytes 1572868
  1.4 4.9 %copy-start.1 = (bf16[512,512]{1,0:T(8,128)(2,1)S(1)}, bf16[512,512]{1,0:T(8,128)(2,1)}, u32[]{:S(2)}) copy-start(bf16[512,512]{1,0:T(8,128)(2,1)} %v_ref.1) | copy-start | bytes 1572868
  1.4 4.3 %collective-permute-start = (f32[264,128]{1,0:T(8,128)S(1)}, f32[264,128]{1,0:T(8,128)S(1)}, u32[]{:S(2)}, u32[]{:S(2)}) collective-permute-start(f32[264,128]{1,0:T(8,128)S(1)} %get-tuple-element.29), channel_id=1, source_target_pairs={{0,4},{4,0},{8,12},{12,8},{16,20},{20,16},{24,28},{28,24},{32,36},... | collective-permute-start | bytes 405512 | tf_op jit(solution)/shard_map/ppermute | solution.py:352
  5.0 1.3 %copy-start.3 = (bf16[512,128]{1,0:T(8,128)(2,1)S(1)}, bf16[512,128]{1,0:T(8,128)(2,1)}, u32[]{:S(2)}) copy-start(bf16[512,128]{1,0:T(8,128)(2,1)} %q_ref.1) | copy-start | bytes 393220
  5.7 5.6 %collective-permute-start.2 = (f32[264,128]{1,0:T(8,128)S(1)}, f32[264,128]{1,0:T(8,128)S(1)}, u32[]{:S(2)}, u32[]{:S(2)}) collective-permute-start(f32[264,128]{1,0:T(8,128)S(1)} %shard_map.86.token_ref.own_ref), channel_id=1, source_target_pairs={{0,12},{4,8},{8,4},{12,0},{16,28},{20,24},{24,20},{28,16},{32,44},... | collective-permute-start | bytes 405512 | tf_op jit(solution)/shard_map/ppermute | solution.py:352
  6.0 8.5 %collective-permute-start.1 = (f32[264,128]{1,0:T(8,128)S(1)}, f32[264,128]{1,0:T(8,128)S(1)}, u32[]{:S(2)}, u32[]{:S(2)}) collective-permute-start(f32[264,128]{1,0:T(8,128)S(1)} %shard_map.84.own_ref), channel_id=1, source_target_pairs={{0,4},{4,0},{8,12},{12,8},{16,20},{20,16},{24,28},{28,24},{32,36},... | collective-permute-start | bytes 405512 | tf_op jit(solution)/shard_map/ppermute | solution.py:352
  6.3 1.0 %copy-start = (f32[512,8,18]{0,1,2:T(8,128)S(1)}, f32[512,8,18]{0,1,2:T(8,128)}, u32[]{:S(2)}) copy-start(f32[512,8,18]{0,1,2:T(8,128)} %param.12) | copy-start | bytes 884740
  6.9 0.7 %copy-start.4 = (f32[8]{0:T(128)S(1)}, f32[8]{0:T(128)}, u32[]{:S(2)}) copy-start(f32[8]{0:T(128)} %skip_ref.7) | copy-start | bytes 100
  11.4 7.5 %collective-permute-start.4 = (f32[264,128]{1,0:T(8,128)S(1)}, f32[264,128]{1,0:T(8,128)S(1)}, u32[]{:S(2)}, u32[]{:S(2)}) collective-permute-start(f32[264,128]{1,0:T(8,128)S(1)} %shard_map.89.token_ref.own_ref), channel_id=1, source_target_pairs={{0,28},{4,24},{8,20},{12,16},{16,12},{20,8},{24,4},{28,0},{32,60},... | collective-permute-start | bytes 405512 | tf_op jit(solution)/shard_map/ppermute | solution.py:352
  14.4 11.8 %collective-permute-start.3 = (f32[264,128]{1,0:T(8,128)S(1)}, f32[264,128]{1,0:T(8,128)S(1)}, u32[]{:S(2)}, u32[]{:S(2)}) collective-permute-start(f32[264,128]{1,0:T(8,128)S(1)} %collective-permute-done.2.rest_0_.got_ref), channel_id=1, source_target_pairs={{0,4},{4,0},{8,12},{12,8},{16,20},{20,16},{24,28},{28,24},{32,36},... | collective-permute-start | bytes 405512 | tf_op jit(solution)/shard_map/ppermute | solution.py:352
  18.9 7.6 %collective-permute-start.5 = (f32[264,128]{1,0:T(8,128)S(1)}, f32[264,128]{1,0:T(8,128)S(1)}, u32[]{:S(2)}, u32[]{:S(2)}) collective-permute-start(f32[264,128]{1,0:T(8,128)S(1)} %collective-permute-done.4.rest_0_.got_ref), channel_id=1, source_target_pairs={{0,4},{4,0},{8,12},{12,8},{16,20},{20,16},{24,28},{28,24},{32,36},... | collective-permute-start | bytes 405512 | tf_op jit(solution)/shard_map/ppermute | solution.py:352
  20.7 10.7 %collective-permute-start.6 = (f32[264,128]{1,0:T(8,128)S(1)}, f32[264,128]{1,0:T(8,128)S(1)}, u32[]{:S(2)}, u32[]{:S(2)}) collective-permute-start(f32[264,128]{1,0:T(8,128)S(1)} %shard_map.92.token_ref.own_ref), channel_id=1, source_target_pairs={{0,60},{4,56},{8,52},{12,48},{16,44},{20,40},{24,36},{28,32},{32,2... | collective-permute-start | bytes 405512 | tf_op jit(solution)/shard_map/ppermute | solution.py:352
  31.5 6.3 %collective-permute-start.8 = (f32[264,128]{1,0:T(8,128)S(1)}, f32[264,128]{1,0:T(8,128)S(1)}, u32[]{:S(2)}, u32[]{:S(2)}) collective-permute-start(f32[264,128]{1,0:T(8,128)S(1)} %shard_map.94.token_ref), channel_id=1, source_target_pairs={{0,64},{4,68},{8,72},{12,76},{16,80},{20,84},{24,88},{28,92},{32,9... | collective-permute-start | bytes 405512 | tf_op jit(solution)/shard_map/ppermute | solution.py:352
  32.8 5.1 %collective-permute-start.7 = (f32[264,128]{1,0:T(8,128)S(1)}, f32[264,128]{1,0:T(8,128)S(1)}, u32[]{:S(2)}, u32[]{:S(2)}) collective-permute-start(f32[264,128]{1,0:T(8,128)S(1)} %collective-permute-done.6.got_ref.rest_0_), channel_id=1, source_target_pairs={{0,4},{4,0},{8,12},{12,8},{16,20},{20,16},{24,28},{28,24},{32,36},... | collective-permute-start | bytes 405512 | tf_op jit(solution)/shard_map/ppermute | solution.py:352
  33.4 8.6 %collective-permute-start.9 = (f32[264,128]{1,0:T(8,128)S(1)}, f32[264,128]{1,0:T(8,128)S(1)}, u32[]{:S(2)}, u32[]{:S(2)}) collective-permute-start(f32[264,128]{1,0:T(8,128)S(1)} %shard_map.94.token_ref), channel_id=1, source_target_pairs={{0,132},{4,128},{8,140},{12,136},{16,148},{20,144},{24,156},{28,15... | collective-permute-start | bytes 405512 | tf_op jit(solution)/shard_map/ppermute | solution.py:352
  35.7 9.2 %collective-permute-start.10 = (f32[264,128]{1,0:T(8,128)S(1)}, f32[264,128]{1,0:T(8,128)S(1)}, u32[]{:S(2)}, u32[]{:S(2)}) collective-permute-start(f32[264,128]{1,0:T(8,128)S(1)} %shard_map.94.token_ref), channel_id=1, source_target_pairs={{0,196},{4,192},{8,204},{12,200},{16,212},{20,208},{24,220},{28,21... | collective-permute-start | bytes 405512 | tf_op jit(solution)/shard_map/ppermute | solution.py:352
  37.7 8.3 %collective-permute-start.11 = (f32[264,128]{1,0:T(8,128)S(1)}, f32[264,128]{1,0:T(8,128)S(1)}, u32[]{:S(2)}, u32[]{:S(2)}) collective-permute-start(f32[264,128]{1,0:T(8,128)S(1)} %collective-permute-done.8.near_ref), channel_id=1, source_target_pairs={{0,4},{4,0},{8,12},{12,8},{16,20},{20,16},{24,28},{28,24},{32,36},... | collective-permute-start | bytes 405512 | tf_op jit(solution)/shard_map/ppermute | solution.py:352
  45.0 1.7 %collective-permute-start.12 = (f32[264,128]{1,0:T(8,128)S(1)}, f32[264,128]{1,0:T(8,128)S(1)}, u32[]{:S(2)}, u32[]{:S(2)}) collective-permute-start(f32[264,128]{1,0:T(8,128)S(1)} %shard_map.97.far_ref), channel_id=1, source_target_pairs={{0,4},{4,0},{8,12},{12,8},{16,20},{20,16},{24,28},{28,24},{32,36},... | collective-permute-start | bytes 405512 | tf_op jit(solution)/shard_map/ppermute | solution.py:352
  47.0 4.8 %collective-permute-start.13 = (f32[1,512]{1,0:T(1,128)S(1)}, f32[1,512]{1,0:T(1,128)S(1)}, u32[]{:S(2)}, u32[]{:S(2)}) collective-permute-start(f32[1,512]{1,0:T(1,128)S(1)} %get-tuple-element.48.a_ref), channel_id=1, source_target_pairs={{0,2},{1,3},{2,0},{3,1},{4,6},{5,7},{6,4},{7,5},{8,10},{9,11},{10,... | collective-permute-start | bytes 6152 | tf_op jit(solution)/shard_map/ppermute | solution.py:352
  50.0 2.4 %collective-permute-start.14 = (f32[1,512]{1,0:T(1,128)S(1)}, f32[1,512]{1,0:T(1,128)S(1)}, u32[]{:S(2)}, u32[]{:S(2)}) collective-permute-start(f32[1,512]{1,0:T(1,128)S(1)} %get-tuple-element.48.a_ref), channel_id=1, source_target_pairs={{0,1},{1,0},{2,3},{3,2},{4,5},{5,4},{6,7},{7,6},{8,9},{9,8},{10,11... | collective-permute-start | bytes 6152 | tf_op jit(solution)/shard_map/ppermute | solution.py:352
  50.4 3.6 %collective-permute-start.15 = (f32[1,512]{1,0:T(1,128)S(1)}, f32[1,512]{1,0:T(1,128)S(1)}, u32[]{:S(2)}, u32[]{:S(2)}) collective-permute-start(f32[1,512]{1,0:T(1,128)S(1)} %get-tuple-element.48.a_ref), channel_id=1, source_target_pairs={{0,3},{1,2},{2,1},{3,0},{4,7},{5,6},{6,5},{7,4},{8,11},{9,10},{10,... | collective-permute-start | bytes 6152 | tf_op jit(solution)/shard_map/ppermute | solution.py:352
  50.8 0.7 %copy-start.5 = (f32[512]{0:T(512)S(1)}, f32[512]{0:T(512)}, u32[]{:S(2)}) copy-start(f32[512]{0:T(512)} %param.15) | copy-start | bytes 6148

commit v9 on v7

--- a/solution.py
+++ b/solution.py
@@ -73,7 +73,7 @@
     me = core_index()
     columns = lambda side: pl.ds(pl.multiple_of(side * ROWS, ROWS), ROWS)
     pairs = (
-        (v_hbm.at[:, columns(1 - me)], theirs_ref), (ld_hbm, ld_ref), (k_hbm, k_ref),
+        (ld_hbm, ld_ref), (v_hbm.at[:, columns(1 - me)], theirs_ref), (k_hbm, k_ref),
         (v_hbm.at[:, columns(me)], mine_ref),
     )
     copies = [pltpu.make_async_copy(a, b, sems.at[i]) for i, (a, b) in enumerate(pairs)]
@@ -82,7 +82,7 @@
     row = lax.broadcasted_iota(jnp.int32, (128, 128), 0)
     col = lax.broadcasted_iota(jnp.int32, (128, 128), 1)
     upto = (row <= col).astype(F32).astype(BF16)
-    copies[1].wait()
+    copies[0].wait()
     terms = []
     for j in range(4):
         ld = ld_ref[:, j * 128 : (j + 1) * 128]
@@ -105,7 +105,7 @@
         cols = slice(j * 128, (j + 1) * 128)
         d_ref[:, cols] = d[j]
         toend_ref[:, cols] = jnp.exp(total - d[j])
-    copies[0].wait()
+    copies[1].wait()
     copies[2].wait()
     product(theirs_ref[...], toend_ref, total, 1 - me, k_ref[...], send_ref)
     copies[3].wait()
@@ -375,11 +375,11 @@
     pair = merge(1, chip, z1, parts[0])
     levels.append((z1, swap(z1)))
     parts.append(close_by(2, pair))
-    acc, lead = step(0, jnp.zeros((HEADS, STATE), F32), levels[0])
     z3 = hop(pair, "tok", Z3)
-    quad = merge(2, pair, z3, parts[1], acc)
+    quad = merge(2, pair, z3, parts[1])
     levels.append((z3, swap(z3)))
     parts.append(close_by(4, quad))
+    acc, lead = step(0, jnp.zeros((HEADS, STATE), F32), levels[0])
     acc, lead = step(1, lead, levels[1], acc, parts[0])
     z7 = hop(quad, "tok", Z7)
     acc, lead = step(2, lead, levels[2], acc, parts[1])
@@ -390,11 +390,12 @@
     x2 = hop(line, "tok", X2)
     x1 = hop(line, "tok", X1)
     x3 = hop(line, "tok", X3)
+    fourth = swap(x1)
     beyond = merge(4, x2, x3, acc)
     other = swap(beyond)
     last = (qt, d, w, lead, acc, gt)
     near_half, part = close(4, 0, *last, x1, beyond)
-    rest, squares = close(4, 1, *last, swap(x1), other, part)
+    rest, squares = close(4, 1, *last, fourth, other, part)
     shares = [hop(squares, "head", 2), hop(squares, "head", 1), hop(squares, "head", 3)]
     turned = turn(near_half, rest, norm_gain[None])
     return finish(HEADS * WIDTH * lax.axis_size("head"), turned, [squares, *shares])

time: 54.9 us -> 54.8 us (level)
  starting transfers between devices: 24.6 us -> 24 us
  waiting for transfers between devices: 17 us -> 17.6 us
    ppermute x16, starting transfers between devices: 24.6 us -> 24 us  [hop(): return lax.ppermute(x, axis, [(i, i ^ flip) for i in range(count)])]
where the time goes in v9:
time: 54.8 us; the launch traced here: 54.7 us
  starting transfers between devices  24 us (44%)
  waiting for transfers between devices  17.6 us (32%)
  Pallas kernels  11.4 us (21%)
  local copies, waits for them, and re-layouts  1.41 us (3%)
    ppermute x16, starting transfers between devices, hop(): return lax.ppermute(x, axis, [(i, i ^ flip) for i in range(count)])  24 us
    ppermute x16, waiting for transfers between devices, hop(): return lax.ppermute(x, axis, [(i, i ^ flip) for i in range(count)])  17.6 us
    pallas_call x4, Pallas kernels, near(): call(functools.partial(near_body, first), sds((2 * WIDTH, BLOCK)), [VM] *...  5.54 us
    pallas_call x4, Pallas kernels, far(): call(functools.partial(far_body, level), [sds((BLOCK, BLOCK)), sds((HEADS...  1.42 us
    unnamed x12, local copies, waits for them, and re-layouts  1.41 us
    pallas_call x1, Pallas kernels, prep(): call(prep_body, outs, [HB] * 3, 10 ** 7, scratch=[pltpu.VMEM((HEADS, BLOC...  1.36 us
  transfers between devices with their start and end apart: 16, of which 9 were waited for; matrix products, arithmetic and copies ran while one was open for 0% of the time, Pallas kernels for 16%

profile of v9, /device:TPU:1, one launch (start us, length us, event | category | flops | bytes accessed | tf_op | source)
XLA Modules:
  0.0 54.7 jit_solution(1537335854302635789)
XLA Ops:
  0.0 0.0 copy-start.2
  0.0 1.4 %shard_map.82 = (f32[8,512]{1,0:T(8,128)S(1)}, f32[8,512]{1,0:T(8,128)S(1)}, f32[8,128]{1,0:T(8,128)S(1)}, f32[264,128]{1,0:T(8,128)S(1)}, bf16[512,256]{1,0:T(8,128)(2,1)S(1)}, /*index=5*/bf16[512,128]{1,0:T(8,128)(2,1)S(1)}) custom-call(f32[8,512]{1,0:T(8,128)} %bitcast.14, bf16[512,512]{1,0:T(8,128)(2,1)} %v_ref.1, bf16[512,128]{1,0:T(8,128)(2,1)} %k_hbm.1), custom_call_target="tpu_custom_call" | custom-call | flops 10000000 | bytes 1048576 | tf_op jit(solution)/shard_map/pallas_call | solution.py:117
  1.4 0.0 copy-start.1
  1.4 3.3 %collective-permute-start = (f32[264,128]{1,0:T(8,128)S(1)}, f32[264,128]{1,0:T(8,128)S(1)}, u32[]{:S(2)}, u32[]{:S(2)}) collective-permute-start(f32[264,128]{1,0:T(8,128)S(1)} %get-tuple-element.29), channel_id=1, source_target_pairs={{0,4},{4,0},{8,12},{12,8},{16,20},{20,16},{24,28},{28,24},{32,36},... | collective-permute-start | bytes 405512 | tf_op jit(solution)/shard_map/ppermute | solution.py:351
  4.7 0.3 shard_map.84.own_ref
  5.0 0.0 copy-start.3
  5.0 0.7 %collective-permute-done.rest_0_.got_ref = f32[264,128]{1,0:T(8,128)S(1)} collective-permute-done((f32[264,128]{1,0:T(8,128)S(1)}, f32[264,128]{1,0:T(8,128)S(1)}, u32[]{:S(2)}, u32[]{:S(2)}) %collective-permute-start) | collective-permute-done | bytes 135200 | tf_op jit(solution)/shard_map/ppermute | solution.py:351
  5.7 0.1 collective-permute-start.2
  5.8 0.0 copy-done.2
  5.8 0.0 copy-done.1
  5.8 0.0 copy-done.3
  5.9 0.0 copy-start
  5.9 0.6 %shard_map.83 = (bf16[256,512]{1,0:T(8,128)(2,1)S(1)}, f32[512,512]{1,0:T(8,128)S(1)}, f32[512,8]{1,0:T(8,128)S(1)}, bf16[512,512]{1,0:T(8,128)(2,1)S(1)}) custom-call(bf16[512,128]{1,0:T(8,128)(2,1)S(1)} %copy-done.3, bf16[512,512]{1,0:T(8,128)(2,1)S(1)} %copy-done.2, f32[8,512]{1,0:T(8,128)S(1)} %get-tuple-element.27.d_ref, bf16[512,512]{1,0:T(8,128)(2,1)S(1)} %copy-done.1), custom_call_target="tpu_custom_call" | custom-call | flops 10000000 | bytes 1048576 | tf_op jit(solution)/shard_map/pallas_call | solution.py:175
  6.5 0.0 copy-start.4
  6.5 0.4 copy-done
  6.8 0.3 copy-done.4
  7.1 1.4 %shard_map.87.rest_3_.refs_0_ = f32[128,512]{1,0:T(8,128)S(1)} custom-call(bf16[512,128]{1,0:T(8,128)(2,1)S(1)} %get-tuple-element.31.k_ref, bf16[256,512]{1,0:T(8,128)(2,1)S(1)} %get-tuple-element.28.qt_ref, bf16[512,512]{1,0:T(8,128)(2,1)S(1)} %get-tuple-element.36.vt_ref, f32[8,512]{1,0:T(8,128)S(1)} %get-tuple-element.27.d_ref, ...), custom_call_target="tpu_custom_call" | custom-call | flops 10000000 | bytes 1048576 | tf_op jit(solution)/shard_map/pallas_call | solution.py:219
  8.5 2.0 %collective-permute-done.2.rest_0_.got_ref = f32[264,128]{1,0:T(8,128)S(1)} collective-permute-done((f32[264,128]{1,0:T(8,128)S(1)}, f32[264,128]{1,0:T(8,128)S(1)}, u32[]{:S(2)}, u32[]{:S(2)}) %collective-permute-start.2) | collective-permute-done | bytes 135200 | tf_op jit(solution)/shard_map/ppermute | solution.py:351
  10.6 2.7 %collective-permute-start.4 = (f32[264,128]{1,0:T(8,128)S(1)}, f32[264,128]{1,0:T(8,128)S(1)}, u32[]{:S(2)}, u32[]{:S(2)}) collective-permute-start(f32[264,128]{1,0:T(8,128)S(1)} %shard_map.89.token_ref.own_ref), channel_id=1, source_target_pairs={{0,24},{4,28},{8,16},{12,20},{16,8},{20,12},{24,0},{28,4},{32,56},... | collective-permute-start | bytes 405512 | tf_op jit(solution)/shard_map/ppermute | solution.py:351
  13.3 1.5 %collective-permute-start.1 = (f32[264,128]{1,0:T(8,128)S(1)}, f32[264,128]{1,0:T(8,128)S(1)}, u32[]{:S(2)}, u32[]{:S(2)}) collective-permute-start(f32[264,128]{1,0:T(8,128)S(1)} %shard_map.84.own_ref), channel_id=1, source_target_pairs={{0,4},{4,0},{8,12},{12,8},{16,20},{20,16},{24,28},{28,24},{32,36},... | collective-permute-start | bytes 405512 | tf_op jit(solution)/shard_map/ppermute | solution.py:351
  14.8 0.0 collective-permute-start.3
  14.8 1.6 %collective-permute-done.4.rest_0_.got_ref = f32[264,128]{1,0:T(8,128)S(1)} collective-permute-done((f32[264,128]{1,0:T(8,128)S(1)}, f32[264,128]{1,0:T(8,128)S(1)}, u32[]{:S(2)}, u32[]{:S(2)}) %collective-permute-start.4) | collective-permute-done | bytes 135200 | tf_op jit(solution)/shard_map/ppermute | solution.py:351
  16.5 2.3 %collective-permute-start.5 = (f32[264,128]{1,0:T(8,128)S(1)}, f32[264,128]{1,0:T(8,128)S(1)}, u32[]{:S(2)}, u32[]{:S(2)}) collective-permute-start(f32[264,128]{1,0:T(8,128)S(1)} %collective-permute-done.4.rest_0_.got_ref), channel_id=1, source_target_pairs={{0,4},{4,0},{8,12},{12,8},{16,20},{20,16},{24,28},{28,24},{32,36},... | collective-permute-start | bytes 405512 | tf_op jit(solution)/shard_map/ppermute | solution.py:351
  18.7 1.4 %shard_map.90.rest_3_.refs_0_ = f32[128,512]{1,0:T(8,128)S(1)} custom-call(bf16[512,128]{1,0:T(8,128)(2,1)S(1)} %get-tuple-element.31.k_ref, bf16[256,512]{1,0:T(8,128)(2,1)S(1)} %get-tuple-element.28.qt_ref, bf16[512,512]{1,0:T(8,128)(2,1)S(1)} %get-tuple-element.36.vt_ref, f32[8,512]{1,0:T(8,128)S(1)} %get-tuple-element.27.d_ref, ...), custom_call_target="tpu_custom_call" | custom-call | flops 10000000 | bytes 1048576 | tf_op jit(solution)/shard_map/pallas_call | solution.py:219
  20.2 4.0 %collective-permute-start.6 = (f32[264,128]{1,0:T(8,128)S(1)}, f32[264,128]{1,0:T(8,128)S(1)}, u32[]{:S(2)}, u32[]{:S(2)}) collective-permute-start(f32[264,128]{1,0:T(8,128)S(1)} %shard_map.92.token_ref.own_ref), channel_id=1, source_target_pairs={{0,56},{4,60},{8,48},{12,52},{16,40},{20,44},{24,32},{28,36},{32,2... | collective-permute-start | bytes 405512 | tf_op jit(solution)/shard_map/ppermute | solution.py:351
  24.1 0.0 collective-permute-done.1.rest_1_
  24.1 0.3 shard_map.85
  24.4 1.4 %shard_map.93.refs_0_.rest_3_ = f32[128,512]{1,0:T(8,128)S(1)} custom-call(bf16[512,128]{1,0:T(8,128)(2,1)S(1)} %get-tuple-element.31.k_ref, bf16[256,512]{1,0:T(8,128)(2,1)S(1)} %get-tuple-element.28.qt_ref, bf16[512,512]{1,0:T(8,128)(2,1)S(1)} %get-tuple-element.36.vt_ref, f32[8,512]{1,0:T(8,128)S(1)} %get-tuple-element.27.d_ref, ...), custom_call_target="tpu_custom_call" | custom-call | flops 10000000 | bytes 1048576 | tf_op jit(solution)/shard_map/pallas_call | solution.py:219
  25.8 0.0 collective-permute-done.3.rest_1_
  25.8 0.4 shard_map.88
  26.2 0.0 collective-permute-done.5.rest_1_
  26.2 0.4 shard_map.91
  26.6 4.4 %collective-permute-done.6.got_ref.rest_0_ = f32[264,128]{1,0:T(8,128)S(1)} collective-permute-done((f32[264,128]{1,0:T(8,128)S(1)}, f32[264,128]{1,0:T(8,128)S(1)}, u32[]{:S(2)}, u32[]{:S(2)}) %collective-permute-start.6) | collective-permute-done | bytes 135200 | tf_op jit(solution)/shard_map/ppermute | solution.py:351
  31.0 1.3 %collective-permute-start.8 = (f32[264,128]{1,0:T(8,128)S(1)}, f32[264,128]{1,0:T(8,128)S(1)}, u32[]{:S(2)}, u32[]{:S(2)}) collective-permute-start(f32[264,128]{1,0:T(8,128)S(1)} %shard_map.94.token_ref), channel_id=1, source_target_pairs={{0,64},{4,68},{8,72},{12,76},{16,80},{20,84},{24,88},{28,92},{32,9... | collective-permute-start | bytes 405512 | tf_op jit(solution)/shard_map/ppermute | solution.py:351
  32.3 0.9 %collective-permute-start.7 = (f32[264,128]{1,0:T(8,128)S(1)}, f32[264,128]{1,0:T(8,128)S(1)}, u32[]{:S(2)}, u32[]{:S(2)}) collective-permute-start(f32[264,128]{1,0:T(8,128)S(1)} %collective-permute-done.6.got_ref.rest_0_), channel_id=1, source_target_pairs={{0,4},{4,0},{8,12},{12,8},{16,20},{20,16},{24,28},{28,24},{32,36},... | collective-permute-start | bytes 405512 | tf_op jit(solution)/shard_map/ppermute | solution.py:351
  33.2 2.4 %collective-permute-start.9 = (f32[264,128]{1,0:T(8,128)S(1)}, f32[264,128]{1,0:T(8,128)S(1)}, u32[]{:S(2)}, u32[]{:S(2)}) collective-permute-start(f32[264,128]{1,0:T(8,128)S(1)} %shard_map.94.token_ref), channel_id=1, source_target_pairs={{0,128},{4,132},{8,136},{12,140},{16,144},{20,148},{24,152},{28,15... | collective-permute-start | bytes 405512 | tf_op jit(solution)/shard_map/ppermute | solution.py:351
  35.6 0.2 collective-permute-start.10
  35.8 1.4 %shard_map.95.rest_4_ = f32[128,512]{1,0:T(8,128)S(1)} custom-call(bf16[512,128]{1,0:T(8,128)(2,1)S(1)} %get-tuple-element.31.k_ref, bf16[256,512]{1,0:T(8,128)(2,1)S(1)} %get-tuple-element.28.qt_ref, bf16[512,512]{1,0:T(8,128)(2,1)S(1)} %get-tuple-element.36.vt_ref, f32[8,512]{1,0:T(8,128)S(1)} %get-tuple-element.27.d_ref, ...), custom_call_target="tpu_custom_call" | custom-call | flops 10000000 | bytes 1048576 | tf_op jit(solution)/shard_map/pallas_call | solution.py:219
  37.2 0.0 collective-permute-done.8.near_ref
  37.2 0.7 %collective-permute-start.11 = (f32[264,128]{1,0:T(8,128)S(1)}, f32[264,128]{1,0:T(8,128)S(1)}, u32[]{:S(2)}, u32[]{:S(2)}) collective-permute-start(f32[264,128]{1,0:T(8,128)S(1)} %collective-permute-done.8.near_ref), channel_id=1, source_target_pairs={{0,4},{4,0},{8,12},{12,8},{16,20},{20,16},{24,28},{28,24},{32,36},... | collective-permute-start | bytes 405512 | tf_op jit(solution)/shard_map/ppermute | solution.py:351
  37.9 0.0 collective-permute-done.7.rest_1_
  37.9 0.4 shard_map.96
  38.2 2.5 %collective-permute-done.9.own_ref = f32[264,128]{1,0:T(8,128)S(1)} collective-permute-done((f32[264,128]{1,0:T(8,128)S(1)}, f32[264,128]{1,0:T(8,128)S(1)}, u32[]{:S(2)}, u32[]{:S(2)}) %collective-permute-start.9) | collective-permute-done | bytes 135200 | tf_op jit(solution)/shard_map/ppermute | solution.py:351
  40.7 3.4 %collective-permute-done.10.got_ref = f32[264,128]{1,0:T(8,128)S(1)} collective-permute-done((f32[264,128]{1,0:T(8,128)S(1)}, f32[264,128]{1,0:T(8,128)S(1)}, u32[]{:S(2)}, u32[]{:S(2)}) %collective-permute-start.10) | collective-permute-done | bytes 135200 | tf_op jit(solution)/shard_map/ppermute | solution.py:351
  44.2 1.0 %collective-permute-start.12 = (f32[264,128]{1,0:T(8,128)S(1)}, f32[264,128]{1,0:T(8,128)S(1)}, u32[]{:S(2)}, u32[]{:S(2)}) collective-permute-start(f32[264,128]{1,0:T(8,128)S(1)} %shard_map.97.far_ref), channel_id=1, source_target_pairs={{0,4},{4,0},{8,12},{12,8},{16,20},{20,16},{24,28},{28,24},{32,36},... | collective-permute-start | bytes 405512 | tf_op jit(solution)/shard_map/ppermute | solution.py:351
  45.2 0.4 shard_map.98
  45.6 0.0 collective-permute-done.11.near_ref
  45.6 0.6 %collective-permute-done.12.far_ref = f32[264,128]{1,0:T(8,128)S(1)} collective-permute-done((f32[264,128]{1,0:T(8,128)S(1)}, f32[264,128]{1,0:T(8,128)S(1)}, u32[]{:S(2)}, u32[]{:S(2)}) %collective-permute-start.12) | collective-permute-done | bytes 135200 | tf_op jit(solution)/shard_map/ppermute | solution.py:351
  46.2 0.4 shard_map.99
  46.6 3.0 %collective-permute-start.13 = (f32[1,512]{1,0:T(1,128)S(1)}, f32[1,512]{1,0:T(1,128)S(1)}, u32[]{:S(2)}, u32[]{:S(2)}) collective-permute-start(f32[1,512]{1,0:T(1,128)S(1)} %get-tuple-element.48.a_ref), channel_id=1, source_target_pairs={{0,2},{1,3},{2,0},{3,1},{4,6},{5,7},{6,4},{7,5},{8,10},{9,11},{10,... | collective-permute-start | bytes 6152 | tf_op jit(solution)/shard_map/ppermute | solution.py:351
  49.6 0.4 collective-permute-start.14
  50.0 0.4 collective-permute-start.15
  50.3 0.0 copy-start.5
  50.3 0.7 %copy-done.5 = f32[512]{0:T(512)S(1)} copy-done((f32[512]{0:T(512)S(1)}, f32[512]{0:T(512)}, u32[]{:S(2)}) %copy-start.5) | copy-done | bytes 2072
  51.0 0.3 shard_map.100.g_ref
  51.4 0.0 collective-permute-done.13.b_ref
  51.4 0.6 %collective-permute-done.14.c_ref = f32[1,512]{1,0:T(1,128)S(1)} collective-permute-done((f32[1,512]{1,0:T(1,128)S(1)}, f32[1,512]{1,0:T(1,128)S(1)}, u32[]{:S(2)}, u32[]{:S(2)}) %collective-permute-start.14) | collective-permute-done | bytes 2080 | tf_op jit(solution)/shard_map/ppermute | solution.py:351
  52.0 1.6 %collective-permute-done.15.e_ref = f32[1,512]{1,0:T(1,128)S(1)} collective-permute-done((f32[1,512]{1,0:T(1,128)S(1)}, f32[1,512]{1,0:T(1,128)S(1)}, u32[]{:S(2)}, u32[]{:S(2)}) %collective-permute-start.15) | collective-permute-done | bytes 2080 | tf_op jit(solution)/shard_map/ppermute | solution.py:351
  53.6 0.9 %shard_map.101 = bf16[512,512]{1,0:T(8,128)(2,1)} custom-call(f32[512,512]{1,0:T(8,128)S(1)} %shard_map.100.g_ref, f32[1,512]{1,0:T(1,128)S(1)} %get-tuple-element.48.a_ref, f32[1,512]{1,0:T(1,128)S(1)} %collective-permute-done.13.b_ref, f32[1,512]{1,0:T(1,128)S(1)} %collective-permute-done.14.c_ref, f32[1,512]{1,0:T(1,128)S(1)} %collective-permute-done.15.e_ref), custom_call_target="tpu_custom_call" | custom-call | flops 100000000 | bytes 1048576 | tf_op jit(solution)/shard_map/pallas_call | solution.py:342
  (6 shorter events, 0.2 us)
Async XLA Ops:
  0.0 5.8 %copy-start.2 = (bf16[512,512]{1,0:T(8,128)(2,1)S(1)}, bf16[512,512]{1,0:T(8,128)(2,1)}, u32[]{:S(2)}) copy-start(bf16[512,512]{1,0:T(8,128)(2,1)} %gate_ref.1) | copy-start | bytes 1572868
  1.4 4.4 %copy-start.1 = (bf16[512,512]{1,0:T(8,128)(2,1)S(1)}, bf16[512,512]{1,0:T(8,128)(2,1)}, u32[]{:S(2)}) copy-start(bf16[512,512]{1,0:T(8,128)(2,1)} %v_ref.1) | copy-start | bytes 1572868
  1.4 4.3 %collective-permute-start = (f32[264,128]{1,0:T(8,128)S(1)}, f32[264,128]{1,0:T(8,128)S(1)}, u32[]{:S(2)}, u32[]{:S(2)}) collective-permute-start(f32[264,128]{1,0:T(8,128)S(1)} %get-tuple-element.29), channel_id=1, source_target_pairs={{0,4},{4,0},{8,12},{12,8},{16,20},{20,16},{24,28},{28,24},{32,36},... | collective-permute-start | bytes 405512 | tf_op jit(solution)/shard_map/ppermute | solution.py:351
  5.0 0.9 %copy-start.3 = (bf16[512,128]{1,0:T(8,128)(2,1)S(1)}, bf16[512,128]{1,0:T(8,128)(2,1)}, u32[]{:S(2)}) copy-start(bf16[512,128]{1,0:T(8,128)(2,1)} %q_ref.1) | copy-start | bytes 393220
  5.7 4.9 %collective-permute-start.2 = (f32[264,128]{1,0:T(8,128)S(1)}, f32[264,128]{1,0:T(8,128)S(1)}, u32[]{:S(2)}, u32[]{:S(2)}) collective-permute-start(f32[264,128]{1,0:T(8,128)S(1)} %shard_map.86.token_ref.own_ref), channel_id=1, source_target_pairs={{0,8},{4,12},{8,0},{12,4},{16,24},{20,28},{24,16},{28,20},{32,40},... | collective-permute-start | bytes 405512 | tf_op jit(solution)/shard_map/ppermute | solution.py:351
  5.9 1.0 %copy-start = (f32[512,8,18]{0,1,2:T(8,128)S(1)}, f32[512,8,18]{0,1,2:T(8,128)}, u32[]{:S(2)}) copy-start(f32[512,8,18]{0,1,2:T(8,128)} %param.12) | copy-start | bytes 884740
  6.5 0.7 %copy-start.4 = (f32[8]{0:T(128)S(1)}, f32[8]{0:T(128)}, u32[]{:S(2)}) copy-start(f32[8]{0:T(128)} %skip_ref.7) | copy-start | bytes 100
  10.6 5.8 %collective-permute-start.4 = (f32[264,128]{1,0:T(8,128)S(1)}, f32[264,128]{1,0:T(8,128)S(1)}, u32[]{:S(2)}, u32[]{:S(2)}) collective-permute-start(f32[264,128]{1,0:T(8,128)S(1)} %shard_map.89.token_ref.own_ref), channel_id=1, source_target_pairs={{0,24},{4,28},{8,16},{12,20},{16,8},{20,12},{24,0},{28,4},{32,56},... | collective-permute-start | bytes 405512 | tf_op jit(solution)/shard_map/ppermute | solution.py:351
  13.3 10.8 %collective-permute-start.1 = (f32[264,128]{1,0:T(8,128)S(1)}, f32[264,128]{1,0:T(8,128)S(1)}, u32[]{:S(2)}, u32[]{:S(2)}) collective-permute-start(f32[264,128]{1,0:T(8,128)S(1)} %shard_map.84.own_ref), channel_id=1, source_target_pairs={{0,4},{4,0},{8,12},{12,8},{16,20},{20,16},{24,28},{28,24},{32,36},... | collective-permute-start | bytes 405512 | tf_op jit(solution)/shard_map/ppermute | solution.py:351
  14.8 11.0 %collective-permute-start.3 = (f32[264,128]{1,0:T(8,128)S(1)}, f32[264,128]{1,0:T(8,128)S(1)}, u32[]{:S(2)}, u32[]{:S(2)}) collective-permute-start(f32[264,128]{1,0:T(8,128)S(1)} %collective-permute-done.2.rest_0_.got_ref), channel_id=1, source_target_pairs={{0,4},{4,0},{8,12},{12,8},{16,20},{20,16},{24,28},{28,24},{32,36},... | collective-permute-start | bytes 405512 | tf_op jit(solution)/shard_map/ppermute | solution.py:351
  16.5 9.7 %collective-permute-start.5 = (f32[264,128]{1,0:T(8,128)S(1)}, f32[264,128]{1,0:T(8,128)S(1)}, u32[]{:S(2)}, u32[]{:S(2)}) collective-permute-start(f32[264,128]{1,0:T(8,128)S(1)} %collective-permute-done.4.rest_0_.got_ref), channel_id=1, source_target_pairs={{0,4},{4,0},{8,12},{12,8},{16,20},{20,16},{24,28},{28,24},{32,36},... | collective-permute-start | bytes 405512 | tf_op jit(solution)/shard_map/ppermute | solution.py:351
  20.2 10.8 %collective-permute-start.6 = (f32[264,128]{1,0:T(8,128)S(1)}, f32[264,128]{1,0:T(8,128)S(1)}, u32[]{:S(2)}, u32[]{:S(2)}) collective-permute-start(f32[264,128]{1,0:T(8,128)S(1)} %shard_map.92.token_ref.own_ref), channel_id=1, source_target_pairs={{0,56},{4,60},{8,48},{12,52},{16,40},{20,44},{24,32},{28,36},{32,2... | collective-permute-start | bytes 405512 | tf_op jit(solution)/shard_map/ppermute | solution.py:351
  31.0 6.2 %collective-permute-start.8 = (f32[264,128]{1,0:T(8,128)S(1)}, f32[264,128]{1,0:T(8,128)S(1)}, u32[]{:S(2)}, u32[]{:S(2)}) collective-permute-start(f32[264,128]{1,0:T(8,128)S(1)} %shard_map.94.token_ref), channel_id=1, source_target_pairs={{0,64},{4,68},{8,72},{12,76},{16,80},{20,84},{24,88},{28,92},{32,9... | collective-permute-start | bytes 405512 | tf_op jit(solution)/shard_map/ppermute | solution.py:351
  32.3 5.6 %collective-permute-start.7 = (f32[264,128]{1,0:T(8,128)S(1)}, f32[264,128]{1,0:T(8,128)S(1)}, u32[]{:S(2)}, u32[]{:S(2)}) collective-permute-start(f32[264,128]{1,0:T(8,128)S(1)} %collective-permute-done.6.got_ref.rest_0_), channel_id=1, source_target_pairs={{0,4},{4,0},{8,12},{12,8},{16,20},{20,16},{24,28},{28,24},{32,36},... | collective-permute-start | bytes 405512 | tf_op jit(solution)/shard_map/ppermute | solution.py:351
  33.2 7.6 %collective-permute-start.9 = (f32[264,128]{1,0:T(8,128)S(1)}, f32[264,128]{1,0:T(8,128)S(1)}, u32[]{:S(2)}, u32[]{:S(2)}) collective-permute-start(f32[264,128]{1,0:T(8,128)S(1)} %shard_map.94.token_ref), channel_id=1, source_target_pairs={{0,128},{4,132},{8,136},{12,140},{16,144},{20,148},{24,152},{28,15... | collective-permute-start | bytes 405512 | tf_op jit(solution)/shard_map/ppermute | solution.py:351
  35.6 8.6 %collective-permute-start.10 = (f32[264,128]{1,0:T(8,128)S(1)}, f32[264,128]{1,0:T(8,128)S(1)}, u32[]{:S(2)}, u32[]{:S(2)}) collective-permute-start(f32[264,128]{1,0:T(8,128)S(1)} %shard_map.94.token_ref), channel_id=1, source_target_pairs={{0,192},{4,196},{8,200},{12,204},{16,208},{20,212},{24,216},{28,22... | collective-permute-start | bytes 405512 | tf_op jit(solution)/shard_map/ppermute | solution.py:351
  37.2 8.4 %collective-permute-start.11 = (f32[264,128]{1,0:T(8,128)S(1)}, f32[264,128]{1,0:T(8,128)S(1)}, u32[]{:S(2)}, u32[]{:S(2)}) collective-permute-start(f32[264,128]{1,0:T(8,128)S(1)} %collective-permute-done.8.near_ref), channel_id=1, source_target_pairs={{0,4},{4,0},{8,12},{12,8},{16,20},{20,16},{24,28},{28,24},{32,36},... | collective-permute-start | bytes 405512 | tf_op jit(solution)/shard_map/ppermute | solution.py:351
  44.2 2.0 %collective-permute-start.12 = (f32[264,128]{1,0:T(8,128)S(1)}, f32[264,128]{1,0:T(8,128)S(1)}, u32[]{:S(2)}, u32[]{:S(2)}) collective-permute-start(f32[264,128]{1,0:T(8,128)S(1)} %shard_map.97.far_ref), channel_id=1, source_target_pairs={{0,4},{4,0},{8,12},{12,8},{16,20},{20,16},{24,28},{28,24},{32,36},... | collective-permute-start | bytes 405512 | tf_op jit(solution)/shard_map/ppermute | solution.py:351
  46.6 4.8 %collective-permute-start.13 = (f32[1,512]{1,0:T(1,128)S(1)}, f32[1,512]{1,0:T(1,128)S(1)}, u32[]{:S(2)}, u32[]{:S(2)}) collective-permute-start(f32[1,512]{1,0:T(1,128)S(1)} %get-tuple-element.48.a_ref), channel_id=1, source_target_pairs={{0,2},{1,3},{2,0},{3,1},{4,6},{5,7},{6,4},{7,5},{8,10},{9,11},{10,... | collective-permute-start | bytes 6152 | tf_op jit(solution)/shard_map/ppermute | solution.py:351
  49.6 2.4 %collective-permute-start.14 = (f32[1,512]{1,0:T(1,128)S(1)}, f32[1,512]{1,0:T(1,128)S(1)}, u32[]{:S(2)}, u32[]{:S(2)}) collective-permute-start(f32[1,512]{1,0:T(1,128)S(1)} %get-tuple-element.48.a_ref), channel_id=1, source_target_pairs={{0,1},{1,0},{2,3},{3,2},{4,5},{5,4},{6,7},{7,6},{8,9},{9,8},{10,11... | collective-permute-start | bytes 6152 | tf_op jit(solution)/shard_map/ppermute | solution.py:351
  50.0 3.6 %collective-permute-start.15 = (f32[1,512]{1,0:T(1,128)S(1)}, f32[1,512]{1,0:T(1,128)S(1)}, u32[]{:S(2)}, u32[]{:S(2)}) collective-permute-start(f32[1,512]{1,0:T(1,128)S(1)} %get-tuple-element.48.a_ref), channel_id=1, source_target_pairs={{0,3},{1,2},{2,1},{3,0},{4,7},{5,6},{6,5},{7,4},{8,11},{9,10},{10,... | collective-permute-start | bytes 6152 | tf_op jit(solution)/shard_map/ppermute | solution.py:351
  50.3 0.7 %copy-start.5 = (f32[512]{0:T(512)S(1)}, f32[512]{0:T(512)}, u32[]{:S(2)}) copy-start(f32[512]{0:T(512)} %param.15) | copy-start | bytes 6148
